TPU v7x, 32 devices: a whole 2x2x4 slice. The times are simulated.
32 devices in a mesh: fsdp: 4 (over x, core), ctx: 2 (over y), tp: 4 (over z).
Axes of the slice: x: 2, y: 2, z: 4, core: 2. Of those that a mesh axis runs over, the one named last changes fastest.
Arguments:
- features: bfloat16 [8, 24, 24, 768], P('fsdp', 'ctx'), may hold values from -6 to 6
- out_grad: float32 [8, 24, 24, 768], P('fsdp', 'ctx'), may hold values from -7 to 7
- regions: int32 [8, 24, 24], P('fsdp', 'ctx'), may hold values from 0 to 3
- rel_index: int32 [144, 144], replicated, may hold values from 0 to 528
- w_qkv: float32 [3, 768, 768], P(None, 'fsdp', 'tp'), may hold values from -0.21875 to 0.21875
- w_proj: float32 [768, 768], P('tp', 'fsdp'), may hold values from -0.875 to 0.875
- w_up: float32 [768, 3072], P('fsdp', 'tp'), may hold values from -0.21875 to 0.21875
- w_down: float32 [3072, 768], P('tp', 'fsdp'), may hold values from -0.109375 to 0.109375
- norm_vecs: float32 [6, 768], P(None, 'fsdp'), may hold values from -2.5 to 2.5
- head_bias: float32 [2, 24, 32], P(None, 'tp', 'fsdp'), may hold values from -3 to 3
- hidden_bias: float32 [96, 32], P('tp', 'fsdp'), may hold values from -3 to 3
- rel_table: float32 [529, 24], P(None, 'tp'), may hold values from -4 to 4
- row_qkv: float32 [3, 768], P(None, 'fsdp'), may hold values from 921.6 to 18432
- col_qkv: float32 [3, 768], P(None, 'tp'), may hold values from 921.6 to 18432
- row_proj: float32 [768], P('tp'), may hold values from 92.16 to 1843.2
- col_proj: float32 [768], P('fsdp'), may hold values from 92.16 to 1843.2
- row_up: float32 [768], P('fsdp'), may hold values from 138.24 to 2304
- col_up: float32 [3072], P('tp'), may hold values from 138.24 to 2304
- row_down: float32 [3072], P('tp'), may hold values from 460.8 to 6912
- col_down: float32 [768], P('fsdp'), may hold values from 460.8 to 6912
- state_norm: float32 [6, 768], P(None, 'fsdp'), may hold values from 230.4 to 23040
- state_heads: float32 [2, 24, 32], P(None, 'tp', 'fsdp'), may hold values from 921.6 to 18432
- state_hidden: float32 [96, 32], P('tp', 'fsdp'), may hold values from 138.24 to 2304
- state_table: float32 [529, 24], P(None, 'tp'), may hold values from 2.304 to 92.16
Outputs:
- block_out: float32 [8, 24, 24, 768], P('fsdp', 'ctx')
- grad_input: float32 [8, 24, 24, 768], P('fsdp', 'ctx')
- grad_qkv: float32 [3, 768, 768], P(None, 'fsdp', 'tp')
- grad_proj: float32 [768, 768], P('tp', 'fsdp')
- grad_up: float32 [768, 3072], P('fsdp', 'tp')
- grad_down: float32 [3072, 768], P('tp', 'fsdp')
- grad_norm: float32 [6, 768], P(None, 'fsdp')
- grad_heads: float32 [2, 24, 32], P(None, 'tp', 'fsdp')
- grad_hidden: float32 [96, 32], P('tp', 'fsdp')
- grad_table: float32 [529, 24], P(None, 'tp')
- new_qkv: float32 [3, 768, 768], P(None, 'fsdp', 'tp')
- new_proj: float32 [768, 768], P('tp', 'fsdp')
- new_up: float32 [768, 3072], P('fsdp', 'tp')
- new_down: float32 [3072, 768], P('tp', 'fsdp')
- new_norm: float32 [6, 768], P(None, 'fsdp')
- new_heads: float32 [2, 24, 32], P(None, 'tp', 'fsdp')
- new_hidden: float32 [96, 32], P('tp', 'fsdp')
- new_table: float32 [529, 24], P(None, 'tp')
- copy_qkv: bfloat16 [3, 768, 768], P(None, 'fsdp', 'tp')
- copy_proj: bfloat16 [768, 768], P('tp', 'fsdp')
- copy_up: bfloat16 [768, 3072], P('fsdp', 'tp')
- copy_down: bfloat16 [3072, 768], P('tp', 'fsdp')
- row_qkv_new: float32 [3, 768], P(None, 'fsdp')
- col_qkv_new: float32 [3, 768], P(None, 'tp')
- row_proj_new: float32 [768], P('tp')
- col_proj_new: float32 [768], P('fsdp')
- row_up_new: float32 [768], P('fsdp')
- col_up_new: float32 [3072], P('tp')
- row_down_new: float32 [3072], P('tp')
- col_down_new: float32 [768], P('fsdp')
- state_norm_new: float32 [6, 768], P(None, 'fsdp')
- state_heads_new: float32 [2, 24, 32], P(None, 'tp', 'fsdp')
- state_hidden_new: float32 [96, 32], P('tp', 'fsdp')
- state_table_new: float32 [529, 24], P(None, 'tp')
- clip_rms: float32 [], replicated
All inputs are finite; a program needn't handle non-finite values.
Results may differ from a plain program's by a relative error of at most 0.012.
The roundings to bfloat16 on the way count: a program that leaves them out, or rounds other values in their place, can miss the bound.
Values may be sent and summed in bfloat16 or wider, within the bound.
A program may use at most 128 MiB of HBM per device.

v0:
```python
import jax
import jax.numpy as jnp
from jax import lax
from jax.sharding import PartitionSpec as P

D = 768
HEADS = 24
HD = 32
FF = 3072
WIN = 12
SHIFT = 6
RELP = 529


DECAY_RATE = 0.5
STAT_EPS = 1e-06
NORM_EPS = 1e-05
MASK_FILL = -100.0
STEP_RATE = 1.0
CLIP_LEVEL = 0.25


def passed_along(x, axis, by):
    count = lax.axis_size(axis)
    return lax.ppermute(x, axis, [(i, (i + by) % count) for i in range(count)])


def layer_norm(values, gain_row, offset):
    mean_val = jnp.mean(values, axis=-1, keepdims=True)
    centred = values - mean_val
    var_val = jnp.mean(centred * centred, axis=-1, keepdims=True)
    return centred * lax.rsqrt(var_val + NORM_EPS) * gain_row + offset


def exact_gelu(values):
    return jax.nn.gelu(values, approximate=False)


def to_windows(values):
    image_count, row_count, col_count, channels = values.shape
    pieces = values.reshape(image_count, row_count // WIN, WIN, col_count // WIN, WIN, channels)
    return pieces.transpose(0, 1, 3, 2, 4, 5).reshape(-1, WIN * WIN, channels)


def from_windows(values, image_count, row_count, col_count):
    channels = values.shape[-1]
    pieces = values.reshape(image_count, row_count // WIN, col_count // WIN, WIN, WIN, channels)
    return pieces.transpose(0, 1, 3, 2, 4, 5).reshape(image_count, row_count, col_count, channels)


def enter_frame(own_rows, received):
    joined = jnp.concatenate([own_rows[:, SHIFT:], received], axis=1)
    return jnp.roll(joined, -SHIFT, axis=2)


def project_heads(normed_low, weights_qkv, bias_query, bias_value, head_shape):
    query_full = (
        jnp.dot(normed_low, weights_qkv[0], preferred_element_type=jnp.float32) + bias_query
    )
    key_full = jnp.dot(normed_low, weights_qkv[1], preferred_element_type=jnp.float32)
    value_full = (
        jnp.dot(normed_low, weights_qkv[2], preferred_element_type=jnp.float32) + bias_value
    )
    return tuple(
        (
            member.astype(jnp.bfloat16).reshape(head_shape)
            for member in (query_full, key_full, value_full)
        )
    )


def attention_scores(query_low, key_low, pos_bias, mask_add):
    products = jnp.einsum("wihc,wjhc->whij", query_low, key_low, preferred_element_type=jnp.float32)
    return products * query_low.shape[-1] ** (-0.5) + pos_bias[None] + mask_add[:, None]


def table_lookup(table_low, rel_index):
    win_tokens = rel_index.shape[0]
    code_ids = jnp.arange(table_low.shape[0], dtype=jnp.int32)
    index_blocks = rel_index.reshape(WIN, -1)

    def lookup(index_block):
        one_hot = (index_block[:, None] == code_ids[None, :]).astype(jnp.bfloat16)
        return jnp.dot(one_hot, table_low, preferred_element_type=jnp.float32)

    looked = lax.map(lookup, index_blocks)
    return looked.reshape(win_tokens, win_tokens, -1).transpose(2, 0, 1)


def table_grad(d_pos, rel_index, table_rows):
    heads_here = d_pos.shape[0]
    code_ids = jnp.arange(table_rows, dtype=jnp.int32)
    index_blocks = rel_index.reshape(WIN, -1)
    grad_blocks = d_pos.transpose(1, 2, 0).reshape(WIN, -1, heads_here)

    def accumulate(running, member):
        index_block, grad_block = member
        one_hot = (index_block[:, None] == code_ids[None, :]).astype(jnp.float32)
        added = lax.dot_general(
            one_hot,
            grad_block,
            (((0,), (0,)), ((), ())),
            precision=lax.Precision.HIGHEST,
            preferred_element_type=jnp.float32,
        )
        return (running + added, None)

    result_pair = lax.scan(
        accumulate, jnp.zeros((table_rows, heads_here), jnp.float32), (index_blocks, grad_blocks)
    )
    return result_pair[0]


def place(part_vec, index_at, whole_len):
    size_of = part_vec.shape[-1]
    base = jnp.zeros(part_vec.shape[:-1] + (whole_len,), jnp.float32)
    return lax.dynamic_update_slice_in_dim(base, part_vec, index_at * size_of, part_vec.ndim - 1)


def own_part(whole_vec, index_at, size_of):
    return lax.dynamic_slice_in_dim(whole_vec, index_at * size_of, size_of, whole_vec.ndim - 1)


def factored(grad, row_local, col_local, row_mean):
    return grad * lax.rsqrt(row_local[..., :, None] * col_local[..., None, :] / row_mean)


def plain_stats(grad, state_old):
    state_new = DECAY_RATE * state_old + (1.0 - DECAY_RATE) * (grad * grad + STAT_EPS)
    return (state_new, grad * lax.rsqrt(state_new))


def shard_sum(grad_list):
    return (
        lax.psum_scatter(grad_list[0], "fsdp", scatter_dimension=1, tiled=True),
        lax.psum_scatter(grad_list[1], "fsdp", scatter_dimension=1, tiled=True),
        lax.psum_scatter(grad_list[2], "fsdp", scatter_dimension=0, tiled=True),
        lax.psum_scatter(grad_list[3], "fsdp", scatter_dimension=1, tiled=True),
        lax.psum_scatter(grad_list[4], "fsdp", scatter_dimension=1, tiled=True),
        lax.psum_scatter(grad_list[5], "fsdp", scatter_dimension=2, tiled=True),
        lax.psum_scatter(grad_list[6], "fsdp", scatter_dimension=1, tiled=True),
    )


def band_sum(grad_list):
    return lax.psum(
        (
            grad_list[0],
            grad_list[1],
            grad_list[2],
            grad_list[3],
            grad_list[4],
            grad_list[5],
            grad_list[6],
        ),
        "ctx",
    )


def per_device(
    features,
    out_grad,
    regions,
    rel_index,
    w_qkv,
    w_proj,
    w_up,
    w_down,
    norm_vecs,
    head_bias,
    hidden_bias,
    rel_table,
    row_qkv,
    col_qkv,
    row_proj,
    col_proj,
    row_up,
    col_up,
    row_down,
    col_down,
    state_norm,
    state_heads,
    state_hidden,
    state_table,
):
    images, band_rows, across, model_width = features.shape
    win_tokens = WIN * WIN
    fsdp_at = lax.axis_index("fsdp")
    ctx_at = lax.axis_index("ctx")
    tp_at = lax.axis_index("tp")
    first_fsdp = (fsdp_at == 0).astype(jnp.float32)
    first_ctx = (ctx_at == 0).astype(jnp.float32)
    first_tp = (tp_at == 0).astype(jnp.float32)
    weights_qkv, weights_proj, weights_up, weights_down, vec_copy, head_copy, hidden_copy = (
        lax.all_gather(w_qkv.astype(jnp.bfloat16), "fsdp", axis=1, tiled=True),
        lax.all_gather(w_proj.astype(jnp.bfloat16), "fsdp", axis=1, tiled=True),
        lax.all_gather(w_up.astype(jnp.bfloat16), "fsdp", axis=0, tiled=True),
        lax.all_gather(w_down.astype(jnp.bfloat16), "fsdp", axis=1, tiled=True),
        lax.all_gather(norm_vecs.astype(jnp.bfloat16), "fsdp", axis=1, tiled=True),
        lax.all_gather(head_bias.astype(jnp.bfloat16), "fsdp", axis=2, tiled=True),
        lax.all_gather(hidden_bias.astype(jnp.bfloat16), "fsdp", axis=1, tiled=True),
    )
    norm_rows = vec_copy.astype(jnp.float32)
    bias_query = head_copy[0].reshape(-1).astype(jnp.float32)
    bias_value = head_copy[1].reshape(-1).astype(jnp.float32)
    bias_hidden = hidden_copy.reshape(-1).astype(jnp.float32)
    table_copy = rel_table.astype(jnp.bfloat16)
    local_width = weights_qkv.shape[2]
    heads_here = local_width // HD
    upper_rows = passed_along(features[:, :SHIFT], "ctx", -1)
    rolled = enter_frame(features, upper_rows).astype(jnp.float32)
    windows = to_windows(rolled)
    win_count = windows.shape[0]
    flat_one = windows.reshape(-1, model_width)
    normed_one, pull_one = jax.vjp(layer_norm, flat_one, norm_rows[0], norm_rows[1])
    normed_one_low = normed_one.astype(jnp.bfloat16)
    head_shape = (win_count, win_tokens, heads_here, HD)
    query_low, key_low, value_low = project_heads(
        normed_one_low, weights_qkv, bias_query, bias_value, head_shape
    )
    pos_bias = table_lookup(table_copy, rel_index)
    region_win = to_windows(regions[..., None])[..., 0]
    mask_add = jnp.where(region_win[:, :, None] == region_win[:, None, :], 0.0, MASK_FILL).astype(
        jnp.float32
    )
    scores = attention_scores(query_low, key_low, pos_bias, mask_add)
    top_score = jnp.max(scores, axis=-1, keepdims=True)
    lifted = jnp.exp(scores - top_score)
    totals = jnp.sum(lifted, axis=-1, keepdims=True)
    log_total = top_score + jnp.log(totals)
    prob_low = (lifted / totals).astype(jnp.bfloat16)
    context = jnp.einsum("whij,wjhc->wihc", prob_low, value_low, preferred_element_type=jnp.float32)
    context_low = context.astype(jnp.bfloat16).reshape(-1, local_width)
    branch_part = jnp.dot(context_low, weights_proj, preferred_element_type=jnp.float32)
    branch_whole = lax.psum(branch_part, "tp")
    branch_band = jnp.roll(
        from_windows(
            branch_whole.reshape(win_count, win_tokens, model_width), images, band_rows, across
        ),
        SHIFT,
        axis=2,
    )
    lower_rows = passed_along(branch_band[:, band_rows - SHIFT :], "ctx", 1)
    branch_home = jnp.concatenate([lower_rows, branch_band[:, : band_rows - SHIFT]], axis=1)
    resid = features.astype(jnp.float32) + branch_home + norm_rows[2]
    flat_two = resid.reshape(-1, model_width)
    normed_two, pull_two = jax.vjp(layer_norm, flat_two, norm_rows[3], norm_rows[4])
    normed_two_low = normed_two.astype(jnp.bfloat16)
    pre_act = jnp.dot(normed_two_low, weights_up, preferred_element_type=jnp.float32) + bias_hidden
    hidden, pull_gelu = jax.vjp(exact_gelu, pre_act)
    hidden_low = hidden.astype(jnp.bfloat16)
    mixed_part = jnp.dot(hidden_low, weights_down, preferred_element_type=jnp.float32)
    mixed_whole = lax.psum(mixed_part.astype(jnp.bfloat16), "tp").astype(jnp.float32)
    block_out = (flat_two + mixed_whole + norm_rows[5]).reshape(features.shape)
    grad_flat = out_grad.reshape(-1, model_width)
    grad_low = grad_flat.astype(jnp.bfloat16)
    grad_down_full = jnp.einsum(
        "tf,td->fd", hidden_low, grad_low, preferred_element_type=jnp.float32
    )
    grad_down_bias = jnp.sum(grad_flat, axis=0)
    d_hidden = jnp.einsum("td,fd->tf", grad_low, weights_down, preferred_element_type=jnp.float32)
    d_pre = pull_gelu(d_hidden)[0]
    d_pre_low = d_pre.astype(jnp.bfloat16)
    grad_hidden_bias = jnp.sum(d_pre, axis=0)
    grad_up_full = jnp.einsum(
        "td,tf->df", normed_two_low, d_pre_low, preferred_element_type=jnp.float32
    )
    d_two_part = jnp.einsum("tf,df->td", d_pre_low, weights_up, preferred_element_type=jnp.float32)
    d_two = lax.psum(d_two_part, "tp")
    d_flat_two, grad_gain_two, grad_offset_two = pull_two(d_two)
    d_resid = grad_flat + d_flat_two
    grad_proj_bias = jnp.sum(d_resid, axis=0)
    d_resid_low = d_resid.astype(jnp.bfloat16).reshape(features.shape)
    upper_grads = passed_along(d_resid_low[:, :SHIFT], "ctx", -1)
    d_branch = to_windows(enter_frame(d_resid_low, upper_grads)).reshape(-1, model_width)
    grad_proj_full = jnp.einsum(
        "tc,td->cd", context_low, d_branch, preferred_element_type=jnp.float32
    )
    d_context = (
        jnp.einsum("td,cd->tc", d_branch, weights_proj, preferred_element_type=jnp.float32)
        .astype(jnp.bfloat16)
        .reshape(head_shape)
    )
    query_use, key_use, value_use = (query_low, key_low, value_low)
    scores_again = attention_scores(query_use, key_use, pos_bias, mask_add)
    prob_rows = jnp.exp(scores_again - log_total)
    prob_again_low = prob_rows.astype(jnp.bfloat16)
    d_probs = jnp.einsum(
        "wihc,wjhc->whij", d_context, value_use, preferred_element_type=jnp.float32
    )
    d_value_low = jnp.einsum(
        "whij,wihc->wjhc", prob_again_low, d_context, preferred_element_type=jnp.float32
    ).astype(jnp.bfloat16)
    d_scores = prob_rows * (d_probs - jnp.sum(prob_rows * d_probs, axis=-1, keepdims=True))
    d_pos = jnp.sum(d_scores, axis=0)
    d_scaled = (d_scores * HD ** (-0.5)).astype(jnp.bfloat16)
    d_query_low = jnp.einsum(
        "whij,wjhc->wihc", d_scaled, key_use, preferred_element_type=jnp.float32
    ).astype(jnp.bfloat16)
    d_key_low = jnp.einsum(
        "whij,wihc->wjhc", d_scaled, query_use, preferred_element_type=jnp.float32
    ).astype(jnp.bfloat16)
    d_heads = jnp.stack([d_query_low, d_key_low, d_value_low]).reshape(3, -1, local_width)
    grad_qkv_full = jnp.einsum(
        "td,ktc->kdc", normed_one_low, d_heads, preferred_element_type=jnp.float32
    )
    grad_head_bias = jnp.stack(
        [
            jnp.sum(d_heads[0].astype(jnp.float32), axis=0),
            jnp.sum(d_heads[2].astype(jnp.float32), axis=0),
        ]
    ).reshape(2, heads_here, HD)
    d_one_part = jnp.einsum("ktc,kdc->td", d_heads, weights_qkv, preferred_element_type=jnp.float32)
    d_one = lax.psum(d_one_part, "tp")
    d_flat_one, grad_gain_one, grad_offset_one = pull_one(d_one)
    d_rolled = jnp.roll(
        from_windows(
            d_flat_one.reshape(win_count, win_tokens, model_width), images, band_rows, across
        ),
        SHIFT,
        axis=2,
    )
    lower_grads = passed_along(
        d_rolled[:, band_rows - SHIFT :].astype(jnp.bfloat16), "ctx", 1
    ).astype(jnp.float32)
    grad_input = d_resid.reshape(features.shape) + jnp.concatenate(
        [lower_grads, d_rolled[:, : band_rows - SHIFT]], axis=1
    )
    table_part = table_grad(d_pos, rel_index, rel_table.shape[0])
    grad_norm_full = jnp.stack(
        [
            grad_gain_one,
            grad_offset_one,
            grad_proj_bias,
            grad_gain_two,
            grad_offset_two,
            grad_down_bias,
        ]
    )
    grad_list = (
        grad_qkv_full,
        grad_proj_full,
        grad_up_full,
        grad_down_full,
        grad_norm_full,
        grad_head_bias,
        grad_hidden_bias.reshape(-1, HD),
    )
    g_qkv, g_proj, g_up, g_down, g_norm, g_heads, g_hidden = shard_sum(band_sum(grad_list))
    d_shard = w_qkv.shape[1]
    hidden_here = w_up.shape[1]
    keep = 1.0 - DECAY_RATE
    sq_qkv = g_qkv * g_qkv
    sq_proj = g_proj * g_proj
    sq_up = g_up * g_up
    sq_down = g_down * g_down
    stat_rq = place(
        (keep * jnp.sum(sq_qkv, axis=2) / D + first_tp * (DECAY_RATE * row_qkv + keep * STAT_EPS))
        * first_ctx,
        fsdp_at,
        D,
    )
    stat_cq = place(
        (keep * jnp.sum(sq_qkv, axis=1) / D + first_fsdp * (DECAY_RATE * col_qkv + keep * STAT_EPS))
        * first_ctx,
        tp_at,
        D,
    )
    stat_rp = place(
        (
            keep * jnp.sum(sq_proj, axis=1) / D
            + first_fsdp * (DECAY_RATE * row_proj + keep * STAT_EPS)
        )
        * first_ctx,
        tp_at,
        D,
    )
    stat_cp = place(
        (keep * jnp.sum(sq_proj, axis=0) / D + first_tp * (DECAY_RATE * col_proj + keep * STAT_EPS))
        * first_ctx,
        fsdp_at,
        D,
    )
    stat_ru = place(
        (keep * jnp.sum(sq_up, axis=1) / FF + first_tp * (DECAY_RATE * row_up + keep * STAT_EPS))
        * first_ctx,
        fsdp_at,
        D,
    )
    stat_cu = place(
        (keep * jnp.sum(sq_up, axis=0) / D + first_fsdp * (DECAY_RATE * col_up + keep * STAT_EPS))
        * first_ctx,
        tp_at,
        FF,
    )
    stat_rd = place(
        (
            keep * jnp.sum(sq_down, axis=1) / D
            + first_fsdp * (DECAY_RATE * row_down + keep * STAT_EPS)
        )
        * first_ctx,
        tp_at,
        FF,
    )
    stat_cd = place(
        (
            keep * jnp.sum(sq_down, axis=0) / FF
            + first_tp * (DECAY_RATE * col_down + keep * STAT_EPS)
        )
        * first_ctx,
        fsdp_at,
        D,
    )
    table_whole = place(table_part, tp_at, HEADS)
    master_sq = jnp.concatenate(
        [
            jnp.stack(
                [
                    jnp.sum(w_qkv * w_qkv),
                    jnp.sum(w_proj * w_proj),
                    jnp.sum(w_up * w_up),
                    jnp.sum(w_down * w_down),
                ]
            )
            * first_ctx,
            jnp.sum(norm_vecs * norm_vecs, axis=1) * first_ctx * first_tp,
            jnp.sum(head_bias * head_bias, axis=(1, 2)) * first_ctx,
            jnp.sum(hidden_bias * hidden_bias)[None] * first_ctx,
            jnp.sum(rel_table * rel_table)[None] * first_ctx * first_fsdp,
        ]
    )
    (
        full_rq,
        full_cq,
        full_rp,
        full_cp,
        full_ru,
        full_cu,
        full_rd,
        full_cd,
        table_sum,
        master_total,
    ) = lax.psum(
        (
            stat_rq,
            stat_cq,
            stat_rp,
            stat_cp,
            stat_ru,
            stat_cu,
            stat_rd,
            stat_cd,
            table_whole,
            master_sq,
        ),
        ("fsdp", "ctx", "tp"),
    )
    u_qkv = factored(
        g_qkv,
        own_part(full_rq, fsdp_at, d_shard),
        own_part(full_cq, tp_at, local_width),
        jnp.mean(full_rq, axis=1)[:, None, None],
    )
    u_proj = factored(
        g_proj,
        own_part(full_rp, tp_at, local_width),
        own_part(full_cp, fsdp_at, d_shard),
        jnp.mean(full_rp),
    )
    u_up = factored(
        g_up,
        own_part(full_ru, fsdp_at, d_shard),
        own_part(full_cu, tp_at, hidden_here),
        jnp.mean(full_ru),
    )
    u_down = factored(
        g_down,
        own_part(full_rd, tp_at, hidden_here),
        own_part(full_cd, fsdp_at, d_shard),
        jnp.mean(full_rd),
    )
    g_table = own_part(table_sum, tp_at, heads_here)
    state_norm_new, u_norm = plain_stats(g_norm, state_norm)
    state_heads_new, u_heads = plain_stats(g_heads, state_heads)
    state_hidden_new, u_hidden = plain_stats(g_hidden, state_hidden)
    state_table_new, u_table = plain_stats(g_table, state_table)
    local_sq = (
        jnp.sum(u_qkv * u_qkv)
        + jnp.sum(u_proj * u_proj)
        + jnp.sum(u_up * u_up)
        + jnp.sum(u_down * u_down)
        + jnp.sum(u_heads * u_heads)
        + jnp.sum(u_hidden * u_hidden)
        + first_tp * jnp.sum(u_norm * u_norm)
        + first_fsdp * jnp.sum(u_table * u_table)
    )
    total_sq = lax.psum(local_sq, ("fsdp", "tp"))
    count_all = 4 * D * D + 2 * D * FF + 8 * D + FF + RELP * HEADS
    clip_rms = jnp.sqrt(total_sq / count_all)
    factor = 1.0 / jnp.maximum(1.0, clip_rms / CLIP_LEVEL)
    counts = jnp.array(
        [3 * D * D, D * D, D * FF, FF * D, D, D, D, D, D, D, D, D, FF, RELP * HEADS], jnp.float32
    )
    scales = jnp.sqrt(master_total / counts + STAT_EPS)
    new_qkv = w_qkv - STEP_RATE * scales[0] * factor * u_qkv
    new_proj = w_proj - STEP_RATE * scales[1] * factor * u_proj
    new_up = w_up - STEP_RATE * scales[2] * factor * u_up
    new_down = w_down - STEP_RATE * scales[3] * factor * u_down
    new_norm = norm_vecs - STEP_RATE * scales[4:10][:, None] * factor * u_norm
    new_heads = head_bias - STEP_RATE * scales[10:12][:, None, None] * factor * u_heads
    new_hidden = hidden_bias - STEP_RATE * scales[12] * factor * u_hidden
    new_table = rel_table - STEP_RATE * scales[13] * factor * u_table
    return (
        block_out,
        grad_input,
        g_qkv,
        g_proj,
        g_up,
        g_down,
        g_norm,
        g_heads,
        g_hidden,
        g_table,
        new_qkv,
        new_proj,
        new_up,
        new_down,
        new_norm,
        new_heads,
        new_hidden,
        new_table,
        new_qkv.astype(jnp.bfloat16),
        new_proj.astype(jnp.bfloat16),
        new_up.astype(jnp.bfloat16),
        new_down.astype(jnp.bfloat16),
        own_part(full_rq, fsdp_at, d_shard),
        own_part(full_cq, tp_at, local_width),
        own_part(full_rp, tp_at, local_width),
        own_part(full_cp, fsdp_at, d_shard),
        own_part(full_ru, fsdp_at, d_shard),
        own_part(full_cu, tp_at, hidden_here),
        own_part(full_rd, tp_at, hidden_here),
        own_part(full_cd, fsdp_at, d_shard),
        state_norm_new,
        state_heads_new,
        state_hidden_new,
        state_table_new,
        clip_rms,
    )


def solution(mesh):
    return jax.shard_map(
        per_device,
        mesh=mesh,
        in_specs=(
            P("fsdp", "ctx", None, None),
            P("fsdp", "ctx", None, None),
            P("fsdp", "ctx", None),
            P(),
            P(None, "fsdp", "tp"),
            P("tp", "fsdp"),
            P("fsdp", "tp"),
            P("tp", "fsdp"),
            P(None, "fsdp"),
            P(None, "tp", "fsdp"),
            P("tp", "fsdp"),
            P(None, "tp"),
            P(None, "fsdp"),
            P(None, "tp"),
            P("tp"),
            P("fsdp"),
            P("fsdp"),
            P("tp"),
            P("tp"),
            P("fsdp"),
            P(None, "fsdp"),
            P(None, "tp", "fsdp"),
            P("tp", "fsdp"),
            P(None, "tp"),
        ),
        out_specs=(
            P("fsdp", "ctx", None, None),
            P("fsdp", "ctx", None, None),
            P(None, "fsdp", "tp"),
            P("tp", "fsdp"),
            P("fsdp", "tp"),
            P("tp", "fsdp"),
            P(None, "fsdp"),
            P(None, "tp", "fsdp"),
            P("tp", "fsdp"),
            P(None, "tp"),
            P(None, "fsdp", "tp"),
            P("tp", "fsdp"),
            P("fsdp", "tp"),
            P("tp", "fsdp"),
            P(None, "fsdp"),
            P(None, "tp", "fsdp"),
            P("tp", "fsdp"),
            P(None, "tp"),
            P(None, "fsdp", "tp"),
            P("tp", "fsdp"),
            P("fsdp", "tp"),
            P("tp", "fsdp"),
            P(None, "fsdp"),
            P(None, "tp"),
            P("tp"),
            P("fsdp"),
            P("fsdp"),
            P("tp"),
            P("tp"),
            P("fsdp"),
            P(None, "fsdp"),
            P(None, "tp", "fsdp"),
            P("tp", "fsdp"),
            P(None, "tp"),
            P(),
        ),
        check_vma=False,
    )
```

profile of v0, /device:TPU:0, one launch (start us, length us, event | category | flops | bytes accessed | tf_op | source)
XLA Modules:
  0.0 811.6 jit_solution(13820860892265158173)
XLA Ops:
  15.2 5.2 all_gather.23
  20.4 5.2 all-gather
  28.9 30.6 %while.22 = (s32[]{:T(128)}, f32[12,1728,6]{1,0,2:T(8,128)S(1)}, s32[12,1728]{1,0:T(8,128)S(1)}, bf16[529,6]{0,1:T(8,128)(2,1)S(1)}, s32[]{:T(128)}, /*index=5*/s32[]{:T(128)}) while((s32[]{:T(128)}, f32[12,1728,6]{1,0,2:T(8,128)S(1)}, s32[12,1728]{1,0:T(8,128)S(1)}, bf16[529,6]{0,1:T(8,128)(2,1)S(1)}, s32[]{:T(128)}, ...), condition=%wide.region_3.4_spmd.clone, body=%wide.region_2.3_spmd.clone.sunk | while | flops 11883458 | bytes 234529 | solution.py:86
  61.9 7.0 all_gather.24
  68.9 11.0 %all_gather.22 = bf16[3,768,192]{2,1,0:T(8,128)(2,1)S(1)} all-gather(bf16[3,192,192]{2,1,0:T(8,128)(2,1)S(1)} %get-tuple-element.433), channel_id=1, replica_groups=mesh['fsdp'=4,'ctx'=2,'tp'=4] {'fsdp'}, dimensions={1}, use_global_device_ids=true | all-gather | bytes 1105920 | tf_op jit(solution)/shard_map/all_gather | solution.py:195
  111.1 72.7 %all-reduce.13.cloned.1.call-done = f32[2,12,24,768]{3,2,1,0:T(8,128)} async-done(((f32[2,12,24,768]{3,2,1,0:T(8,128)}), f32[2,12,24,768]{3,2,1,0:T(8,128)}) %all-reduce.13.cloned.1.call-update) | async-done | bytes 1769488 | tf_op jit(solution)/shard_map/psum | solution.py:235
  190.9 5.2 all_gather.26
  196.8 3.3 fusion.97
  200.1 7.8 collective-permute-done.1
  217.6 3.9 fusion.84
  221.6 8.6 %fusion.91 = (f32[768]{0:T(1024)}, bf16[576,768]{1,0:T(8,128)(2,1)S(1)}, f32[576,768]{1,0:T(8,128)}) fusion(f32[576,768]{1,0:T(8,128)} %fusion.84, f32[768]{0:T(1024)S(1)} %copy-done.77, bf16[576,768]{1,0:T(8,128)(2,1)} %get-tuple-element.427, bf16[768,768]{0,1:T(8,128)(2,1)} %all-gather.6.cloned.1.call-done), kind=kOutput, calls=%fused_computation.227 | convolution fusion | flops 712211712 | bytes 6494208 | tf_op jit(solution)/shard_map/td,fd->tf/dot_general | solution.py:261
  237.9 71.3 %all-reduce.17.cloned.1.call-done = f32[576,768]{1,0:T(8,128)} async-done(((f32[576,768]{1,0:T(8,128)}), f32[576,768]{1,0:T(8,128)}) %all-reduce.17.cloned.1.call-update) | async-done | bytes 1769488 | tf_op jit(solution)/shard_map/psum | solution.py:269
  322.9 6.2 collective-permute-done.2
  340.1 3.6 fusion.69
  345.8 5.4 fusion.41
  359.3 6.0 convert_reduce_fusion.1
  373.1 3.4 convolution_bitcast_fusion
  381.6 3.4 copy.338
  391.3 3.9 convolution_bitcast_fusion.1
  395.2 4.3 copy.363
  399.5 4.7 reshape.441
  404.3 4.0 fusion.107
  426.7 4.4 fusion.64
  431.2 3.3 fusion.24
  440.7 11.1 %all-reduce.3 = (f32[2,6,32]{2,1,0:T(8,128)S(1)}, f32[24,32]{1,0:T(8,128)S(1)}) all-reduce(f32[2,6,32]{2,1,0:T(8,128)S(1)} %pad_maximum_fusion.4, f32[24,32]{1,0:T(8,128)S(1)} %copy-done.50), channel_id=7, replica_groups=mesh['fsdp'=4,'ctx'=2,'tp'=4] {'fsdp'}, use_global_device_ids=true, to_apply=%region_36.37.clone | all-reduce | flops 1152 | bytes 9216
  452.4 29.3 %while.23 = (s32[]{:T(128)}, f32[529,6]{0,1:T(8,128)S(1)}, s32[12,1728]{1,0:T(8,128)}, f32[12,1728,6]{1,0,2:T(8,128)S(1)}, s32[]{:T(128)}, /*index=5*/s32[]{:T(128)}) while((s32[]{:T(128)}, f32[529,6]{0,1:T(8,128)S(1)}, s32[12,1728]{1,0:T(8,128)}, f32[12,1728,6]{1,0,2:T(8,128)S(1)}, s32[]{:T(128)}, /*index=5*/s32[]{:T(128)}) %tuple.138), condition=%wide.region_42.43_spmd.clone, body=%wide.region_41.42_spmd.clone.sunk | while | flops 66736528 | bytes 170639 | solution.py:108
  493.0 13.6 %reduce-scatter.14.cloned.1.call-done = f32[192,768]{1,0:T(8,128)} async-done(((f32[768,768]{1,0:T(8,128)}), f32[192,768]{1,0:T(8,128)}) %reduce-scatter.14.cloned.1.call-update) | async-done | bytes 589840 | tf_op jit(solution)/shard_map/reduce_scatter | solution.py:137
  516.7 13.7 %reduce-scatter.22.cloned.1.call-done = f32[192,6]{1,0:T(8,128)} async-done(((f32[768,6]{1,0:T(8,128)}), f32[192,6]{1,0:T(8,128)}) %reduce-scatter.22.cloned.1.call-update) | async-done | bytes 4624
  531.3 10.6 %all-reduce.4 = (f32[6,192]{1,0:T(8,128)S(1)}, f32[2,6,8]{2,1,0:T(8,128)S(1)}, f32[24,8]{1,0:T(8,128)S(1)}) all-reduce(f32[6,192]{1,0:T(8,128)S(1)} %copy.368, f32[2,6,8]{2,1,0:T(8,128)S(1)} %copy-done.64, f32[24,8]{1,0:T(8,128)S(1)} %copy-done.49), channel_id=1, replica_groups=mesh['fsdp'=4,'ctx'=2,'tp'=4] {'ctx'}, use_global_device_ids=true, to_apply=%region_31.32 | all-reduce | flops 1440 | bytes 11520 | tf_op jit(solution)/shard_map/psum | solution.py:146
  550.0 27.2 %all-reduce.23.cloned.1.call-done = (f32[3,192,192]{1,2,0:T(8,128)}, f32[192,192]{1,0:T(8,128)}, f32[192,768]{1,0:T(8,128)}, f32[768,192]{0,1:T(8,128)}) async-done(((f32[3,192,192]{1,2,0:T(8,128)}, f32[192,192]{1,0:T(8,128)}, f32[192,768]{1,0:T(8,128)}, f32[768,192]{0,1:T(8,128)}), (f32[3,192,192]{1,2,0:T(8,128)}, f32[192,192]{1,0:T(8,128)}, f32[192,768]{1,0:T(8,128)}, ...) | async-done | bytes 1769488 | tf_op jit(solution)/shard_map/psum | solution.py:146
  604.9 124.4 %all-reduce.21.cloned.1.call-done = (f32[529,24]{0,1:T(8,128)}, f32[14]{0:T(128)}, f32[3,768]{1,0:T(4,128)}, f32[3,768]{1,0:T(4,128)}, f32[768]{0:T(1024)}, /*in...) async-done(((f32[529,24]{0,1:T(8,128)}, f32[14]{0:T(128)}, f32[3,768]{1,0:T(4,128)}, f32[3,768]{1,0:T(4,128)}, f32[768]{0:T(1024)}, ...) | async-done | bytes 106152 | tf_op jit(solution)/shard_map/psum | solution.py:443
  752.8 31.7 %psum.175 = f32[]{:T(128)} all-reduce(f32[]{:T(128)S(6)} %add.427), channel_id=1, replica_groups=mesh['fsdp'=4,'ctx'=2,'tp'=4] {'fsdp','tp'}, use_global_device_ids=true, to_apply=%region_81.82 | all-reduce | flops 1 | bytes 8 | tf_op jit(solution)/shard_map/psum | solution.py:497
  (538 shorter events, 292.6 us)
Async XLA Ops:
  8.1 175.6 %all-reduce.13.cloned.1.call-start = ((), (), s32[]{:S(2)}) async-start(), calls=%async_computation.5 | async-start | bytes 3538944 | tf_op jit(solution)/shard_map/psum | solution.py:235
  10.3 69.7 %collective-permute-start = (bf16[2,6,24,768]{3,2,1,0:T(8,128)(2,1)}, bf16[2,6,24,768]{3,2,1,0:T(8,128)(2,1)S(1)}, u32[]{:S(2)}, u32[]{:S(2)}) collective-permute-start(bf16[2,6,24,768]{3,2,1,0:T(8,128)(2,1)} %get-tuple-element.431), channel_id=1, source_target_pairs={{0,4},{4,0},{1,5},{5,1},{2,6},{6,2},{3,7},{7,3},{8,12},{12,8},{9,1... | collective-permute-start | bytes 1327112 | tf_op jit(solution)/shard_map/ppermute | solution.py:25
  107.8 109.8 %all-gather.4.cloned.1.call-start = ((), (), s32[]{:S(2)}) async-start(), calls=%async_computation.6 | async-start | bytes 1474560 | tf_op jit(solution)/shard_map/all_gather | solution.py:197
  111.0 110.6 %all-gather.6.cloned.1.call-start = ((), (), s32[]{:S(2)}) async-start(), calls=%async_computation.7 | async-start | bytes 1474560 | tf_op jit(solution)/shard_map/all_gather | solution.py:198
  187.3 20.5 %collective-permute-start.1 = (f32[2,6,24,768]{3,2,1,0:T(8,128)}, f32[2,6,24,768]{3,2,1,0:T(8,128)}, u32[]{:S(2)}, u32[]{:S(2)}) collective-permute-start(f32[2,6,24,768]{3,2,1,0:T(8,128)} %fusion.48), channel_id=1, source_target_pairs={{0,4},{4,0},{1,5},{5,1},{2,6},{6,2},{3,7},{7,3},{8,12},{12,8},{9,1... | collective-permute-start | bytes 2654216 | tf_op jit(solution)/shard_map/ppermute | solution.py:25
  190.2 119.0 %all-reduce.17.cloned.1.call-start = ((), (), s32[]{:S(2)}) async-start(), calls=%async_computation.9 | async-start | bytes 3538944 | tf_op jit(solution)/shard_map/psum | solution.py:269
  214.7 99.0 %copy-start.63 = (f32[576]{0:T(1024)}, f32[576]{0:T(1024)S(1)}, u32[]{:S(2)}) copy-start(f32[576]{0:T(1024)S(1)} %rsqrt.48) | copy-start | bytes 6916
  233.3 197.9 %all-reduce.15.cloned.1.call-start = ((), (), s32[]{:S(2)}) async-start(), calls=%async_computation.8 | async-start | bytes 1769472 | tf_op jit(solution)/shard_map/psum | solution.py:253
  237.9 74.4 %copy-start.61 = (f32[576]{0:T(1024)S(1)}, f32[576]{0:T(1024)}, u32[]{:S(2)}) copy-start(f32[576]{0:T(1024)} %add.372) | copy-start | bytes 6916
  318.0 11.1 %collective-permute-start.2 = (bf16[2,6,24,768]{3,0,2,1:T(2,128)(2,1)}, bf16[2,6,24,768]{3,0,2,1:T(2,128)(2,1)}, u32[]{:S(2)}, u32[]{:S(2)}) collective-permute-start(bf16[2,6,24,768]{3,0,2,1:T(2,128)(2,1)} %copy.381), channel_id=1, source_target_pairs={{0,4},{4,0},{1,5},{5,1},{2,6},{6,2},{3,7},{7,3},{8,12},{12,8},{9,1... | collective-permute-start | bytes 1327112 | tf_op jit(solution)/shard_map/ppermute | solution.py:25
  321.3 160.4 %all-reduce.19.cloned.1.call-start = ((), (), s32[]{:S(2)}) async-start(), calls=%async_computation.10 | async-start | bytes 3538944 | tf_op jit(solution)/shard_map/psum | solution.py:314
  376.6 110.1 %reduce-scatter.20.cloned.1.call-start = ((), (), s32[]{:S(2)}) async-start(), calls=%async_computation.14 | async-start | bytes 983040
  379.4 109.0 %reduce-scatter.18.cloned.1.call-start = ((), (), s32[]{:S(2)}) async-start(), calls=%async_computation.13 | async-start | bytes 2457600
  404.2 88.8 %reduce-scatter.16.cloned.1.call-start = ((), (), s32[]{:S(2)}) async-start(), calls=%async_computation.12 | async-start | bytes 2949120 | tf_op jit(solution)/shard_map/reduce_scatter | solution.py:138
  408.3 98.3 %reduce-scatter.14.cloned.1.call-start = ((), (), s32[]{:S(2)}) async-start(), calls=%async_computation.11 | async-start | bytes 2949120 | tf_op jit(solution)/shard_map/reduce_scatter | solution.py:137
  431.1 99.3 %reduce-scatter.22.cloned.1.call-start = ((), (), s32[]{:S(2)}) async-start(), calls=%async_computation.15 | async-start | bytes 491520
  485.7 91.5 %all-reduce.23.cloned.1.call-start = ((), (), s32[]{:S(2)}) async-start(), calls=%async_computation.17 | async-start | bytes 3932160 | tf_op jit(solution)/shard_map/psum | solution.py:146
  506.7 222.7 %all-reduce.21.cloned.1.call-start = ((), (), s32[]{:S(2)}) async-start(), calls=%async_computation.16 | async-start | bytes 254976 | tf_op jit(solution)/shard_map/psum | solution.py:443
  515.2 32.4 %collective-permute-start.3 = (bf16[2,6,24,768]{3,0,2,1:T(2,128)(2,1)}, bf16[2,6,24,768]{3,0,2,1:T(2,128)(2,1)}, u32[]{:S(2)}, u32[]{:S(2)}) collective-permute-start(bf16[2,6,24,768]{3,0,2,1:T(2,128)(2,1)} %fusion.55), channel_id=1, source_target_pairs={{0,4},{4,0},{1,5},{5,1},{2,6},{6,2},{3,7},{7,3},{8,12},{12,8},{9,1... | collective-permute-start | bytes 1327112 | tf_op jit(solution)/shard_map/ppermute | solution.py:25
  602.4 139.7 %copy-start.75 = (f32[529,6]{0,1:T(8,128)S(1)}, f32[529,6]{0,1:T(8,128)}, u32[]{:S(2)}) copy-start(f32[529,6]{0,1:T(8,128)} %param.52) | copy-start | bytes 38092
  602.4 141.8 %copy-start.99 = (f32[14]{0:T(128)S(1)}, f32[14]{0:T(128)}, u32[]{:S(2)}) copy-start(f32[14]{0:T(128)} %constant.199) | copy-start | bytes 172
  602.5 142.4 %copy-start.19 = (f32[192,192]{1,0:T(8,128)S(1)}, f32[192,192]{1,0:T(8,128)}, u32[]{:S(2)}) copy-start(f32[192,192]{1,0:T(8,128)} %get-tuple-element.560) | copy-start | bytes 442372
  603.8 143.9 %copy-start.10 = (f32[192,768]{1,0:T(8,128)S(1)}, f32[192,768]{1,0:T(8,128)}, u32[]{:S(2)}) copy-start(f32[192,768]{1,0:T(8,128)} %get-tuple-element.561) | copy-start | bytes 1769476
  603.8 145.5 %copy-start.9 = (f32[768,192]{0,1:T(8,128)S(1)}, f32[768,192]{0,1:T(8,128)}, u32[]{:S(2)}) copy-start(f32[768,192]{0,1:T(8,128)} %get-tuple-element.562) | copy-start | bytes 1769476
  603.8 185.5 %copy-start.38 = (f32[24,8]{1,0:T(8,128)S(1)}, f32[24,8]{1,0:T(8,128)}, u32[]{:S(2)}) copy-start(f32[24,8]{1,0:T(8,128)} %copy-done.37) | copy-start | bytes 2308
  603.8 185.5 %copy-start.51 = (f32[24,8]{1,0:T(8,128)S(1)}, f32[24,8]{1,0:T(8,128)}, u32[]{:S(2)}) copy-start(f32[24,8]{1,0:T(8,128)} %copy.348) | copy-start | bytes 2308
  603.8 186.1 %copy-start.45 = (f32[2,6,8]{2,1,0:T(8,128)S(1)}, f32[2,6,8]{2,1,0:T(8,128)}, u32[]{:S(2)}) copy-start(f32[2,6,8]{2,1,0:T(8,128)} %copy-done.44) | copy-start | bytes 1156
  603.8 186.1 %copy-start.71 = (f32[2,6,8]{2,0,1:T(2,128)S(1)}, f32[2,6,8]{2,0,1:T(2,128)}, u32[]{:S(2)}) copy-start(f32[2,6,8]{2,0,1:T(2,128)} %param.38) | copy-start | bytes 1156
  603.9 186.1 %copy-start.73 = (f32[2,6,8]{2,0,1:T(2,128)S(1)}, f32[2,6,8]{2,0,1:T(2,128)}, u32[]{:S(2)}) copy-start(f32[2,6,8]{2,0,1:T(2,128)} %param.50) | copy-start | bytes 1156
  603.9 186.8 %copy-start.23 = (f32[3,192,192]{1,2,0:T(8,128)S(1)}, f32[3,192,192]{1,2,0:T(8,128)}, u32[]{:S(2)}) copy-start(f32[3,192,192]{1,2,0:T(8,128)} %copy.346) | copy-start | bytes 1327108
  730.1 67.7 %copy-start.56 = (f32[768]{0:T(1024)}, f32[768]{0:T(1024)S(1)}, u32[]{:S(2)}) copy-start(f32[768]{0:T(1024)S(1)} %dynamic_slice.53) | copy-start | bytes 9220
  732.2 64.5 %copy-start.90 = (f32[192]{0:T(256)}, f32[192]{0:T(256)S(1)}, u32[]{:S(2)}) copy-start(f32[192]{0:T(256)S(1)} %dynamic_slice.51) | copy-start | bytes 2308
  (86 other events, 1189.5 us)
Sparse Core Ops, SparseCore 0:
  108.0 75.7 all-reduce.12
  233.4 75.7 all-reduce.16
  321.4 44.8 all-reduce.14
  376.7 75.6 all-reduce.18
  506.8 70.3 all-reduce.22
  599.9 129.3 all-reduce.20
Sparse Core Ops, SparseCore 1:
  111.1 17.6 all-gather.3
  190.3 15.4 all-gather.5
  379.6 23.3 reduce-scatter.19
  405.6 30.4 reduce-scatter.17
  438.6 32.7 reduce-scatter.15
  473.9 32.7 reduce-scatter.13
  509.6 20.7 reduce-scatter.21
where the time goes:
time: 819 us; the launch traced here: 812 us
  waiting for transfers between devices  337 us (41%)
  local copies, waits for them, and re-layouts  157 us (19%)
  other arithmetic  96.3 us (12%)
  matrix products  91.7 us (11%)
  blocking collectives  86.9 us (11%)
  between operations  32.3 us (4%)
  starting transfers between devices  9.02 us (1%)
    psum x1, waiting for transfers between devices, per_device(): lax.psum((stat_rq, stat_cq, stat_rp, stat_cp, stat_ru, stat_cu, stat_rd,...  124 us
    psum x1, waiting for transfers between devices, per_device(): branch_whole = lax.psum(branch_part, 'tp')  72.7 us
    psum x1, waiting for transfers between devices, per_device(): d_two = lax.psum(d_two_part, 'tp')  71.3 us
    unnamed x235, local copies, waits for them, and re-layouts  45.5 us
    psum x1, blocking collectives, per_device(): total_sq = lax.psum(local_sq, ('fsdp', 'tp'))  31.7 us
    psum x1, waiting for transfers between devices, band_sum(): lax.psum((grad_list[0], grad_list[1], grad_list[2], grad_list[3], grad_li...  27.2 us
    dynamic_update_slice x24, local copies, waits for them, and re-layouts, table_lookup(): looked = lax.map(lookup, index_blocks)  18.4 us
    dot_general x12, matrix products, accumulate(): lax.dot_general(one_hot, grad_block, (((0,), (0,)), ((), ())), precision=...  18.3 us
  transfers between devices with their start and end apart: 17, of which 8 were waited for; matrix products, arithmetic and copies ran while one was open for 30% of the time, Pallas kernels for 0%

commit v1 on v0

--- a/solution.py
+++ b/solution.py
@@ -207,11 +207,25 @@
     table_copy = rel_table.astype(jnp.bfloat16)
     local_width = weights_qkv.shape[2]
     heads_here = local_width // HD
-    upper_rows = passed_along(features[:, :SHIFT], "ctx", -1)
-    rolled = enter_frame(features, upper_rows).astype(jnp.float32)
-    windows = to_windows(rolled)
-    win_count = windows.shape[0]
-    flat_one = windows.reshape(-1, model_width)
+
+    def roll_in(home):
+        received = passed_along(home[:, :SHIFT], "ctx", -1)
+        return to_windows(enter_frame(home, received)).reshape(-1, model_width)
+
+    def roll_out(rolled_flat):
+        band = jnp.roll(
+            from_windows(
+                rolled_flat.reshape(-1, win_tokens, model_width), images, band_rows, across
+            ),
+            SHIFT,
+            axis=2,
+        )
+        lower = passed_along(band[:, band_rows - SHIFT :], "ctx", 1)
+        return jnp.concatenate([lower, band[:, : band_rows - SHIFT]], axis=1)
+
+    flat_one = roll_in(features).astype(jnp.float32)
+    grad_flat = roll_in(out_grad)
+    win_count = flat_one.shape[0] // win_tokens
     normed_one, pull_one = jax.vjp(layer_norm, flat_one, norm_rows[0], norm_rows[1])
     normed_one_low = normed_one.astype(jnp.bfloat16)
     head_shape = (win_count, win_tokens, heads_here, HD)
@@ -226,24 +240,13 @@
     scores = attention_scores(query_low, key_low, pos_bias, mask_add)
     top_score = jnp.max(scores, axis=-1, keepdims=True)
     lifted = jnp.exp(scores - top_score)
-    totals = jnp.sum(lifted, axis=-1, keepdims=True)
-    log_total = top_score + jnp.log(totals)
-    prob_low = (lifted / totals).astype(jnp.bfloat16)
+    prob_rows = lifted / jnp.sum(lifted, axis=-1, keepdims=True)
+    prob_low = prob_rows.astype(jnp.bfloat16)
     context = jnp.einsum("whij,wjhc->wihc", prob_low, value_low, preferred_element_type=jnp.float32)
     context_low = context.astype(jnp.bfloat16).reshape(-1, local_width)
     branch_part = jnp.dot(context_low, weights_proj, preferred_element_type=jnp.float32)
-    branch_whole = lax.psum(branch_part, "tp")
-    branch_band = jnp.roll(
-        from_windows(
-            branch_whole.reshape(win_count, win_tokens, model_width), images, band_rows, across
-        ),
-        SHIFT,
-        axis=2,
-    )
-    lower_rows = passed_along(branch_band[:, band_rows - SHIFT :], "ctx", 1)
-    branch_home = jnp.concatenate([lower_rows, branch_band[:, : band_rows - SHIFT]], axis=1)
-    resid = features.astype(jnp.float32) + branch_home + norm_rows[2]
-    flat_two = resid.reshape(-1, model_width)
+    branch = lax.psum(branch_part.astype(jnp.bfloat16), "tp").astype(jnp.float32) + norm_rows[2]
+    flat_two = flat_one + branch
     normed_two, pull_two = jax.vjp(layer_norm, flat_two, norm_rows[3], norm_rows[4])
     normed_two_low = normed_two.astype(jnp.bfloat16)
     pre_act = jnp.dot(normed_two_low, weights_up, preferred_element_type=jnp.float32) + bias_hidden
@@ -251,8 +254,9 @@
     hidden_low = hidden.astype(jnp.bfloat16)
     mixed_part = jnp.dot(hidden_low, weights_down, preferred_element_type=jnp.float32)
     mixed_whole = lax.psum(mixed_part.astype(jnp.bfloat16), "tp").astype(jnp.float32)
-    block_out = (flat_two + mixed_whole + norm_rows[5]).reshape(features.shape)
-    grad_flat = out_grad.reshape(-1, model_width)
+    block_out = features.astype(jnp.float32) + roll_out(
+        (branch + mixed_whole + norm_rows[5]).astype(jnp.bfloat16)
+    ).astype(jnp.float32)
     grad_low = grad_flat.astype(jnp.bfloat16)
     grad_down_full = jnp.einsum(
         "tf,td->fd", hidden_low, grad_low, preferred_element_type=jnp.float32
@@ -266,13 +270,11 @@
         "td,tf->df", normed_two_low, d_pre_low, preferred_element_type=jnp.float32
     )
     d_two_part = jnp.einsum("tf,df->td", d_pre_low, weights_up, preferred_element_type=jnp.float32)
-    d_two = lax.psum(d_two_part, "tp")
+    d_two = lax.psum(d_two_part.astype(jnp.bfloat16), "tp").astype(jnp.float32)
     d_flat_two, grad_gain_two, grad_offset_two = pull_two(d_two)
     d_resid = grad_flat + d_flat_two
     grad_proj_bias = jnp.sum(d_resid, axis=0)
-    d_resid_low = d_resid.astype(jnp.bfloat16).reshape(features.shape)
-    upper_grads = passed_along(d_resid_low[:, :SHIFT], "ctx", -1)
-    d_branch = to_windows(enter_frame(d_resid_low, upper_grads)).reshape(-1, model_width)
+    d_branch = d_resid.astype(jnp.bfloat16)
     grad_proj_full = jnp.einsum(
         "tc,td->cd", context_low, d_branch, preferred_element_type=jnp.float32
     )
@@ -281,24 +283,20 @@
         .astype(jnp.bfloat16)
         .reshape(head_shape)
     )
-    query_use, key_use, value_use = (query_low, key_low, value_low)
-    scores_again = attention_scores(query_use, key_use, pos_bias, mask_add)
-    prob_rows = jnp.exp(scores_again - log_total)
-    prob_again_low = prob_rows.astype(jnp.bfloat16)
     d_probs = jnp.einsum(
-        "wihc,wjhc->whij", d_context, value_use, preferred_element_type=jnp.float32
+        "wihc,wjhc->whij", d_context, value_low, preferred_element_type=jnp.float32
     )
     d_value_low = jnp.einsum(
-        "whij,wihc->wjhc", prob_again_low, d_context, preferred_element_type=jnp.float32
+        "whij,wihc->wjhc", prob_low, d_context, preferred_element_type=jnp.float32
     ).astype(jnp.bfloat16)
     d_scores = prob_rows * (d_probs - jnp.sum(prob_rows * d_probs, axis=-1, keepdims=True))
     d_pos = jnp.sum(d_scores, axis=0)
     d_scaled = (d_scores * HD ** (-0.5)).astype(jnp.bfloat16)
     d_query_low = jnp.einsum(
-        "whij,wjhc->wihc", d_scaled, key_use, preferred_element_type=jnp.float32
+        "whij,wjhc->wihc", d_scaled, key_low, preferred_element_type=jnp.float32
     ).astype(jnp.bfloat16)
     d_key_low = jnp.einsum(
-        "whij,wihc->wjhc", d_scaled, query_use, preferred_element_type=jnp.float32
+        "whij,wihc->wjhc", d_scaled, query_low, preferred_element_type=jnp.float32
     ).astype(jnp.bfloat16)
     d_heads = jnp.stack([d_query_low, d_key_low, d_value_low]).reshape(3, -1, local_width)
     grad_qkv_full = jnp.einsum(
@@ -311,20 +309,10 @@
         ]
     ).reshape(2, heads_here, HD)
     d_one_part = jnp.einsum("ktc,kdc->td", d_heads, weights_qkv, preferred_element_type=jnp.float32)
-    d_one = lax.psum(d_one_part, "tp")
+    d_one = lax.psum(d_one_part.astype(jnp.bfloat16), "tp").astype(jnp.float32)
     d_flat_one, grad_gain_one, grad_offset_one = pull_one(d_one)
-    d_rolled = jnp.roll(
-        from_windows(
-            d_flat_one.reshape(win_count, win_tokens, model_width), images, band_rows, across
-        ),
-        SHIFT,
-        axis=2,
-    )
-    lower_grads = passed_along(
-        d_rolled[:, band_rows - SHIFT :].astype(jnp.bfloat16), "ctx", 1
-    ).astype(jnp.float32)
-    grad_input = d_resid.reshape(features.shape) + jnp.concatenate(
-        [lower_grads, d_rolled[:, : band_rows - SHIFT]], axis=1
+    grad_input = out_grad + roll_out((d_flat_two + d_flat_one).astype(jnp.bfloat16)).astype(
+        jnp.float32
     )
     table_part = table_grad(d_pos, rel_index, rel_table.shape[0])
     grad_norm_full = jnp.stack(

time: 819 us -> 784 us (0.957)
  waiting for transfers between devices: 337 us -> 272 us
  blocking collectives: 86.9 us -> 112 us
  matrix products: 91.7 us -> 116 us
  other arithmetic: 96.3 us -> 74.7 us
    psum x3 -> x2, waiting for transfers between devices: 144 us -> 55.8 us  [the longest x1 42.2 us: per_device(): d_two = lax.psum(d_two_part.astype(jnp.bfloat16), 'tp').astype(jnp.float32)]
    psum x1, waiting for transfers between devices: 0.02 us -> 65.7 us  [per_device(): lax.psum(mixed_part.astype(jnp.bfloat16), 'tp').astype(jnp.float32)]
    psum x1, blocking collectives: 10.6 us -> 35.6 us  [band_sum(): lax.psum((grad_list[0], grad_list[1], grad_list[2], grad_list[3], grad_li...]
    dot_general x12, matrix products: 18.3 us -> 33.8 us  [accumulate(): lax.dot_general(one_hot, grad_block, (((0,), (0,)), ((), ())), precision=...]
    unnamed x16 -> x15, waiting for transfers between devices: 13.9 us -> 0.23 us
    reduce_scatter x1, waiting for transfers between devices: 13.6 us -> 0.01 us  [shard_sum(): lax.psum_scatter(grad_list[2], 'fsdp', scatter_dimension=0, tiled=True)]
    dynamic_slice x12, local copies, waits for them, and re-layouts: 0.49 us -> 12.2 us  [table_grad(): lax.scan(accumulate, jnp.zeros((table_rows, heads_here), jnp.float32), (i...]
    psum x1, waiting for transfers between devices: 27.2 us -> 17.9 us  [band_sum(): lax.psum((grad_list[0], grad_list[1], grad_list[2], grad_list[3], grad_li...]
  transfers between devices with their start and end apart: 17 -> 16, of which waited for: 8 -> 6; matrix products, arithmetic and copies ran while one was open for 30% -> 30% of each run, Pallas kernels for 0% -> 0%
where the time goes in v1:
time: 784 us; the launch traced here: 776 us
  waiting for transfers between devices  272 us (35%)
  local copies, waits for them, and re-layouts  162 us (21%)
  matrix products  116 us (15%)
  blocking collectives  112 us (14%)
  other arithmetic  74.7 us (10%)
  between operations  31.7 us (4%)
    psum x1, waiting for transfers between devices, per_device(): lax.psum((stat_rq, stat_cq, stat_rp, stat_cp, stat_ru, stat_cu, stat_rd,...  125 us
    psum x1, waiting for transfers between devices, per_device(): lax.psum(mixed_part.astype(jnp.bfloat16), 'tp').astype(jnp.float32)  65.7 us
    unnamed x230, local copies, waits for them, and re-layouts  49 us
    psum x1, waiting for transfers between devices, per_device(): d_two = lax.psum(d_two_part.astype(jnp.bfloat16), 'tp').astype(jnp.float32)  42.2 us
    psum x1, blocking collectives, band_sum(): lax.psum((grad_list[0], grad_list[1], grad_list[2], grad_list[3], grad_li...  35.6 us
    dot_general x12, matrix products, accumulate(): lax.dot_general(one_hot, grad_block, (((0,), (0,)), ((), ())), precision=...  33.8 us
    psum x1, blocking collectives, per_device(): total_sq = lax.psum(local_sq, ('fsdp', 'tp'))  31.7 us
    dynamic_update_slice x24, local copies, waits for them, and re-layouts, table_lookup(): looked = lax.map(lookup, index_blocks)  18.4 us
  transfers between devices with their start and end apart: 16, of which 6 were waited for; matrix products, arithmetic and copies ran while one was open for 30% of the time, Pallas kernels for 0%

profile of v1, /device:TPU:0, one launch (start us, length us, event | category | flops | bytes accessed | tf_op | source)
XLA Modules:
  0.0 775.9 jit_solution(9777298492413612432)
XLA Ops:
  15.3 5.2 all_gather.23
  20.5 5.2 all-gather
  29.0 30.6 %while.22 = (s32[]{:T(128)}, f32[12,1728,6]{1,0,2:T(8,128)S(1)}, s32[12,1728]{1,0:T(8,128)S(1)}, bf16[529,6]{0,1:T(8,128)(2,1)S(1)}, s32[]{:T(128)}, /*index=5*/s32[]{:T(128)}) while((s32[]{:T(128)}, f32[12,1728,6]{1,0,2:T(8,128)S(1)}, s32[12,1728]{1,0:T(8,128)S(1)}, bf16[529,6]{0,1:T(8,128)(2,1)S(1)}, s32[]{:T(128)}, ...), condition=%wide.region_3.4_spmd.clone, body=%wide.region_2.3_spmd.clone.sunk | while | flops 11883458 | bytes 234529 | solution.py:86
  62.0 6.5 all_gather.24
  68.5 11.4 %all_gather.22 = bf16[3,768,192]{2,1,0:T(8,128)(2,1)} all-gather(bf16[3,192,192]{2,1,0:T(8,128)(2,1)S(1)} %get-tuple-element.397), channel_id=1, replica_groups=mesh['fsdp'=4,'ctx'=2,'tp'=4] {'fsdp'}, dimensions={1}, use_global_device_ids=true | all-gather | bytes 1105920 | tf_op jit(solution)/shard_map/all_gather | solution.py:195
  97.0 4.8 fusion.117
  114.7 5.8 all_gather.26
  126.7 7.5 collective-permute-done.2
  141.7 13.6 %all-reduce.13.cloned.1.call-done = bf16[576,768]{1,0:T(8,128)(2,1)} async-done(((bf16[576,768]{1,0:T(8,128)(2,1)}), bf16[576,768]{1,0:T(8,128)(2,1)}) %all-reduce.13.cloned.1.call-update) | async-done | bytes 884752 | tf_op jit(solution)/shard_map/psum | solution.py:248
  157.7 7.2 multiply_convert_fusion.1
  164.9 4.9 fusion.125
  173.0 3.3 convolution_convert_fusion.1
  176.3 42.2 %all-reduce.15.cloned.1.call-done = bf16[576,768]{1,0:T(8,128)(2,1)} async-done(((bf16[576,768]{1,0:T(8,128)(2,1)}), bf16[576,768]{1,0:T(8,128)(2,1)}) %all-reduce.15.cloned.1.call-update) | async-done | bytes 884752 | tf_op jit(solution)/shard_map/psum | solution.py:273
  227.7 4.2 convert_reduce_fusion.2
  234.3 7.1 fusion.36
  241.4 7.7 convert_reduce_fusion.3
  265.1 3.2 bitcast_convert_fusion
  277.4 65.7 %all-reduce.21.cloned.1.call-done = (bf16[576,768]{1,0:T(8,128)(2,1)}, bf16[576,768]{1,0:T(8,128)(2,1)}) async-done(((bf16[576,768]{1,0:T(8,128)(2,1)}, bf16[576,768]{1,0:T(8,128)(2,1)}), (bf16[576,768]{1,0:T(8,128)(2,1)}, bf16[576,768]{1,0:T(8,128)(2,1)})) %all-reduce.21.cloned.1.call-update) | async-done | bytes 1769488 | tf_op jit(solution)/shard_map/psum | solution.py:256
  349.0 4.2 copy.295
  353.2 4.7 reshape.396
  358.6 4.0 fusion.64
  371.7 3.2 maximum_multiply_fusion
  381.1 3.7 fusion.67
  385.6 6.2 fusion.122
  396.0 10.8 %all-reduce.3 = (f32[2,6,32]{2,1,0:T(8,128)}, f32[24,32]{1,0:T(8,128)S(1)}) all-reduce(f32[2,6,32]{2,1,0:T(8,128)S(1)} %pad_maximum_fusion.5, f32[24,32]{1,0:T(8,128)} %reshape.383), channel_id=7, replica_groups=mesh['fsdp'=4,'ctx'=2,'tp'=4] {'fsdp'}, use_global_device_ids=true, to_apply=%region_37.38.clone | all-reduce | flops 1152 | bytes 9216
  407.6 56.3 %while.23 = (s32[]{:T(128)}, f32[529,6]{0,1:T(8,128)}, s32[12,1728]{1,0:T(8,128)}, f32[12,1728,6]{1,0,2:T(8,128)}, s32[]{:T(128)}, /*index=5*/s32[]{:T(128)}) while((s32[]{:T(128)}, f32[529,6]{0,1:T(8,128)}, s32[12,1728]{1,0:T(8,128)}, f32[12,1728,6]{1,0,2:T(8,128)}, s32[]{:T(128)}, /*index=5*/s32[]{:T(128)}) %tuple.139), condition=%wide.region_43.44_spmd.clone, body=%wide.region_42.43_spmd.clone.sunk | while | flops 66736528 | bytes 170639 | solution.py:108
  465.1 4.0 fusion.24
  494.0 35.6 %all-reduce.4 = (f32[6,192]{1,0:T(8,128)S(1)}, f32[2,6,8]{2,1,0:T(8,128)S(1)}, f32[24,8]{1,0:T(8,128)S(1)}) all-reduce(f32[6,192]{1,0:T(8,128)S(1)} %copy.300, f32[2,6,8]{2,1,0:T(8,128)S(1)} %copy-done.59, f32[24,8]{1,0:T(8,128)S(1)} %copy-done.42), channel_id=1, replica_groups=mesh['fsdp'=4,'ctx'=2,'tp'=4] {'ctx'}, use_global_device_ids=true, to_apply=%region_32.33 | all-reduce | flops 1440 | bytes 11520 | tf_op jit(solution)/shard_map/psum | solution.py:146
  534.7 3.5 convert_add_fusion
  538.4 17.9 %all-reduce.19.cloned.1.call-done = (f32[3,192,192]{1,2,0:T(8,128)}, f32[192,192]{1,0:T(8,128)}, f32[192,768]{1,0:T(8,128)}, f32[768,192]{0,1:T(8,128)}) async-done(((f32[3,192,192]{1,2,0:T(8,128)}, f32[192,192]{1,0:T(8,128)}, f32[192,768]{1,0:T(8,128)}, f32[768,192]{0,1:T(8,128)}), (f32[3,192,192]{1,2,0:T(8,128)}, f32[192,192]{1,0:T(8,128)}, f32[192,768]{1,0:T(8,128)}, ...) | async-done | bytes 1769488 | tf_op jit(solution)/shard_map/psum | solution.py:146
  569.4 124.7 %all-reduce.17.cloned.1.call-done = (f32[529,24]{0,1:T(8,128)}, f32[14]{0:T(128)}, f32[3,768]{1,0:T(4,128)}, f32[3,768]{1,0:T(4,128)}, f32[768]{0:T(1024)}, /*in...) async-done(((f32[529,24]{0,1:T(8,128)}, f32[14]{0:T(128)}, f32[3,768]{1,0:T(4,128)}, f32[3,768]{1,0:T(4,128)}, f32[768]{0:T(1024)}, ...) | async-done | bytes 106152 | tf_op jit(solution)/shard_map/psum | solution.py:431
  717.6 31.7 %psum.175 = f32[]{:T(128)} all-reduce(f32[]{:T(128)S(6)} %add.414), channel_id=1, replica_groups=mesh['fsdp'=4,'ctx'=2,'tp'=4] {'fsdp','tp'}, use_global_device_ids=true, to_apply=%region_82.83 | all-reduce | flops 1 | bytes 8 | tf_op jit(solution)/shard_map/psum | solution.py:485
  (520 shorter events, 283.8 us)
Async XLA Ops:
  8.1 147.1 %all-reduce.13.cloned.1.call-start = ((), (), s32[]{:S(2)}) async-start(), calls=%async_computation.5 | async-start | bytes 1769472 | tf_op jit(solution)/shard_map/psum | solution.py:248
  10.3 69.7 %collective-permute-start = (bf16[2,6,24,768]{3,2,1,0:T(8,128)(2,1)}, bf16[2,6,24,768]{3,2,1,0:T(8,128)(2,1)S(1)}, u32[]{:S(2)}, u32[]{:S(2)}) collective-permute-start(bf16[2,6,24,768]{3,2,1,0:T(8,128)(2,1)} %get-tuple-element.395), channel_id=1, source_target_pairs={{0,4},{4,0},{1,5},{5,1},{2,6},{6,2},{3,7},{7,3},{8,12},{12,8},{9,1... | collective-permute-start | bytes 1327112 | tf_op jit(solution)/shard_map/ppermute | solution.py:25
  26.4 128.9 %copy-start.58 = (f32[768]{0:T(1024)}, f32[768]{0:T(1024)S(1)}, u32[]{:S(2)}) copy-start(f32[768]{0:T(1024)S(1)} %get-tuple-element.327) | copy-start | bytes 9220
  26.4 194.8 %copy-start.52 = (f32[768]{0:T(1024)}, f32[768]{0:T(1024)S(1)}, u32[]{:S(2)}) copy-start(f32[768]{0:T(1024)S(1)} %get-tuple-element.326) | copy-start | bytes 9220
  108.0 49.7 %all-gather.4.cloned.1.call-start = ((), (), s32[]{:S(2)}) async-start(), calls=%async_computation.6 | async-start | bytes 1474560 | tf_op jit(solution)/shard_map/all_gather | solution.py:197
  109.5 55.3 %all-gather.6.cloned.1.call-start = ((), (), s32[]{:S(2)}) async-start(), calls=%async_computation.7 | async-start | bytes 1474560 | tf_op jit(solution)/shard_map/all_gather | solution.py:198
  112.2 22.1 %collective-permute-start.2 = (f32[2,6,24,768]{3,2,1,0:T(8,128)}, f32[2,6,24,768]{3,2,1,0:T(8,128)S(1)}, u32[]{:S(2)}, u32[]{:S(2)}) collective-permute-start(f32[2,6,24,768]{3,2,1,0:T(8,128)} %get-tuple-element.393), channel_id=1, source_target_pairs={{0,4},{4,0},{1,5},{5,1},{2,6},{6,2},{3,7},{7,3},{8,12},{12,8},{9,1... | collective-permute-start | bytes 2654216 | tf_op jit(solution)/shard_map/ppermute | solution.py:25
  114.1 104.5 %all-reduce.15.cloned.1.call-start = ((), (), s32[]{:S(2)}) async-start(), calls=%async_computation.8 | async-start | bytes 1769472 | tf_op jit(solution)/shard_map/psum | solution.py:273
  172.5 170.5 %all-reduce.21.cloned.1.call-start = ((), (), s32[]{:S(2)}) async-start(), calls=%async_computation.16 | async-start | bytes 3538944 | tf_op jit(solution)/shard_map/psum | solution.py:256
  268.3 205.1 %reduce-scatter.20.cloned.1.call-start = ((), (), s32[]{:S(2)}) async-start(), calls=%async_computation.12 | async-start | bytes 983040
  271.1 204.0 %reduce-scatter.18.cloned.1.call-start = ((), (), s32[]{:S(2)}) async-start(), calls=%async_computation.11 | async-start | bytes 2457600
  274.1 75.0 %copy-start.41 = (f32[576]{0:T(1024)}, f32[576]{0:T(1024)S(1)}, u32[]{:S(2)}) copy-start(f32[576]{0:T(1024)S(1)} %div.137) | copy-start | bytes 6916
  357.9 121.8 %reduce-scatter.14.cloned.1.call-start = ((), (), s32[]{:S(2)}) async-start(), calls=%async_computation.9 | async-start | bytes 2949120 | tf_op jit(solution)/shard_map/reduce_scatter | solution.py:137
  362.6 117.1 %reduce-scatter.16.cloned.1.call-start = ((), (), s32[]{:S(2)}) async-start(), calls=%async_computation.10 | async-start | bytes 2949120 | tf_op jit(solution)/shard_map/reduce_scatter | solution.py:138
  384.9 108.2 %reduce-scatter.22.cloned.1.call-start = ((), (), s32[]{:S(2)}) async-start(), calls=%async_computation.13 | async-start | bytes 491520
  394.0 71.1 %copy-start.16 = (bf16[576,768]{1,0:T(8,128)(2,1)S(1)}, bf16[576,768]{1,0:T(8,128)(2,1)}, u32[]{:S(2)}) copy-start(bf16[576,768]{1,0:T(8,128)(2,1)} %all-reduce.13.cloned.1.call-done) | copy-start | bytes 2654212
  470.8 85.4 %all-reduce.19.cloned.1.call-start = ((), (), s32[]{:S(2)}) async-start(), calls=%async_computation.15 | async-start | bytes 3932160 | tf_op jit(solution)/shard_map/psum | solution.py:146
  479.8 214.3 %all-reduce.17.cloned.1.call-start = ((), (), s32[]{:S(2)}) async-start(), calls=%async_computation.14 | async-start | bytes 254976 | tf_op jit(solution)/shard_map/psum | solution.py:431
  490.4 71.9 %collective-permute-start.3 = (bf16[2,6,24,768]{3,0,2,1:T(2,128)(2,1)}, bf16[2,6,24,768]{3,0,2,1:T(2,128)(2,1)}, u32[]{:S(2)}, u32[]{:S(2)}) collective-permute-start(bf16[2,6,24,768]{3,0,2,1:T(2,128)(2,1)} %fusion.60), channel_id=1, source_target_pairs={{0,4},{4,0},{1,5},{5,1},{2,6},{6,2},{3,7},{7,3},{8,12},{12,8},{9,1... | collective-permute-start | bytes 1327112 | tf_op jit(solution)/shard_map/ppermute | solution.py:25
  492.5 42.2 %collective-permute-start.1 = (bf16[2,6,24,768]{3,0,2,1:T(2,128)(2,1)S(1)}, bf16[2,6,24,768]{3,0,2,1:T(2,128)(2,1)}, u32[]{:S(2)}, u32[]{:S(2)}) collective-permute-start(bf16[2,6,24,768]{3,0,2,1:T(2,128)(2,1)S(1)} %fusion.61), channel_id=1, source_target_pairs={{0,4},{4,0},{1,5},{5,1},{2,6},{6,2},{3,7},{7,3},{8,12},{12,8},{9,1... | collective-permute-start | bytes 1327112 | tf_op jit(solution)/shard_map/ppermute | solution.py:25
  529.7 234.0 %copy-start.60 = (f32[6,192]{1,0:T(8,128)}, f32[6,192]{1,0:T(8,128)S(1)}, u32[]{:S(2)}) copy-start(f32[6,192]{1,0:T(8,128)S(1)} %get-tuple-element.534) | copy-start | bytes 13828
  534.1 229.7 %copy-start.61 = (f32[6,192]{1,0:T(8,128)}, f32[6,192]{1,0:T(8,128)S(1)}, u32[]{:S(2)}) copy-start(f32[6,192]{1,0:T(8,128)S(1)} %get-tuple-element.558) | copy-start | bytes 13828
  567.0 139.9 %copy-start.67 = (f32[529,6]{0,1:T(8,128)S(1)}, f32[529,6]{0,1:T(8,128)}, u32[]{:S(2)}) copy-start(f32[529,6]{0,1:T(8,128)} %param.52) | copy-start | bytes 38092
  567.0 142.0 %copy-start.95 = (f32[14]{0:T(128)S(1)}, f32[14]{0:T(128)}, u32[]{:S(2)}) copy-start(f32[14]{0:T(128)} %constant.199) | copy-start | bytes 172
  567.0 142.7 %copy-start.18 = (f32[192,192]{1,0:T(8,128)S(1)}, f32[192,192]{1,0:T(8,128)}, u32[]{:S(2)}) copy-start(f32[192,192]{1,0:T(8,128)} %get-tuple-element.531) | copy-start | bytes 442372
  568.3 144.2 %copy-start.5 = (f32[192,768]{1,0:T(8,128)S(1)}, f32[192,768]{1,0:T(8,128)}, u32[]{:S(2)}) copy-start(f32[192,768]{1,0:T(8,128)} %get-tuple-element.532) | copy-start | bytes 1769476
  568.3 145.8 %copy-start.4 = (f32[768,192]{0,1:T(8,128)S(1)}, f32[768,192]{0,1:T(8,128)}, u32[]{:S(2)}) copy-start(f32[768,192]{0,1:T(8,128)} %get-tuple-element.533) | copy-start | bytes 1769476
  568.3 185.7 %copy-start.43 = (f32[24,8]{1,0:T(8,128)S(1)}, f32[24,8]{1,0:T(8,128)}, u32[]{:S(2)}) copy-start(f32[24,8]{1,0:T(8,128)} %copy.279) | copy-start | bytes 2308
  568.3 186.4 %copy-start.65 = (f32[2,6,8]{2,0,1:T(2,128)S(1)}, f32[2,6,8]{2,0,1:T(2,128)}, u32[]{:S(2)}) copy-start(f32[2,6,8]{2,0,1:T(2,128)} %param.38) | copy-start | bytes 1156
  568.3 187.1 %copy-start.23 = (f32[3,192,192]{1,2,0:T(8,128)S(1)}, f32[3,192,192]{1,2,0:T(8,128)}, u32[]{:S(2)}) copy-start(f32[3,192,192]{1,2,0:T(8,128)} %copy.277) | copy-start | bytes 1327108
  694.9 67.7 %copy-start.48 = (f32[768]{0:T(1024)}, f32[768]{0:T(1024)S(1)}, u32[]{:S(2)}) copy-start(f32[768]{0:T(1024)S(1)} %dynamic_slice.53) | copy-start | bytes 9220
  697.0 64.5 %copy-start.81 = (f32[192]{0:T(256)}, f32[192]{0:T(256)S(1)}, u32[]{:S(2)}) copy-start(f32[192]{0:T(256)S(1)} %dynamic_slice.51) | copy-start | bytes 2308
  (83 other events, 1194.6 us)
Sparse Core Ops, SparseCore 0:
  108.2 47.0 all-reduce.12
  172.7 45.8 all-reduce.14
  268.4 74.5 all-reduce.20
  479.9 76.2 all-reduce.18
  564.8 129.3 all-reduce.16
Sparse Core Ops, SparseCore 1:
  110.7 17.5 all-gather.3
  130.3 17.3 all-gather.5
  271.3 22.2 reduce-scatter.19
  358.0 29.4 reduce-scatter.17
  390.0 32.7 reduce-scatter.13
  425.3 32.7 reduce-scatter.15
  470.9 20.7 reduce-scatter.21

commit v2 on v1

--- a/solution.py
+++ b/solution.py
@@ -1,7 +1,12 @@
+import functools
+
 import jax
 import jax.numpy as jnp
 from jax import lax
+from jax.experimental import pallas as pl
+from jax.experimental.pallas import tpu as pltpu
 from jax.sharding import PartitionSpec as P
+
 
 D = 768
 HEADS = 24
@@ -157,7 +162,429 @@
     )
 
 
-def per_device(
+BF = jnp.bfloat16
+F32 = jnp.float32
+MESH = pl.DeviceIdType.MESH
+TOK = WIN * WIN
+HALF = D // 2
+VMEM_LIMIT = 66_000_000
+
+
+def dot(a, b):
+    return lax.dot_general(a, b, (((1,), (0,)), ((), ())), preferred_element_type=F32)
+
+
+def dot_t(a, b):
+    return lax.dot_general(a, b, (((1,), (1,)), ((), ())), preferred_element_type=F32)
+
+
+def t_dot(a, b):
+    return lax.dot_general(a, b, (((0,), (0,)), ((), ())), preferred_element_type=F32)
+
+
+def row_mean(x):
+    return jnp.sum(x, axis=-1, keepdims=True) * (1.0 / x.shape[-1])
+
+
+def remote(src, dst, send, recv, where):
+    return pltpu.make_async_remote_copy(
+        src_ref=src, dst_ref=dst, send_sem=send, recv_sem=recv, device_id=where, device_id_type=MESH
+    )
+
+
+def greet(barrier, places):
+    for place_of in places:
+        pl.semaphore_signal(barrier, inc=1, device_id=place_of, device_id_type=MESH)
+
+
+class LineSum:
+    def __init__(self, part, send, from_outer, from_mid, total, sems):
+        self.part, self.send, self.from_outer, self.from_mid, self.total = (
+            part, send, from_outer, from_mid, total,
+        )
+        self.s_out, self.r_out, self.s_mid, self.r_mid, self.s_tot, self.r_tot, self.s_cross = sems
+        z = lax.axis_index("tp")
+        self.is_mid = jnp.logical_and(z > 0, z < 3)
+        self.is_outer = jnp.logical_not(self.is_mid)
+        self.outer = jnp.where(z < 2, 0, 3)
+        self.mid = jnp.where(z < 2, 1, 2)
+        self.other_mid = 3 - self.mid
+        self.own = self.mid - 1
+        self.other = 1 - self.own
+
+    @staticmethod
+    def scratch(count):
+        return [
+            pltpu.VMEM((count, 2, TOK, HALF), F32),
+            pltpu.VMEM((count, 2, TOK, HALF), BF),
+            pltpu.VMEM((count, 2, TOK, HALF), BF),
+            pltpu.VMEM((count, TOK, HALF), BF),
+            pltpu.SemaphoreType.DMA((count, 2)),
+            pltpu.SemaphoreType.DMA((count, 2)),
+            pltpu.SemaphoreType.DMA((count,)),
+            pltpu.SemaphoreType.DMA((count,)),
+            pltpu.SemaphoreType.DMA((count, 2)),
+            pltpu.SemaphoreType.DMA((count, 2)),
+            pltpu.SemaphoreType.DMA((count,)),
+        ]
+
+    @staticmethod
+    def build(refs, total):
+        return LineSum(refs[0], refs[1], refs[2], refs[3], total, refs[4:11])
+
+    @staticmethod
+    def peers():
+        return 2
+
+    def greet(self, barrier):
+        pl.semaphore_signal(
+            barrier, inc=1, device_id={"tp": jnp.where(self.is_mid, self.outer, self.mid)},
+            device_id_type=MESH,
+        )
+
+        @pl.when(self.is_mid)
+        def _():
+            pl.semaphore_signal(
+                barrier, inc=1, device_id={"tp": self.other_mid}, device_id_type=MESH
+            )
+
+    def greet_count(self):
+        return jnp.where(self.is_mid, 2, 1)
+
+    def _to_mid(self, w, h):
+        return remote(self.send.at[w, h], self.from_outer.at[w, h], self.s_out.at[w, h],
+                      self.r_out.at[w, h], {"tp": self.mid})
+
+    def _across(self, w):
+        return remote(self.send.at[w, self.other], self.from_mid.at[w], self.s_mid.at[w],
+                      self.r_mid.at[w], {"tp": self.other_mid})
+
+    def _total_across(self, w, h):
+        return remote(self.total.at[w, h], self.total.at[w, h], self.s_cross.at[w],
+                      self.r_tot.at[w, h], {"tp": self.other_mid})
+
+    def _total_out(self, w, h):
+        return remote(self.total.at[w, h], self.total.at[w, h], self.s_tot.at[w, h],
+                      self.r_tot.at[w, h], {"tp": self.outer})
+
+    def put(self, w, value):
+        self.part[w, 0] = value[:, :HALF]
+        self.part[w, 1] = value[:, HALF:]
+
+    def start(self, w):
+        @pl.when(self.is_outer)
+        def _():
+            self.send[w, self.other] = self.part[w, self.other].astype(BF)
+            self._to_mid(w, self.other).start()
+            self.send[w, self.own] = self.part[w, self.own].astype(BF)
+            self._to_mid(w, self.own).start()
+
+    def cross(self, w):
+        @pl.when(self.is_mid)
+        def _():
+            self._to_mid(w, self.other).wait_recv()
+            self.send[w, self.other] = (
+                self.part[w, self.other] + self.from_outer[w, self.other].astype(F32)
+            ).astype(BF)
+            self._across(w).start()
+
+    def settle(self, w):
+        @pl.when(self.is_mid)
+        def _():
+            self._to_mid(w, self.own).wait_recv()
+            self._across(w).wait_recv()
+            self.total[w, self.own] = (
+                self.part[w, self.own]
+                + self.from_outer[w, self.own].astype(F32)
+                + self.from_mid[w].astype(F32)
+            ).astype(BF)
+            self._total_across(w, self.own).start()
+            self._total_out(w, self.own).start()
+
+    def hand(self, w):
+        @pl.when(self.is_mid)
+        def _():
+            self._total_across(w, self.other).wait_recv()
+            self._total_out(w, self.other).start()
+
+    def arrive(self, w):
+        @pl.when(self.is_outer)
+        def _():
+            self._total_out(w, 0).wait_recv()
+            self._total_out(w, 1).wait_recv()
+
+    def drain(self, w):
+        @pl.when(self.is_outer)
+        def _():
+            self._to_mid(w, 0).wait_send()
+            self._to_mid(w, 1).wait_send()
+
+        @pl.when(self.is_mid)
+        def _():
+            self._across(w).wait_send()
+            self._total_across(w, self.own).wait_send()
+            self._total_out(w, 0).wait_send()
+            self._total_out(w, 1).wait_send()
+
+
+def window_rows(row_of, row_tmp, image, dst):
+    for r in range(WIN):
+        row_tmp[...] = row_of(image, r).astype(F32)
+        dst[2 * image, r * WIN : (r + 1) * WIN, :] = row_tmp[SHIFT : SHIFT + WIN, :]
+        dst[2 * image + 1, r * WIN : r * WIN + SHIFT, :] = row_tmp[SHIFT + WIN :, :]
+        dst[2 * image + 1, r * WIN + SHIFT : (r + 1) * WIN, :] = row_tmp[:SHIFT, :]
+
+
+def attention_forward_body(
+    feat, og, wq, wp, wu, wd, small, table_t, ridx, regr, regc,
+    wq_o, wp_o, wu_o, wd_o, rows_o, xw_o, ogw_o, n1_o, q_o, k_o, v_o, probs_o, ctx_o, br_o,
+    sm_g, wp_g, wd_g, fh, gh, bias_s, row_tmp,
+    ls_a, ls_b, ls_c, ls_d, ls_e, ls_f, ls_g, ls_h, ls_i, ls_j, ls_k,
+    w_send, w_recv, h_send, h_recv,
+):
+    windows = xw_o.shape[0]
+    images = windows // 2
+    f = lax.axis_index("fsdp")
+    c = lax.axis_index("ctx")
+    near, far = f + 1 - 2 * lax.rem(f, 2), lax.rem(f + 2, 4)
+    line = LineSum.build((ls_a, ls_b, ls_c, ls_d, ls_e, ls_f, ls_g, ls_h, ls_i, ls_j, ls_k), br_o)
+    barrier = pltpu.get_barrier_semaphore()
+    greet(barrier, [{"fsdp": near}, {"fsdp": far}, {"ctx": 1 - c}])
+    line.greet(barrier)
+
+    shard = wq.shape[1]
+
+    def block(at):
+        return pl.ds(pl.multiple_of(at * shard, shard), shard)
+
+    wq_o[:, block(f), :] = wq[...].astype(BF)
+    sm_g[f] = small[...].astype(BF)
+    wp_g[f] = wp[...].astype(BF)
+    wu_o[block(f), :] = wu[...].astype(BF)
+    wd_g[f] = wd[...].astype(BF)
+    pl.semaphore_wait(barrier, 3 + line.greet_count())
+
+    items = [
+        lambda at: sm_g.at[at],
+        lambda at: wq_o.at[:, block(at), :],
+        lambda at: wp_g.at[at],
+        lambda at: wu_o.at[block(at), :],
+        lambda at: wd_g.at[at],
+    ]
+
+    def copy_of(n, kind, at, where):
+        ref = items[n](at)
+        return remote(ref, ref, w_send.at[n, kind], w_recv.at[n, kind], {"fsdp": where})
+
+    halo_f = [
+        remote(feat.at[i, 0:SHIFT], fh.at[i], h_send.at[i], h_recv.at[i], {"ctx": 1 - c})
+        for i in range(images)
+    ]
+    halo_g = [
+        remote(og.at[i, 0:SHIFT], gh.at[i], h_send.at[images + i], h_recv.at[images + i], {"ctx": 1 - c})
+        for i in range(images)
+    ]
+    for copy in halo_f:
+        copy.start()
+    for n in range(len(items)):
+        copy_of(n, 0, f, far).start()
+        copy_of(n, 1, f, near).start()
+    for copy in halo_g:
+        copy.start()
+
+    def relay(n):
+        copy_of(n, 0, f, far).wait_recv()
+        copy_of(n, 2, far, near).start()
+
+    def gathered(n):
+        copy_of(n, 1, f, near).wait_recv()
+        copy_of(n, 2, far, near).wait_recv()
+
+    relay(0)
+
+    def bias_rows(step, carry):
+        rows = pl.ds(pl.multiple_of(step * 8, 8), 8)
+        for part in range(2):
+            idx = ridx[rows, part * 128 : (part + 1) * 128]
+            low = jnp.bitwise_and(idx, 127)
+            high = jnp.right_shift(idx, 7)
+            picks = [high == n for n in range(5)]
+            for h in range(bias_s.shape[0]):
+                found = jnp.zeros((8, 128), F32)
+                for n in range(5):
+                    tab = jnp.broadcast_to(table_t[h : h + 1, n * 128 : (n + 1) * 128], (8, 128))
+                    got = jnp.take_along_axis(tab, low, axis=1, mode="promise_in_bounds")
+                    found = jnp.where(picks[n], got, found)
+                bias_s[h, rows, part * 128 : (part + 1) * 128] = found
+        return carry
+
+    lax.fori_loop(0, TOK // 8, bias_rows, 0)
+    gathered(0)
+    relay(1)
+    lanes = rows_o.shape[1]
+    rows_o[...] = jnp.concatenate([sm_g[n].astype(F32) for n in range(4)], axis=1)
+    unit = lax.broadcasted_iota(jnp.int32, (shard, lanes), 0)
+    lane = lax.broadcasted_iota(jnp.int32, (shard, lanes), 1)
+    biases = jnp.zeros((16, lanes), F32)
+    for n in range(4):
+        same = jnp.logical_and(
+            jnp.right_shift(lane, 5) == jnp.right_shift(unit, 3),
+            jnp.bitwise_and(lane, 31) == jnp.bitwise_and(unit, 7) + n * 8,
+        )
+        biases = biases + dot(sm_g[n], jnp.where(same, 1.0, 0.0).astype(BF))
+    rows_o[8:16, :] = biases[8:16, :]
+
+    for i in range(images):
+        halo_f[i].wait_recv()
+        window_rows(
+            lambda im, r: feat[im, SHIFT + r] if r < SHIFT else fh[im, r - SHIFT], row_tmp, i, xw_o
+        )
+    gain, offset = rows_o[0:1, :], rows_o[1:2, :]
+    width = q_o.shape[2]
+    bias_q, bias_v = rows_o[9:10, :width], rows_o[10:11, :width]
+    head_of = jnp.right_shift(lax.broadcasted_iota(jnp.int32, (1, width), 1), 5)
+    heads = width // HD
+    gathered(1)
+
+    def window(w, carry):
+        x = xw_o[w]
+        mean_val = row_mean(x)
+        centred = x - mean_val
+        var_val = row_mean(centred * centred)
+        n1 = (centred * lax.rsqrt(var_val + NORM_EPS) * gain + offset).astype(BF)
+        n1_o[w] = n1
+        q = (dot(n1, wq_o[0]) + bias_q).astype(BF)
+        k = dot(n1, wq_o[1]).astype(BF)
+        v = (dot(n1, wq_o[2]) + bias_v).astype(BF)
+        q_o[w] = q
+        k_o[w] = k
+        v_o[w] = v
+        mask = jnp.where(regc[w] == regr[w], 0.0, MASK_FILL)
+
+        @pl.when(w >= 1)
+        def _():
+            line.cross(w - 1)
+
+        @pl.when(w == 0)
+        def _():
+            relay(2)
+            gathered(2)
+            wp_o[...] = jnp.concatenate([wp_g[n] for n in range(4)], axis=1)
+
+        context = jnp.zeros((TOK, width), F32)
+        for h in range(heads):
+            pick = jnp.where(head_of == h, 1.0, 0.0).astype(BF)
+            scores = dot_t(q * pick, k) * HD ** (-0.5) + bias_s[h, :, :TOK] + mask
+            lifted = jnp.exp(scores - jnp.max(scores, axis=-1, keepdims=True))
+            probs = lifted / jnp.sum(lifted, axis=-1, keepdims=True)
+            probs_o[w, h] = probs
+            context = context + dot(probs.astype(BF), v * pick)
+        ctx = context.astype(BF)
+        ctx_o[w] = ctx
+        line.put(w, dot(ctx, wp_o[...]))
+        line.start(w)
+
+        @pl.when(w >= 1)
+        def _():
+            line.settle(w - 1)
+
+        @pl.when(w >= 2)
+        def _():
+            line.hand(w - 2)
+
+        return carry
+
+    lax.fori_loop(0, windows, window, 0)
+    line.cross(windows - 1)
+    line.hand(windows - 2)
+    relay(3)
+    line.settle(windows - 1)
+    relay(4)
+    line.hand(windows - 1)
+    gathered(3)
+    gathered(4)
+    wd_o[...] = jnp.concatenate([wd_g[n] for n in range(4)], axis=1)
+    for i in range(images):
+        halo_g[i].wait_recv()
+        window_rows(
+            lambda im, r: og[im, SHIFT + r] if r < SHIFT else gh[im, r - SHIFT], row_tmp, i, ogw_o
+        )
+    for w in range(windows):
+        line.arrive(w)
+        line.drain(w)
+    for copy in halo_f + halo_g:
+        copy.wait_send()
+    for n in range(len(items)):
+        copy_of(n, 0, f, far).wait_send()
+        copy_of(n, 1, f, near).wait_send()
+        copy_of(n, 2, far, near).wait_send()
+
+
+def vmem_call(body, outs, scratch, name, collective_id):
+    def call(*args):
+        return pl.pallas_call(
+            body,
+            out_shape=[jax.ShapeDtypeStruct(s, t) for s, t in outs],
+            in_specs=[pl.BlockSpec(memory_space=pltpu.VMEM)] * len(args),
+            out_specs=[pl.BlockSpec(memory_space=pltpu.VMEM)] * len(outs),
+            scratch_shapes=scratch,
+            compiler_params=pltpu.CompilerParams(
+                collective_id=collective_id, has_side_effects=True, vmem_limit_bytes=VMEM_LIMIT
+            ),
+            name=name,
+        )(*args)
+
+    return call
+
+
+def attention_forward(features, out_grad, regions, rel_index, w_qkv, w_proj, w_up, w_down,
+                      norm_vecs, head_bias, hidden_bias, rel_table):
+    images = features.shape[0]
+    windows = 2 * images
+    shard, width = w_qkv.shape[1], w_qkv.shape[2]
+    hidden = w_up.shape[1]
+    heads = width // HD
+    small = jnp.concatenate(
+        [
+            norm_vecs,
+            jnp.zeros((2, shard), F32),
+            hidden_bias.reshape(1, shard),
+            jnp.pad(head_bias.reshape(2, -1), ((0, 5), (0, shard - head_bias[0].size))),
+        ],
+        axis=0,
+    )
+    table_t = jnp.pad(
+        rel_table.astype(BF).astype(F32).T, ((0, 8 - heads), (0, 640 - rel_table.shape[0]))
+    )
+    ridx = jnp.pad(rel_index, ((0, 0), (0, 256 - TOK)))
+    region_win = to_windows(regions[..., None])[..., 0]
+    outs = [
+        ((3, D, width), BF), ((width, D), BF), ((D, hidden), BF), ((hidden, D), BF), ((16, D), F32),
+        ((windows, TOK, D), F32), ((windows, TOK, D), F32), ((windows, TOK, D), BF),
+        ((windows, TOK, width), BF), ((windows, TOK, width), BF), ((windows, TOK, width), BF),
+        ((windows, heads, TOK, TOK), F32), ((windows, TOK, width), BF),
+        ((windows, 2, TOK, HALF), BF),
+    ]
+    scratch = [
+        pltpu.VMEM((4, 16, shard), BF),
+        pltpu.VMEM((4, width, shard), BF),
+        pltpu.VMEM((4, hidden, shard), BF),
+        pltpu.VMEM((images, SHIFT, 24, D), BF),
+        pltpu.VMEM((images, SHIFT, 24, D), F32),
+        pltpu.VMEM((heads, TOK, 256), F32),
+        pltpu.VMEM((24, D), F32),
+        *LineSum.scratch(windows),
+        pltpu.SemaphoreType.DMA((5, 3)),
+        pltpu.SemaphoreType.DMA((5, 3)),
+        pltpu.SemaphoreType.DMA((2 * images,)),
+        pltpu.SemaphoreType.DMA((2 * images,)),
+    ]
+    call = vmem_call(attention_forward_body, outs, scratch, "attention_forward", 1)
+    return call(features, out_grad, w_qkv, w_proj, w_up, w_down, small, table_t, ridx,
+                region_win[:, None, :], region_win[:, :, None])
+
+
+def per_device_plain(
     features,
     out_grad,
     regions,
@@ -537,9 +964,364 @@
     )
 
 
+def per_device(
+    features,
+    out_grad,
+    regions,
+    rel_index,
+    w_qkv,
+    w_proj,
+    w_up,
+    w_down,
+    norm_vecs,
+    head_bias,
+    hidden_bias,
+    rel_table,
+    row_qkv,
+    col_qkv,
+    row_proj,
+    col_proj,
+    row_up,
+    col_up,
+    row_down,
+    col_down,
+    state_norm,
+    state_heads,
+    state_hidden,
+    state_table,
+):
+    images, band_rows, across, model_width = features.shape
+    win_tokens = WIN * WIN
+    fsdp_at = lax.axis_index("fsdp")
+    ctx_at = lax.axis_index("ctx")
+    tp_at = lax.axis_index("tp")
+    first_fsdp = (fsdp_at == 0).astype(jnp.float32)
+    first_ctx = (ctx_at == 0).astype(jnp.float32)
+    first_tp = (tp_at == 0).astype(jnp.float32)
+    (weights_qkv, weights_proj, weights_up, weights_down, rows, xw, ogw, n1, query_low, key_low, value_low,
+     prob_rows, context_low, br) = attention_forward(
+        features, out_grad, regions, rel_index, w_qkv, w_proj, w_up, w_down,
+        norm_vecs, head_bias, hidden_bias, rel_table)
+    norm_rows = rows[:6]
+    bias_hidden = rows[8]
+    local_width = weights_qkv.shape[2]
+    heads_here = local_width // HD
+    win_count = xw.shape[0]
+    head_shape = (win_count, win_tokens, heads_here, HD)
+    flat_one = xw.reshape(-1, model_width)
+    grad_flat = ogw.reshape(-1, model_width)
+    normed_one_low = n1.reshape(-1, model_width)
+    _, pull_one = jax.vjp(layer_norm, flat_one, norm_rows[0], norm_rows[1])
+    query_low, key_low, value_low = (u.reshape(head_shape) for u in (query_low, key_low, value_low))
+    prob_low = prob_rows.astype(jnp.bfloat16)
+    context_low = context_low.reshape(-1, local_width)
+    branch = br.transpose(0, 2, 1, 3).reshape(-1, model_width).astype(jnp.float32) + norm_rows[2]
+    def roll_out(rolled_flat):
+        band = jnp.roll(
+            from_windows(
+                rolled_flat.reshape(-1, win_tokens, model_width), images, band_rows, across
+            ),
+            SHIFT,
+            axis=2,
+        )
+        lower = passed_along(band[:, band_rows - SHIFT :], "ctx", 1)
+        return jnp.concatenate([lower, band[:, : band_rows - SHIFT]], axis=1)
+
+    flat_two = flat_one + branch
+    normed_two, pull_two = jax.vjp(layer_norm, flat_two, norm_rows[3], norm_rows[4])
+    normed_two_low = normed_two.astype(jnp.bfloat16)
+    pre_act = jnp.dot(normed_two_low, weights_up, preferred_element_type=jnp.float32) + bias_hidden
+    hidden, pull_gelu = jax.vjp(exact_gelu, pre_act)
+    hidden_low = hidden.astype(jnp.bfloat16)
+    mixed_part = jnp.dot(hidden_low, weights_down, preferred_element_type=jnp.float32)
+    mixed_whole = lax.psum(mixed_part.astype(jnp.bfloat16), "tp").astype(jnp.float32)
+    block_out = features.astype(jnp.float32) + roll_out(
+        (branch + mixed_whole + norm_rows[5]).astype(jnp.bfloat16)
+    ).astype(jnp.float32)
+    grad_low = grad_flat.astype(jnp.bfloat16)
+    grad_down_full = jnp.einsum(
+        "tf,td->fd", hidden_low, grad_low, preferred_element_type=jnp.float32
+    )
+    grad_down_bias = jnp.sum(grad_flat, axis=0)
+    d_hidden = jnp.einsum("td,fd->tf", grad_low, weights_down, preferred_element_type=jnp.float32)
+    d_pre = pull_gelu(d_hidden)[0]
+    d_pre_low = d_pre.astype(jnp.bfloat16)
+    grad_hidden_bias = jnp.sum(d_pre, axis=0)
+    grad_up_full = jnp.einsum(
+        "td,tf->df", normed_two_low, d_pre_low, preferred_element_type=jnp.float32
+    )
+    d_two_part = jnp.einsum("tf,df->td", d_pre_low, weights_up, preferred_element_type=jnp.float32)
+    d_two = lax.psum(d_two_part.astype(jnp.bfloat16), "tp").astype(jnp.float32)
+    d_flat_two, grad_gain_two, grad_offset_two = pull_two(d_two)
+    d_resid = grad_flat + d_flat_two
+    grad_proj_bias = jnp.sum(d_resid, axis=0)
+    d_branch = d_resid.astype(jnp.bfloat16)
+    grad_proj_full = jnp.einsum(
+        "tc,td->cd", context_low, d_branch, preferred_element_type=jnp.float32
+    )
+    d_context = (
+        jnp.einsum("td,cd->tc", d_branch, weights_proj, preferred_element_type=jnp.float32)
+        .astype(jnp.bfloat16)
+        .reshape(head_shape)
+    )
+    d_probs = jnp.einsum(
+        "wihc,wjhc->whij", d_context, value_low, preferred_element_type=jnp.float32
+    )
+    d_value_low = jnp.einsum(
+        "whij,wihc->wjhc", prob_low, d_context, preferred_element_type=jnp.float32
+    ).astype(jnp.bfloat16)
+    d_scores = prob_rows * (d_probs - jnp.sum(prob_rows * d_probs, axis=-1, keepdims=True))
+    d_pos = jnp.sum(d_scores, axis=0)
+    d_scaled = (d_scores * HD ** (-0.5)).astype(jnp.bfloat16)
+    d_query_low = jnp.einsum(
+        "whij,wjhc->wihc", d_scaled, key_low, preferred_element_type=jnp.float32
+    ).astype(jnp.bfloat16)
+    d_key_low = jnp.einsum(
+        "whij,wihc->wjhc", d_scaled, query_low, preferred_element_type=jnp.float32
+    ).astype(jnp.bfloat16)
+    d_heads = jnp.stack([d_query_low, d_key_low, d_value_low]).reshape(3, -1, local_width)
+    grad_qkv_full = jnp.einsum(
+        "td,ktc->kdc", normed_one_low, d_heads, preferred_element_type=jnp.float32
+    )
+    grad_head_bias = jnp.stack(
+        [
+            jnp.sum(d_heads[0].astype(jnp.float32), axis=0),
+            jnp.sum(d_heads[2].astype(jnp.float32), axis=0),
+        ]
+    ).reshape(2, heads_here, HD)
+    d_one_part = jnp.einsum("ktc,kdc->td", d_heads, weights_qkv, preferred_element_type=jnp.float32)
+    d_one = lax.psum(d_one_part.astype(jnp.bfloat16), "tp").astype(jnp.float32)
+    d_flat_one, grad_gain_one, grad_offset_one = pull_one(d_one)
+    grad_input = out_grad + roll_out((d_flat_two + d_flat_one).astype(jnp.bfloat16)).astype(
+        jnp.float32
+    )
+    table_part = table_grad(d_pos, rel_index, rel_table.shape[0])
+    grad_norm_full = jnp.stack(
+        [
+            grad_gain_one,
+            grad_offset_one,
+            grad_proj_bias,
+            grad_gain_two,
+            grad_offset_two,
+            grad_down_bias,
+        ]
+    )
+    grad_list = (
+        grad_qkv_full,
+        grad_proj_full,
+        grad_up_full,
+        grad_down_full,
+        grad_norm_full,
+        grad_head_bias,
+        grad_hidden_bias.reshape(-1, HD),
+    )
+    g_qkv, g_proj, g_up, g_down, g_norm, g_heads, g_hidden = shard_sum(band_sum(grad_list))
+    d_shard = w_qkv.shape[1]
+    hidden_here = w_up.shape[1]
+    keep = 1.0 - DECAY_RATE
+    sq_qkv = g_qkv * g_qkv
+    sq_proj = g_proj * g_proj
+    sq_up = g_up * g_up
+    sq_down = g_down * g_down
+    stat_rq = place(
+        (keep * jnp.sum(sq_qkv, axis=2) / D + first_tp * (DECAY_RATE * row_qkv + keep * STAT_EPS))
+        * first_ctx,
+        fsdp_at,
+        D,
+    )
+    stat_cq = place(
+        (keep * jnp.sum(sq_qkv, axis=1) / D + first_fsdp * (DECAY_RATE * col_qkv + keep * STAT_EPS))
+        * first_ctx,
+        tp_at,
+        D,
+    )
+    stat_rp = place(
+        (
+            keep * jnp.sum(sq_proj, axis=1) / D
+            + first_fsdp * (DECAY_RATE * row_proj + keep * STAT_EPS)
+        )
+        * first_ctx,
+        tp_at,
+        D,
+    )
+    stat_cp = place(
+        (keep * jnp.sum(sq_proj, axis=0) / D + first_tp * (DECAY_RATE * col_proj + keep * STAT_EPS))
+        * first_ctx,
+        fsdp_at,
+        D,
+    )
+    stat_ru = place(
+        (keep * jnp.sum(sq_up, axis=1) / FF + first_tp * (DECAY_RATE * row_up + keep * STAT_EPS))
+        * first_ctx,
+        fsdp_at,
+        D,
+    )
+    stat_cu = place(
+        (keep * jnp.sum(sq_up, axis=0) / D + first_fsdp * (DECAY_RATE * col_up + keep * STAT_EPS))
+        * first_ctx,
+        tp_at,
+        FF,
+    )
+    stat_rd = place(
+        (
+            keep * jnp.sum(sq_down, axis=1) / D
+            + first_fsdp * (DECAY_RATE * row_down + keep * STAT_EPS)
+        )
+        * first_ctx,
+        tp_at,
+        FF,
+    )
+    stat_cd = place(
+        (
+            keep * jnp.sum(sq_down, axis=0) / FF
+            + first_tp * (DECAY_RATE * col_down + keep * STAT_EPS)
+        )
+        * first_ctx,
+        fsdp_at,
+        D,
+    )
+    table_whole = place(table_part, tp_at, HEADS)
+    master_sq = jnp.concatenate(
+        [
+            jnp.stack(
+                [
+                    jnp.sum(w_qkv * w_qkv),
+                    jnp.sum(w_proj * w_proj),
+                    jnp.sum(w_up * w_up),
+                    jnp.sum(w_down * w_down),
+                ]
+            )
+            * first_ctx,
+            jnp.sum(norm_vecs * norm_vecs, axis=1) * first_ctx * first_tp,
+            jnp.sum(head_bias * head_bias, axis=(1, 2)) * first_ctx,
+            jnp.sum(hidden_bias * hidden_bias)[None] * first_ctx,
+            jnp.sum(rel_table * rel_table)[None] * first_ctx * first_fsdp,
+        ]
+    )
+    (
+        full_rq,
+        full_cq,
+        full_rp,
+        full_cp,
+        full_ru,
+        full_cu,
+        full_rd,
+        full_cd,
+        table_sum,
+        master_total,
+    ) = lax.psum(
+        (
+            stat_rq,
+            stat_cq,
+            stat_rp,
+            stat_cp,
+            stat_ru,
+            stat_cu,
+            stat_rd,
+            stat_cd,
+            table_whole,
+            master_sq,
+        ),
+        ("fsdp", "ctx", "tp"),
+    )
+    u_qkv = factored(
+        g_qkv,
+        own_part(full_rq, fsdp_at, d_shard),
+        own_part(full_cq, tp_at, local_width),
+        jnp.mean(full_rq, axis=1)[:, None, None],
+    )
+    u_proj = factored(
+        g_proj,
+        own_part(full_rp, tp_at, local_width),
+        own_part(full_cp, fsdp_at, d_shard),
+        jnp.mean(full_rp),
+    )
+    u_up = factored(
+        g_up,
+        own_part(full_ru, fsdp_at, d_shard),
+        own_part(full_cu, tp_at, hidden_here),
+        jnp.mean(full_ru),
+    )
+    u_down = factored(
+        g_down,
+        own_part(full_rd, tp_at, hidden_here),
+        own_part(full_cd, fsdp_at, d_shard),
+        jnp.mean(full_rd),
+    )
+    g_table = own_part(table_sum, tp_at, heads_here)
+    state_norm_new, u_norm = plain_stats(g_norm, state_norm)
+    state_heads_new, u_heads = plain_stats(g_heads, state_heads)
+    state_hidden_new, u_hidden = plain_stats(g_hidden, state_hidden)
+    state_table_new, u_table = plain_stats(g_table, state_table)
+    local_sq = (
+        jnp.sum(u_qkv * u_qkv)
+        + jnp.sum(u_proj * u_proj)
+        + jnp.sum(u_up * u_up)
+        + jnp.sum(u_down * u_down)
+        + jnp.sum(u_heads * u_heads)
+        + jnp.sum(u_hidden * u_hidden)
+        + first_tp * jnp.sum(u_norm * u_norm)
+        + first_fsdp * jnp.sum(u_table * u_table)
+    )
+    total_sq = lax.psum(local_sq, ("fsdp", "tp"))
+    count_all = 4 * D * D + 2 * D * FF + 8 * D + FF + RELP * HEADS
+    clip_rms = jnp.sqrt(total_sq / count_all)
+    factor = 1.0 / jnp.maximum(1.0, clip_rms / CLIP_LEVEL)
+    counts = jnp.array(
+        [3 * D * D, D * D, D * FF, FF * D, D, D, D, D, D, D, D, D, FF, RELP * HEADS], jnp.float32
+    )
+    scales = jnp.sqrt(master_total / counts + STAT_EPS)
+    new_qkv = w_qkv - STEP_RATE * scales[0] * factor * u_qkv
+    new_proj = w_proj - STEP_RATE * scales[1] * factor * u_proj
+    new_up = w_up - STEP_RATE * scales[2] * factor * u_up
+    new_down = w_down - STEP_RATE * scales[3] * factor * u_down
+    new_norm = norm_vecs - STEP_RATE * scales[4:10][:, None] * factor * u_norm
+    new_heads = head_bias - STEP_RATE * scales[10:12][:, None, None] * factor * u_heads
+    new_hidden = hidden_bias - STEP_RATE * scales[12] * factor * u_hidden
+    new_table = rel_table - STEP_RATE * scales[13] * factor * u_table
+    return (
+        block_out,
+        grad_input,
+        g_qkv,
+        g_proj,
+        g_up,
+        g_down,
+        g_norm,
+        g_heads,
+        g_hidden,
+        g_table,
+        new_qkv,
+        new_proj,
+        new_up,
+        new_down,
+        new_norm,
+        new_heads,
+        new_hidden,
+        new_table,
+        new_qkv.astype(jnp.bfloat16),
+        new_proj.astype(jnp.bfloat16),
+        new_up.astype(jnp.bfloat16),
+        new_down.astype(jnp.bfloat16),
+        own_part(full_rq, fsdp_at, d_shard),
+        own_part(full_cq, tp_at, local_width),
+        own_part(full_rp, tp_at, local_width),
+        own_part(full_cp, fsdp_at, d_shard),
+        own_part(full_ru, fsdp_at, d_shard),
+        own_part(full_cu, tp_at, hidden_here),
+        own_part(full_rd, tp_at, hidden_here),
+        own_part(full_cd, fsdp_at, d_shard),
+        state_norm_new,
+        state_heads_new,
+        state_hidden_new,
+        state_table_new,
+        clip_rms,
+    )
+
+
 def solution(mesh):
+    line_of_four = mesh.shape["fsdp"] == 4 and mesh.shape["tp"] == 4 and mesh.shape["ctx"] == 2
     return jax.shard_map(
-        per_device,
+        per_device if line_of_four else per_device_plain,
         mesh=mesh,
         in_specs=(
             P("fsdp", "ctx", None, None),

time: 784 us -> 702 us (0.90)
  Pallas kernels: 0 us -> 63.9 us
  blocking collectives: 112 us -> 53.5 us
  waiting for transfers between devices: 272 us -> 235 us
  matrix products: 116 us -> 88.2 us
  local copies, waits for them, and re-layouts: 162 us -> 137 us
    psum x1, waiting for transfers between devices: 65.7 us -> 0.01 us  [per_device(): lax.psum(mixed_part.astype(jnp.bfloat16), 'tp').astype(jnp.float32)]
    pallas_call x0 -> x1, Pallas kernels: none -> 63.9 us  [call(): pl.pallas_call(body, out_shape=[jax.ShapeDtypeStruct(s, t) for s, t in ou...]
    all_gather x5 -> x0, blocking collectives: 34.2 us -> none  [the longest x1 11.4 us: per_device(): lax.all_gather(w_qkv.astype(jnp.bfloat16), 'fsdp', axis=1, tiled=True)]
    psum x1, waiting for transfers between devices: 17.9 us -> 46.1 us  [band_sum(): lax.psum((grad_list[0], grad_list[1], grad_list[2], grad_list[3], grad_li...]
    psum x1, blocking collectives: 35.6 us -> 8.6 us  [band_sum(): lax.psum((grad_list[0], grad_list[1], grad_list[2], grad_list[3], grad_li...]
    dot_general x17 -> x0, matrix products: 21.6 us -> none  [the longest x12 11.4 us: lookup(): return jnp.dot(one_hot, table_low, preferred_element_type=jnp.float32)]
    reduce_scatter x1, waiting for transfers between devices: 0.01 us -> 19.1 us  [shard_sum(): lax.psum_scatter(grad_list[3], 'fsdp', scatter_dimension=1, tiled=True)]
    dynamic_update_slice x24 -> x0, local copies, waits for them, and re-layouts: 18.4 us -> none  [table_lookup(): looked = lax.map(lookup, index_blocks)]
  transfers between devices with their start and end apart: 16 -> 11, of which waited for: 6 -> 5; matrix products, arithmetic and copies ran while one was open for 30% -> 30% of each run, Pallas kernels for 0% -> 0%
where the time goes in v2:
time: 702 us; the launch traced here: 690 us
  waiting for transfers between devices  235 us (33%)
  local copies, waits for them, and re-layouts  137 us (20%)
  matrix products  88.2 us (13%)
  other arithmetic  78.5 us (11%)
  Pallas kernels  63.9 us (9%)
  blocking collectives  53.5 us (8%)
  between operations  30.3 us (4%)
    psum x1, waiting for transfers between devices, per_device(): lax.psum((stat_rq, stat_cq, stat_rp, stat_cp, stat_ru, stat_cu, stat_rd,...  125 us
    pallas_call x1, Pallas kernels, call(): pl.pallas_call(body, out_shape=[jax.ShapeDtypeStruct(s, t) for s, t in ou...  63.9 us
    unnamed x216, local copies, waits for them, and re-layouts  49.2 us
    psum x1, waiting for transfers between devices, band_sum(): lax.psum((grad_list[0], grad_list[1], grad_list[2], grad_list[3], grad_li...  46.1 us
    dot_general x12, matrix products, accumulate(): lax.dot_general(one_hot, grad_block, (((0,), (0,)), ((), ())), precision=...  35.1 us
    psum x1, waiting for transfers between devices, per_device(): d_two = lax.psum(d_two_part.astype(jnp.bfloat16), 'tp').astype(jnp.float32)  33.7 us
    psum x1, blocking collectives, per_device(): total_sq = lax.psum(local_sq, ('fsdp', 'tp'))  31.7 us
    dynamic_slice x24, local copies, waits for them, and re-layouts, table_grad(): lax.scan(accumulate, jnp.zeros((table_rows, heads_here), jnp.float32), (i...  29.8 us
  transfers between devices with their start and end apart: 11, of which 5 were waited for; matrix products, arithmetic and copies ran while one was open for 30% of the time, Pallas kernels for 0%

profile of v2, /device:TPU:0, one launch (start us, length us, event | category | flops | bytes accessed | tf_op | source)
XLA Modules:
  0.0 689.7 jit_solution(1886462317903238949)
XLA Ops:
  14.8 63.9 %attention_forward.1 = (bf16[3,768,192]{2,1,0:T(8,128)(2,1)}, bf16[192,768]{1,0:T(8,128)(2,1)}, bf16[768,768]{1,0:T(8,128)(2,1)}, bf16[768,768]{1,0:T(8,128)(2,1...) custom-call(bf16[2,12,24,768]{3,2,1,0:T(8,128)(2,1)} %feat.1, ...), custom_call_target="tpu_custom_call" | custom-call | tf_op jit(solution)/shard_map/attention_forward/pallas_call | solution.py:525
  96.4 3.0 fusion.60
  99.4 6.3 fusion.66
  119.5 33.7 %all-reduce.15.cloned.1.call-done = bf16[576,768]{1,0:T(8,128)(2,1)} async-done(((bf16[576,768]{1,0:T(8,128)(2,1)}), bf16[576,768]{1,0:T(8,128)(2,1)}) %all-reduce.15.cloned.1.call-update) | async-done | bytes 884752 | tf_op jit(solution)/shard_map/psum | solution.py:1054
  153.2 3.2 fusion.16
  162.9 3.6 fusion.52
  166.5 7.4 %convert_reduce_fusion.3 = (f32[6,32]{1,0:T(8,128)}, bf16[4,144,6,32]{1,3,2,0:T(8,128)(2,1)}) fusion(bf16[4,144,6,32]{1,3,2,0:T(8,128)(2,1)} %bitcast.131, f32[4,6,144,144]{3,2,1,0:T(8,128)} %get-tuple-element.83, f32[4,6,144,144]{3,2,1,0:T(8,128)} %fusion.52), kind=kOutput, calls=%fused_computation.82 | convolution fusion | flops 34674000 | bytes 4424448 | tf_op jit(solution)/shard_map/whij,wjhc->wihc/dot_general | solution.py:1076
  180.8 6.9 %fusion.32 = bf16[4,144,6,32]{1,3,2,0:T(8,128)(2,1)} fusion(bf16[4,144,6,32]{1,3,2,0:T(8,128)(2,1)} %bitcast.130, f32[4,6,144,144]{3,2,1,0:T(8,128)} %get-tuple-element.83, f32[4,6,144,144]{3,2,1,0:T(8,128)} %fusion.52), kind=kOutput, calls=%fused_computation.71 | convolution fusion | flops 34453008 | bytes 4423680 | tf_op jit(solution)/shard_map/whij,wihc->wjhc/dot_general | solution.py:1079
  191.8 3.2 convert_reduce_fusion.2
  201.9 3.2 bitcast_convert_fusion
  205.1 3.5 convolution_bitcast_fusion
  208.6 4.2 copy.160
  212.8 4.7 reshape.307
  217.8 4.6 fusion.48
  222.5 4.0 fusion.75
  252.7 6.9 fusion.72
  263.8 64.9 %while.11 = (s32[]{:T(128)}, f32[529,6]{0,1:T(8,128)}, s32[12,1728]{1,0:T(8,128)}, f32[12,1728,6]{1,0,2:T(8,128)}, s32[]{:T(128)}, /*index=5*/s32[]{:T(128)}) while((s32[]{:T(128)}, f32[529,6]{0,1:T(8,128)}, s32[12,1728]{1,0:T(8,128)}, f32[12,1728,6]{1,0,2:T(8,128)}, s32[]{:T(128)}, /*index=5*/s32[]{:T(128)}) %tuple.73), condition=%wide.region_37.38_spmd.clone, body=%wide.region_36.37_spmd.clone.sunk | while | flops 66736528 | bytes 170639 | solution.py:113
  266.3 2.9 fusion.98
  271.7 2.9 fusion.98
  277.1 2.9 fusion.98
  282.6 2.9 fusion.98
  288.0 2.9 fusion.98
  298.8 2.9 fusion.98
  320.4 2.9 fusion.98
  331.5 13.2 %all-reduce.6 = (f32[2,6,32]{2,1,0:T(8,128)}, f32[24,32]{1,0:T(8,128)}) all-reduce(f32[2,6,32]{2,1,0:T(8,128)S(1)} %pad_maximum_fusion.2, f32[24,32]{1,0:T(8,128)} %reshape.300), channel_id=7, replica_groups=mesh['fsdp'=4,'ctx'=2,'tp'=4] {'fsdp'}, use_global_device_ids=true, to_apply=%region_31.32.clone | all-reduce | flops 1152 | bytes 9216
  364.9 19.1 %reduce-scatter.16.cloned.1.call-done = f32[768,192]{0,1:T(8,128)} async-done(((f32[768,768]{0,1:T(8,128)}), f32[768,192]{0,1:T(8,128)}) %reduce-scatter.16.cloned.1.call-update) | async-done | bytes 589840 | tf_op jit(solution)/shard_map/reduce_scatter | solution.py:143
  396.1 11.8 %reduce-scatter.22.cloned.1.call-done = f32[192,6]{1,0:T(8,128)} async-done(((f32[768,6]{1,0:T(8,128)}), f32[192,6]{1,0:T(8,128)}) %reduce-scatter.22.cloned.1.call-update) | async-done | bytes 4624
  408.9 8.6 %all-reduce.7 = (f32[6,192]{1,0:T(8,128)S(1)}, f32[2,6,8]{2,1,0:T(8,128)S(1)}, f32[24,8]{1,0:T(8,128)S(1)}) all-reduce(f32[6,192]{1,0:T(8,128)S(1)} %copy.165, f32[2,6,8]{2,1,0:T(8,128)S(1)} %copy-done.58, f32[24,8]{1,0:T(8,128)S(1)} %copy-done.40), channel_id=1, replica_groups=mesh['fsdp'=4,'ctx'=2,'tp'=4] {'ctx'}, use_global_device_ids=true, to_apply=%region_26.27 | all-reduce | flops 1440 | bytes 11520 | tf_op jit(solution)/shard_map/psum | solution.py:151
  425.0 46.1 %all-reduce.19.cloned.1.call-done = (f32[3,192,192]{1,2,0:T(8,128)}, f32[192,192]{1,0:T(8,128)}, f32[192,768]{1,0:T(8,128)}, f32[768,192]{0,1:T(8,128)}) async-done(((f32[3,192,192]{1,2,0:T(8,128)}, f32[192,192]{1,0:T(8,128)}, f32[192,768]{1,0:T(8,128)}, f32[768,192]{0,1:T(8,128)}), (f32[3,192,192]{1,2,0:T(8,128)}, f32[192,192]{1,0:T(8,128)}, f32[192,768]{1,0:T(8,128)}, ...) | async-done | bytes 1769488 | tf_op jit(solution)/shard_map/psum | solution.py:151
  476.9 4.0 copy_add_fusion
  484.7 124.6 %all-reduce.17.cloned.1.call-done = (f32[529,24]{0,1:T(8,128)}, f32[14]{0:T(128)}, f32[3,768]{1,0:T(4,128)}, f32[3,768]{1,0:T(4,128)}, f32[768]{0:T(1024)}, /*in...) async-done(((f32[529,24]{0,1:T(8,128)}, f32[14]{0:T(128)}, f32[3,768]{1,0:T(4,128)}, f32[3,768]{1,0:T(4,128)}, f32[768]{0:T(1024)}, ...) | async-done | bytes 106152 | tf_op jit(solution)/shard_map/psum | solution.py:1212
  632.7 31.7 %psum.167 = f32[]{:T(128)} all-reduce(f32[]{:T(128)S(6)} %add.372), channel_id=1, replica_groups=mesh['fsdp'=4,'ctx'=2,'tp'=4] {'fsdp','tp'}, use_global_device_ids=true, to_apply=%region_76.77 | all-reduce | flops 1 | bytes 8 | tf_op jit(solution)/shard_map/psum | solution.py:1266
  (416 shorter events, 217.6 us)
Async XLA Ops:
  7.3 145.9 %all-reduce.15.cloned.1.call-start = ((), (), s32[]{:S(2)}) async-start(), calls=%async_computation.5 | async-start | bytes 1769472 | tf_op jit(solution)/shard_map/psum | solution.py:1054
  108.5 239.0 %reduce-scatter.20.cloned.1.call-start = ((), (), s32[]{:S(2)}) async-start(), calls=%async_computation.9 | async-start | bytes 983040
  180.7 168.5 %all-reduce.21.cloned.1.call-start = ((), (), s32[]{:S(2)}) async-start(), calls=%async_computation.13 | async-start | bytes 3538944 | tf_op jit(solution)/shard_map/psum | solution.py:1037
  205.1 157.3 %reduce-scatter.18.cloned.1.call-start = ((), (), s32[]{:S(2)}) async-start(), calls=%async_computation.8 | async-start | bytes 2457600
  217.5 147.3 %reduce-scatter.14.cloned.1.call-start = ((), (), s32[]{:S(2)}) async-start(), calls=%async_computation.6 | async-start | bytes 2949120 | tf_op jit(solution)/shard_map/reduce_scatter | solution.py:142
  222.4 161.6 %reduce-scatter.16.cloned.1.call-start = ((), (), s32[]{:S(2)}) async-start(), calls=%async_computation.7 | async-start | bytes 2949120 | tf_op jit(solution)/shard_map/reduce_scatter | solution.py:143
  226.5 181.4 %reduce-scatter.22.cloned.1.call-start = ((), (), s32[]{:S(2)}) async-start(), calls=%async_computation.10 | async-start | bytes 491520
  359.6 111.5 %all-reduce.19.cloned.1.call-start = ((), (), s32[]{:S(2)}) async-start(), calls=%async_computation.12 | async-start | bytes 3932160 | tf_op jit(solution)/shard_map/psum | solution.py:151
  384.0 225.2 %all-reduce.17.cloned.1.call-start = ((), (), s32[]{:S(2)}) async-start(), calls=%async_computation.11 | async-start | bytes 254976 | tf_op jit(solution)/shard_map/psum | solution.py:1212
  392.7 29.9 %collective-permute-start = (bf16[2,6,24,768]{3,0,2,1:T(2,128)(2,1)S(1)}, bf16[2,6,24,768]{3,0,2,1:T(2,128)(2,1)S(1)}, u32[]{:S(2)}, u32[]{:S(2)}) collective-permute-start(bf16[2,6,24,768]{3,0,2,1:T(2,128)(2,1)S(1)} %fusion.45), channel_id=1, source_target_pairs={{0,4},{4,0},{1,5},{5,1},{2,6},{6,2},{3,7},{7,3},{8,12},{12,8},{9,1... | collective-permute-start | bytes 1327112 | tf_op jit(solution)/shard_map/ppermute | solution.py:30
  395.5 81.4 %collective-permute-start.1 = (bf16[2,6,24,768]{3,0,2,1:T(2,128)(2,1)}, bf16[2,6,24,768]{3,0,2,1:T(2,128)(2,1)}, u32[]{:S(2)}, u32[]{:S(2)}) collective-permute-start(bf16[2,6,24,768]{3,0,2,1:T(2,128)(2,1)} %fusion.44), channel_id=1, source_target_pairs={{0,4},{4,0},{1,5},{5,1},{2,6},{6,2},{3,7},{7,3},{8,12},{12,8},{9,1... | collective-permute-start | bytes 1327112 | tf_op jit(solution)/shard_map/ppermute | solution.py:30
  417.5 260.5 %copy-start.59 = (f32[6,192]{1,0:T(8,128)}, f32[6,192]{1,0:T(8,128)S(1)}, u32[]{:S(2)}) copy-start(f32[6,192]{1,0:T(8,128)S(1)} %get-tuple-element.370) | copy-start | bytes 13828
  421.9 256.1 %copy-start.60 = (f32[6,192]{1,0:T(8,128)}, f32[6,192]{1,0:T(8,128)S(1)}, u32[]{:S(2)}) copy-start(f32[6,192]{1,0:T(8,128)S(1)} %get-tuple-element.394) | copy-start | bytes 13828
  425.0 50.8 %copy-start.85 = (f32[192]{0:T(256)S(1)}, f32[192]{0:T(256)}, u32[]{:S(2)}) copy-start(f32[192]{0:T(256)} %param.43) | copy-start | bytes 2308
  425.0 50.9 %copy-start.79 = (f32[768]{0:T(1024)S(1)}, f32[768]{0:T(1024)}, u32[]{:S(2)}) copy-start(f32[768]{0:T(1024)} %param.44) | copy-start | bytes 9220
  425.0 51.0 %copy-start.86 = (f32[192]{0:T(256)S(1)}, f32[192]{0:T(256)}, u32[]{:S(2)}) copy-start(f32[192]{0:T(256)} %param.46) | copy-start | bytes 2308
  425.0 51.1 %copy-start.80 = (f32[768]{0:T(1024)S(1)}, f32[768]{0:T(1024)}, u32[]{:S(2)}) copy-start(f32[768]{0:T(1024)} %param.45) | copy-start | bytes 9220
  482.3 139.1 %copy-start.62 = (f32[529,6]{0,1:T(8,128)S(1)}, f32[529,6]{0,1:T(8,128)}, u32[]{:S(2)}) copy-start(f32[529,6]{0,1:T(8,128)} %param.50) | copy-start | bytes 38092
  482.3 140.5 %copy-start.90 = (f32[14]{0:T(128)S(1)}, f32[14]{0:T(128)}, u32[]{:S(2)}) copy-start(f32[14]{0:T(128)} %constant.196) | copy-start | bytes 172
  483.6 140.7 %copy-start.17 = (f32[192,192]{1,0:T(8,128)S(1)}, f32[192,192]{1,0:T(8,128)}, u32[]{:S(2)}) copy-start(f32[192,192]{1,0:T(8,128)} %get-tuple-element.367) | copy-start | bytes 442372
  483.6 142.8 %copy-start.7 = (f32[192,768]{1,0:T(8,128)S(1)}, f32[192,768]{1,0:T(8,128)}, u32[]{:S(2)}) copy-start(f32[192,768]{1,0:T(8,128)} %get-tuple-element.368) | copy-start | bytes 1769476
  483.6 182.3 %copy-start.18 = (f32[3,192,192]{1,2,0:T(8,128)S(1)}, f32[3,192,192]{1,2,0:T(8,128)}, u32[]{:S(2)}) copy-start(f32[3,192,192]{1,2,0:T(8,128)} %copy.144) | copy-start | bytes 1327108
  610.0 57.1 %copy-start.45 = (f32[3,192]{1,0:T(4,128)}, f32[3,192]{1,0:T(4,128)S(1)}, u32[]{:S(2)}) copy-start(f32[3,192]{1,0:T(4,128)S(1)} %constant_dynamic-slice_fusion.4) | copy-start | bytes 6916
  611.6 55.5 %copy-start.46 = (f32[3,192]{1,0:T(4,128)}, f32[3,192]{1,0:T(4,128)S(1)}, u32[]{:S(2)}) copy-start(f32[3,192]{1,0:T(4,128)S(1)} %constant_dynamic-slice_fusion.3) | copy-start | bytes 6916
  612.4 57.5 %copy-start.74 = (f32[192]{0:T(256)}, f32[192]{0:T(256)S(1)}, u32[]{:S(2)}) copy-start(f32[192]{0:T(256)S(1)} %dynamic_slice.46) | copy-start | bytes 2308
  614.4 55.5 %copy-start.75 = (f32[192]{0:T(256)}, f32[192]{0:T(256)S(1)}, u32[]{:S(2)}) copy-start(f32[192]{0:T(256)S(1)} %dynamic_slice.47) | copy-start | bytes 2308
  615.2 56.3 %copy-start.76 = (f32[192]{0:T(256)}, f32[192]{0:T(256)S(1)}, u32[]{:S(2)}) copy-start(f32[192]{0:T(256)S(1)} %dynamic_slice.48) | copy-start | bytes 2308
  618.6 52.9 %copy-start.47 = (f32[768]{0:T(1024)}, f32[768]{0:T(1024)S(1)}, u32[]{:S(2)}) copy-start(f32[768]{0:T(1024)S(1)} %dynamic_slice.49) | copy-start | bytes 9220
  619.3 54.0 %copy-start.48 = (f32[768]{0:T(1024)}, f32[768]{0:T(1024)S(1)}, u32[]{:S(2)}) copy-start(f32[768]{0:T(1024)S(1)} %dynamic_slice.50) | copy-start | bytes 9220
  621.4 51.9 %copy-start.77 = (f32[192]{0:T(256)}, f32[192]{0:T(256)S(1)}, u32[]{:S(2)}) copy-start(f32[192]{0:T(256)S(1)} %dynamic_slice.51) | copy-start | bytes 2308
  622.8 55.9 %copy-start.33 = (f32[529,6]{0,1:T(8,128)}, f32[529,6]{0,1:T(8,128)S(1)}, u32[]{:S(2)}) copy-start(f32[529,6]{0,1:T(8,128)S(1)} %get-tuple-element.397) | copy-start | bytes 38092
  622.8 55.9 %copy-start.34 = (f32[529,6]{0,1:T(8,128)}, f32[529,6]{0,1:T(8,128)S(1)}, u32[]{:S(2)}) copy-start(f32[529,6]{0,1:T(8,128)S(1)} %get-tuple-element.373) | copy-start | bytes 38092
  (71 other events, 575.0 us)
Sparse Core Ops, SparseCore 0:
  108.6 44.5 all-reduce.14
  180.9 22.2 reduce-scatter.19
  205.6 75.4 all-reduce.20
  283.6 29.3 reduce-scatter.17
  315.4 33.3 reduce-scatter.13
  351.2 32.8 reduce-scatter.15
  387.1 20.8 reduce-scatter.21
  411.0 60.1 all-reduce.18
  479.9 129.3 all-reduce.16

commit v3 on v2

--- a/solution.py
+++ b/solution.py
@@ -338,7 +338,7 @@
 def attention_forward_body(
     feat, og, wq, wp, wu, wd, small, table_t, ridx, regr, regc,
     wq_o, wp_o, wu_o, wd_o, rows_o, xw_o, ogw_o, n1_o, q_o, k_o, v_o, probs_o, ctx_o, br_o,
-    sm_g, wp_g, wd_g, fh, gh, bias_s, row_tmp,
+    sm_g, wp_g, fh, gh, bias_s, row_tmp,
     ls_a, ls_b, ls_c, ls_d, ls_e, ls_f, ls_g, ls_h, ls_i, ls_j, ls_k,
     w_send, w_recv, h_send, h_recv,
 ):
@@ -361,7 +361,7 @@
     sm_g[f] = small[...].astype(BF)
     wp_g[f] = wp[...].astype(BF)
     wu_o[block(f), :] = wu[...].astype(BF)
-    wd_g[f] = wd[...].astype(BF)
+    wd_o[block(f), :] = wd[...].astype(BF)
     pl.semaphore_wait(barrier, 3 + line.greet_count())
 
     items = [
@@ -369,7 +369,7 @@
         lambda at: wq_o.at[:, block(at), :],
         lambda at: wp_g.at[at],
         lambda at: wu_o.at[block(at), :],
-        lambda at: wd_g.at[at],
+        lambda at: wd_o.at[block(at), :],
     ]
 
     def copy_of(n, kind, at, where):
@@ -503,7 +503,6 @@
     line.hand(windows - 1)
     gathered(3)
     gathered(4)
-    wd_o[...] = jnp.concatenate([wd_g[n] for n in range(4)], axis=1)
     for i in range(images):
         halo_g[i].wait_recv()
         window_rows(
@@ -559,7 +558,7 @@
     ridx = jnp.pad(rel_index, ((0, 0), (0, 256 - TOK)))
     region_win = to_windows(regions[..., None])[..., 0]
     outs = [
-        ((3, D, width), BF), ((width, D), BF), ((D, hidden), BF), ((hidden, D), BF), ((16, D), F32),
+        ((3, D, width), BF), ((width, D), BF), ((D, hidden), BF), ((D, hidden), BF), ((16, D), F32),
         ((windows, TOK, D), F32), ((windows, TOK, D), F32), ((windows, TOK, D), BF),
         ((windows, TOK, width), BF), ((windows, TOK, width), BF), ((windows, TOK, width), BF),
         ((windows, heads, TOK, TOK), F32), ((windows, TOK, width), BF),
@@ -568,7 +567,6 @@
     scratch = [
         pltpu.VMEM((4, 16, shard), BF),
         pltpu.VMEM((4, width, shard), BF),
-        pltpu.VMEM((4, hidden, shard), BF),
         pltpu.VMEM((images, SHIFT, 24, D), BF),
         pltpu.VMEM((images, SHIFT, 24, D), F32),
         pltpu.VMEM((heads, TOK, 256), F32),
@@ -580,8 +578,766 @@
         pltpu.SemaphoreType.DMA((2 * images,)),
     ]
     call = vmem_call(attention_forward_body, outs, scratch, "attention_forward", 1)
-    return call(features, out_grad, w_qkv, w_proj, w_up, w_down, small, table_t, ridx,
+    return call(features, out_grad, w_qkv, w_proj, w_up, w_down.T, small, table_t, ridx,
                 region_win[:, None, :], region_win[:, :, None])
+
+
+def feed_forward_body(
+    rows, wu, wd, xw, ogw, br,
+    gu_o, gd_o, dft_o, dbr_o, mix_o, sums_o,
+    n2_s, hid_s, dpl_s, ol_s, xhat_s, rstd_s, tot,
+    ls_a, ls_b, ls_c, ls_d, ls_e, ls_f, ls_g, ls_h, ls_i, ls_j, ls_k,
+):
+    windows = xw.shape[0]
+    line = LineSum.build((ls_a, ls_b, ls_c, ls_d, ls_e, ls_f, ls_g, ls_h, ls_i, ls_j, ls_k), tot)
+    barrier = pltpu.get_barrier_semaphore()
+    line.greet(barrier)
+    pl.semaphore_wait(barrier, line.greet_count())
+    sums_o[...] = jnp.zeros_like(sums_o)
+    bias_proj, gain, offset = rows[2:3, :], rows[3:4, :], rows[4:5, :]
+    bias_hidden = rows[8:9, :]
+
+    def spot(w):
+        return pl.ds(pl.multiple_of(w * TOK, TOK), TOK)
+
+    def window(w, carry):
+        resid = xw[w] + (jnp.concatenate([br[w, 0], br[w, 1]], axis=1).astype(F32) + bias_proj)
+        centred = resid - row_mean(resid)
+        rstd = lax.rsqrt(row_mean(centred * centred) + NORM_EPS)
+        xhat = centred * rstd
+        xhat_s[w] = xhat
+        rstd_s[w] = jnp.broadcast_to(rstd, (TOK, 128))
+        n2 = (xhat * gain + offset).astype(BF)
+        n2_s[spot(w), :] = n2
+        pre = dot(n2, wu[...]) + bias_hidden
+        cdf = 0.5 * (1.0 + lax.erf(pre * 0.7071067811865476))
+        slope = cdf + pre * (jnp.exp(-0.5 * (pre * pre)) * 0.3989422804014327)
+        hid_s[spot(w), :] = (pre * cdf).astype(BF)
+        ol = ogw[w].astype(BF)
+        ol_s[spot(w), :] = ol
+        d_pre = dot(ol, wd[...]) * slope
+        sums_o[6:7, :] = sums_o[6:7, :] + jnp.sum(d_pre, axis=0, keepdims=True)
+        dpl = d_pre.astype(BF)
+        dpl_s[spot(w), :] = dpl
+
+        @pl.when(w >= 1)
+        def _():
+            line.cross(w - 1)
+
+        line.put(w, dot_t(dpl, wu[...]))
+        line.start(w)
+        mixed = dot_t(hid_s[spot(w), :], wd[...])
+        mix_o[w, 0] = mixed[:, :HALF]
+        mix_o[w, 1] = mixed[:, HALF:]
+
+        @pl.when(w >= 1)
+        def _():
+            line.settle(w - 1)
+
+        @pl.when(w >= 2)
+        def _():
+            line.hand(w - 2)
+
+        return carry
+
+    def back(w):
+        line.arrive(w)
+        d_two = jnp.concatenate([tot[w, 0], tot[w, 1]], axis=1).astype(F32)
+        xhat = xhat_s[w]
+        e = d_two * gain
+        d_flat = (e - row_mean(e) - xhat * row_mean(e * xhat)) * rstd_s[w, :, 0:1]
+        og = ogw[w]
+        d_resid = og + d_flat
+        dft_o[w] = d_flat
+        dbr_o[w] = d_resid.astype(BF)
+        for n, term in ((2, d_resid), (3, d_two * xhat), (4, d_two), (5, og)):
+            sums_o[n : n + 1, :] = sums_o[n : n + 1, :] + jnp.sum(term, axis=0, keepdims=True)
+
+    def grad_chunk(m, carry):
+        part = pl.ds(pl.multiple_of(m * 256, 256), 256)
+        gd_o[part, :] = t_dot(ol_s[:, part], hid_s[...])
+        gu_o[part, :] = t_dot(n2_s[:, part], dpl_s[...])
+        return carry
+
+    lax.fori_loop(0, windows, window, 0)
+    chunks = hid_s.shape[1] // 256
+    line.cross(windows - 1)
+    line.hand(windows - 2)
+    lax.fori_loop(0, 1, grad_chunk, 0)
+    line.settle(windows - 1)
+    lax.fori_loop(1, 2, grad_chunk, 0)
+    line.hand(windows - 1)
+    lax.fori_loop(2, chunks, grad_chunk, 0)
+    for w in range(windows):
+        back(w)
+    for w in range(windows):
+        line.drain(w)
+
+
+def feed_forward(rows, wu, wd, xw, ogw, br):
+    windows, hidden = xw.shape[0], wu.shape[1]
+    outs = [
+        ((D, hidden), F32), ((D, hidden), F32), ((windows, TOK, D), F32),
+        ((windows, TOK, D), BF), ((windows, 2, TOK, HALF), F32), ((8, D), F32),
+    ]
+    scratch = [
+        pltpu.VMEM((windows * TOK, D), BF),
+        pltpu.VMEM((windows * TOK, hidden), BF),
+        pltpu.VMEM((windows * TOK, hidden), BF),
+        pltpu.VMEM((windows * TOK, D), BF),
+        pltpu.VMEM((windows, TOK, D), F32),
+        pltpu.VMEM((windows, TOK, 128), F32),
+        pltpu.VMEM((windows, 2, TOK, HALF), BF),
+        *LineSum.scratch(windows),
+    ]
+    return vmem_call(feed_forward_body, outs, scratch, "feed_forward", 2)(
+        rows, wu, wd, xw, ogw, br
+    )
+
+
+class ShardSum:
+    def __init__(self, block_of, out, refs):
+        self.block_of, self.out = block_of, out
+        self.snd1, self.rcv1, self.snd2, self.rcv2, self.snd3, self.rcv3, self.s, self.r = refs
+        f = lax.axis_index("fsdp")
+        core = lax.rem(f, 2)
+        self.f, self.core = f, core
+        self.near, self.far = f + 1 - 2 * core, lax.rem(f + 2, 4)
+        self.ctx = 1 - lax.axis_index("ctx")
+
+    @staticmethod
+    def scratch(shape):
+        return [
+            pltpu.VMEM((2, *shape), BF), pltpu.VMEM((2, *shape), BF),
+            pltpu.VMEM(shape, BF), pltpu.VMEM(shape, BF),
+            pltpu.VMEM(shape, BF), pltpu.VMEM(shape, BF),
+            pltpu.SemaphoreType.DMA((4,)), pltpu.SemaphoreType.DMA((4,)),
+        ]
+
+    def _near(self, x):
+        return remote(self.snd1.at[x], self.rcv1.at[x], self.s.at[x], self.r.at[x], {"fsdp": self.near})
+
+    def _far(self):
+        return remote(self.snd2, self.rcv2, self.s.at[2], self.r.at[2], {"fsdp": self.far})
+
+    def _ctx(self):
+        return remote(self.snd3, self.rcv3, self.s.at[3], self.r.at[3], {"ctx": self.ctx})
+
+    def start(self):
+        for x in range(2):
+            self.snd1[x] = self.block_of(2 * x + 1 - self.core).astype(BF)
+            self._near(x).start()
+
+    def pair(self):
+        for x in range(2):
+            self._near(x).wait_recv()
+        other = lax.div(self.far, 2)
+        self.snd2[...] = (self.block_of(self.far) + self.rcv1[other].astype(F32)).astype(BF)
+        self._far().start()
+
+    def cross(self):
+        self._far().wait_recv()
+        mine = lax.div(self.f, 2)
+        self.snd3[...] = (
+            self.block_of(self.f) + self.rcv1[mine].astype(F32) + self.rcv2[...].astype(F32)
+        ).astype(BF)
+        self._ctx().start()
+
+    def finish(self):
+        self._ctx().wait_recv()
+        self.out[...] = self.snd3[...].astype(F32) + self.rcv3[...].astype(F32)
+
+    def drain(self):
+        for x in range(2):
+            self._near(x).wait_send()
+        self._far().wait_send()
+        self._ctx().wait_send()
+
+
+def home_row(delta, row_tmp, image, r):
+    row_tmp[SHIFT : SHIFT + WIN, :] = delta[2 * image, r * WIN : (r + 1) * WIN, :]
+    row_tmp[SHIFT + WIN :, :] = delta[2 * image + 1, r * WIN : r * WIN + SHIFT, :]
+    row_tmp[:SHIFT, :] = delta[2 * image + 1, r * WIN + SHIFT : (r + 1) * WIN, :]
+    return row_tmp[...]
+
+
+def attention_backward_body(
+    rows, wq, wp, n1, q, k, v, probs, ctx, dbr, dft, xw, og, gu, gd, ridx_t, sums, mix,
+    gin_o, gq_o, gp_o, small_o, gu_o, gd_o, mixed_o,
+    dh_s, dpos_s, delta, row_tmp, halo_s, halo_r, tot, hist_s,
+    ls_a, ls_b, ls_c, ls_d, ls_e, ls_f, ls_g, ls_h, ls_i, ls_j, ls_k,
+    ua, ub, uc, ud, ue, uf, ug, uh,
+    da, db, dc, dd, de, df, dg, dh,
+    ms_b, ms_c, ms_d, ms_e, ms_f, ms_g, ms_h, ms_i, ms_j, ms_k,
+    h_send, h_recv,
+):
+    windows, heads = probs.shape[0], probs.shape[1]
+    images = windows // 2
+    width = q.shape[2]
+    c = lax.axis_index("ctx")
+    line = LineSum.build((ls_a, ls_b, ls_c, ls_d, ls_e, ls_f, ls_g, ls_h, ls_i, ls_j, ls_k), tot)
+    mix_line = LineSum.build((mix, ms_b, ms_c, ms_d, ms_e, ms_f, ms_g, ms_h, ms_i, ms_j, ms_k), mixed_o)
+    shard = gu_o.shape[0]
+    up = ShardSum(
+        lambda at: gu[pl.ds(pl.multiple_of(at * shard, shard), shard), :], gu_o,
+        (ua, ub, uc, ud, ue, uf, ug, uh),
+    )
+    down = ShardSum(
+        lambda at: gd[pl.ds(pl.multiple_of(at * shard, shard), shard), :], gd_o,
+        (da, db, dc, dd, de, df, dg, dh),
+    )
+    barrier = pltpu.get_barrier_semaphore()
+    greet(barrier, [{"fsdp": up.near}, {"fsdp": up.far}, {"ctx": 1 - c}])
+    line.greet(barrier)
+    dpos_s[...] = jnp.zeros_like(dpos_s)
+    small_o[...] = jnp.zeros_like(small_o)
+    small_o[0:8, :] = sums[...]
+    pl.semaphore_wait(barrier, 3 + line.greet_count())
+    down.start()
+    up.start()
+    gain = rows[0:1, :]
+    head_of = jnp.right_shift(lax.broadcasted_iota(jnp.int32, (1, width), 1), 5)
+
+    def window(w, carry):
+        d_branch = dbr[w]
+        d_ctx = dot_t(d_branch, wp[...]).astype(BF)
+        q_w, k_w, v_w = q[w], k[w], v[w]
+        d_q = jnp.zeros((TOK, width), F32)
+        d_k = jnp.zeros((TOK, width), F32)
+        d_v = jnp.zeros((TOK, width), F32)
+        for h in range(heads):
+            pick = jnp.where(head_of == h, 1.0, 0.0).astype(BF)
+            d_ctx_h = d_ctx * pick
+            p = probs[w, h]
+            d_p = dot_t(d_ctx_h, v_w)
+            d_v = d_v + t_dot(p.astype(BF), d_ctx_h)
+            d_s = p * (d_p - jnp.sum(p * d_p, axis=-1, keepdims=True))
+            dpos_s[h, :, :TOK] = dpos_s[h, :, :TOK] + d_s
+            d_l = (d_s * HD ** (-0.5)).astype(BF)
+            d_q = d_q + dot(d_l, k_w * pick)
+            d_k = d_k + t_dot(d_l, q_w * pick)
+            if h == heads // 2 - 1:
+
+                @pl.when(w >= 1)
+                def _():
+                    line.cross(w - 1)
+
+        part = jnp.zeros((TOK, D), F32)
+        for n, d_n in enumerate((d_q, d_k, d_v)):
+            low = d_n.astype(BF)
+            dh_s[n, pl.ds(pl.multiple_of(w * TOK, TOK), TOK), :] = low
+            part = part + dot_t(low, wq[n])
+            if n != 1:
+                at = 8 + n // 2
+                small_o[at : at + 1, :width] = small_o[at : at + 1, :width] + jnp.sum(
+                    low.astype(F32), axis=0, keepdims=True
+                )
+        line.put(w, part)
+        line.start(w)
+        mix_line.start(w)
+
+        @pl.when(w == 0)
+        def _():
+            down.pair()
+            up.pair()
+
+        @pl.when(w == 1)
+        def _():
+            down.cross()
+
+        @pl.when(w == 2)
+        def _():
+            up.cross()
+
+        @pl.when(w >= 1)
+        def _():
+            line.settle(w - 1)
+            mix_line.cross(w - 1)
+
+        @pl.when(w >= 2)
+        def _():
+            line.hand(w - 2)
+            mix_line.settle(w - 2)
+
+        return carry
+
+    def back(w):
+        line.arrive(w)
+        x = xw[w]
+        centred = x - row_mean(x)
+        rstd = lax.rsqrt(row_mean(centred * centred) + NORM_EPS)
+        xhat = centred * rstd
+        d_one = jnp.concatenate([tot[w, 0], tot[w, 1]], axis=1).astype(F32)
+        e = d_one * gain
+        delta[w] = dft[w] + (e - row_mean(e) - xhat * row_mean(e * xhat)) * rstd
+        for n, term in ((0, d_one * xhat), (1, d_one)):
+            small_o[n : n + 1, :] = small_o[n : n + 1, :] + jnp.sum(term, axis=0, keepdims=True)
+
+    halo = [
+        remote(halo_s.at[i], halo_r.at[i], h_send.at[i], h_recv.at[i], {"ctx": 1 - c})
+        for i in range(images)
+    ]
+
+    def go_home(i):
+        for r in range(SHIFT, WIN):
+            halo_s[i, r - SHIFT] = home_row(delta, row_tmp, i, r).astype(BF)
+        halo[i].start()
+        for r in range(SHIFT):
+            gin_o[i, SHIFT + r] = og[i, SHIFT + r] + home_row(delta, row_tmp, i, r)
+
+    ident = lax.broadcasted_iota(jnp.int32, (TOK, 640), 1)
+
+    def bin_row(i, acc):
+        col = ridx_t[i]
+        hot = jnp.where(jnp.broadcast_to(col, (TOK, 640)) == ident, 1.0, 0.0).astype(BF)
+        vals = jnp.concatenate([dpos_s[h, pl.ds(i, 1), :TOK] for h in range(heads)]
+                               + [jnp.zeros((8 - heads, TOK), F32)], axis=0)
+        high = vals.astype(BF)
+        rest = vals - high.astype(F32)
+        mid = rest.astype(BF)
+        return acc + dot(high, hot) + dot(mid, hot)
+
+    lax.fori_loop(0, windows, window, 0)
+    hist = jnp.zeros((8, 640), F32)
+    line.cross(windows - 1)
+    line.hand(windows - 2)
+    for n in range(3):
+        gq_o[n] = t_dot(n1[...], dh_s[n])
+    down.finish()
+    up.finish()
+    line.settle(windows - 1)
+    hist = lax.fori_loop(0, TOK // 2, bin_row, hist)
+    line.hand(windows - 1)
+    mix_line.cross(windows - 1)
+    mix_line.hand(0)
+    mix_line.settle(windows - 2)
+    back(0)
+    back(1)
+    go_home(0)
+    gp = t_dot(ctx[...], dbr[...].reshape(windows * TOK, D))
+    for n in range(4):
+        gp_o[n] = gp[:, n * shard : (n + 1) * shard]
+    mix_line.settle(windows - 1)
+    mix_line.hand(1)
+    mix_line.hand(2)
+    back(2)
+    back(3)
+    mix_line.hand(windows - 1)
+    go_home(1)
+    hist = lax.fori_loop(TOK // 2, TOK, bin_row, hist)
+    small_o[16:24, :640] = hist
+    for i in range(images):
+        halo[i].wait_recv()
+        for r in range(SHIFT):
+            gin_o[i, r] = og[i, r] + halo_r[i, r].astype(F32)
+    for w in range(windows):
+        line.drain(w)
+        mix_line.arrive(w)
+        mix_line.drain(w)
+    for copy in halo:
+        copy.wait_send()
+    up.drain()
+    down.drain()
+
+
+def attention_backward(rows, wq, wp, n1, q, k, v, probs, ctx, dbr, dft, xw, og, gu, gd, rel_index, sums, mix):
+    windows, heads = probs.shape[0], probs.shape[1]
+    images, width, shard = windows // 2, q.shape[2], gd.shape[0] // 4
+    hidden = gu.shape[1]
+    outs = [
+        (og.shape, F32), ((3, D, width), F32), ((4, width, shard), F32), ((24, D), F32),
+        ((shard, hidden), F32), ((shard, hidden), F32),
+        ((windows, 2, TOK, HALF), BF),
+    ]
+    scratch = [
+        pltpu.VMEM((3, windows * TOK, width), BF),
+        pltpu.VMEM((heads, TOK, 256), F32),
+        pltpu.VMEM((windows, TOK, D), F32),
+        pltpu.VMEM((24, D), F32),
+        pltpu.VMEM((images, SHIFT, 24, D), BF),
+        pltpu.VMEM((images, SHIFT, 24, D), BF),
+        pltpu.VMEM((windows, 2, TOK, HALF), BF),
+        pltpu.VMEM((8, 640), F32),
+        *LineSum.scratch(windows),
+        *ShardSum.scratch((shard, hidden)),
+        *ShardSum.scratch((shard, hidden)),
+        *LineSum.scratch(windows)[1:],
+        pltpu.SemaphoreType.DMA((images,)),
+        pltpu.SemaphoreType.DMA((images,)),
+    ]
+    return vmem_call(attention_backward_body, outs, scratch, "attention_backward", 3)(
+        rows, wq, wp, n1.reshape(-1, D), q, k, v, probs, ctx.reshape(-1, width), dbr, dft, xw, og,
+        gu, gd, rel_index[:, :, None], sums, mix,
+    )
+
+
+def total_of(x):
+    return jnp.sum(jnp.sum(x, axis=1, keepdims=True), axis=0, keepdims=True)
+
+
+def exact(a, b, dims):
+    return lax.dot_general(
+        a, b, (dims, ((), ())), precision=lax.Precision.HIGHEST, preferred_element_type=F32
+    )
+
+
+def lane_sums(squares):
+    return exact(jnp.ones((8, squares.shape[1]), F32), squares, ((1,), (1,)))[0:1]
+
+
+def as_column(row):
+    n = row.shape[1]
+    step = 64
+    eye = lax.broadcasted_iota(jnp.int32, (step, step), 0) == lax.broadcasted_iota(
+        jnp.int32, (step, step), 1
+    )
+    return jnp.concatenate(
+        [
+            jnp.sum(
+                jnp.where(eye, jnp.broadcast_to(row[:, at : at + step], (step, step)), 0.0),
+                axis=1, keepdims=True,
+            )
+            for at in range(0, n, step)
+        ],
+        axis=0,
+    )
+
+
+def lane_pack(values):
+    lane = lax.broadcasted_iota(jnp.int32, (8, 128), 1)
+    packed = jnp.zeros((8, 128), F32)
+    for n, value in enumerate(values):
+        packed = packed + jnp.where(lane == n, jnp.broadcast_to(value, (8, 128)), 0.0)
+    return packed
+
+
+def optimizer_body(
+    gq, gp, g_up, g_down, small, rows, feat, br, mixed,
+    w_qkv, w_proj, w_up, w_down, w_norm, w_heads, w_hidden, w_table,
+    row_qkv, col_qkv, row_proj, col_proj, row_up, col_up, row_down, col_down,
+    s_norm, s_heads, s_hidden, s_table,
+    out_o, gq_o, gp_o, gn_o, gh_o, gu_o, gt_o,
+    nq_o, np_o, nu_o, nd_o, nn_o, nh_o, nx_o, nt_o,
+    cq_o, cp_o, cu_o, cd_o,
+    rq_o, kq_o, rp_o, kp_o, ru_o, ku_o, rd_o, kd_o,
+    sn_o, sh_o, sx_o, st_o, clip_o,
+    qa, qb, qc, qd, qe, qf, qg, qh,
+    pa, pb, pc, pd, pe, pf, pg, ph,
+    sm_s, sm_r, t_s, f_s, z_s, c_s, delta, row_tmp, halo_s, halo_r,
+    sm_send, sm_recv, t_send, t_recv, f_send, f_recv, z_send, z_recv, c_send, c_recv, h_send, h_recv,
+):
+    f, c, t = lax.axis_index("fsdp"), lax.axis_index("ctx"), lax.axis_index("tp")
+    images = feat.shape[0]
+    windows = 2 * images
+    shard, width = w_qkv.shape[1], w_qkv.shape[2]
+    me = f * 4 + t
+    first_f = jnp.where(f == 0, 1.0, 0.0)
+    first_t = jnp.where(t == 0, 1.0, 0.0)
+
+    def other(n):
+        at = lax.rem(me + n, 16)
+        return {"fsdp": lax.div(at, 4), "tp": lax.rem(at, 4)}
+
+    barrier = pltpu.get_barrier_semaphore()
+    greet(barrier, [{"ctx": 1 - c}] + [other(n) for n in range(1, 16)])
+    qkv = ShardSum(
+        lambda at: gq[:, pl.ds(pl.multiple_of(at * shard, shard), shard), :], gq_o,
+        (qa, qb, qc, qd, qe, qf, qg, qh),
+    )
+    proj = ShardSum(lambda at: gp[at], gp_o, (pa, pb, pc, pd, pe, pf, pg, ph))
+    sm_s[0] = small[...]
+
+    def swap(n):
+        where = ({"fsdp": qkv.near}, {"fsdp": qkv.far}, {"ctx": 1 - c})[n]
+        return remote(sm_s.at[n], sm_r.at[n], sm_send.at[n], sm_recv.at[n], where)
+
+    pl.semaphore_wait(barrier, 16)
+    swap(0).start()
+    qkv.start()
+    proj.start()
+
+    keep = 1.0 - DECAY_RATE
+    t_s[t] = jnp.zeros((8, shard), F32)
+    f_s[f] = jnp.zeros((8, f_s.shape[2]), F32)
+    sq_up = g_up[...] * g_up[...]
+    sq_down = g_down[...] * g_down[...]
+    t_s[t, 4:5, :] = lane_sums(sq_up)
+    t_s[t, 5:6, :] = lane_sums(sq_down)
+    f_s[f, 4:5, :] = jnp.sum(sq_up, axis=0, keepdims=True)
+    f_s[f, 5:6, :] = jnp.sum(sq_down, axis=0, keepdims=True)
+    tot_up, tot_down = total_of(sq_up), total_of(sq_down)
+    old_rows = [
+        first_t * jnp.sum(row_qkv[0:1, :], axis=1, keepdims=True),
+        first_t * jnp.sum(row_qkv[1:2, :], axis=1, keepdims=True),
+        first_t * jnp.sum(row_qkv[2:3, :], axis=1, keepdims=True),
+        first_f * jnp.sum(row_proj[...], axis=1, keepdims=True),
+        first_t * jnp.sum(row_up[...], axis=1, keepdims=True),
+        first_f * jnp.sum(row_down[...], axis=1, keepdims=True),
+    ]
+    masters = [
+        sum(total_of(w_qkv[n] * w_qkv[n]) for n in range(3)),
+        total_of(w_proj[...] * w_proj[...]),
+        total_of(w_up[...] * w_up[...]),
+        total_of(w_down[...] * w_down[...]),
+        *[
+            first_t * jnp.sum(w_norm[n : n + 1, :] * w_norm[n : n + 1, :], axis=1, keepdims=True)
+            for n in range(6)
+        ],
+        *[total_of(w_heads[n] * w_heads[n]) for n in range(2)],
+        total_of(w_hidden[...] * w_hidden[...]),
+        first_f * total_of(w_table[...] * w_table[...]),
+    ]
+
+    qkv.pair()
+    proj.pair()
+    swap(0).wait_recv()
+    sm_s[1] = sm_s[0] + sm_r[0]
+    swap(1).start()
+
+    bias_two, bias_five = rows[2:3, :], rows[5:6, :]
+    for w in range(windows):
+        delta[w] = (
+            jnp.concatenate([br[w, 0], br[w, 1]], axis=1).astype(F32) + bias_two
+            + jnp.concatenate([mixed[w, 0], mixed[w, 1]], axis=1).astype(F32) + bias_five
+        )
+    halo = [
+        remote(halo_s.at[i], halo_r.at[i], h_send.at[i], h_recv.at[i], {"ctx": 1 - c})
+        for i in range(images)
+    ]
+    qkv.cross()
+    proj.cross()
+    swap(1).wait_recv()
+    sm_s[2] = sm_s[1] + sm_r[1]
+    swap(2).start()
+    for i in range(images):
+        for r in range(SHIFT, WIN):
+            halo_s[i, r - SHIFT] = home_row(delta, row_tmp, i, r).astype(BF)
+        for r in range(SHIFT):
+            out_o[i, SHIFT + r] = feat[i, SHIFT + r].astype(F32) + home_row(delta, row_tmp, i, r)
+    qkv.finish()
+    proj.finish()
+
+    tot_q = []
+    for n in range(3):
+        sq = gq_o[n] * gq_o[n]
+        t_s[t, n : n + 1, :] = lane_sums(sq)
+        f_s[f, n : n + 1, :width] = jnp.sum(sq, axis=0, keepdims=True)
+        tot_q.append(total_of(sq))
+    sq = gp_o[...] * gp_o[...]
+    f_s[f, 3:4, :shard] = lane_sums(sq)
+    t_s[t, 3:4, :] = jnp.sum(sq, axis=0, keepdims=True)
+    z_s[me] = lane_pack([*tot_q, total_of(sq), tot_up, tot_down, *old_rows, *masters])
+
+    def t_copy(n):
+        return remote(t_s.at[t], t_s.at[t], t_send.at[n], t_recv.at[n], {"tp": lax.rem(t + n, 4)})
+
+    def f_copy(n):
+        return remote(f_s.at[f], f_s.at[f], f_send.at[n], f_recv.at[n], {"fsdp": lax.rem(f + n, 4)})
+
+    def z_copy(n):
+        return remote(z_s.at[me], z_s.at[me], z_send.at[n], z_recv.at[n], other(n))
+
+    def c_copy(n):
+        return remote(c_s.at[me], c_s.at[me], c_send.at[n], c_recv.at[n], other(n))
+
+    for n in range(1, 4):
+        t_copy(n).start()
+        f_copy(n).start()
+    for n in range(1, 16):
+        z_copy(n).start()
+    for i in range(images):
+        halo[i].start()
+
+    swap(2).wait_recv()
+    sm = sm_s[2] + sm_r[2]
+
+    def own_lanes(x, size):
+        out = x[:, :size]
+        for n in range(1, 4):
+            out = jnp.where(f == n, x[:, n * size : (n + 1) * size], out)
+        return out
+
+    gn = own_lanes(sm[0:6, :], shard)
+    gn_o[...] = gn
+    part = HD // 4
+
+    def spread(row, count):
+        lanes = count * HD
+        lane = lax.broadcasted_iota(jnp.int32, (count, lanes), 1)
+        unit = lax.broadcasted_iota(jnp.int32, (count, lanes), 0)
+        only = jnp.where(
+            jnp.right_shift(lane, 5) == unit, jnp.broadcast_to(row, (count, lanes)), 0.0
+        )
+        at = lax.broadcasted_iota(jnp.int32, (lanes, part), 0)
+        k = lax.broadcasted_iota(jnp.int32, (lanes, part), 1)
+        pick = jnp.where(jnp.bitwise_and(at, HD - 1) == f * part + k, 1.0, 0.0)
+        return exact(only, pick, ((1,), (0,)))
+
+    heads = width // HD
+    gh = [spread(sm[8 + n : 9 + n, :width], heads) for n in range(2)]
+    gx = spread(sm[6:7, :], nx_o.shape[0])
+    gu_o[...] = gx
+    eye = jnp.where(
+        lax.broadcasted_iota(jnp.int32, (8, 8), 0) == lax.broadcasted_iota(jnp.int32, (8, 8), 1),
+        1.0, 0.0,
+    )
+    gt = exact(sm[16:24, :640], eye, ((0,), (0,)))[: w_table.shape[0], :heads]
+    gt_o[...] = gt
+
+    def plain(grad, state):
+        new = DECAY_RATE * state + keep * (grad * grad + STAT_EPS)
+        return new, grad * lax.rsqrt(new)
+
+    sn, un = plain(gn, s_norm[...])
+    sn_o[...] = sn
+    uh = []
+    for n in range(2):
+        gh_o[n] = gh[n]
+        sh, u = plain(gh[n], s_heads[n])
+        sh_o[n] = sh
+        uh.append(u)
+    sx, ux = plain(gx, s_hidden[...])
+    sx_o[...] = sx
+    st, ut = plain(gt, s_table[...])
+    st_o[...] = st
+    small_sq = (
+        first_t * total_of(un * un) + total_of(uh[0] * uh[0]) + total_of(uh[1] * uh[1])
+        + total_of(ux * ux) + first_f * total_of(ut * ut)
+    )
+
+    for n in range(1, 4):
+        t_copy(n).wait_recv()
+        f_copy(n).wait_recv()
+    t_sum = t_s[0] + t_s[1] + t_s[2] + t_s[3]
+    f_sum = f_s[0] + f_s[1] + f_s[2] + f_s[3]
+    for n in range(1, 16):
+        z_copy(n).wait_recv()
+    z_sum = z_s[0]
+    for n in range(1, 16):
+        z_sum = z_sum + z_s[n]
+    lane8 = lax.broadcasted_iota(jnp.int32, (8, 128), 1)
+
+    def scalar(n):
+        return jnp.sum(jnp.where(lane8 == n, z_sum, 0.0)[0:1], axis=1, keepdims=True)
+
+    def fresh(old, summed, count):
+        return DECAY_RATE * old + keep * (summed / count + STAT_EPS)
+
+    hidden = f_s.shape[2]
+    ff = 4 * hidden
+    rq = fresh(row_qkv[...], t_sum[0:3, :], D)
+    kq = fresh(col_qkv[...], f_sum[0:3, :width], D)
+    rp = fresh(row_proj[...], f_sum[3:4, :width], D)
+    kp = fresh(col_proj[...], t_sum[3:4, :], D)
+    ru = fresh(row_up[...], t_sum[4:5, :], ff)
+    ku = fresh(col_up[...], f_sum[4:5, :], D)
+    rd = fresh(row_down[...], f_sum[5:6, :], D)
+    kd = fresh(col_down[...], t_sum[5:6, :], ff)
+    for ref, val in (
+        (rq_o, rq), (kq_o, kq), (rp_o, rp), (kp_o, kp), (ru_o, ru), (ku_o, ku), (rd_o, rd), (kd_o, kd)
+    ):
+        ref[...] = val
+
+    def mean_row(n, rows_all, cols_all):
+        return (DECAY_RATE * scalar(6 + n) + keep * (scalar(n) / cols_all + rows_all * STAT_EPS)) / rows_all
+
+    scale_q = [
+        as_column(lax.rsqrt(rq[n : n + 1, :] / mean_row(n, D, D))) * lax.rsqrt(kq[n : n + 1, :])
+        for n in range(3)
+    ]
+    scale_p = as_column(lax.rsqrt(rp / mean_row(3, D, D))) * lax.rsqrt(kp)
+    scale_u = as_column(lax.rsqrt(ru / mean_row(4, D, ff))) * lax.rsqrt(ku)
+    scale_d = as_column(lax.rsqrt(kd)) * lax.rsqrt(rd / mean_row(5, ff, D))
+    big_sq = small_sq
+    for n in range(3):
+        u = gq_o[n] * scale_q[n]
+        nq_o[n] = u
+        big_sq = big_sq + total_of(u * u)
+    for grad, scale, ref in ((gp_o, scale_p, np_o), (g_up, scale_u, nu_o), (g_down, scale_d, nd_o)):
+        u = grad[...] * scale
+        ref[...] = u
+        big_sq = big_sq + total_of(u * u)
+    c_s[me] = jnp.broadcast_to(big_sq, (8, 128))
+    for n in range(1, 16):
+        c_copy(n).start()
+    for i in range(images):
+        halo[i].wait_recv()
+        for r in range(SHIFT):
+            out_o[i, r] = feat[i, r].astype(F32) + halo_r[i, r].astype(F32)
+    counts = [3 * D * D, D * D, D * ff, ff * D] + [D] * 8 + [ff, RELP * HEADS]
+    sizes = [jnp.sqrt(scalar(12 + n) / counts[n] + STAT_EPS) for n in range(14)]
+    for n in range(1, 16):
+        c_copy(n).wait_recv()
+    all_sq = c_s[0]
+    for n in range(1, 16):
+        all_sq = all_sq + c_s[n]
+    count_all = 4 * D * D + 2 * D * ff + 8 * D + ff + RELP * HEADS
+    clip = jnp.sqrt(all_sq[0:1, 0:1] / count_all)
+    clip_o[...] = clip
+    factor = STEP_RATE / jnp.maximum(1.0, clip / CLIP_LEVEL)
+
+    for n in range(3):
+        new = w_qkv[n] - sizes[0] * factor * nq_o[n]
+        nq_o[n] = new
+        cq_o[n] = new.astype(BF)
+    for master, size, ref, low in (
+        (w_proj, sizes[1], np_o, cp_o), (w_up, sizes[2], nu_o, cu_o), (w_down, sizes[3], nd_o, cd_o)
+    ):
+        new = master[...] - size * factor * ref[...]
+        ref[...] = new
+        low[...] = new.astype(BF)
+    for n in range(6):
+        nn_o[n : n + 1, :] = w_norm[n : n + 1, :] - sizes[4 + n] * factor * un[n : n + 1, :]
+    for n in range(2):
+        nh_o[n] = w_heads[n] - sizes[10 + n] * factor * uh[n]
+    nx_o[...] = w_hidden[...] - sizes[12] * factor * ux
+    nt_o[...] = w_table[...] - sizes[13] * factor * ut
+
+    for n in range(3):
+        swap(n).wait_send()
+    for n in range(1, 4):
+        t_copy(n).wait_send()
+        f_copy(n).wait_send()
+    for n in range(1, 16):
+        z_copy(n).wait_send()
+        c_copy(n).wait_send()
+    for copy in halo:
+        copy.wait_send()
+    qkv.drain()
+    proj.drain()
+
+
+def optimizer(gq, gp, g_up, g_down, small, rows, feat, br, mixed, masters, stats, states):
+    w_qkv, w_proj, w_up, w_down, w_norm, w_heads, w_hidden, w_table = masters
+    images = feat.shape[0]
+    windows = 2 * images
+    shard, width = w_qkv.shape[1], w_qkv.shape[2]
+    hidden = w_up.shape[1]
+    stats = [u if u.ndim == 2 else u[None] for u in stats]
+    like = lambda u: (u.shape, F32)
+    mats = (w_qkv, w_proj, w_up, w_down)
+    small_ps = (w_norm, w_heads, w_hidden, w_table)
+    outs = [
+        (feat.shape, F32), like(w_qkv), like(w_proj), like(w_norm), like(w_heads), like(w_hidden),
+        like(w_table), *map(like, masters), *[(u.shape, BF) for u in mats], *map(like, stats),
+        *map(like, small_ps), ((1, 1), F32),
+    ]
+    scratch = [
+        *ShardSum.scratch((3, shard, width)),
+        *ShardSum.scratch((width, shard)),
+        pltpu.VMEM((3, 24, D), F32), pltpu.VMEM((3, 24, D), F32),
+        pltpu.VMEM((4, 8, shard), F32), pltpu.VMEM((4, 8, hidden), F32),
+        pltpu.VMEM((16, 8, 128), F32), pltpu.VMEM((16, 8, 128), F32),
+        pltpu.VMEM((windows, TOK, D), F32), pltpu.VMEM((24, D), F32),
+        pltpu.VMEM((images, SHIFT, 24, D), BF), pltpu.VMEM((images, SHIFT, 24, D), BF),
+        pltpu.SemaphoreType.DMA((3,)), pltpu.SemaphoreType.DMA((3,)),
+        *[pltpu.SemaphoreType.DMA((4,)) for _ in range(4)],
+        *[pltpu.SemaphoreType.DMA((16,)) for _ in range(4)],
+        pltpu.SemaphoreType.DMA((images,)), pltpu.SemaphoreType.DMA((images,)),
+    ]
+    return vmem_call(optimizer_body, outs, scratch, "optimizer", 4)(
+        gq, gp, g_up, g_down, small, rows, feat, br, mixed, *masters, *stats, *states
+    )
 
 
 def per_device_plain(
@@ -990,331 +1746,27 @@
     state_hidden,
     state_table,
 ):
-    images, band_rows, across, model_width = features.shape
-    win_tokens = WIN * WIN
-    fsdp_at = lax.axis_index("fsdp")
-    ctx_at = lax.axis_index("ctx")
-    tp_at = lax.axis_index("tp")
-    first_fsdp = (fsdp_at == 0).astype(jnp.float32)
-    first_ctx = (ctx_at == 0).astype(jnp.float32)
-    first_tp = (tp_at == 0).astype(jnp.float32)
     (weights_qkv, weights_proj, weights_up, weights_down, rows, xw, ogw, n1, query_low, key_low, value_low,
-     prob_rows, context_low, br) = attention_forward(
+     prob_rows, ctx, br) = attention_forward(
         features, out_grad, regions, rel_index, w_qkv, w_proj, w_up, w_down,
         norm_vecs, head_bias, hidden_bias, rel_table)
-    norm_rows = rows[:6]
-    bias_hidden = rows[8]
-    local_width = weights_qkv.shape[2]
-    heads_here = local_width // HD
-    win_count = xw.shape[0]
-    head_shape = (win_count, win_tokens, heads_here, HD)
-    flat_one = xw.reshape(-1, model_width)
-    grad_flat = ogw.reshape(-1, model_width)
-    normed_one_low = n1.reshape(-1, model_width)
-    _, pull_one = jax.vjp(layer_norm, flat_one, norm_rows[0], norm_rows[1])
-    query_low, key_low, value_low = (u.reshape(head_shape) for u in (query_low, key_low, value_low))
-    prob_low = prob_rows.astype(jnp.bfloat16)
-    context_low = context_low.reshape(-1, local_width)
-    branch = br.transpose(0, 2, 1, 3).reshape(-1, model_width).astype(jnp.float32) + norm_rows[2]
-    def roll_out(rolled_flat):
-        band = jnp.roll(
-            from_windows(
-                rolled_flat.reshape(-1, win_tokens, model_width), images, band_rows, across
-            ),
-            SHIFT,
-            axis=2,
-        )
-        lower = passed_along(band[:, band_rows - SHIFT :], "ctx", 1)
-        return jnp.concatenate([lower, band[:, : band_rows - SHIFT]], axis=1)
-
-    flat_two = flat_one + branch
-    normed_two, pull_two = jax.vjp(layer_norm, flat_two, norm_rows[3], norm_rows[4])
-    normed_two_low = normed_two.astype(jnp.bfloat16)
-    pre_act = jnp.dot(normed_two_low, weights_up, preferred_element_type=jnp.float32) + bias_hidden
-    hidden, pull_gelu = jax.vjp(exact_gelu, pre_act)
-    hidden_low = hidden.astype(jnp.bfloat16)
-    mixed_part = jnp.dot(hidden_low, weights_down, preferred_element_type=jnp.float32)
-    mixed_whole = lax.psum(mixed_part.astype(jnp.bfloat16), "tp").astype(jnp.float32)
-    block_out = features.astype(jnp.float32) + roll_out(
-        (branch + mixed_whole + norm_rows[5]).astype(jnp.bfloat16)
-    ).astype(jnp.float32)
-    grad_low = grad_flat.astype(jnp.bfloat16)
-    grad_down_full = jnp.einsum(
-        "tf,td->fd", hidden_low, grad_low, preferred_element_type=jnp.float32
-    )
-    grad_down_bias = jnp.sum(grad_flat, axis=0)
-    d_hidden = jnp.einsum("td,fd->tf", grad_low, weights_down, preferred_element_type=jnp.float32)
-    d_pre = pull_gelu(d_hidden)[0]
-    d_pre_low = d_pre.astype(jnp.bfloat16)
-    grad_hidden_bias = jnp.sum(d_pre, axis=0)
-    grad_up_full = jnp.einsum(
-        "td,tf->df", normed_two_low, d_pre_low, preferred_element_type=jnp.float32
-    )
-    d_two_part = jnp.einsum("tf,df->td", d_pre_low, weights_up, preferred_element_type=jnp.float32)
-    d_two = lax.psum(d_two_part.astype(jnp.bfloat16), "tp").astype(jnp.float32)
-    d_flat_two, grad_gain_two, grad_offset_two = pull_two(d_two)
-    d_resid = grad_flat + d_flat_two
-    grad_proj_bias = jnp.sum(d_resid, axis=0)
-    d_branch = d_resid.astype(jnp.bfloat16)
-    grad_proj_full = jnp.einsum(
-        "tc,td->cd", context_low, d_branch, preferred_element_type=jnp.float32
-    )
-    d_context = (
-        jnp.einsum("td,cd->tc", d_branch, weights_proj, preferred_element_type=jnp.float32)
-        .astype(jnp.bfloat16)
-        .reshape(head_shape)
-    )
-    d_probs = jnp.einsum(
-        "wihc,wjhc->whij", d_context, value_low, preferred_element_type=jnp.float32
-    )
-    d_value_low = jnp.einsum(
-        "whij,wihc->wjhc", prob_low, d_context, preferred_element_type=jnp.float32
-    ).astype(jnp.bfloat16)
-    d_scores = prob_rows * (d_probs - jnp.sum(prob_rows * d_probs, axis=-1, keepdims=True))
-    d_pos = jnp.sum(d_scores, axis=0)
-    d_scaled = (d_scores * HD ** (-0.5)).astype(jnp.bfloat16)
-    d_query_low = jnp.einsum(
-        "whij,wjhc->wihc", d_scaled, key_low, preferred_element_type=jnp.float32
-    ).astype(jnp.bfloat16)
-    d_key_low = jnp.einsum(
-        "whij,wihc->wjhc", d_scaled, query_low, preferred_element_type=jnp.float32
-    ).astype(jnp.bfloat16)
-    d_heads = jnp.stack([d_query_low, d_key_low, d_value_low]).reshape(3, -1, local_width)
-    grad_qkv_full = jnp.einsum(
-        "td,ktc->kdc", normed_one_low, d_heads, preferred_element_type=jnp.float32
-    )
-    grad_head_bias = jnp.stack(
-        [
-            jnp.sum(d_heads[0].astype(jnp.float32), axis=0),
-            jnp.sum(d_heads[2].astype(jnp.float32), axis=0),
-        ]
-    ).reshape(2, heads_here, HD)
-    d_one_part = jnp.einsum("ktc,kdc->td", d_heads, weights_qkv, preferred_element_type=jnp.float32)
-    d_one = lax.psum(d_one_part.astype(jnp.bfloat16), "tp").astype(jnp.float32)
-    d_flat_one, grad_gain_one, grad_offset_one = pull_one(d_one)
-    grad_input = out_grad + roll_out((d_flat_two + d_flat_one).astype(jnp.bfloat16)).astype(
-        jnp.float32
-    )
-    table_part = table_grad(d_pos, rel_index, rel_table.shape[0])
-    grad_norm_full = jnp.stack(
-        [
-            grad_gain_one,
-            grad_offset_one,
-            grad_proj_bias,
-            grad_gain_two,
-            grad_offset_two,
-            grad_down_bias,
-        ]
-    )
-    grad_list = (
-        grad_qkv_full,
-        grad_proj_full,
-        grad_up_full,
-        grad_down_full,
-        grad_norm_full,
-        grad_head_bias,
-        grad_hidden_bias.reshape(-1, HD),
-    )
-    g_qkv, g_proj, g_up, g_down, g_norm, g_heads, g_hidden = shard_sum(band_sum(grad_list))
-    d_shard = w_qkv.shape[1]
-    hidden_here = w_up.shape[1]
-    keep = 1.0 - DECAY_RATE
-    sq_qkv = g_qkv * g_qkv
-    sq_proj = g_proj * g_proj
-    sq_up = g_up * g_up
-    sq_down = g_down * g_down
-    stat_rq = place(
-        (keep * jnp.sum(sq_qkv, axis=2) / D + first_tp * (DECAY_RATE * row_qkv + keep * STAT_EPS))
-        * first_ctx,
-        fsdp_at,
-        D,
-    )
-    stat_cq = place(
-        (keep * jnp.sum(sq_qkv, axis=1) / D + first_fsdp * (DECAY_RATE * col_qkv + keep * STAT_EPS))
-        * first_ctx,
-        tp_at,
-        D,
-    )
-    stat_rp = place(
-        (
-            keep * jnp.sum(sq_proj, axis=1) / D
-            + first_fsdp * (DECAY_RATE * row_proj + keep * STAT_EPS)
-        )
-        * first_ctx,
-        tp_at,
-        D,
-    )
-    stat_cp = place(
-        (keep * jnp.sum(sq_proj, axis=0) / D + first_tp * (DECAY_RATE * col_proj + keep * STAT_EPS))
-        * first_ctx,
-        fsdp_at,
-        D,
-    )
-    stat_ru = place(
-        (keep * jnp.sum(sq_up, axis=1) / FF + first_tp * (DECAY_RATE * row_up + keep * STAT_EPS))
-        * first_ctx,
-        fsdp_at,
-        D,
-    )
-    stat_cu = place(
-        (keep * jnp.sum(sq_up, axis=0) / D + first_fsdp * (DECAY_RATE * col_up + keep * STAT_EPS))
-        * first_ctx,
-        tp_at,
-        FF,
-    )
-    stat_rd = place(
-        (
-            keep * jnp.sum(sq_down, axis=1) / D
-            + first_fsdp * (DECAY_RATE * row_down + keep * STAT_EPS)
-        )
-        * first_ctx,
-        tp_at,
-        FF,
-    )
-    stat_cd = place(
-        (
-            keep * jnp.sum(sq_down, axis=0) / FF
-            + first_tp * (DECAY_RATE * col_down + keep * STAT_EPS)
-        )
-        * first_ctx,
-        fsdp_at,
-        D,
-    )
-    table_whole = place(table_part, tp_at, HEADS)
-    master_sq = jnp.concatenate(
-        [
-            jnp.stack(
-                [
-                    jnp.sum(w_qkv * w_qkv),
-                    jnp.sum(w_proj * w_proj),
-                    jnp.sum(w_up * w_up),
-                    jnp.sum(w_down * w_down),
-                ]
-            )
-            * first_ctx,
-            jnp.sum(norm_vecs * norm_vecs, axis=1) * first_ctx * first_tp,
-            jnp.sum(head_bias * head_bias, axis=(1, 2)) * first_ctx,
-            jnp.sum(hidden_bias * hidden_bias)[None] * first_ctx,
-            jnp.sum(rel_table * rel_table)[None] * first_ctx * first_fsdp,
-        ]
-    )
-    (
-        full_rq,
-        full_cq,
-        full_rp,
-        full_cp,
-        full_ru,
-        full_cu,
-        full_rd,
-        full_cd,
-        table_sum,
-        master_total,
-    ) = lax.psum(
-        (
-            stat_rq,
-            stat_cq,
-            stat_rp,
-            stat_cp,
-            stat_ru,
-            stat_cu,
-            stat_rd,
-            stat_cd,
-            table_whole,
-            master_sq,
-        ),
-        ("fsdp", "ctx", "tp"),
-    )
-    u_qkv = factored(
-        g_qkv,
-        own_part(full_rq, fsdp_at, d_shard),
-        own_part(full_cq, tp_at, local_width),
-        jnp.mean(full_rq, axis=1)[:, None, None],
-    )
-    u_proj = factored(
-        g_proj,
-        own_part(full_rp, tp_at, local_width),
-        own_part(full_cp, fsdp_at, d_shard),
-        jnp.mean(full_rp),
-    )
-    u_up = factored(
-        g_up,
-        own_part(full_ru, fsdp_at, d_shard),
-        own_part(full_cu, tp_at, hidden_here),
-        jnp.mean(full_ru),
-    )
-    u_down = factored(
-        g_down,
-        own_part(full_rd, tp_at, hidden_here),
-        own_part(full_cd, fsdp_at, d_shard),
-        jnp.mean(full_rd),
-    )
-    g_table = own_part(table_sum, tp_at, heads_here)
-    state_norm_new, u_norm = plain_stats(g_norm, state_norm)
-    state_heads_new, u_heads = plain_stats(g_heads, state_heads)
-    state_hidden_new, u_hidden = plain_stats(g_hidden, state_hidden)
-    state_table_new, u_table = plain_stats(g_table, state_table)
-    local_sq = (
-        jnp.sum(u_qkv * u_qkv)
-        + jnp.sum(u_proj * u_proj)
-        + jnp.sum(u_up * u_up)
-        + jnp.sum(u_down * u_down)
-        + jnp.sum(u_heads * u_heads)
-        + jnp.sum(u_hidden * u_hidden)
-        + first_tp * jnp.sum(u_norm * u_norm)
-        + first_fsdp * jnp.sum(u_table * u_table)
-    )
-    total_sq = lax.psum(local_sq, ("fsdp", "tp"))
-    count_all = 4 * D * D + 2 * D * FF + 8 * D + FF + RELP * HEADS
-    clip_rms = jnp.sqrt(total_sq / count_all)
-    factor = 1.0 / jnp.maximum(1.0, clip_rms / CLIP_LEVEL)
-    counts = jnp.array(
-        [3 * D * D, D * D, D * FF, FF * D, D, D, D, D, D, D, D, D, FF, RELP * HEADS], jnp.float32
-    )
-    scales = jnp.sqrt(master_total / counts + STAT_EPS)
-    new_qkv = w_qkv - STEP_RATE * scales[0] * factor * u_qkv
-    new_proj = w_proj - STEP_RATE * scales[1] * factor * u_proj
-    new_up = w_up - STEP_RATE * scales[2] * factor * u_up
-    new_down = w_down - STEP_RATE * scales[3] * factor * u_down
-    new_norm = norm_vecs - STEP_RATE * scales[4:10][:, None] * factor * u_norm
-    new_heads = head_bias - STEP_RATE * scales[10:12][:, None, None] * factor * u_heads
-    new_hidden = hidden_bias - STEP_RATE * scales[12] * factor * u_hidden
-    new_table = rel_table - STEP_RATE * scales[13] * factor * u_table
+    gu, gd, dft, dbr, mix, sums = feed_forward(rows, weights_up, weights_down, xw, ogw, br)
+    grad_input, gq, gp, small, g_up, g_down, mixed = attention_backward(
+        rows, weights_qkv, weights_proj, n1, query_low, key_low, value_low, prob_rows, ctx, dbr, dft,
+        xw, out_grad, gu, gd, rel_index, sums, mix)
+    (block_out, g_qkv, g_proj, g_norm, g_heads, g_hidden, g_table,
+     new_qkv, new_proj, new_up, new_down, new_norm, new_heads, new_hidden, new_table,
+     copy_qkv, copy_proj, copy_up, copy_down, *stats, clip_rms) = optimizer(
+        gq, gp, g_up, g_down, small, rows, features, br, mixed,
+        (w_qkv, w_proj, w_up, w_down.T, norm_vecs, head_bias, hidden_bias, rel_table),
+        (row_qkv, col_qkv, row_proj, col_proj, row_up, col_up, row_down, col_down),
+        (state_norm, state_heads, state_hidden, state_table))
+    factors, states = stats[:8], stats[8:]
+    factors = factors[:2] + [u[0] for u in factors[2:]]
     return (
-        block_out,
-        grad_input,
-        g_qkv,
-        g_proj,
-        g_up,
-        g_down,
-        g_norm,
-        g_heads,
-        g_hidden,
-        g_table,
-        new_qkv,
-        new_proj,
-        new_up,
-        new_down,
-        new_norm,
-        new_heads,
-        new_hidden,
-        new_table,
-        new_qkv.astype(jnp.bfloat16),
-        new_proj.astype(jnp.bfloat16),
-        new_up.astype(jnp.bfloat16),
-        new_down.astype(jnp.bfloat16),
-        own_part(full_rq, fsdp_at, d_shard),
-        own_part(full_cq, tp_at, local_width),
-        own_part(full_rp, tp_at, local_width),
-        own_part(full_cp, fsdp_at, d_shard),
-        own_part(full_ru, fsdp_at, d_shard),
-        own_part(full_cu, tp_at, hidden_here),
-        own_part(full_rd, tp_at, hidden_here),
-        own_part(full_cd, fsdp_at, d_shard),
-        state_norm_new,
-        state_heads_new,
-        state_hidden_new,
-        state_table_new,
-        clip_rms,
+        block_out, grad_input, g_qkv, g_proj, g_up, g_down.T, g_norm, g_heads, g_hidden, g_table,
+        new_qkv, new_proj, new_up, new_down.T, new_norm, new_heads, new_hidden, new_table,
+        copy_qkv, copy_proj, copy_up, copy_down.T, *factors, *states, clip_rms[0, 0],
     )
 
 

time: 702 us -> 306 us (0.44); the launches traced: 690 us -> 305 us
  waiting for transfers between devices: 235 us -> 0 us
  Pallas kernels: 63.9 us -> 250 us
  local copies, waits for them, and re-layouts: 137 us -> 47.4 us
  matrix products: 88.2 us -> 0 us
  other arithmetic: 78.5 us -> 5.28 us
  blocking collectives: 53.5 us -> 0 us
  between operations: 30.3 us -> 2.64 us
    psum x4 -> x0, waiting for transfers between devices: 204 us -> none  [the longest x1 125 us: per_device(): lax.psum((stat_rq, stat_cq, stat_rp, stat_cp, stat_ru, stat_cu, stat_rd,...]
    pallas_call x1 -> x4, Pallas kernels: 63.9 us -> 250 us  [call(): pl.pallas_call(body, out_shape=[jax.ShapeDtypeStruct(s, t) for s, t in ou...]
    dot_general x25 -> x0, matrix products: 85.5 us -> none  [the longest x12 35.1 us: accumulate(): lax.dot_general(one_hot, grad_block, (((0,), (0,)), ((), ())), precision=...]
    psum x2 -> x0, blocking collectives: 40.3 us -> none  [the longest x1 31.7 us: per_device(): total_sq = lax.psum(local_sq, ('fsdp', 'tp'))]
    dynamic_slice x32 -> x0, local copies, waits for them, and re-layouts: 35.9 us -> none  [the longest x24 29.8 us: table_grad(): lax.scan(accumulate, jnp.zeros((table_rows, heads_here), jnp.float32), (i...]
    reduce_sum x29 -> x0, other arithmetic: 34.2 us -> none  [the longest x2 5.77 us: layer_norm(): return centred * lax.rsqrt(var_val + NORM_EPS) * gain_row + offset]
    reduce_scatter x2 -> x0, waiting for transfers between devices: 19.1 us -> none  [the longest x1 19.1 us: shard_sum(): lax.psum_scatter(grad_list[3], 'fsdp', scatter_dimension=1, tiled=True)]
    unnamed x1 -> x0, blocking collectives: 13.2 us -> none
  transfers between devices with their start and end apart: 11 -> 0, of which waited for: 5 -> 0; matrix products, arithmetic and copies ran while one was open for 30% -> 0% of each run, Pallas kernels for 0% -> 0%
where the time goes in v3:
time: 306 us; the launch traced here: 305 us
  Pallas kernels  250 us (82%)
  local copies, waits for them, and re-layouts  47.4 us (15%)
  other arithmetic  5.28 us (2%)
    pallas_call x4, Pallas kernels, call(): pl.pallas_call(body, out_shape=[jax.ShapeDtypeStruct(s, t) for s, t in ou...  250 us
    unnamed x100, local copies, waits for them, and re-layouts  36.3 us

profile of v3, /device:TPU:0, one launch (start us, length us, event | category | flops | bytes accessed | tf_op | source)
XLA Modules:
  0.0 305.4 jit_solution(1965443034614201848)
XLA Ops:
  0.7 0.8 copy.77.w_hidden
  2.4 1.4 select_maximum_fusion.small
  3.8 0.8 reshape_broadcast_in_dim.3
  4.6 0.9 broadcast_in_dim_squeeze_reshape.9.regc
  6.1 1.6 pad.17.ridx
  7.7 0.7 convert_bitcast_fusion
  9.0 64.0 %attention_forward.1 = (bf16[3,768,192]{2,1,0:T(8,128)(2,1)}, bf16[192,768]{1,0:T(8,128)(2,1)}, bf16[768,768]{1,0:T(8,128)(2,1)}, bf16[768,768]{1,0:T(8,128)(2,1...) custom-call(bf16[2,12,24,768]{3,2,1,0:T(8,128)(2,1)} %feat.3, ...), custom_call_target="tpu_custom_call" | custom-call | tf_op jit(solution)/shard_map/attention_forward/pallas_call | solution.py:524
  73.1 44.8 %feed_forward.1 = (f32[768,768]{1,0:T(8,128)}, f32[768,768]{1,0:T(8,128)}, f32[4,144,768]{2,1,0:T(8,128)}, bf16[4,144,768]{2,1,0:T(8,128)(2,1)}, f32[4,2,144,384]{3,2,1,0:T(8,128)}, /*index=5*/f32[8,768]{1,0:T(8,128)}) custom-call(f32[16,768]{1,0:T(8,128)} %get-tuple-element.94.rows, bf16[768,768]{1,0:T(8,128)(2,1)} %get-tuple-element.103.wu, ...), custom_call_target="tpu_custom_call" | custom-call | tf_op jit(solution)/shard_map/feed_forward/pallas_call | solution.py:524
  117.9 5.8 %copy.82.ridx_t = s32[144,144,1]{2,1,0:T(8,128)} copy(s32[144,144,1]{1,0,2:T(8,128)S(1)} %bitcast.32) | data formatting | bytes 165888 | tf_op jit(solution)/shard_map/broadcast_in_dim | solution.py:970
  123.8 96.5 %attention_backward.1 = (f32[2,12,24,768]{3,2,1,0:T(8,128)}, f32[3,768,192]{2,1,0:T(8,128)}, f32[4,192,192]{2,1,0:T(8,128)}, f32[24,768]{1,0:T(8,128)}, f32[192,...) custom-call(f32[16,768]{1,0:T(8,128)} %get-tuple-element.94.rows, ...), custom_call_target="tpu_custom_call" | custom-call | tf_op jit(solution)/shard_map/attention_backward/pallas_call | solution.py:524
  220.3 0.9 copy.85.w_table
  221.2 0.9 copy.88.s_table
  224.5 44.7 %optimizer.1 = (f32[2,12,24,768]{3,2,1,0:T(8,128)}, f32[3,192,192]{2,1,0:T(8,128)}, f32[192,192]{1,0:T(8,128)}, f32[6,192]{1,0:T(8,128)}, f32[2,6,8]{2,1,0:T(8,1...) custom-call(f32[3,768,192]{2,1,0:T(8,128)} %get-tuple-element.114.gq, ...), custom_call_target="tpu_custom_call" | custom-call | tf_op jit(solution)/shard_map/optimizer/pallas_call | solution.py:524
  269.2 1.7 copy.91
  270.9 1.7 copy.94
  272.6 1.7 copy.97
  274.3 1.3 copy.89
  275.6 1.3 copy.92
  276.9 1.3 copy.95
  278.2 1.4 copy.90
  279.5 1.4 copy.93
  280.9 1.4 copy.96
  282.3 1.3 reduce
  283.6 1.3 reduce.1
  284.8 2.9 copy.124
  287.8 1.2 copy.125
  289.2 0.8 copy.126
  290.7 0.8 copy.128
  291.6 0.8 copy.129
  293.0 0.8 copy.131
  294.5 0.8 copy.133
  295.4 0.8 copy.134
  (89 shorter events, 14.4 us)
Async XLA Ops:
  1.4 71.6 %copy-start.13 = (f32[24,8]{1,0:T(8,128)}, f32[24,8]{1,0:T(8,128)S(1)}, u32[]{:S(2)}) copy-start(f32[24,8]{1,0:T(8,128)S(1)} %copy.77.w_hidden) | copy-start | bytes 2308
  2.2 70.9 %copy-start.16 = (f32[2,6,8]{2,1,0:T(8,128)}, f32[2,6,8]{2,1,0:T(8,128)S(1)}, u32[]{:S(2)}) copy-start(f32[2,6,8]{2,1,0:T(8,128)S(1)} %copy.78.w_heads) | copy-start | bytes 1156
  73.1 44.8 %copy-start.7 = (s32[144,144]{1,0:T(8,128)S(1)}, s32[144,144]{1,0:T(8,128)}, u32[]{:S(2)}) copy-start(s32[144,144]{1,0:T(8,128)} %param.27) | copy-start | bytes 248836
  123.7 96.5 %copy-start.15 = (f32[529,6]{0,1:T(8,128)S(1)}, f32[529,6]{0,1:T(8,128)}, u32[]{:S(2)}) copy-start(f32[529,6]{0,1:T(8,128)} %param.35) | copy-start | bytes 38092
  123.8 97.4 %copy-start.17 = (f32[529,6]{0,1:T(8,128)S(1)}, f32[529,6]{0,1:T(8,128)}, u32[]{:S(2)}) copy-start(f32[529,6]{0,1:T(8,128)} %param.47) | copy-start | bytes 38092
  123.8 98.3 %copy-start.26 = (f32[24,8]{0,1:T(8,128)S(1)}, f32[24,8]{0,1:T(8,128)}, u32[]{:S(2)}) copy-start(f32[24,8]{0,1:T(8,128)} %param.46) | copy-start | bytes 2308
  123.8 98.9 %copy-start.21 = (f32[2,6,8]{2,0,1:T(2,128)S(1)}, f32[2,6,8]{2,0,1:T(2,128)}, u32[]{:S(2)}) copy-start(f32[2,6,8]{2,0,1:T(2,128)} %param.45) | copy-start | bytes 1156
  123.8 99.5 %copy-start.22 = (f32[768]{0:T(1024)S(1)}, f32[768]{0:T(1024)}, u32[]{:S(2)}) copy-start(f32[768]{0:T(1024)} %param.41) | copy-start | bytes 9220
  123.8 100.1 %copy-start.23 = (f32[768]{0:T(1024)S(1)}, f32[768]{0:T(1024)}, u32[]{:S(2)}) copy-start(f32[768]{0:T(1024)} %param.42) | copy-start | bytes 9220
  284.8 2.9 copy-start.2
  287.8 1.4 copy-start.6
  287.8 2.3 copy-start.12
  287.8 2.9 copy-start.1
  289.2 2.3 copy-start
  289.2 3.1 %copy-start.20 = (f32[6,192]{1,0:T(8,128)S(1)}, f32[6,192]{1,0:T(8,128)}, u32[]{:S(2)}) copy-start(f32[6,192]{1,0:T(8,128)} %get-tuple-element.264) | copy-start | bytes 13828
  289.2 3.7 %copy-start.5 = (f32[3,192,192]{2,1,0:T(8,128)S(1)}, f32[3,192,192]{2,1,0:T(8,128)}, u32[]{:S(2)}) copy-start(f32[3,192,192]{2,1,0:T(8,128)} %get-tuple-element.268) | copy-start | bytes 1327108
  290.7 3.1 %copy-start.11 = (f32[192,192]{1,0:T(8,128)S(1)}, f32[192,192]{1,0:T(8,128)}, u32[]{:S(2)}) copy-start(f32[192,192]{1,0:T(8,128)} %get-tuple-element.269) | copy-start | bytes 442372
  290.7 3.7 %copy-start.4 = (f32[192,768]{1,0:T(8,128)S(1)}, f32[192,768]{1,0:T(8,128)}, u32[]{:S(2)}) copy-start(f32[192,768]{1,0:T(8,128)} %get-tuple-element.270) | copy-start | bytes 1769476
  291.6 3.7 %copy-start.3 = (f32[192,768]{1,0:T(8,128)S(1)}, f32[192,768]{1,0:T(8,128)}, u32[]{:S(2)}) copy-start(f32[192,768]{1,0:T(8,128)} %get-tuple-element.131) | copy-start | bytes 1769476
  293.0 3.2 %copy-start.19 = (f32[6,192]{1,0:T(8,128)S(1)}, f32[6,192]{1,0:T(8,128)}, u32[]{:S(2)}) copy-start(f32[6,192]{1,0:T(8,128)} %get-tuple-element.272) | copy-start | bytes 13828
  293.0 3.8 %copy-start.10 = (bf16[3,192,192]{2,1,0:T(8,128)(2,1)S(1)}, bf16[3,192,192]{2,1,0:T(8,128)(2,1)}, u32[]{:S(2)}) copy-start(bf16[3,192,192]{2,1,0:T(8,128)(2,1)} %get-tuple-element.276) | copy-start | bytes 663556
  293.8 3.7 %copy-start.14 = (bf16[192,192]{1,0:T(8,128)(2,1)S(1)}, bf16[192,192]{1,0:T(8,128)(2,1)}, u32[]{:S(2)}) copy-start(bf16[192,192]{1,0:T(8,128)(2,1)} %get-tuple-element.277) | copy-start | bytes 221188
  293.8 4.3 %copy-start.9 = (bf16[192,768]{1,0:T(8,128)(2,1)S(1)}, bf16[192,768]{1,0:T(8,128)(2,1)}, u32[]{:S(2)}) copy-start(bf16[192,768]{1,0:T(8,128)(2,1)} %get-tuple-element.278) | copy-start | bytes 884740
  294.5 4.4 %copy-start.8 = (bf16[192,768]{1,0:T(8,128)(2,1)S(1)}, bf16[192,768]{1,0:T(8,128)(2,1)}, u32[]{:S(2)}) copy-start(bf16[192,768]{1,0:T(8,128)(2,1)} %get-tuple-element.139) | copy-start | bytes 884740
  295.3 4.3 %copy-start.25 = (f32[3,192]{1,0:T(4,128)S(1)}, f32[3,192]{1,0:T(4,128)}, u32[]{:S(2)}) copy-start(f32[3,192]{1,0:T(4,128)} %get-tuple-element.280) | copy-start | bytes 6916
  295.3 4.9 %copy-start.24 = (f32[3,192]{1,0:T(4,128)S(1)}, f32[3,192]{1,0:T(4,128)}, u32[]{:S(2)}) copy-start(f32[3,192]{1,0:T(4,128)} %get-tuple-element.281) | copy-start | bytes 6916
  295.3 5.5 %copy-start.30 = (f32[1,192]{1,0:T(1,128)S(1)}, f32[1,192]{1,0:T(1,128)}, u32[]{:S(2)}) copy-start(f32[1,192]{1,0:T(1,128)} %get-tuple-element.142) | copy-start | bytes 2308
  295.3 6.0 %copy-start.29 = (f32[1,192]{1,0:T(1,128)S(1)}, f32[1,192]{1,0:T(1,128)}, u32[]{:S(2)}) copy-start(f32[1,192]{1,0:T(1,128)} %get-tuple-element.143) | copy-start | bytes 2308
  295.3 6.6 %copy-start.28 = (f32[1,192]{1,0:T(1,128)S(1)}, f32[1,192]{1,0:T(1,128)}, u32[]{:S(2)}) copy-start(f32[1,192]{1,0:T(1,128)} %get-tuple-element.144) | copy-start | bytes 2308
  295.3 7.1 %copy-start.27 = (f32[1,192]{1,0:T(1,128)S(1)}, f32[1,192]{1,0:T(1,128)}, u32[]{:S(2)}) copy-start(f32[1,192]{1,0:T(1,128)} %get-tuple-element.147) | copy-start | bytes 2308
  295.3 7.7 %copy-start.18 = (f32[6,192]{1,0:T(8,128)S(1)}, f32[6,192]{1,0:T(8,128)}, u32[]{:S(2)}) copy-start(f32[6,192]{1,0:T(8,128)} %get-tuple-element.288) | copy-start | bytes 13828

commit v4 on v1

--- a/solution.py
+++ b/solution.py
@@ -1,7 +1,12 @@
+import functools
+
 import jax
 import jax.numpy as jnp
 from jax import lax
+from jax.experimental import pallas as pl
+from jax.experimental.pallas import tpu as pltpu
 from jax.sharding import PartitionSpec as P
+
 
 D = 768
 HEADS = 24
@@ -157,7 +162,1195 @@
     )
 
 
-def per_device(
+BF = jnp.bfloat16
+F32 = jnp.float32
+MESH = pl.DeviceIdType.MESH
+TOK = WIN * WIN
+HALF = D // 2
+VMEM_LIMIT = 66_000_000
+
+
+def dot(a, b):
+    return lax.dot_general(a, b, (((1,), (0,)), ((), ())), preferred_element_type=F32)
+
+
+def dot_t(a, b):
+    return lax.dot_general(a, b, (((1,), (1,)), ((), ())), preferred_element_type=F32)
+
+
+def t_dot(a, b):
+    return lax.dot_general(a, b, (((0,), (0,)), ((), ())), preferred_element_type=F32)
+
+
+def row_mean(x):
+    return jnp.sum(x, axis=-1, keepdims=True) * (1.0 / x.shape[-1])
+
+
+def remote(src, dst, send, recv, where):
+    return pltpu.make_async_remote_copy(
+        src_ref=src, dst_ref=dst, send_sem=send, recv_sem=recv, device_id=where, device_id_type=MESH
+    )
+
+
+def greet(barrier, places):
+    for place_of in places:
+        pl.semaphore_signal(barrier, inc=1, device_id=place_of, device_id_type=MESH)
+
+
+class LineSum:
+    def __init__(self, part, send, from_outer, from_mid, total, sems):
+        self.part, self.send, self.from_outer, self.from_mid, self.total = (
+            part, send, from_outer, from_mid, total,
+        )
+        self.s_out, self.r_out, self.s_mid, self.r_mid, self.s_tot, self.r_tot, self.s_cross = sems
+        z = lax.axis_index("tp")
+        self.is_mid = jnp.logical_and(z > 0, z < 3)
+        self.is_outer = jnp.logical_not(self.is_mid)
+        self.outer = jnp.where(z < 2, 0, 3)
+        self.mid = jnp.where(z < 2, 1, 2)
+        self.other_mid = 3 - self.mid
+        self.own = self.mid - 1
+        self.other = 1 - self.own
+
+    @staticmethod
+    def scratch(count):
+        return [
+            pltpu.VMEM((count, 2, TOK, HALF), BF),
+            pltpu.VMEM((count, 2, TOK, HALF), BF),
+            pltpu.VMEM((count, TOK, HALF), BF),
+            pltpu.SemaphoreType.DMA((count, 2)),
+            pltpu.SemaphoreType.DMA((count, 2)),
+            pltpu.SemaphoreType.DMA((count,)),
+            pltpu.SemaphoreType.DMA((count,)),
+            pltpu.SemaphoreType.DMA((count, 2)),
+            pltpu.SemaphoreType.DMA((count, 2)),
+            pltpu.SemaphoreType.DMA((count,)),
+        ]
+
+    @staticmethod
+    def build(part, refs, total):
+        return LineSum(part, refs[0], refs[1], refs[2], total, refs[3:10])
+
+    @staticmethod
+    def peers():
+        return 2
+
+    def greet(self, barrier):
+        pl.semaphore_signal(
+            barrier, inc=1, device_id={"tp": jnp.where(self.is_mid, self.outer, self.mid)},
+            device_id_type=MESH,
+        )
+
+        @pl.when(self.is_mid)
+        def _():
+            pl.semaphore_signal(
+                barrier, inc=1, device_id={"tp": self.other_mid}, device_id_type=MESH
+            )
+
+    def greet_count(self):
+        return jnp.where(self.is_mid, 2, 1)
+
+    def _to_mid(self, w, h):
+        return remote(self.send.at[w, h], self.from_outer.at[w, h], self.s_out.at[w, h],
+                      self.r_out.at[w, h], {"tp": self.mid})
+
+    def _across(self, w):
+        return remote(self.send.at[w, self.other], self.from_mid.at[w], self.s_mid.at[w],
+                      self.r_mid.at[w], {"tp": self.other_mid})
+
+    def _total_across(self, w, h):
+        return remote(self.total.at[w, h], self.total.at[w, h], self.s_cross.at[w],
+                      self.r_tot.at[w, h], {"tp": self.other_mid})
+
+    def _total_out(self, w, h):
+        return remote(self.total.at[w, h], self.total.at[w, h], self.s_tot.at[w, h],
+                      self.r_tot.at[w, h], {"tp": self.outer})
+
+    def put(self, w, value):
+        self.part[w, 0] = value[:, :HALF]
+        self.part[w, 1] = value[:, HALF:]
+
+    def start(self, w):
+        @pl.when(self.is_outer)
+        def _():
+            self.send[w, self.other] = self.part[w, self.other].astype(BF)
+            self._to_mid(w, self.other).start()
+            self.send[w, self.own] = self.part[w, self.own].astype(BF)
+            self._to_mid(w, self.own).start()
+
+    def cross(self, w):
+        @pl.when(self.is_mid)
+        def _():
+            self._to_mid(w, self.other).wait_recv()
+            self.send[w, self.other] = (
+                self.part[w, self.other] + self.from_outer[w, self.other].astype(F32)
+            ).astype(BF)
+            self._across(w).start()
+
+    def settle(self, w):
+        @pl.when(self.is_mid)
+        def _():
+            self._to_mid(w, self.own).wait_recv()
+            self._across(w).wait_recv()
+            self.total[w, self.own] = (
+                self.part[w, self.own]
+                + self.from_outer[w, self.own].astype(F32)
+                + self.from_mid[w].astype(F32)
+            ).astype(BF)
+            self._total_across(w, self.own).start()
+            self._total_out(w, self.own).start()
+
+    def hand(self, w):
+        @pl.when(self.is_mid)
+        def _():
+            self._total_across(w, self.other).wait_recv()
+            self._total_out(w, self.other).start()
+
+    def arrive(self, w):
+        @pl.when(self.is_outer)
+        def _():
+            self._total_out(w, 0).wait_recv()
+            self._total_out(w, 1).wait_recv()
+
+    def drain(self, w):
+        @pl.when(self.is_outer)
+        def _():
+            self._to_mid(w, 0).wait_send()
+            self._to_mid(w, 1).wait_send()
+
+        @pl.when(self.is_mid)
+        def _():
+            self._across(w).wait_send()
+            self._total_across(w, self.own).wait_send()
+            self._total_out(w, 0).wait_send()
+            self._total_out(w, 1).wait_send()
+
+
+class ShardSum:
+    def __init__(self, block_of, out, refs):
+        self.block_of, self.out = block_of, out
+        self.snd1, self.rcv1, self.snd2, self.rcv2, self.snd3, self.rcv3, self.s, self.r = refs
+        f = lax.axis_index("fsdp")
+        core = lax.rem(f, 2)
+        self.f, self.core = f, core
+        self.near, self.far = f + 1 - 2 * core, lax.rem(f + 2, 4)
+        self.ctx = 1 - lax.axis_index("ctx")
+
+    @staticmethod
+    def scratch(shape):
+        return [
+            pltpu.VMEM((2, *shape), BF), pltpu.VMEM((2, *shape), BF),
+            pltpu.VMEM(shape, BF), pltpu.VMEM(shape, BF),
+            pltpu.VMEM(shape, BF), pltpu.VMEM(shape, BF),
+            pltpu.SemaphoreType.DMA((4,)), pltpu.SemaphoreType.DMA((4,)),
+        ]
+
+    def _near(self, x):
+        return remote(self.snd1.at[x], self.rcv1.at[x], self.s.at[x], self.r.at[x], {"fsdp": self.near})
+
+    def _far(self):
+        return remote(self.snd2, self.rcv2, self.s.at[2], self.r.at[2], {"fsdp": self.far})
+
+    def _ctx(self):
+        return remote(self.snd3, self.rcv3, self.s.at[3], self.r.at[3], {"ctx": self.ctx})
+
+    def start(self):
+        for x in range(2):
+            self.snd1[x] = self.block_of(2 * x + 1 - self.core).astype(BF)
+            self._near(x).start()
+
+    def pair(self):
+        for x in range(2):
+            self._near(x).wait_recv()
+        other = lax.div(self.far, 2)
+        self.snd2[...] = (self.block_of(self.far) + self.rcv1[other].astype(F32)).astype(BF)
+        self._far().start()
+
+    def cross(self):
+        self._far().wait_recv()
+        mine = lax.div(self.f, 2)
+        self.snd3[...] = (
+            self.block_of(self.f) + self.rcv1[mine].astype(F32) + self.rcv2[...].astype(F32)
+        ).astype(BF)
+        self._ctx().start()
+
+    def finish(self):
+        self._ctx().wait_recv()
+        self.out[...] = self.snd3[...].astype(F32) + self.rcv3[...].astype(F32)
+
+    def drain(self):
+        for x in range(2):
+            self._near(x).wait_send()
+        self._far().wait_send()
+        self._ctx().wait_send()
+
+
+def vmem_call(body, outs, scratch, name, collective_id):
+    remote_kernel = {} if collective_id is None else dict(
+        collective_id=collective_id, has_side_effects=True
+    )
+
+    def call(*args):
+        return pl.pallas_call(
+            body,
+            out_shape=[jax.ShapeDtypeStruct(s, t) for s, t in outs],
+            in_specs=[pl.BlockSpec(memory_space=pltpu.VMEM)] * len(args),
+            out_specs=[pl.BlockSpec(memory_space=pltpu.VMEM)] * len(outs),
+            scratch_shapes=scratch,
+            compiler_params=pltpu.CompilerParams(vmem_limit_bytes=VMEM_LIMIT, **remote_kernel),
+            name=name,
+        )(*args)
+
+    return call
+
+
+def take(refs, counts):
+    groups, at = [], 0
+    for n in counts:
+        groups.append(refs[at : at + n])
+        at += n
+    return groups
+
+
+def window_rows(row_of, row_tmp, image, dst):
+    for r in range(WIN):
+        row_tmp[...] = row_of(image, r).astype(F32)
+        dst[2 * image, r * WIN : (r + 1) * WIN, :] = row_tmp[SHIFT : SHIFT + WIN, :]
+        dst[2 * image + 1, r * WIN : r * WIN + SHIFT, :] = row_tmp[SHIFT + WIN :, :]
+        dst[2 * image + 1, r * WIN + SHIFT : (r + 1) * WIN, :] = row_tmp[:SHIFT, :]
+
+
+def home_row(delta, row_tmp, image, r):
+    row_tmp[SHIFT : SHIFT + WIN, :] = delta[2 * image, r * WIN : (r + 1) * WIN, :]
+    row_tmp[SHIFT + WIN :, :] = delta[2 * image + 1, r * WIN : r * WIN + SHIFT, :]
+    row_tmp[:SHIFT, :] = delta[2 * image + 1, r * WIN + SHIFT : (r + 1) * WIN, :]
+    return row_tmp[...].astype(BF)
+
+
+class HomeRows:
+    def __init__(self, delta, row_tmp, out, halo, send, recv):
+        self.delta, self.row_tmp, self.out, self.halo, self.s, self.r = (
+            delta, row_tmp, out, halo, send, recv,
+        )
+
+    def _copy(self, i):
+        return remote(self.halo.at[i], self.out.at[i, 0:SHIFT], self.s.at[i], self.r.at[i],
+                      {"ctx": 1 - lax.axis_index("ctx")})
+
+    def go(self, i):
+        for r in range(SHIFT, WIN):
+            self.halo[i, r - SHIFT] = home_row(self.delta, self.row_tmp, i, r)
+        self._copy(i).start()
+        for r in range(SHIFT):
+            self.out[i, SHIFT + r] = home_row(self.delta, self.row_tmp, i, r)
+
+    def wait(self, i):
+        self._copy(i).wait_recv()
+        self._copy(i).wait_send()
+
+
+class TableSum:
+    def __init__(self, part, refs):
+        self.part = part
+        self.snd1, self.rcv1, self.snd2, self.rcv2, self.snd3, self.rcv3, self.s, self.r = refs
+        f = lax.axis_index("fsdp")
+        self.core, self.x, self.c = lax.rem(f, 2), lax.div(f, 2), lax.axis_index("ctx")
+        self.near, self.far = f + 1 - 2 * self.core, lax.rem(f + 2, 4)
+
+    @staticmethod
+    def scratch(heads):
+        shapes = [(heads, 2, 2, 24, 256)] * 2 + [(heads, 2, 24, 256)] * 2 + [(heads, 24, 256)] * 2
+        return [*[pltpu.VMEM(s, BF) for s in shapes], pltpu.SemaphoreType.DMA((3,)),
+                pltpu.SemaphoreType.DMA((3,))]
+
+    def _copy(self, n):
+        src, dst = ((self.snd1, self.rcv1), (self.snd2, self.rcv2), (self.snd3, self.rcv3))[n]
+        where = ({"fsdp": self.near}, {"fsdp": self.far}, {"ctx": 1 - self.c})[n]
+        return remote(src, dst, self.s.at[n], self.r.at[n], where)
+
+    def rows(self, core, x, c):
+        return pl.ds(pl.multiple_of(core * 96 + x * 48 + c * 24, 8), 24)
+
+    def start(self):
+        for x in range(2):
+            for c in range(2):
+                self.snd1[:, x, c] = self.part[:, self.rows(1 - self.core, x, c), :].astype(BF)
+        self._copy(0).start()
+
+    def pair(self):
+        self._copy(0).wait_recv()
+        x = 1 - self.x
+        for c in range(2):
+            self.snd2[:, c] = (
+                self.part[:, self.rows(self.core, x, c), :] + self.rcv1[:, x, c].astype(F32)
+            ).astype(BF)
+        self._copy(1).start()
+
+    def cross(self):
+        self._copy(1).wait_recv()
+        c = 1 - self.c
+        self.snd3[...] = (
+            self.part[:, self.rows(self.core, self.x, c), :] + self.rcv1[:, self.x, c].astype(F32)
+            + self.rcv2[:, c].astype(F32)
+        ).astype(BF)
+        self._copy(2).start()
+
+    def finish(self, out):
+        self._copy(2).wait_recv()
+        out[...] = (
+            self.part[:, self.rows(self.core, self.x, self.c), :]
+            + self.rcv1[:, self.x, self.c].astype(F32)
+            + self.rcv2[:, self.c].astype(F32) + self.rcv3[...].astype(F32)
+        )
+
+    def first_row(self):
+        return self.core * 96 + self.x * 48 + self.c * 24
+
+    def drain(self):
+        for n in range(3):
+            self._copy(n).wait_send()
+
+
+def main_body(*refs):
+    (
+        (feat, og, wq_m, wp_m, wu_m, wd_m, small_m, table_t, ridx, regr, regc),
+        (gin_o, gq_o, gp_o, small_o, gu_o, gd_o, rows, br, mix_o),
+        (sm_g, wq, wp_g, wp, wu, wd, fh, gh, bias_s, row_tmp, xw, ogw, n1, q, k, v, probs, ctx, part),
+        (n2_s, hid_s, dpl_s, ol_s, xhat_s, rstd_s, tot_two, gu, gd, dft, dbr),
+        (dh_s, dpos_s, chunk_s, halo_s, tot_one),
+        ls_one, ls_two, ls_four, up_refs, down_refs, table_refs,
+        (w_send, w_recv, h_send, h_recv, o_send, o_recv),
+    ) = take(refs, (11, 9, 19, 11, 5, 10, 10, 10, 8, 8, 8, 6))
+    windows, heads = probs.shape[0], probs.shape[1]
+    images = windows // 2
+    width = q.shape[2]
+    shard = wq_m.shape[1]
+    f, c = lax.axis_index("fsdp"), lax.axis_index("ctx")
+    near, far = f + 1 - 2 * lax.rem(f, 2), lax.rem(f + 2, 4)
+    one = LineSum.build(part, ls_one, br)
+    two = LineSum.build(part, ls_two, tot_two)
+    four = LineSum.build(part, ls_four, tot_one)
+
+    def block(at):
+        return pl.ds(pl.multiple_of(at * shard, shard), shard)
+
+    up = ShardSum(lambda at: gu[block(at), :], gu_o, up_refs)
+    down = ShardSum(lambda at: gd[block(at), :], gd_o, down_refs)
+    table = TableSum(dpos_s, table_refs)
+    barrier = pltpu.get_barrier_semaphore()
+    greet(barrier, [{"fsdp": near}, {"fsdp": far}, {"ctx": 1 - c}])
+    one.greet(barrier)
+    wq[:, block(f), :] = wq_m[...].astype(BF)
+    sm_g[f] = small_m[...].astype(BF)
+    wp_g[f] = wp_m[...].astype(BF)
+    wu[block(f), :] = wu_m[...].astype(BF)
+    wd[block(f), :] = wd_m[...].astype(BF)
+    pl.semaphore_wait(barrier, 3 + one.greet_count())
+
+    items = [
+        lambda at: sm_g.at[at],
+        lambda at: wq.at[:, block(at), :],
+        lambda at: wp_g.at[at],
+        lambda at: wu.at[block(at), :],
+        lambda at: wd.at[block(at), :],
+    ]
+
+    def copy_of(n, kind, at, where):
+        ref = items[n](at)
+        return remote(ref, ref, w_send.at[n, kind], w_recv.at[n, kind], {"fsdp": where})
+
+    halo_f = [
+        remote(feat.at[i, 0:SHIFT], fh.at[i], h_send.at[i], h_recv.at[i], {"ctx": 1 - c})
+        for i in range(images)
+    ]
+    halo_g = [
+        remote(og.at[i, 0:SHIFT], gh.at[i], h_send.at[images + i], h_recv.at[images + i], {"ctx": 1 - c})
+        for i in range(images)
+    ]
+    for copy in halo_f:
+        copy.start()
+    for n in range(len(items)):
+        copy_of(n, 0, f, far).start()
+        copy_of(n, 1, f, near).start()
+    for copy in halo_g:
+        copy.start()
+
+    def relay(n):
+        copy_of(n, 0, f, far).wait_recv()
+        copy_of(n, 2, far, near).start()
+
+    def gathered(n):
+        copy_of(n, 1, f, near).wait_recv()
+        copy_of(n, 2, far, near).wait_recv()
+
+    relay(0)
+
+    table_low = table_t[...].astype(BF).astype(F32)
+
+    def bias_rows(step, carry):
+        rows_at = pl.ds(pl.multiple_of(step * 8, 8), 8)
+        for half in range(2):
+            lanes_at = slice(half * 128, (half + 1) * 128)
+            idx = ridx[rows_at, lanes_at]
+            low = jnp.bitwise_and(idx, 127)
+            high = jnp.right_shift(idx, 7)
+            picks = [high == n for n in range(5)]
+            for h in range(heads):
+                found = jnp.zeros((8, 128), F32)
+                for n in range(5):
+                    tab = jnp.broadcast_to(
+                        table_low[h : h + 1, n * 128 : (n + 1) * 128], (8, 128)
+                    )
+                    got = jnp.take_along_axis(tab, low, axis=1, mode="promise_in_bounds")
+                    found = jnp.where(picks[n], got, found)
+                bias_s[h, rows_at, lanes_at] = found
+        return carry
+
+    lax.fori_loop(0, TOK // 8, bias_rows, 0)
+    gathered(0)
+    lanes = rows.shape[1]
+    rows[...] = jnp.concatenate([sm_g[n].astype(F32) for n in range(4)], axis=1)
+    unit = lax.broadcasted_iota(jnp.int32, (shard, lanes), 0)
+    lane = lax.broadcasted_iota(jnp.int32, (shard, lanes), 1)
+    biases = jnp.zeros((16, lanes), F32)
+    for n in range(4):
+        same = jnp.logical_and(
+            jnp.right_shift(lane, 5) == jnp.right_shift(unit, 3),
+            jnp.bitwise_and(lane, 31) == jnp.bitwise_and(unit, 7) + n * 8,
+        )
+        biases = biases + dot(sm_g[n], jnp.where(same, 1.0, 0.0).astype(BF))
+    rows[8:16, :] = biases[8:16, :]
+    dpos_s[...] = jnp.zeros_like(dpos_s)
+    small_o[...] = jnp.zeros_like(small_o)
+    for i in range(images):
+        halo_f[i].wait_recv()
+        window_rows(
+            lambda im, r: feat[im, SHIFT + r] if r < SHIFT else fh[im, r - SHIFT], row_tmp, i, xw
+        )
+    relay(1)
+    gain_one, offset_one = rows[0:1, :], rows[1:2, :]
+    bias_proj, gain_two, offset_two = rows[2:3, :], rows[3:4, :], rows[4:5, :]
+    bias_hidden = rows[8:9, :]
+    bias_q, bias_v = rows[9:10, :width], rows[10:11, :width]
+    head_of = jnp.right_shift(lax.broadcasted_iota(jnp.int32, (1, width), 1), 5)
+    picks_of = [jnp.where(head_of == h, 1.0, 0.0).astype(BF) for h in range(heads)]
+    gathered(1)
+    relay(2)
+    gathered(2)
+    wp[...] = jnp.concatenate([wp_g[n] for n in range(4)], axis=1)
+
+    def spot(w):
+        return pl.ds(pl.multiple_of(w * TOK, TOK), TOK)
+
+    def add_rows(n, term):
+        small_o[n : n + 1, : term.shape[1]] = small_o[n : n + 1, : term.shape[1]] + jnp.sum(
+            term, axis=0, keepdims=True
+        )
+
+    def serve(w, line, before):
+        @pl.when(w == 0)
+        def _():
+            if before is not None:
+                before.cross(windows - 1)
+                before.settle(windows - 1)
+                before.hand(windows - 2)
+
+        @pl.when(w == 1)
+        def _():
+            if before is not None:
+                before.hand(windows - 1)
+
+        @pl.when(w >= 1)
+        def _():
+            line.cross(w - 1)
+            line.settle(w - 1)
+
+        @pl.when(w >= 2)
+        def _():
+            line.hand(w - 2)
+
+    def forward(w, carry):
+        x = xw[w]
+        centred = x - row_mean(x)
+        xhat = centred * lax.rsqrt(row_mean(centred * centred) + NORM_EPS)
+        normed = (xhat * gain_one + offset_one).astype(BF)
+        n1[spot(w), :] = normed
+        q_w = (dot(normed, wq[0]) + bias_q).astype(BF)
+        k_w = dot(normed, wq[1]).astype(BF)
+        v_w = (dot(normed, wq[2]) + bias_v).astype(BF)
+        q[w] = q_w
+        k[w] = k_w
+        v[w] = v_w
+        mask = jnp.where(regc[w] == regr[w], 0.0, MASK_FILL)
+        context = jnp.zeros((TOK, width), F32)
+        for h in range(heads):
+            scores = dot_t(q_w * picks_of[h], k_w) * HD ** (-0.5) + bias_s[h, :, :TOK] + mask
+            lifted = jnp.exp(scores - jnp.max(scores, axis=-1, keepdims=True))
+            p = lifted / jnp.sum(lifted, axis=-1, keepdims=True)
+            probs[w, h] = p
+            context = context + dot(p.astype(BF), v_w * picks_of[h])
+        low = context.astype(BF)
+        ctx[spot(w), :] = low
+        one.put(w, dot(low, wp[...]))
+        one.start(w)
+        serve(w, one, None)
+        return carry
+
+    lax.fori_loop(0, windows, forward, 0)
+    relay(3)
+    relay(4)
+    gathered(3)
+    gathered(4)
+
+    def middle(w, carry):
+        one.arrive(w)
+        resid = xw[w] + (jnp.concatenate([br[w, 0], br[w, 1]], axis=1).astype(F32) + bias_proj)
+        centred = resid - row_mean(resid)
+        rstd = lax.rsqrt(row_mean(centred * centred) + NORM_EPS)
+        xhat = centred * rstd
+        xhat_s[w] = xhat
+        rstd_s[w] = jnp.broadcast_to(rstd, (TOK, 128))
+        normed = (xhat * gain_two + offset_two).astype(BF)
+        n2_s[spot(w), :] = normed
+        pre = dot(normed, wu[...]) + bias_hidden
+        cdf = 0.5 * (1.0 + lax.erf(pre * 0.7071067811865476))
+        slope = cdf + pre * (jnp.exp(-0.5 * (pre * pre)) * 0.3989422804014327)
+        hid = (pre * cdf).astype(BF)
+        hid_s[spot(w), :] = hid
+
+        @pl.when(w % 2 == 0)
+        def _():
+            i = w // 2
+            for n in range(images):
+
+                @pl.when(i == n)
+                def _():
+                    halo_g[n].wait_recv()
+                    window_rows(
+                        lambda im, r: og[im, SHIFT + r] if r < SHIFT else gh[im, r - SHIFT],
+                        row_tmp, n, ogw,
+                    )
+
+        low = ogw[w].astype(BF)
+        ol_s[spot(w), :] = low
+        d_pre = dot(low, wd[...]) * slope
+        add_rows(6, d_pre)
+        dpl = d_pre.astype(BF)
+        dpl_s[spot(w), :] = dpl
+        two.put(w, dot_t(dpl, wu[...]))
+        two.start(w)
+        mixed = dot_t(hid, wd[...])
+        mix_o[w, 0] = mixed[:, :HALF]
+        mix_o[w, 1] = mixed[:, HALF:]
+        serve(w, two, one)
+        return carry
+
+    lax.fori_loop(0, windows, middle, 0)
+
+    def grad_chunk(m, carry):
+        chunk = pl.ds(pl.multiple_of(m * 256, 256), 256)
+        gd[chunk, :] = t_dot(ol_s[:, chunk], hid_s[...])
+        gu[chunk, :] = t_dot(n2_s[:, chunk], dpl_s[...])
+        return carry
+
+    lax.fori_loop(0, D // 256, grad_chunk, 0)
+    down.start()
+    up.start()
+
+    def backward(w, carry):
+        two.arrive(w)
+        d_two = jnp.concatenate([tot_two[w, 0], tot_two[w, 1]], axis=1).astype(F32)
+        xhat = xhat_s[w]
+        e = d_two * gain_two
+        d_flat = (e - row_mean(e) - xhat * row_mean(e * xhat)) * rstd_s[w, :, 0:1]
+        og_w = ogw[w]
+        d_resid = og_w + d_flat
+        dft[w] = d_flat
+        d_branch = d_resid.astype(BF)
+        dbr[spot(w), :] = d_branch
+        for n, term in ((2, d_resid), (3, d_two * xhat), (4, d_two), (5, og_w)):
+            add_rows(n, term)
+        d_ctx = dot_t(d_branch, wp[...]).astype(BF)
+        q_w, k_w, v_w = q[w], k[w], v[w]
+        d_q = jnp.zeros((TOK, width), F32)
+        d_k = jnp.zeros((TOK, width), F32)
+        d_v = jnp.zeros((TOK, width), F32)
+        for h in range(heads):
+            d_ctx_h = d_ctx * picks_of[h]
+            p = probs[w, h]
+            d_p = dot_t(d_ctx_h, v_w)
+            d_v = d_v + t_dot(p.astype(BF), d_ctx_h)
+            d_s = p * (d_p - jnp.sum(p * d_p, axis=-1, keepdims=True))
+            dpos_s[h, :TOK, :TOK] = dpos_s[h, :TOK, :TOK] + d_s
+            d_l = (d_s * HD ** (-0.5)).astype(BF)
+            d_q = d_q + dot(d_l, k_w * picks_of[h])
+            d_k = d_k + t_dot(d_l, q_w * picks_of[h])
+        partial = jnp.zeros((TOK, D), F32)
+        for n, d_n in enumerate((d_q, d_k, d_v)):
+            low = d_n.astype(BF)
+            dh_s[n, spot(w), :] = low
+            partial = partial + dot_t(low, wq[n])
+            if n != 1:
+                add_rows(8 + n // 2, low.astype(F32))
+        four.put(w, partial)
+        four.start(w)
+        serve(w, four, two)
+
+        @pl.when(w == 1)
+        def _():
+            down.pair()
+            up.pair()
+
+        @pl.when(w == windows - 1)
+        def _():
+            down.cross()
+            up.cross()
+
+        return carry
+
+    lax.fori_loop(0, windows, backward, 0)
+    table.start()
+    for n in range(3):
+        gq_o[n] = t_dot(n1[...], dh_s[n])
+    four.cross(windows - 1)
+    table.pair()
+    gp = t_dot(ctx[...], dbr[...])
+    for n in range(4):
+        gp_o[n] = gp[:, n * shard : (n + 1) * shard]
+    four.hand(windows - 2)
+    four.settle(windows - 1)
+    table.cross()
+
+    home = HomeRows(xhat_s, row_tmp, gin_o, halo_s, o_send, o_recv)
+
+    def back(w):
+        four.arrive(w)
+        x = xw[w]
+        centred = x - row_mean(x)
+        rstd = lax.rsqrt(row_mean(centred * centred) + NORM_EPS)
+        xhat = centred * rstd
+        d_one = jnp.concatenate([tot_one[w, 0], tot_one[w, 1]], axis=1).astype(F32)
+        e = d_one * gain_one
+        xhat_s[w] = dft[w] + (e - row_mean(e) - xhat * row_mean(e * xhat)) * rstd
+        for n, term in ((0, d_one * xhat), (1, d_one)):
+            add_rows(n, term)
+
+    back(0)
+    back(1)
+    home.go(0)
+    table.finish(chunk_s)
+    first = table.first_row()
+    ident = lax.broadcasted_iota(jnp.int32, (640, TOK), 0)
+
+    def bin_row(i, acc):
+        hot = jnp.where(ident == ridx[pl.ds(first + i, 1), :TOK], 1.0, 0.0).astype(BF)
+        vals = jnp.concatenate(
+            [chunk_s[h, pl.ds(i, 1), :TOK] for h in range(heads)] + [jnp.zeros((8 - heads, TOK), F32)],
+            axis=0,
+        )
+        high = vals.astype(BF)
+        low = (vals - high.astype(F32)).astype(BF)
+        return acc + dot_t(jnp.concatenate([high, low], axis=0), hot)
+
+    hist = lax.fori_loop(0, 24, bin_row, jnp.zeros((16, 640), F32))
+    small_o[16:24, :640] = hist[0:8] + hist[8:16]
+    four.hand(windows - 1)
+    down.finish()
+    up.finish()
+    back(2)
+    back(3)
+    home.go(1)
+    for i in range(images):
+        home.wait(i)
+    for w in range(windows):
+        for line in (one, two, four):
+            line.drain(w)
+    for copy in halo_f + halo_g:
+        copy.wait_send()
+    for n in range(len(items)):
+        copy_of(n, 0, f, far).wait_send()
+        copy_of(n, 1, f, near).wait_send()
+        copy_of(n, 2, far, near).wait_send()
+    up.drain()
+    down.drain()
+    table.drain()
+
+
+def forward_backward(features, out_grad, regions, rel_index, w_qkv, w_proj, w_up, w_down_t,
+                     norm_vecs, head_bias, hidden_bias, rel_table):
+    images = features.shape[0]
+    windows = 2 * images
+    shard, width = w_qkv.shape[1], w_qkv.shape[2]
+    hidden = w_up.shape[1]
+    heads = width // HD
+    small = jnp.concatenate(
+        [
+            norm_vecs,
+            jnp.zeros((2, shard), F32),
+            hidden_bias.reshape(1, shard),
+            jnp.pad(head_bias.reshape(2, -1), ((0, 5), (0, shard - head_bias[0].size))),
+        ],
+        axis=0,
+    )
+    table_t = jnp.pad(
+        rel_table.T, ((0, 8 - heads), (0, 640 - rel_table.shape[0]))
+    )
+    ridx = jnp.pad(rel_index, ((0, 192 - TOK), (0, 256 - TOK)))
+    region_win = to_windows(regions[..., None])[..., 0]
+    halves = (windows, 2, TOK, HALF)
+    outs = [
+        (features.shape, BF), ((3, D, width), F32), ((4, width, shard), F32), ((24, D), F32),
+        ((shard, hidden), F32), ((shard, hidden), F32), ((16, D), F32), (halves, BF), (halves, F32),
+    ]
+    vm = pltpu.VMEM
+    flat = windows * TOK
+    scratch = [
+        vm((4, 16, shard), BF), vm((3, D, width), BF), vm((4, width, shard), BF), vm((width, D), BF),
+        vm((D, hidden), BF), vm((D, hidden), BF), vm((images, SHIFT, 24, D), BF),
+        vm((images, SHIFT, 24, D), F32), vm((heads, TOK, 256), F32), vm((24, D), F32),
+        vm((windows, TOK, D), F32), vm((windows, TOK, D), F32), vm((flat, D), BF),
+        vm((windows, TOK, width), BF), vm((windows, TOK, width), BF), vm((windows, TOK, width), BF),
+        vm((windows, heads, TOK, TOK), F32), vm((flat, width), BF), vm(halves, F32),
+        vm((flat, D), BF), vm((flat, hidden), BF), vm((flat, hidden), BF), vm((flat, D), BF),
+        vm((windows, TOK, D), F32), vm((windows, TOK, 128), F32), vm(halves, BF),
+        vm((D, hidden), F32), vm((D, hidden), F32), vm((windows, TOK, D), F32), vm((flat, D), BF),
+        vm((3, flat, width), BF), vm((heads, 192, 256), F32), vm((heads, 24, 256), F32),
+        vm((images, SHIFT, 24, D), BF), vm(halves, BF),
+        *LineSum.scratch(windows), *LineSum.scratch(windows), *LineSum.scratch(windows),
+        *ShardSum.scratch((shard, hidden)), *ShardSum.scratch((shard, hidden)),
+        *TableSum.scratch(heads),
+        *[pltpu.SemaphoreType.DMA((5, 3))] * 2,
+        *[pltpu.SemaphoreType.DMA((2 * images,))] * 2,
+        *[pltpu.SemaphoreType.DMA((images,))] * 2,
+    ]
+    return vmem_call(main_body, outs, scratch, "forward_backward", 1)(
+        features, out_grad, w_qkv, w_proj, w_up, w_down_t, small, table_t, ridx,
+        region_win[:, None, :], region_win[:, :, None],
+    )
+
+
+def total_of(x):
+    return jnp.sum(jnp.sum(x, axis=1, keepdims=True), axis=0, keepdims=True)
+
+
+def exact(a, b, dims):
+    return lax.dot_general(
+        a, b, (dims, ((), ())), precision=lax.Precision.HIGHEST, preferred_element_type=F32
+    )
+
+
+def lane_sums(squares):
+    return exact(jnp.ones((8, squares.shape[1]), F32), squares, ((1,), (1,)))[0:1]
+
+
+def as_column(row):
+    n = row.shape[1]
+    step = 64
+    eye = lax.broadcasted_iota(jnp.int32, (step, step), 0) == lax.broadcasted_iota(
+        jnp.int32, (step, step), 1
+    )
+    return jnp.concatenate(
+        [
+            jnp.sum(
+                jnp.where(eye, jnp.broadcast_to(row[:, at : at + step], (step, step)), 0.0),
+                axis=1, keepdims=True,
+            )
+            for at in range(0, n, step)
+        ],
+        axis=0,
+    )
+
+
+def lane_pack(values):
+    lane = lax.broadcasted_iota(jnp.int32, (8, 128), 1)
+    packed = jnp.zeros((8, 128), F32)
+    for n, value in enumerate(values):
+        packed = packed + jnp.where(lane == n, jnp.broadcast_to(value, (8, 128)), 0.0)
+    return packed
+
+
+def wide(ref):
+    if ref.shape[1] != 128:
+        return ref[...]
+    return jnp.concatenate([ref[n : n + 1, :] for n in range(ref.shape[0])], axis=1)
+
+
+def put_wide(ref, row):
+    if ref.shape[1] != 128:
+        ref[...] = row
+    else:
+        for n in range(ref.shape[0]):
+            ref[n : n + 1, :] = row[:, n * 128 : (n + 1) * 128]
+
+
+def plain(grad, state):
+    new = DECAY_RATE * state + (1.0 - DECAY_RATE) * (grad * grad + STAT_EPS)
+    return new, grad * lax.rsqrt(new)
+
+
+def optimizer_body(*refs):
+    (
+        (gq, gp, g_up, g_down, small, rows, br, mix),
+        (w_qkv, w_proj, w_up, w_down, w_norm, w_heads, w_hidden, w_table),
+        (row_qkv, col_qkv, row_proj, col_proj, row_up, col_up, row_down, col_down),
+        (s_norm, s_heads, s_hidden, s_table),
+        (home_o, gq_o, gp_o, gn_o, gh_o, gx_o, gt_o, uq_o, up_o, uu_o, ud_o),
+        (rq_o, kq_o, rp_o, kp_o, ru_o, ku_o, rd_o, kd_o, size_o),
+        qkv_refs, proj_refs, line_refs,
+        (mixed, sm_s, sm_r, t_s, f_s, z_s, c_s, delta, row_tmp, halo_s),
+        (sm_send, sm_recv, t_send, t_recv, f_send, f_recv, z_send, z_recv, c_send, c_recv,
+         o_send, o_recv),
+    ) = take(refs, (8, 8, 8, 4, 11, 9, 8, 8, 10, 10, 12))
+    f, c, t = lax.axis_index("fsdp"), lax.axis_index("ctx"), lax.axis_index("tp")
+    windows = br.shape[0]
+    images = windows // 2
+    shard, width = w_qkv.shape[1], w_qkv.shape[2]
+    hidden = f_s.shape[2]
+    ff = 4 * hidden
+    heads = width // HD
+    me = f * 4 + t
+    first_f = jnp.where(f == 0, 1.0, 0.0)
+    first_t = jnp.where(t == 0, 1.0, 0.0)
+
+    def other(n):
+        at = lax.rem(me + n, 16)
+        return {"fsdp": lax.div(at, 4), "tp": lax.rem(at, 4)}
+
+    barrier = pltpu.get_barrier_semaphore()
+    greet(barrier, [{"ctx": 1 - c}] + [other(n) for n in range(1, 16)])
+    qkv = ShardSum(
+        lambda at: gq[:, pl.ds(pl.multiple_of(at * shard, shard), shard), :], gq_o, qkv_refs
+    )
+    proj = ShardSum(lambda at: gp[at], gp_o, proj_refs)
+    line = LineSum.build(mix, line_refs, mixed)
+    sm_s[0] = small[...]
+
+    def swap(n):
+        where = ({"fsdp": qkv.near}, {"fsdp": qkv.far}, {"ctx": 1 - c})[n]
+        return remote(sm_s.at[n], sm_r.at[n], sm_send.at[n], sm_recv.at[n], where)
+
+    pl.semaphore_wait(barrier, 16)
+    swap(0).start()
+    qkv.start()
+    proj.start()
+    for w in range(windows):
+        line.start(w)
+
+    keep = 1.0 - DECAY_RATE
+    t_s[t] = jnp.zeros((8, shard), F32)
+    f_s[f] = jnp.zeros((8, hidden), F32)
+    sq_up = g_up[...] * g_up[...]
+    sq_down = g_down[...] * g_down[...]
+    t_s[t, 4:5, :] = lane_sums(sq_up)
+    t_s[t, 5:6, :] = lane_sums(sq_down)
+    f_s[f, 4:5, :] = jnp.sum(sq_up, axis=0, keepdims=True)
+    f_s[f, 5:6, :] = jnp.sum(sq_down, axis=0, keepdims=True)
+    tot_up, tot_down = total_of(sq_up), total_of(sq_down)
+
+    qkv.pair()
+    proj.pair()
+    swap(0).wait_recv()
+    sm_s[1] = sm_s[0] + sm_r[0]
+    swap(1).start()
+    line.cross(0)
+
+    old_rows = [
+        first_t * jnp.sum(row_qkv[0:1, :], axis=1, keepdims=True),
+        first_t * jnp.sum(row_qkv[1:2, :], axis=1, keepdims=True),
+        first_t * jnp.sum(row_qkv[2:3, :], axis=1, keepdims=True),
+        first_f * total_of(row_proj[...]),
+        first_t * total_of(row_up[...]),
+        first_f * total_of(row_down[...]),
+    ]
+    masters = [
+        sum(total_of(w_qkv[n] * w_qkv[n]) for n in range(3)),
+        total_of(w_proj[...] * w_proj[...]),
+        total_of(w_up[...] * w_up[...]),
+        total_of(w_down[...] * w_down[...]),
+        *[
+            first_t * jnp.sum(w_norm[n : n + 1, :] * w_norm[n : n + 1, :], axis=1, keepdims=True)
+            for n in range(6)
+        ],
+        *[total_of(w_heads[:, n, :] * w_heads[:, n, :]) for n in range(2)],
+        total_of(w_hidden[...] * w_hidden[...]),
+        first_f * total_of(w_table[...] * w_table[...]),
+    ]
+    line.settle(0)
+    line.cross(1)
+    qkv.cross()
+    proj.cross()
+    swap(1).wait_recv()
+    sm_s[2] = sm_s[1] + sm_r[1]
+    swap(2).start()
+    line.hand(0)
+    line.settle(1)
+    line.cross(2)
+    qkv.finish()
+    proj.finish()
+
+    tot_q = []
+    for n in range(3):
+        sq = gq_o[n] * gq_o[n]
+        t_s[t, n : n + 1, :] = lane_sums(sq)
+        f_s[f, n : n + 1, :width] = jnp.sum(sq, axis=0, keepdims=True)
+        tot_q.append(total_of(sq))
+    sq = gp_o[...] * gp_o[...]
+    f_s[f, 3:4, :shard] = lane_sums(sq)
+    t_s[t, 3:4, :] = jnp.sum(sq, axis=0, keepdims=True)
+    z_s[me] = lane_pack([*tot_q, total_of(sq), tot_up, tot_down, *old_rows, *masters])
+
+    def t_copy(n):
+        return remote(t_s.at[t], t_s.at[t], t_send.at[n], t_recv.at[n], {"tp": lax.rem(t + n, 4)})
+
+    def f_copy(n):
+        return remote(f_s.at[f], f_s.at[f], f_send.at[n], f_recv.at[n], {"fsdp": lax.rem(f + n, 4)})
+
+    def z_copy(n):
+        return remote(z_s.at[me], z_s.at[me], z_send.at[n], z_recv.at[n], other(n))
+
+    def c_copy(n):
+        return remote(c_s.at[me], c_s.at[me], c_send.at[n], c_recv.at[n], other(n))
+
+    for n in range(1, 4):
+        t_copy(n).start()
+        f_copy(n).start()
+    for n in range(1, 16):
+        z_copy(n).start()
+    line.hand(1)
+    line.settle(2)
+    line.cross(3)
+
+    swap(2).wait_recv()
+    sm = sm_s[2] + sm_r[2]
+
+    def own_lanes(x, size):
+        out = x[:, :size]
+        for n in range(1, 4):
+            out = jnp.where(f == n, x[:, n * size : (n + 1) * size], out)
+        return out
+
+    part = HD // 4
+
+    def own_units(row, count):
+        lanes = count * HD
+        lane = lax.broadcasted_iota(jnp.int32, (count, lanes), 1)
+        unit = lax.broadcasted_iota(jnp.int32, (count, lanes), 0)
+        only = jnp.where(
+            jnp.right_shift(lane, 5) == unit, jnp.broadcast_to(row, (count, lanes)), 0.0
+        )
+        at = lax.broadcasted_iota(jnp.int32, (lanes, part), 0)
+        k = lax.broadcasted_iota(jnp.int32, (lanes, part), 1)
+        pick = jnp.where(jnp.bitwise_and(at, HD - 1) == f * part + k, 1.0, 0.0)
+        return only, pick
+
+    gn = own_lanes(sm[0:6, :], shard)
+    gh = [exact(*own_units(sm[8 + n : 9 + n, :width], heads), ((1,), (0,))) for n in range(2)]
+    only, pick = own_units(sm[6:7, :], hidden // HD)
+    gx = exact(pick, only, ((0,), (1,)))
+    gt = sm[16 : 16 + heads, : w_table.shape[1]]
+    gn_o[...] = gn
+    gx_o[...] = gx
+    gt_o[...] = gt
+    small_sq = first_t * total_of(plain(gn, s_norm[...])[1] ** 2)
+    for n in range(2):
+        gh_o[:, n, :] = gh[n]
+        small_sq = small_sq + total_of(plain(gh[n], s_heads[:, n, :])[1] ** 2)
+    small_sq = small_sq + total_of(plain(gx, s_hidden[...])[1] ** 2)
+    small_sq = small_sq + first_f * total_of(plain(gt, s_table[...])[1] ** 2)
+
+    for n in range(1, 4):
+        t_copy(n).wait_recv()
+        f_copy(n).wait_recv()
+    t_sum = t_s[0] + t_s[1] + t_s[2] + t_s[3]
+    f_sum = f_s[0] + f_s[1] + f_s[2] + f_s[3]
+    for n in range(1, 16):
+        z_copy(n).wait_recv()
+    z_sum = z_s[0]
+    for n in range(1, 16):
+        z_sum = z_sum + z_s[n]
+    lane8 = lax.broadcasted_iota(jnp.int32, (8, 128), 1)
+
+    def scalar(n):
+        return jnp.sum(jnp.where(lane8 == n, z_sum, 0.0)[0:1], axis=1, keepdims=True)
+
+    def fresh(old, summed, count):
+        return DECAY_RATE * old + keep * (summed / count + STAT_EPS)
+
+    rq = fresh(row_qkv[...], t_sum[0:3, :], D)
+    kq = fresh(col_qkv[...], f_sum[0:3, :width], D)
+    rp = fresh(wide(row_proj), f_sum[3:4, :width], D)
+    kp = fresh(wide(col_proj), t_sum[3:4, :], D)
+    ru = fresh(wide(row_up), t_sum[4:5, :], ff)
+    ku = fresh(wide(col_up), f_sum[4:5, :], D)
+    rd = fresh(wide(row_down), f_sum[5:6, :], D)
+    kd = fresh(wide(col_down), t_sum[5:6, :], ff)
+
+    def mean_row(n, rows_all, cols_all):
+        return (
+            DECAY_RATE * scalar(6 + n) + keep * (scalar(n) / cols_all + rows_all * STAT_EPS)
+        ) / rows_all
+
+    scale_q = [
+        as_column(lax.rsqrt(rq[n : n + 1, :] / mean_row(n, D, D))) * lax.rsqrt(kq[n : n + 1, :])
+        for n in range(3)
+    ]
+    scale_p = as_column(lax.rsqrt(rp / mean_row(3, D, D))) * lax.rsqrt(kp)
+    scale_u = as_column(lax.rsqrt(ru / mean_row(4, D, ff))) * lax.rsqrt(ku)
+    scale_d = as_column(lax.rsqrt(kd)) * lax.rsqrt(rd / mean_row(5, ff, D))
+    big_sq = small_sq
+    for n in range(3):
+        u = gq_o[n] * scale_q[n]
+        uq_o[n] = u
+        big_sq = big_sq + total_of(u * u)
+    for grad, scale, ref in ((gp_o, scale_p, up_o), (g_up, scale_u, uu_o), (g_down, scale_d, ud_o)):
+        u = grad[...] * scale
+        ref[...] = u
+        big_sq = big_sq + total_of(u * u)
+    c_s[me] = jnp.broadcast_to(big_sq, (8, 128))
+    for n in range(1, 16):
+        c_copy(n).start()
+    line.hand(2)
+    line.settle(3)
+    rq_o[...] = rq
+    kq_o[...] = kq
+    for ref, row in ((rp_o, rp), (kp_o, kp), (ru_o, ru), (ku_o, ku), (rd_o, rd), (kd_o, kd)):
+        put_wide(ref, row)
+
+    home = HomeRows(delta, row_tmp, home_o, halo_s, o_send, o_recv)
+    both_bias = rows[2:3, :] + rows[5:6, :]
+
+    def lift(w):
+        line.arrive(w)
+        delta[w] = (
+            jnp.concatenate([br[w, 0], br[w, 1]], axis=1).astype(F32)
+            + jnp.concatenate([mixed[w, 0], mixed[w, 1]], axis=1).astype(F32) + both_bias
+        )
+
+    lift(0)
+    lift(1)
+    home.go(0)
+    line.hand(3)
+    lift(2)
+    lift(3)
+    home.go(1)
+
+    counts = [3 * D * D, D * D, D * ff, ff * D] + [D] * 8 + [ff, RELP * HEADS]
+    sizes = [jnp.sqrt(scalar(12 + n) / counts[n] + STAT_EPS) for n in range(14)]
+    for n in range(1, 16):
+        c_copy(n).wait_recv()
+    all_sq = c_s[0]
+    for n in range(1, 16):
+        all_sq = all_sq + c_s[n]
+    count_all = 4 * D * D + 2 * D * ff + 8 * D + ff + RELP * HEADS
+    clip = jnp.sqrt(all_sq[0:1, 0:1] / count_all)
+    factor = STEP_RATE / jnp.maximum(1.0, clip / CLIP_LEVEL)
+    size_o[...] = lane_pack([size * factor for size in sizes] + [clip])
+    for i in range(images):
+        home.wait(i)
+    for n in range(3):
+        swap(n).wait_send()
+    for n in range(1, 4):
+        t_copy(n).wait_send()
+        f_copy(n).wait_send()
+    for n in range(1, 16):
+        z_copy(n).wait_send()
+        c_copy(n).wait_send()
+    for w in range(windows):
+        line.drain(w)
+    qkv.drain()
+    proj.drain()
+
+
+def finish_body(*refs):
+    (
+        (home_out, feat, home_in, og, gq, gp, g_up, g_down, gn, gh, gx, gt, uq, up, uu, ud),
+        (w_qkv, w_proj, w_up, w_down, w_norm, w_heads, w_hidden, w_table),
+        (s_norm, s_heads, s_hidden, s_table),
+        stats, (size,),
+        (out_o, gin_o, gq_o, gp_o, gu_o, gd_o, gn_o, gh_o, gx_o, gt_o),
+        (nq_o, np_o, nu_o, nd_o, nn_o, nh_o, nx_o, nt_o),
+        (cq_o, cp_o, cu_o, cd_o),
+        stats_o, (sn_o, sh_o, sx_o, st_o), (clip_o,),
+    ) = take(refs, (16, 8, 4, 8, 1, 10, 8, 4, 8, 4, 1))
+    lane8 = lax.broadcasted_iota(jnp.int32, (8, 128), 1)
+    table = size[...]
+
+    def step(n):
+        return jnp.sum(jnp.where(lane8 == n, table, 0.0)[0:1], axis=1, keepdims=True)
+
+    out_o[...] = feat[...].astype(F32) + home_out[...].astype(F32)
+    gin_o[...] = og[...] + home_in[...].astype(F32)
+    for src, dst in (
+        (gq, gq_o), (gp, gp_o), (g_up, gu_o), (g_down, gd_o), (gn, gn_o), (gh, gh_o), (gx, gx_o),
+        (gt, gt_o), *zip(stats, stats_o),
+    ):
+        dst[...] = src[...]
+    for n, (master, u, new_o, low_o) in enumerate(
+        ((w_qkv, uq, nq_o, cq_o), (w_proj, up, np_o, cp_o), (w_up, uu, nu_o, cu_o), (w_down, ud, nd_o, cd_o))
+    ):
+        new = master[...] - step(n) * u[...]
+        new_o[...] = new
+        low_o[...] = new.astype(BF)
+    sn, un = plain(gn[...], s_norm[...])
+    sn_o[...] = sn
+    for n in range(6):
+        nn_o[n : n + 1, :] = w_norm[n : n + 1, :] - step(4 + n) * un[n : n + 1, :]
+    for n in range(2):
+        sh, uh = plain(gh[:, n, :], s_heads[:, n, :])
+        sh_o[:, n, :] = sh
+        nh_o[:, n, :] = w_heads[:, n, :] - step(10 + n) * uh
+    sx, ux = plain(gx[...], s_hidden[...])
+    sx_o[...] = sx
+    nx_o[...] = w_hidden[...] - step(12) * ux
+    st, ut = plain(gt[...], s_table[...])
+    st_o[...] = st
+    nt_o[...] = w_table[...] - step(13) * ut
+    clip_o[...] = step(14)
+
+
+def optimizer(gq, gp, g_up, g_down, small, rows, br, mix, home_in, feat, og, masters, stats, states):
+    w_qkv, w_proj, w_up, w_down, w_norm, w_heads, w_hidden, w_table = masters
+    windows = br.shape[0]
+    images = windows // 2
+    shard, width = w_qkv.shape[1], w_qkv.shape[2]
+    hidden = w_up.shape[1]
+    stats = [
+        u if u.ndim == 2 else (u.reshape(-1, 128) if u.shape[0] % 512 == 0 or u.shape[0] == hidden
+                               else u[None])
+        for u in stats
+    ]
+    like = lambda u: (u.shape, F32)
+    mats = (w_qkv, w_proj, w_up, w_down)
+    smalls = (w_norm, w_heads, w_hidden, w_table)
+    vm, dma = pltpu.VMEM, pltpu.SemaphoreType.DMA
+    outs = [
+        (feat.shape, BF), like(w_qkv), like(w_proj), *map(like, smalls), *map(like, mats),
+        *map(like, stats), ((8, 128), F32),
+    ]
+    halves = (windows, 2, TOK, HALF)
+    scratch = [
+        *ShardSum.scratch((3, shard, width)), *ShardSum.scratch((width, shard)),
+        *LineSum.scratch(windows),
+        vm(halves, BF), vm((3, 24, D), F32), vm((3, 24, D), F32), vm((4, 8, shard), F32),
+        vm((4, 8, hidden), F32), vm((16, 8, 128), F32), vm((16, 8, 128), F32),
+        vm((windows, TOK, D), F32), vm((24, D), F32), vm((images, SHIFT, 24, D), BF),
+        dma((3,)), dma((3,)), *[dma((4,))] * 4, *[dma((16,))] * 4, *[dma((images,))] * 2,
+    ]
+    got = vmem_call(optimizer_body, outs, scratch, "optimizer", 4)(
+        gq, gp, g_up, g_down, small, rows, br, mix, *masters, *stats, *states
+    )
+    home_out, g_qkv, g_proj, gn, gh, gx, gt, uq, up, uu, ud, *new_stats, size = got
+    outs = [
+        like(og), like(og), *map(like, mats), *map(like, smalls), *map(like, masters),
+        *[(u.shape, BF) for u in mats], *map(like, stats), *map(like, smalls), ((1, 1), F32),
+    ]
+    return vmem_call(finish_body, outs, [], "finish", None)(
+        home_out, feat, home_in, og, g_qkv, g_proj, g_up, g_down, gn, gh, gx, gt, uq, up, uu, ud,
+        *masters, *states, *new_stats, size,
+    )
+
+
+def per_device_plain(
     features,
     out_grad,
     regions,
@@ -537,9 +1730,57 @@
     )
 
 
+def per_device(
+    features,
+    out_grad,
+    regions,
+    rel_index,
+    w_qkv,
+    w_proj,
+    w_up,
+    w_down,
+    norm_vecs,
+    head_bias,
+    hidden_bias,
+    rel_table,
+    row_qkv,
+    col_qkv,
+    row_proj,
+    col_proj,
+    row_up,
+    col_up,
+    row_down,
+    col_down,
+    state_norm,
+    state_heads,
+    state_hidden,
+    state_table,
+):
+    home_in, gq, gp, small, g_up, g_down, rows, br, mix = forward_backward(
+        features, out_grad, regions, rel_index, w_qkv, w_proj, w_up, w_down.T,
+        norm_vecs, head_bias, hidden_bias, rel_table)
+    flip = lambda u: u.transpose(1, 0, 2)
+    (block_out, grad_input, g_qkv, g_proj, g_up, g_down, g_norm, g_heads, g_hidden, g_table,
+     new_qkv, new_proj, new_up, new_down, new_norm, new_heads, new_hidden, new_table,
+     copy_qkv, copy_proj, copy_up, copy_down, *rest) = optimizer(
+        gq, gp, g_up, g_down, small, rows, br, mix, home_in, features, out_grad,
+        (w_qkv, w_proj, w_up, w_down.T, norm_vecs, flip(head_bias), hidden_bias.T, rel_table.T),
+        (row_qkv, col_qkv, row_proj, col_proj, row_up, col_up, row_down, col_down),
+        (state_norm, flip(state_heads), state_hidden.T, state_table.T))
+    factors, states, clip_rms = rest[:8], rest[8:12], rest[12]
+    factors = list(factors[:2]) + [u.reshape(-1) for u in factors[2:]]
+    return (
+        block_out, grad_input, g_qkv, g_proj, g_up, g_down.T, g_norm, flip(g_heads), g_hidden.T,
+        g_table.T, new_qkv, new_proj, new_up, new_down.T, new_norm, flip(new_heads), new_hidden.T,
+        new_table.T, copy_qkv, copy_proj, copy_up, copy_down.T, *factors,
+        states[0], flip(states[1]), states[2].T, states[3].T, clip_rms[0, 0],
+    )
+
+
 def solution(mesh):
+    line_of_four = mesh.shape["fsdp"] == 4 and mesh.shape["tp"] == 4 and mesh.shape["ctx"] == 2
     return jax.shard_map(
-        per_device,
+        per_device if line_of_four else per_device_plain,
         mesh=mesh,
         in_specs=(
             P("fsdp", "ctx", None, None),

time: 784 us -> 209 us (0.27)
  waiting for transfers between devices: 272 us -> 0 us
  Pallas kernels: 0 us -> 199 us
  local copies, waits for them, and re-layouts: 162 us -> 6.97 us
  matrix products: 116 us -> 0 us
  blocking collectives: 112 us -> 0 us
  other arithmetic: 74.7 us -> 1.38 us
  between operations: 31.7 us -> 0.88 us
    psum x5 -> x0, waiting for transfers between devices: 264 us -> none  [the longest x1 125 us: per_device(): lax.psum((stat_rq, stat_cq, stat_rp, stat_cp, stat_ru, stat_cu, stat_rd,...]
    pallas_call x0 -> x3, Pallas kernels: none -> 199 us  [call(): pl.pallas_call(body, out_shape=[jax.ShapeDtypeStruct(s, t) for s, t in ou...]
    dot_general x42 -> x0, matrix products: 108 us -> none  [the longest x12 33.8 us: accumulate(): lax.dot_general(one_hot, grad_block, (((0,), (0,)), ((), ())), precision=...]
    psum x2 -> x0, blocking collectives: 67.3 us -> none  [the longest x1 35.6 us: band_sum(): lax.psum((grad_list[0], grad_list[1], grad_list[2], grad_list[3], grad_li...]
    unnamed x230 -> x2, local copies, waits for them, and re-layouts: 49 us -> 1.45 us
    reduce_sum x34 -> x0, other arithmetic: 37.9 us -> none  [the longest x3 9 us: layer_norm(): return centred * lax.rsqrt(var_val + NORM_EPS) * gain_row + offset]
    all_gather x5 -> x0, blocking collectives: 34.2 us -> none  [the longest x1 11.4 us: per_device(): lax.all_gather(w_qkv.astype(jnp.bfloat16), 'fsdp', axis=1, tiled=True)]
    dynamic_slice x44 -> x0, local copies, waits for them, and re-layouts: 28.9 us -> none  [the longest x12 12.2 us: table_grad(): lax.scan(accumulate, jnp.zeros((table_rows, heads_here), jnp.float32), (i...]
  transfers between devices with their start and end apart: 16 -> 0, of which waited for: 6 -> 0; matrix products, arithmetic and copies ran while one was open for 30% -> 0% of each run, Pallas kernels for 0% -> 0%
where the time goes in v4:
time: 209 us
  Pallas kernels  199 us (95%)
  local copies, waits for them, and re-layouts  6.97 us (3%)
    pallas_call x3, Pallas kernels, call(): pl.pallas_call(body, out_shape=[jax.ShapeDtypeStruct(s, t) for s, t in ou...  199 us

profile of v4, /device:TPU:0, one launch (start us, length us, event | category | flops | bytes accessed | tf_op | source)
XLA Modules:
  0.0 208.6 jit_solution(15314003051452944641)
XLA Ops:
  0.7 0.1 pad.16.clone
  0.8 0.7 copy.63
  1.5 0.1 reshape.101
  1.5 0.8 copy.62
  2.3 0.1 reshape.100
  2.4 1.4 select_maximum_fusion.refs_6_
  3.8 1.3 pad.13.refs_7_
  5.1 0.8 reshape_broadcast_in_dim.3
  5.9 0.7 broadcast_in_dim_squeeze_reshape.8.refs_9_
  6.6 1.6 pad.14.refs_8_
  8.2 0.8 broadcast_in_dim_squeeze_reshape.9.refs_10_
  9.1 136.8 %forward_backward.1 = (bf16[2,12,24,768]{3,2,1,0:T(8,128)(2,1)}, f32[3,768,192]{2,1,0:T(8,128)}, f32[4,192,192]{2,1,0:T(8,128)}, f32[24,768]{1,0:T(8,128)}, f32[...) custom-call(bf16[2,12,24,768]{3,2,1,0:T(8,128)(2,1)} %refs_1_.3, ...), custom_call_target="tpu_custom_call" | custom-call | tf_op jit(solution)/shard_map/forward_backward/pallas_call | solution.py:394
  145.9 54.8 %optimizer.1 = (bf16[2,12,24,768]{3,2,1,0:T(8,128)(2,1)}, f32[3,192,192]{2,1,0:T(8,128)}, f32[192,192]{1,0:T(8,128)}, f32[6,192]{1,0:T(8,128)}, f32[6,2,8]{2,1,0...) custom-call(f32[3,768,192]{2,1,0:T(8,128)} %get-tuple-element.99.ref, ...), custom_call_target="tpu_custom_call" | custom-call | tf_op jit(solution)/shard_map/optimizer/pallas_call | solution.py:394
  200.7 7.7 %finish.1 = (f32[2,12,24,768]{3,2,1,0:T(8,128)}, f32[2,12,24,768]{3,2,1,0:T(8,128)}, f32[3,192,192]{2,1,0:T(8,128)}, f32[192,192]{1,0:T(8,128)}, f32[192,768]{1,...) custom-call(bf16[2,12,24,768]{3,2,1,0:T(8,128)(2,1)} %get-tuple-elem, ...), custom_call_target="tpu_custom_call" | custom-call | tf_op jit(solution)/shard_map/finish/pallas_call | solution.py:394
  (2 shorter events, 0.0 us)

commit v5 on v4

--- a/solution.py
+++ b/solution.py
@@ -167,7 +167,8 @@
 MESH = pl.DeviceIdType.MESH
 TOK = WIN * WIN
 HALF = D // 2
-VMEM_LIMIT = 66_000_000
+ROWS = TOK // 2
+VMEM_LIMIT = 67_043_328
 
 
 def dot(a, b):
@@ -215,9 +216,9 @@
     @staticmethod
     def scratch(count):
         return [
-            pltpu.VMEM((count, 2, TOK, HALF), BF),
-            pltpu.VMEM((count, 2, TOK, HALF), BF),
-            pltpu.VMEM((count, TOK, HALF), BF),
+            pltpu.VMEM((count, 2, ROWS, HALF), BF),
+            pltpu.VMEM((count, 2, ROWS, HALF), BF),
+            pltpu.VMEM((count, ROWS, HALF), BF),
             pltpu.SemaphoreType.DMA((count, 2)),
             pltpu.SemaphoreType.DMA((count, 2)),
             pltpu.SemaphoreType.DMA((count,)),
@@ -267,63 +268,79 @@
                       self.r_tot.at[w, h], {"tp": self.outer})
 
     def put(self, w, value):
-        self.part[w, 0] = value[:, :HALF]
-        self.part[w, 1] = value[:, HALF:]
+        for s in range(2):
+            for h in range(2):
+                self.part[2 * w + s, h] = value[s * ROWS : (s + 1) * ROWS, h * HALF : (h + 1) * HALF]
+
+    def get(self, w):
+        return jnp.concatenate(
+            [
+                jnp.concatenate([self.total[2 * w + s, h].astype(F32) for h in range(2)], axis=1)
+                for s in range(2)
+            ],
+            axis=0,
+        )
 
     def start(self, w):
         @pl.when(self.is_outer)
         def _():
-            self.send[w, self.other] = self.part[w, self.other].astype(BF)
-            self._to_mid(w, self.other).start()
-            self.send[w, self.own] = self.part[w, self.own].astype(BF)
-            self._to_mid(w, self.own).start()
+            for j in (2 * w, 2 * w + 1):
+                for h in (self.other, self.own):
+                    self.send[j, h] = self.part[j, h].astype(BF)
+                    self._to_mid(j, h).start()
 
     def cross(self, w):
         @pl.when(self.is_mid)
         def _():
-            self._to_mid(w, self.other).wait_recv()
-            self.send[w, self.other] = (
-                self.part[w, self.other] + self.from_outer[w, self.other].astype(F32)
-            ).astype(BF)
-            self._across(w).start()
+            for j in (2 * w, 2 * w + 1):
+                self._to_mid(j, self.other).wait_recv()
+                self.send[j, self.other] = (
+                    self.part[j, self.other] + self.from_outer[j, self.other].astype(F32)
+                ).astype(BF)
+                self._across(j).start()
 
     def settle(self, w):
         @pl.when(self.is_mid)
         def _():
-            self._to_mid(w, self.own).wait_recv()
-            self._across(w).wait_recv()
-            self.total[w, self.own] = (
-                self.part[w, self.own]
-                + self.from_outer[w, self.own].astype(F32)
-                + self.from_mid[w].astype(F32)
-            ).astype(BF)
-            self._total_across(w, self.own).start()
-            self._total_out(w, self.own).start()
+            for j in (2 * w, 2 * w + 1):
+                self._to_mid(j, self.own).wait_recv()
+                self._across(j).wait_recv()
+                self.total[j, self.own] = (
+                    self.part[j, self.own]
+                    + self.from_outer[j, self.own].astype(F32)
+                    + self.from_mid[j].astype(F32)
+                ).astype(BF)
+                self._total_across(j, self.own).start()
+                self._total_out(j, self.own).start()
 
     def hand(self, w):
         @pl.when(self.is_mid)
         def _():
-            self._total_across(w, self.other).wait_recv()
-            self._total_out(w, self.other).start()
+            for j in (2 * w, 2 * w + 1):
+                self._total_across(j, self.other).wait_recv()
+                self._total_out(j, self.other).start()
 
     def arrive(self, w):
         @pl.when(self.is_outer)
         def _():
-            self._total_out(w, 0).wait_recv()
-            self._total_out(w, 1).wait_recv()
+            for j in (2 * w, 2 * w + 1):
+                self._total_out(j, 0).wait_recv()
+                self._total_out(j, 1).wait_recv()
 
     def drain(self, w):
         @pl.when(self.is_outer)
         def _():
-            self._to_mid(w, 0).wait_send()
-            self._to_mid(w, 1).wait_send()
+            for j in (2 * w, 2 * w + 1):
+                self._to_mid(j, 0).wait_send()
+                self._to_mid(j, 1).wait_send()
 
         @pl.when(self.is_mid)
         def _():
-            self._across(w).wait_send()
-            self._total_across(w, self.own).wait_send()
-            self._total_out(w, 0).wait_send()
-            self._total_out(w, 1).wait_send()
+            for j in (2 * w, 2 * w + 1):
+                self._across(j).wait_send()
+                self._total_across(j, self.own).wait_send()
+                self._total_out(j, 0).wait_send()
+                self._total_out(j, 1).wait_send()
 
 
 class ShardSum:
@@ -511,46 +528,159 @@
             self._copy(n).wait_send()
 
 
-def main_body(*refs):
+def total_of(x):
+    return jnp.sum(jnp.sum(x, axis=1, keepdims=True), axis=0, keepdims=True)
+
+
+def exact(a, b, dims):
+    return lax.dot_general(
+        a, b, (dims, ((), ())), precision=lax.Precision.HIGHEST, preferred_element_type=F32
+    )
+
+
+def lane_sums(squares):
+    return exact(jnp.ones((8, squares.shape[1]), F32), squares, ((1,), (1,)))[0:1]
+
+
+def as_column(row):
+    n = row.shape[1]
+    step = 64
+    eye = lax.broadcasted_iota(jnp.int32, (step, step), 0) == lax.broadcasted_iota(
+        jnp.int32, (step, step), 1
+    )
+    return jnp.concatenate(
+        [
+            jnp.sum(
+                jnp.where(eye, jnp.broadcast_to(row[:, at : at + step], (step, step)), 0.0),
+                axis=1, keepdims=True,
+            )
+            for at in range(0, n, step)
+        ],
+        axis=0,
+    )
+
+
+def lane_pack(values):
+    lane = lax.broadcasted_iota(jnp.int32, (8, 128), 1)
+    packed = jnp.zeros((8, 128), F32)
+    for n, value in enumerate(values):
+        packed = packed + jnp.where(lane == n, jnp.broadcast_to(value, (8, 128)), 0.0)
+    return packed
+
+
+def wide(ref):
+    if ref.shape[1] != 128:
+        return ref[...]
+    return jnp.concatenate([ref[n : n + 1, :] for n in range(ref.shape[0])], axis=1)
+
+
+def put_wide(ref, row):
+    if ref.shape[1] != 128:
+        ref[...] = row
+    else:
+        for n in range(ref.shape[0]):
+            ref[n : n + 1, :] = row[:, n * 128 : (n + 1) * 128]
+
+
+def plain(grad, state):
+    new = DECAY_RATE * state + (1.0 - DECAY_RATE) * (grad * grad + STAT_EPS)
+    return new, grad * lax.rsqrt(new)
+
+
+def step_body(*refs):
     (
-        (feat, og, wq_m, wp_m, wu_m, wd_m, small_m, table_t, ridx, regr, regc),
-        (gin_o, gq_o, gp_o, small_o, gu_o, gd_o, rows, br, mix_o),
-        (sm_g, wq, wp_g, wp, wu, wd, fh, gh, bias_s, row_tmp, xw, ogw, n1, q, k, v, probs, ctx, part),
-        (n2_s, hid_s, dpl_s, ol_s, xhat_s, rstd_s, tot_two, gu, gd, dft, dbr),
-        (dh_s, dpos_s, chunk_s, halo_s, tot_one),
-        ls_one, ls_two, ls_four, up_refs, down_refs, table_refs,
-        (w_send, w_recv, h_send, h_recv, o_send, o_recv),
-    ) = take(refs, (11, 9, 19, 11, 5, 10, 10, 10, 8, 8, 8, 6))
+        (feat, og, regions, ridx_m, w_qkv, w_proj, w_up, w_down, w_norm, w_heads, w_hidden, w_table),
+        (row_qkv, col_qkv, row_proj, col_proj, row_up, col_up, row_down, col_down),
+        (s_norm, s_heads, s_hidden, s_table),
+        (home_o, gin_o, gq_o, gp_o, gu_o, gd_o, gn_o, gh_o, gx_o, gt_o, uq_o, up_o, uu_o, ud_o),
+        (rq_o, kq_o, rp_o, kp_o, ru_o, ku_o, rd_o, kd_o, size_o),
+        (sm_g, wq, wp_g, wp, wu, wd, fh, gh, og_low, bias_s, row_tmp, rows, ridx, table_t, small),
+        (xw, ogw, n1, q, k, v, probs, ctx, part),
+        (n2_s, hid_s, dpl_s, xhat_s, rstd_s, tot_two, gu, gd, dft, dbr, mix),
+        (dh_s, dpos_s, chunk_s, tot_four),
+        ls_two, ls_four, up_refs, down_refs, qkv_refs, proj_refs, table_refs,
+        (sm_s, sm_r, t_s, f_s, z_s, c_s),
+        (w_send, w_recv, p_send, p_recv, v_send, v_recv, h_send, h_recv, a_send, a_recv,
+         b_send, b_recv, x_send, x_recv),
+        (sm_send, sm_recv, t_send, t_recv, f_send, f_recv, z_send, z_recv, c_send, c_recv),
+    ) = take(refs, (12, 8, 4, 14, 9, 15, 9, 11, 4, 10, 10, 8, 8, 8, 8, 8, 6, 14, 10))
     windows, heads = probs.shape[0], probs.shape[1]
     images = windows // 2
     width = q.shape[2]
-    shard = wq_m.shape[1]
-    f, c = lax.axis_index("fsdp"), lax.axis_index("ctx")
+    shard = w_qkv.shape[1]
+    hidden = w_up.shape[1]
+    ff = 4 * hidden
+    f, c, t = lax.axis_index("fsdp"), lax.axis_index("ctx"), lax.axis_index("tp")
     near, far = f + 1 - 2 * lax.rem(f, 2), lax.rem(f + 2, 4)
-    one = LineSum.build(part, ls_one, br)
+    me = f * 4 + t
     two = LineSum.build(part, ls_two, tot_two)
-    four = LineSum.build(part, ls_four, tot_one)
+    four = LineSum.build(part, ls_four, tot_four)
+    mixl = LineSum.build(mix, ls_two, tot_two)
 
     def block(at):
         return pl.ds(pl.multiple_of(at * shard, shard), shard)
 
+    def band(at):
+        return pl.ds(pl.multiple_of(at * width, width), width)
+
+    def other(n):
+        at = lax.rem(me + n, 16)
+        return {"fsdp": lax.div(at, 4), "tp": lax.rem(at, 4)}
+
     up = ShardSum(lambda at: gu[block(at), :], gu_o, up_refs)
     down = ShardSum(lambda at: gd[block(at), :], gd_o, down_refs)
+    qkv = ShardSum(
+        lambda at: jnp.stack([gu[block(at), n * 256 : n * 256 + width] for n in range(3)]),
+        gq_o, qkv_refs,
+    )
+    proj = ShardSum(lambda at: gd[block(at), :shard], gp_o, proj_refs)
     table = TableSum(dpos_s, table_refs)
     barrier = pltpu.get_barrier_semaphore()
-    greet(barrier, [{"fsdp": near}, {"fsdp": far}, {"ctx": 1 - c}])
-    one.greet(barrier)
-    wq[:, block(f), :] = wq_m[...].astype(BF)
-    sm_g[f] = small_m[...].astype(BF)
-    wp_g[f] = wp_m[...].astype(BF)
-    wu[block(f), :] = wu_m[...].astype(BF)
-    wd[block(f), :] = wd_m[...].astype(BF)
-    pl.semaphore_wait(barrier, 3 + one.greet_count())
+    greet(barrier, [{"ctx": 1 - c}] + [other(n) for n in range(1, 16)])
+
+    part_of = HD // 4
+
+    def ints(shape, axis):
+        return lax.broadcasted_iota(jnp.int32, shape, axis)
+
+    def ones_where(cond):
+        return jnp.where(cond, 1.0, 0.0).astype(BF)
+
+    def flat_units(values, count):
+        lanes = count * part_of
+        spread = dot(values, ones_where(jnp.bitwise_and(ints((part_of, lanes), 1), 7) == ints((part_of, lanes), 0)))
+        return jnp.sum(
+            jnp.where(jnp.right_shift(ints((count, lanes), 1), 3) == ints((count, lanes), 0), spread, 0.0),
+            axis=0, keepdims=True,
+        )
+
+    wq[:, block(f), :] = w_qkv[...].astype(BF)
+    wp_g[f, band(t), :] = w_proj[...].astype(BF)
+    units = hidden // HD
+    lanes = units * part_of
+    spread = dot(
+        w_hidden[...].astype(BF),
+        ones_where(jnp.right_shift(ints((units, lanes), 1), 3) == ints((units, lanes), 0)),
+    )
+    hidden_row = jnp.sum(
+        jnp.where(jnp.bitwise_and(ints((8, lanes), 1), 7) == ints((8, lanes), 0), spread, 0.0),
+        axis=0, keepdims=True,
+    )
+    own = jnp.concatenate([w_norm[...], jnp.zeros((2, shard), F32), hidden_row, jnp.zeros((7, shard), F32)], axis=0)
+    small[0:16, :shard] = own
+    small[0:16, shard:] = jnp.zeros((16, D - shard), F32)
+    for n in range(2):
+        small[9 + n : 10 + n, : heads * part_of] = flat_units(w_heads[:, n, :].astype(BF), heads)
+    sm_g[f] = small[0:16, :shard].astype(BF)
+    wu[block(f), :] = w_up[...].astype(BF)
+    wd[block(f), :] = w_down[...].astype(BF)
+    for i in range(images):
+        og_low[i] = og[i, 0:SHIFT].astype(BF)
+    pl.semaphore_wait(barrier, 16)
 
     items = [
         lambda at: sm_g.at[at],
         lambda at: wq.at[:, block(at), :],
-        lambda at: wp_g.at[at],
         lambda at: wu.at[block(at), :],
         lambda at: wd.at[block(at), :],
     ]
@@ -558,22 +688,39 @@
     def copy_of(n, kind, at, where):
         ref = items[n](at)
         return remote(ref, ref, w_send.at[n, kind], w_recv.at[n, kind], {"fsdp": where})
+
+    def proj_copy(n, kind, at, where):
+        ref = wp_g.at[at, band(lax.rem(t - n + 4, 4))]
+        return remote(ref, ref, p_send.at[n, kind], p_recv.at[n, kind], {"fsdp": where})
+
+    def proj_line(n):
+        ref = wp_g.at[f, band(t)]
+        return remote(ref, ref, v_send.at[n], v_recv.at[n], {"tp": lax.rem(t + n, 4)})
 
     halo_f = [
         remote(feat.at[i, 0:SHIFT], fh.at[i], h_send.at[i], h_recv.at[i], {"ctx": 1 - c})
         for i in range(images)
     ]
     halo_g = [
-        remote(og.at[i, 0:SHIFT], gh.at[i], h_send.at[images + i], h_recv.at[images + i], {"ctx": 1 - c})
+        remote(og_low.at[i], gh.at[i], h_send.at[images + i], h_recv.at[images + i], {"ctx": 1 - c})
         for i in range(images)
     ]
+
+    def send_both(n):
+        copy_of(n, 0, f, far).start()
+        copy_of(n, 1, f, near).start()
+
+    def proj_both(n):
+        proj_copy(n, 0, f, far).start()
+        proj_copy(n, 1, f, near).start()
+
+    send_both(0)
     for copy in halo_f:
         copy.start()
-    for n in range(len(items)):
-        copy_of(n, 0, f, far).start()
-        copy_of(n, 1, f, near).start()
-    for copy in halo_g:
-        copy.start()
+    for n in range(1, 4):
+        proj_line(n).start()
+    send_both(1)
+    proj_both(0)
 
     def relay(n):
         copy_of(n, 0, f, far).wait_recv()
@@ -583,9 +730,10 @@
         copy_of(n, 1, f, near).wait_recv()
         copy_of(n, 2, far, near).wait_recv()
 
-    relay(0)
-
-    table_low = table_t[...].astype(BF).astype(F32)
+    ridx[...] = jnp.zeros_like(ridx)
+    ridx[:TOK, :TOK] = ridx_m[...]
+    table_t[...] = jnp.zeros_like(table_t)
+    table_t[:heads, : w_table.shape[1]] = w_table[...].astype(BF).astype(F32)
 
     def bias_rows(step, carry):
         rows_at = pl.ds(pl.multiple_of(step * 8, 8), 8)
@@ -598,78 +746,87 @@
             for h in range(heads):
                 found = jnp.zeros((8, 128), F32)
                 for n in range(5):
-                    tab = jnp.broadcast_to(
-                        table_low[h : h + 1, n * 128 : (n + 1) * 128], (8, 128)
-                    )
+                    tab = jnp.broadcast_to(table_t[h : h + 1, n * 128 : (n + 1) * 128], (8, 128))
                     got = jnp.take_along_axis(tab, low, axis=1, mode="promise_in_bounds")
                     found = jnp.where(picks[n], got, found)
                 bias_s[h, rows_at, lanes_at] = found
         return carry
 
     lax.fori_loop(0, TOK // 8, bias_rows, 0)
+    relay(0)
+    dpos_s[...] = jnp.zeros_like(dpos_s)
+    for n in range(1, 4):
+        proj_line(n).wait_recv()
+        proj_both(n)
+    send_both(2)
+    send_both(3)
+    for copy in halo_g:
+        copy.start()
     gathered(0)
-    lanes = rows.shape[1]
     rows[...] = jnp.concatenate([sm_g[n].astype(F32) for n in range(4)], axis=1)
-    unit = lax.broadcasted_iota(jnp.int32, (shard, lanes), 0)
-    lane = lax.broadcasted_iota(jnp.int32, (shard, lanes), 1)
-    biases = jnp.zeros((16, lanes), F32)
+    unit = ints((shard, D), 0)
+    lane = ints((shard, D), 1)
+    biases = jnp.zeros((16, D), F32)
     for n in range(4):
         same = jnp.logical_and(
             jnp.right_shift(lane, 5) == jnp.right_shift(unit, 3),
             jnp.bitwise_and(lane, 31) == jnp.bitwise_and(unit, 7) + n * 8,
         )
-        biases = biases + dot(sm_g[n], jnp.where(same, 1.0, 0.0).astype(BF))
+        biases = biases + dot(sm_g[n], ones_where(same))
     rows[8:16, :] = biases[8:16, :]
-    dpos_s[...] = jnp.zeros_like(dpos_s)
-    small_o[...] = jnp.zeros_like(small_o)
-    for i in range(images):
+    small[...] = jnp.zeros_like(small)
+    relay(1)
+
+    def enter(i):
         halo_f[i].wait_recv()
         window_rows(
             lambda im, r: feat[im, SHIFT + r] if r < SHIFT else fh[im, r - SHIFT], row_tmp, i, xw
         )
-    relay(1)
+
+    enter(0)
     gain_one, offset_one = rows[0:1, :], rows[1:2, :]
     bias_proj, gain_two, offset_two = rows[2:3, :], rows[3:4, :], rows[4:5, :]
     bias_hidden = rows[8:9, :]
     bias_q, bias_v = rows[9:10, :width], rows[10:11, :width]
-    head_of = jnp.right_shift(lax.broadcasted_iota(jnp.int32, (1, width), 1), 5)
-    picks_of = [jnp.where(head_of == h, 1.0, 0.0).astype(BF) for h in range(heads)]
-    gathered(1)
-    relay(2)
-    gathered(2)
-    wp[...] = jnp.concatenate([wp_g[n] for n in range(4)], axis=1)
+    head_of = jnp.right_shift(ints((1, width), 1), 5)
+    picks_of = [ones_where(head_of == h) for h in range(heads)]
+
+    def over(p):
+        return jnp.right_shift(p * 171, 11)
+
+    def region_forms(w):
+        i, j = lax.div(w, 2), lax.rem(w, 2)
+        both = regions[i].astype(F32)
+        square = jnp.where(j == 0, both[:, :WIN], both[:, WIN:]).astype(BF)
+        p_row, r_row = ints((WIN, TOK), 1), ints((WIN, TOK), 0)
+        spread_row = dot(square, ones_where(p_row - WIN * over(p_row) == r_row))
+        row = jnp.sum(jnp.where(over(p_row) == r_row, spread_row, 0.0), axis=0, keepdims=True)
+        p_col, r_col = ints((TOK, WIN), 0), ints((TOK, WIN), 1)
+        spread_col = dot(ones_where(over(p_col) == r_col), square)
+        col = jnp.sum(
+            jnp.where(p_col - WIN * over(p_col) == r_col, spread_col, 0.0), axis=1, keepdims=True
+        )
+        return row, col
 
     def spot(w):
         return pl.ds(pl.multiple_of(w * TOK, TOK), TOK)
 
     def add_rows(n, term):
-        small_o[n : n + 1, : term.shape[1]] = small_o[n : n + 1, : term.shape[1]] + jnp.sum(
+        small[n : n + 1, : term.shape[1]] = small[n : n + 1, : term.shape[1]] + jnp.sum(
             term, axis=0, keepdims=True
         )
 
-    def serve(w, line, before):
-        @pl.when(w == 0)
+    def ctx_copy(w, n):
+        ref = ctx.at[w, t]
+        return remote(ref, ref, x_send.at[w, n], x_recv.at[w, n], {"tp": lax.rem(t + n, 4)})
+
+    gathered(1)
+
+    def forward(w, carry):
+        @pl.when(w == 2)
         def _():
-            if before is not None:
-                before.cross(windows - 1)
-                before.settle(windows - 1)
-                before.hand(windows - 2)
-
-        @pl.when(w == 1)
-        def _():
-            if before is not None:
-                before.hand(windows - 1)
-
-        @pl.when(w >= 1)
-        def _():
-            line.cross(w - 1)
-            line.settle(w - 1)
-
-        @pl.when(w >= 2)
-        def _():
-            line.hand(w - 2)
-
-    def forward(w, carry):
+            enter(1)
+
         x = xw[w]
         centred = x - row_mean(x)
         xhat = centred * lax.rsqrt(row_mean(centred * centred) + NORM_EPS)
@@ -681,7 +838,8 @@
         q[w] = q_w
         k[w] = k_w
         v[w] = v_w
-        mask = jnp.where(regc[w] == regr[w], 0.0, MASK_FILL)
+        reg_row, reg_col = region_forms(w)
+        mask = jnp.where(reg_col == reg_row, 0.0, MASK_FILL)
         context = jnp.zeros((TOK, width), F32)
         for h in range(heads):
             scores = dot_t(q_w * picks_of[h], k_w) * HD ** (-0.5) + bias_s[h, :, :TOK] + mask
@@ -689,22 +847,31 @@
             p = lifted / jnp.sum(lifted, axis=-1, keepdims=True)
             probs[w, h] = p
             context = context + dot(p.astype(BF), v_w * picks_of[h])
-        low = context.astype(BF)
-        ctx[spot(w), :] = low
-        one.put(w, dot(low, wp[...]))
-        one.start(w)
-        serve(w, one, None)
+        ctx[w, t] = context.astype(BF)
+        for n in (2, 1, 3):
+            ctx_copy(w, n).start()
         return carry
 
     lax.fori_loop(0, windows, forward, 0)
+    for n in range(4):
+        proj_copy(n, 0, f, far).wait_recv()
+        proj_copy(n, 2, far, near).start()
+    relay(2)
     relay(3)
-    relay(4)
+    for n in range(4):
+        proj_copy(n, 1, f, near).wait_recv()
+        proj_copy(n, 2, far, near).wait_recv()
+    wp[...] = jnp.concatenate([wp_g[n] for n in range(4)], axis=1)
+    gathered(2)
     gathered(3)
-    gathered(4)
 
     def middle(w, carry):
-        one.arrive(w)
-        resid = xw[w] + (jnp.concatenate([br[w, 0], br[w, 1]], axis=1).astype(F32) + bias_proj)
+        for n in range(1, 4):
+            ctx_copy(w, n).wait_recv()
+        branch = jnp.zeros((TOK, D), F32) + bias_proj
+        for n in range(4):
+            branch = branch + dot(ctx[w, n], wp[n * width : (n + 1) * width, :])
+        resid = xw[w] + branch
         centred = resid - row_mean(resid)
         rstd = lax.rsqrt(row_mean(centred * centred) + NORM_EPS)
         xhat = centred * rstd
@@ -718,48 +885,73 @@
         hid = (pre * cdf).astype(BF)
         hid_s[spot(w), :] = hid
 
-        @pl.when(w % 2 == 0)
+        for n in range(images):
+
+            @pl.when(w == 2 * n)
+            def _():
+                halo_g[n].wait_recv()
+                window_rows(
+                    lambda im, r: og[im, SHIFT + r] if r < SHIFT else gh[im, r - SHIFT],
+                    row_tmp, n, ogw,
+                )
+
+        @pl.when(w >= 1)
         def _():
-            i = w // 2
-            for n in range(images):
-
-                @pl.when(i == n)
-                def _():
-                    halo_g[n].wait_recv()
-                    window_rows(
-                        lambda im, r: og[im, SHIFT + r] if r < SHIFT else gh[im, r - SHIFT],
-                        row_tmp, n, ogw,
-                    )
+            two.cross(w - 1)
 
         low = ogw[w].astype(BF)
-        ol_s[spot(w), :] = low
         d_pre = dot(low, wd[...]) * slope
         add_rows(6, d_pre)
         dpl = d_pre.astype(BF)
         dpl_s[spot(w), :] = dpl
         two.put(w, dot_t(dpl, wu[...]))
         two.start(w)
-        mixed = dot_t(hid, wd[...])
-        mix_o[w, 0] = mixed[:, :HALF]
-        mix_o[w, 1] = mixed[:, HALF:]
-        serve(w, two, one)
+        mixl.put(w, dot_t(hid, wd[...]))
+
+        @pl.when(two.is_mid)
+        def _():
+            whole = branch + rows[5:6, :]
+            for s in range(2):
+                for h in range(2):
+
+                    @pl.when(two.own == h)
+                    def _():
+                        mix[2 * w + s, h] = (
+                            mix[2 * w + s, h]
+                            + whole[s * ROWS : (s + 1) * ROWS, h * HALF : (h + 1) * HALF]
+                        )
+
+        @pl.when(w >= 1)
+        def _():
+            two.settle(w - 1)
+
+        @pl.when(w >= 2)
+        def _():
+            two.hand(w - 2)
+
         return carry
 
     lax.fori_loop(0, windows, middle, 0)
+    two.cross(windows - 1)
 
     def grad_chunk(m, carry):
         chunk = pl.ds(pl.multiple_of(m * 256, 256), 256)
-        gd[chunk, :] = t_dot(ol_s[:, chunk], hid_s[...])
+        low = jnp.concatenate([ogw[w, :, chunk] for w in range(windows)], axis=0).astype(BF)
+        gd[chunk, :] = t_dot(low, hid_s[...])
         gu[chunk, :] = t_dot(n2_s[:, chunk], dpl_s[...])
         return carry
 
-    lax.fori_loop(0, D // 256, grad_chunk, 0)
+    lax.fori_loop(0, 1, grad_chunk, 0)
+    two.hand(windows - 2)
+    lax.fori_loop(1, 2, grad_chunk, 0)
+    two.settle(windows - 1)
+    lax.fori_loop(2, D // 256, grad_chunk, 0)
     down.start()
     up.start()
 
     def backward(w, carry):
         two.arrive(w)
-        d_two = jnp.concatenate([tot_two[w, 0], tot_two[w, 1]], axis=1).astype(F32)
+        d_two = two.get(w)
         xhat = xhat_s[w]
         e = d_two * gain_two
         d_flat = (e - row_mean(e) - xhat * row_mean(e * xhat)) * rstd_s[w, :, 0:1]
@@ -770,12 +962,22 @@
         dbr[spot(w), :] = d_branch
         for n, term in ((2, d_resid), (3, d_two * xhat), (4, d_two), (5, og_w)):
             add_rows(n, term)
-        d_ctx = dot_t(d_branch, wp[...]).astype(BF)
+        d_ctx = dot_t(d_branch, wp[band(t), :]).astype(BF)
         q_w, k_w, v_w = q[w], k[w], v[w]
         d_q = jnp.zeros((TOK, width), F32)
         d_k = jnp.zeros((TOK, width), F32)
         d_v = jnp.zeros((TOK, width), F32)
         for h in range(heads):
+            if h == heads // 2:
+
+                @pl.when(w >= 1)
+                def _():
+                    four.cross(w - 1)
+
+                @pl.when(w == 0)
+                def _():
+                    two.hand(windows - 1)
+
             d_ctx_h = d_ctx * picks_of[h]
             p = probs[w, h]
             d_p = dot_t(d_ctx_h, v_w)
@@ -794,7 +996,14 @@
                 add_rows(8 + n // 2, low.astype(F32))
         four.put(w, partial)
         four.start(w)
-        serve(w, four, two)
+
+        @pl.when(w >= 1)
+        def _():
+            four.settle(w - 1)
+
+        @pl.when(w >= 2)
+        def _():
+            four.hand(w - 2)
 
         @pl.when(w == 1)
         def _():
@@ -809,251 +1018,25 @@
         return carry
 
     lax.fori_loop(0, windows, backward, 0)
+    for n in range(3):
+        gu[:, n * 256 : n * 256 + width] = t_dot(n1[...], dh_s[n])
+    qkv.start()
+    ctx_own = jnp.concatenate([ctx[w, t] for w in range(windows)], axis=0)
+    gp = t_dot(ctx_own, dbr[...])
+    for n in range(4):
+        gd[n * width : (n + 1) * width, :shard] = gp[:, n * shard : (n + 1) * shard]
+    proj.start()
+    four.cross(windows - 1)
     table.start()
-    for n in range(3):
-        gq_o[n] = t_dot(n1[...], dh_s[n])
-    four.cross(windows - 1)
-    table.pair()
-    gp = t_dot(ctx[...], dbr[...])
-    for n in range(4):
-        gp_o[n] = gp[:, n * shard : (n + 1) * shard]
+    for w in range(windows):
+        two.drain(w)
+        mixl.start(w)
     four.hand(windows - 2)
     four.settle(windows - 1)
-    table.cross()
-
-    home = HomeRows(xhat_s, row_tmp, gin_o, halo_s, o_send, o_recv)
-
-    def back(w):
-        four.arrive(w)
-        x = xw[w]
-        centred = x - row_mean(x)
-        rstd = lax.rsqrt(row_mean(centred * centred) + NORM_EPS)
-        xhat = centred * rstd
-        d_one = jnp.concatenate([tot_one[w, 0], tot_one[w, 1]], axis=1).astype(F32)
-        e = d_one * gain_one
-        xhat_s[w] = dft[w] + (e - row_mean(e) - xhat * row_mean(e * xhat)) * rstd
-        for n, term in ((0, d_one * xhat), (1, d_one)):
-            add_rows(n, term)
-
-    back(0)
-    back(1)
-    home.go(0)
-    table.finish(chunk_s)
-    first = table.first_row()
-    ident = lax.broadcasted_iota(jnp.int32, (640, TOK), 0)
-
-    def bin_row(i, acc):
-        hot = jnp.where(ident == ridx[pl.ds(first + i, 1), :TOK], 1.0, 0.0).astype(BF)
-        vals = jnp.concatenate(
-            [chunk_s[h, pl.ds(i, 1), :TOK] for h in range(heads)] + [jnp.zeros((8 - heads, TOK), F32)],
-            axis=0,
-        )
-        high = vals.astype(BF)
-        low = (vals - high.astype(F32)).astype(BF)
-        return acc + dot_t(jnp.concatenate([high, low], axis=0), hot)
-
-    hist = lax.fori_loop(0, 24, bin_row, jnp.zeros((16, 640), F32))
-    small_o[16:24, :640] = hist[0:8] + hist[8:16]
-    four.hand(windows - 1)
-    down.finish()
-    up.finish()
-    back(2)
-    back(3)
-    home.go(1)
-    for i in range(images):
-        home.wait(i)
-    for w in range(windows):
-        for line in (one, two, four):
-            line.drain(w)
-    for copy in halo_f + halo_g:
-        copy.wait_send()
-    for n in range(len(items)):
-        copy_of(n, 0, f, far).wait_send()
-        copy_of(n, 1, f, near).wait_send()
-        copy_of(n, 2, far, near).wait_send()
-    up.drain()
-    down.drain()
-    table.drain()
-
-
-def forward_backward(features, out_grad, regions, rel_index, w_qkv, w_proj, w_up, w_down_t,
-                     norm_vecs, head_bias, hidden_bias, rel_table):
-    images = features.shape[0]
-    windows = 2 * images
-    shard, width = w_qkv.shape[1], w_qkv.shape[2]
-    hidden = w_up.shape[1]
-    heads = width // HD
-    small = jnp.concatenate(
-        [
-            norm_vecs,
-            jnp.zeros((2, shard), F32),
-            hidden_bias.reshape(1, shard),
-            jnp.pad(head_bias.reshape(2, -1), ((0, 5), (0, shard - head_bias[0].size))),
-        ],
-        axis=0,
-    )
-    table_t = jnp.pad(
-        rel_table.T, ((0, 8 - heads), (0, 640 - rel_table.shape[0]))
-    )
-    ridx = jnp.pad(rel_index, ((0, 192 - TOK), (0, 256 - TOK)))
-    region_win = to_windows(regions[..., None])[..., 0]
-    halves = (windows, 2, TOK, HALF)
-    outs = [
-        (features.shape, BF), ((3, D, width), F32), ((4, width, shard), F32), ((24, D), F32),
-        ((shard, hidden), F32), ((shard, hidden), F32), ((16, D), F32), (halves, BF), (halves, F32),
-    ]
-    vm = pltpu.VMEM
-    flat = windows * TOK
-    scratch = [
-        vm((4, 16, shard), BF), vm((3, D, width), BF), vm((4, width, shard), BF), vm((width, D), BF),
-        vm((D, hidden), BF), vm((D, hidden), BF), vm((images, SHIFT, 24, D), BF),
-        vm((images, SHIFT, 24, D), F32), vm((heads, TOK, 256), F32), vm((24, D), F32),
-        vm((windows, TOK, D), F32), vm((windows, TOK, D), F32), vm((flat, D), BF),
-        vm((windows, TOK, width), BF), vm((windows, TOK, width), BF), vm((windows, TOK, width), BF),
-        vm((windows, heads, TOK, TOK), F32), vm((flat, width), BF), vm(halves, F32),
-        vm((flat, D), BF), vm((flat, hidden), BF), vm((flat, hidden), BF), vm((flat, D), BF),
-        vm((windows, TOK, D), F32), vm((windows, TOK, 128), F32), vm(halves, BF),
-        vm((D, hidden), F32), vm((D, hidden), F32), vm((windows, TOK, D), F32), vm((flat, D), BF),
-        vm((3, flat, width), BF), vm((heads, 192, 256), F32), vm((heads, 24, 256), F32),
-        vm((images, SHIFT, 24, D), BF), vm(halves, BF),
-        *LineSum.scratch(windows), *LineSum.scratch(windows), *LineSum.scratch(windows),
-        *ShardSum.scratch((shard, hidden)), *ShardSum.scratch((shard, hidden)),
-        *TableSum.scratch(heads),
-        *[pltpu.SemaphoreType.DMA((5, 3))] * 2,
-        *[pltpu.SemaphoreType.DMA((2 * images,))] * 2,
-        *[pltpu.SemaphoreType.DMA((images,))] * 2,
-    ]
-    return vmem_call(main_body, outs, scratch, "forward_backward", 1)(
-        features, out_grad, w_qkv, w_proj, w_up, w_down_t, small, table_t, ridx,
-        region_win[:, None, :], region_win[:, :, None],
-    )
-
-
-def total_of(x):
-    return jnp.sum(jnp.sum(x, axis=1, keepdims=True), axis=0, keepdims=True)
-
-
-def exact(a, b, dims):
-    return lax.dot_general(
-        a, b, (dims, ((), ())), precision=lax.Precision.HIGHEST, preferred_element_type=F32
-    )
-
-
-def lane_sums(squares):
-    return exact(jnp.ones((8, squares.shape[1]), F32), squares, ((1,), (1,)))[0:1]
-
-
-def as_column(row):
-    n = row.shape[1]
-    step = 64
-    eye = lax.broadcasted_iota(jnp.int32, (step, step), 0) == lax.broadcasted_iota(
-        jnp.int32, (step, step), 1
-    )
-    return jnp.concatenate(
-        [
-            jnp.sum(
-                jnp.where(eye, jnp.broadcast_to(row[:, at : at + step], (step, step)), 0.0),
-                axis=1, keepdims=True,
-            )
-            for at in range(0, n, step)
-        ],
-        axis=0,
-    )
-
-
-def lane_pack(values):
-    lane = lax.broadcasted_iota(jnp.int32, (8, 128), 1)
-    packed = jnp.zeros((8, 128), F32)
-    for n, value in enumerate(values):
-        packed = packed + jnp.where(lane == n, jnp.broadcast_to(value, (8, 128)), 0.0)
-    return packed
-
-
-def wide(ref):
-    if ref.shape[1] != 128:
-        return ref[...]
-    return jnp.concatenate([ref[n : n + 1, :] for n in range(ref.shape[0])], axis=1)
-
-
-def put_wide(ref, row):
-    if ref.shape[1] != 128:
-        ref[...] = row
-    else:
-        for n in range(ref.shape[0]):
-            ref[n : n + 1, :] = row[:, n * 128 : (n + 1) * 128]
-
-
-def plain(grad, state):
-    new = DECAY_RATE * state + (1.0 - DECAY_RATE) * (grad * grad + STAT_EPS)
-    return new, grad * lax.rsqrt(new)
-
-
-def optimizer_body(*refs):
-    (
-        (gq, gp, g_up, g_down, small, rows, br, mix),
-        (w_qkv, w_proj, w_up, w_down, w_norm, w_heads, w_hidden, w_table),
-        (row_qkv, col_qkv, row_proj, col_proj, row_up, col_up, row_down, col_down),
-        (s_norm, s_heads, s_hidden, s_table),
-        (home_o, gq_o, gp_o, gn_o, gh_o, gx_o, gt_o, uq_o, up_o, uu_o, ud_o),
-        (rq_o, kq_o, rp_o, kp_o, ru_o, ku_o, rd_o, kd_o, size_o),
-        qkv_refs, proj_refs, line_refs,
-        (mixed, sm_s, sm_r, t_s, f_s, z_s, c_s, delta, row_tmp, halo_s),
-        (sm_send, sm_recv, t_send, t_recv, f_send, f_recv, z_send, z_recv, c_send, c_recv,
-         o_send, o_recv),
-    ) = take(refs, (8, 8, 8, 4, 11, 9, 8, 8, 10, 10, 12))
-    f, c, t = lax.axis_index("fsdp"), lax.axis_index("ctx"), lax.axis_index("tp")
-    windows = br.shape[0]
-    images = windows // 2
-    shard, width = w_qkv.shape[1], w_qkv.shape[2]
-    hidden = f_s.shape[2]
-    ff = 4 * hidden
-    heads = width // HD
-    me = f * 4 + t
+
+    keep = 1.0 - DECAY_RATE
     first_f = jnp.where(f == 0, 1.0, 0.0)
     first_t = jnp.where(t == 0, 1.0, 0.0)
-
-    def other(n):
-        at = lax.rem(me + n, 16)
-        return {"fsdp": lax.div(at, 4), "tp": lax.rem(at, 4)}
-
-    barrier = pltpu.get_barrier_semaphore()
-    greet(barrier, [{"ctx": 1 - c}] + [other(n) for n in range(1, 16)])
-    qkv = ShardSum(
-        lambda at: gq[:, pl.ds(pl.multiple_of(at * shard, shard), shard), :], gq_o, qkv_refs
-    )
-    proj = ShardSum(lambda at: gp[at], gp_o, proj_refs)
-    line = LineSum.build(mix, line_refs, mixed)
-    sm_s[0] = small[...]
-
-    def swap(n):
-        where = ({"fsdp": qkv.near}, {"fsdp": qkv.far}, {"ctx": 1 - c})[n]
-        return remote(sm_s.at[n], sm_r.at[n], sm_send.at[n], sm_recv.at[n], where)
-
-    pl.semaphore_wait(barrier, 16)
-    swap(0).start()
-    qkv.start()
-    proj.start()
-    for w in range(windows):
-        line.start(w)
-
-    keep = 1.0 - DECAY_RATE
-    t_s[t] = jnp.zeros((8, shard), F32)
-    f_s[f] = jnp.zeros((8, hidden), F32)
-    sq_up = g_up[...] * g_up[...]
-    sq_down = g_down[...] * g_down[...]
-    t_s[t, 4:5, :] = lane_sums(sq_up)
-    t_s[t, 5:6, :] = lane_sums(sq_down)
-    f_s[f, 4:5, :] = jnp.sum(sq_up, axis=0, keepdims=True)
-    f_s[f, 5:6, :] = jnp.sum(sq_down, axis=0, keepdims=True)
-    tot_up, tot_down = total_of(sq_up), total_of(sq_down)
-
-    qkv.pair()
-    proj.pair()
-    swap(0).wait_recv()
-    sm_s[1] = sm_s[0] + sm_r[0]
-    swap(1).start()
-    line.cross(0)
-
     old_rows = [
         first_t * jnp.sum(row_qkv[0:1, :], axis=1, keepdims=True),
         first_t * jnp.sum(row_qkv[1:2, :], axis=1, keepdims=True),
@@ -1075,16 +1058,83 @@
         total_of(w_hidden[...] * w_hidden[...]),
         first_f * total_of(w_table[...] * w_table[...]),
     ]
-    line.settle(0)
-    line.cross(1)
+    qkv.pair()
+    proj.pair()
+    table.pair()
+    down.finish()
+    up.finish()
+    t_s[t] = jnp.zeros((8, shard), F32)
+    f_s[f] = jnp.zeros((8, hidden), F32)
+    sq_up = gu_o[...] * gu_o[...]
+    sq_down = gd_o[...] * gd_o[...]
+    t_s[t, 4:5, :] = lane_sums(sq_up)
+    t_s[t, 5:6, :] = lane_sums(sq_down)
+    f_s[f, 4:5, :] = jnp.sum(sq_up, axis=0, keepdims=True)
+    f_s[f, 5:6, :] = jnp.sum(sq_down, axis=0, keepdims=True)
+    tot_up, tot_down = total_of(sq_up), total_of(sq_down)
+
+    for copy in halo_g:
+        copy.wait_send()
+    home_in = HomeRows(xhat_s, row_tmp, gin_o, og_low, a_send, a_recv)
+
+    def back(w):
+        four.arrive(w)
+        x = xw[w]
+        centred = x - row_mean(x)
+        rstd = lax.rsqrt(row_mean(centred * centred) + NORM_EPS)
+        xhat = centred * rstd
+        d_one = four.get(w)
+        e = d_one * gain_one
+        xhat_s[w] = dft[w] + (e - row_mean(e) - xhat * row_mean(e * xhat)) * rstd
+        for n, term in ((0, d_one * xhat), (1, d_one)):
+            add_rows(n, term)
+
+    back(0)
+    back(1)
+    home_in.go(0)
+    four.hand(windows - 1)
+    table.cross()
+    mixl.cross(0)
     qkv.cross()
     proj.cross()
-    swap(1).wait_recv()
-    sm_s[2] = sm_s[1] + sm_r[1]
-    swap(2).start()
-    line.hand(0)
-    line.settle(1)
-    line.cross(2)
+    mixl.settle(0)
+    mixl.cross(1)
+    table.finish(chunk_s)
+    first = table.first_row()
+    ident = ints((640, TOK), 0)
+
+    def bin_row(step, acc):
+        for n in range(4):
+            i = step * 4 + n
+            hot = ones_where(ident == ridx[pl.ds(first + i, 1), :TOK])
+            vals = jnp.concatenate(
+                [chunk_s[h, pl.ds(i, 1), :TOK] for h in range(heads)]
+                + [jnp.zeros((8 - heads, TOK), F32)],
+                axis=0,
+            )
+            high = vals.astype(BF)
+            low = (vals - high.astype(F32)).astype(BF)
+            acc = acc + dot_t(jnp.concatenate([high, low], axis=0), hot)
+        return acc
+
+    hist = lax.fori_loop(0, 6, bin_row, jnp.zeros((16, 640), F32))
+    small[16:24, :640] = hist[0:8] + hist[8:16]
+    back(2)
+    back(3)
+    sm_s[0] = small[...]
+
+    def swap(n):
+        where = ({"fsdp": near}, {"fsdp": far}, {"ctx": 1 - c})[n]
+        return remote(sm_s.at[n], sm_r.at[n], sm_send.at[n], sm_recv.at[n], where)
+
+    swap(0).start()
+    home_in.go(1)
+    mixl.settle(1)
+    mixl.hand(0)
+    mixl.cross(2)
+    swap(0).wait_recv()
+    sm_s[1] = sm_s[0] + sm_r[0]
+    swap(1).start()
     qkv.finish()
     proj.finish()
 
@@ -1116,9 +1166,12 @@
         f_copy(n).start()
     for n in range(1, 16):
         z_copy(n).start()
-    line.hand(1)
-    line.settle(2)
-    line.cross(3)
+    swap(1).wait_recv()
+    sm_s[2] = sm_s[1] + sm_r[1]
+    swap(2).start()
+    mixl.settle(2)
+    mixl.hand(1)
+    mixl.cross(3)
 
     swap(2).wait_recv()
     sm = sm_s[2] + sm_r[2]
@@ -1129,22 +1182,22 @@
             out = jnp.where(f == n, x[:, n * size : (n + 1) * size], out)
         return out
 
-    part = HD // 4
-
     def own_units(row, count):
-        lanes = count * HD
-        lane = lax.broadcasted_iota(jnp.int32, (count, lanes), 1)
-        unit = lax.broadcasted_iota(jnp.int32, (count, lanes), 0)
+        all_lanes = count * HD
+        at_lane = ints((count, all_lanes), 1)
         only = jnp.where(
-            jnp.right_shift(lane, 5) == unit, jnp.broadcast_to(row, (count, lanes)), 0.0
+            jnp.right_shift(at_lane, 5) == ints((count, all_lanes), 0),
+            jnp.broadcast_to(row, (count, all_lanes)), 0.0,
         )
-        at = lax.broadcasted_iota(jnp.int32, (lanes, part), 0)
-        k = lax.broadcasted_iota(jnp.int32, (lanes, part), 1)
-        pick = jnp.where(jnp.bitwise_and(at, HD - 1) == f * part + k, 1.0, 0.0)
+        pick = jnp.where(
+            jnp.bitwise_and(ints((all_lanes, part_of), 0), HD - 1)
+            == f * part_of + ints((all_lanes, part_of), 1),
+            1.0, 0.0,
+        )
         return only, pick
 
     gn = own_lanes(sm[0:6, :], shard)
-    gh = [exact(*own_units(sm[8 + n : 9 + n, :width], heads), ((1,), (0,))) for n in range(2)]
+    gh_new = [exact(*own_units(sm[8 + n : 9 + n, :width], heads), ((1,), (0,))) for n in range(2)]
     only, pick = own_units(sm[6:7, :], hidden // HD)
     gx = exact(pick, only, ((0,), (1,)))
     gt = sm[16 : 16 + heads, : w_table.shape[1]]
@@ -1153,8 +1206,8 @@
     gt_o[...] = gt
     small_sq = first_t * total_of(plain(gn, s_norm[...])[1] ** 2)
     for n in range(2):
-        gh_o[:, n, :] = gh[n]
-        small_sq = small_sq + total_of(plain(gh[n], s_heads[:, n, :])[1] ** 2)
+        gh_o[:, n, :] = gh_new[n]
+        small_sq = small_sq + total_of(plain(gh_new[n], s_heads[:, n, :])[1] ** 2)
     small_sq = small_sq + total_of(plain(gx, s_hidden[...])[1] ** 2)
     small_sq = small_sq + first_f * total_of(plain(gt, s_table[...])[1] ** 2)
 
@@ -1168,7 +1221,7 @@
     z_sum = z_s[0]
     for n in range(1, 16):
         z_sum = z_sum + z_s[n]
-    lane8 = lax.broadcasted_iota(jnp.int32, (8, 128), 1)
+    lane8 = ints((8, 128), 1)
 
     def scalar(n):
         return jnp.sum(jnp.where(lane8 == n, z_sum, 0.0)[0:1], axis=1, keepdims=True)
@@ -1202,37 +1255,33 @@
         u = gq_o[n] * scale_q[n]
         uq_o[n] = u
         big_sq = big_sq + total_of(u * u)
-    for grad, scale, ref in ((gp_o, scale_p, up_o), (g_up, scale_u, uu_o), (g_down, scale_d, ud_o)):
+    for grad, scale, ref in ((gp_o, scale_p, up_o), (gu_o, scale_u, uu_o), (gd_o, scale_d, ud_o)):
         u = grad[...] * scale
         ref[...] = u
         big_sq = big_sq + total_of(u * u)
     c_s[me] = jnp.broadcast_to(big_sq, (8, 128))
     for n in range(1, 16):
         c_copy(n).start()
-    line.hand(2)
-    line.settle(3)
+    mixl.settle(3)
+    mixl.hand(2)
     rq_o[...] = rq
     kq_o[...] = kq
     for ref, row in ((rp_o, rp), (kp_o, kp), (ru_o, ru), (ku_o, ku), (rd_o, rd), (kd_o, kd)):
         put_wide(ref, row)
 
-    home = HomeRows(delta, row_tmp, home_o, halo_s, o_send, o_recv)
-    both_bias = rows[2:3, :] + rows[5:6, :]
+    home_out = HomeRows(dft, row_tmp, home_o, fh, b_send, b_recv)
 
     def lift(w):
-        line.arrive(w)
-        delta[w] = (
-            jnp.concatenate([br[w, 0], br[w, 1]], axis=1).astype(F32)
-            + jnp.concatenate([mixed[w, 0], mixed[w, 1]], axis=1).astype(F32) + both_bias
-        )
+        mixl.arrive(w)
+        dft[w] = mixl.get(w)
 
     lift(0)
     lift(1)
-    home.go(0)
-    line.hand(3)
+    home_out.go(0)
+    mixl.hand(3)
     lift(2)
     lift(3)
-    home.go(1)
+    home_out.go(1)
 
     counts = [3 * D * D, D * D, D * ff, ff * D] + [D] * 8 + [ff, RELP * HEADS]
     sizes = [jnp.sqrt(scalar(12 + n) / counts[n] + STAT_EPS) for n in range(14)]
@@ -1246,21 +1295,33 @@
     factor = STEP_RATE / jnp.maximum(1.0, clip / CLIP_LEVEL)
     size_o[...] = lane_pack([size * factor for size in sizes] + [clip])
     for i in range(images):
-        home.wait(i)
+        home_in.wait(i)
+        home_out.wait(i)
     for n in range(3):
         swap(n).wait_send()
     for n in range(1, 4):
         t_copy(n).wait_send()
         f_copy(n).wait_send()
+        proj_line(n).wait_send()
+        for w in range(windows):
+            ctx_copy(w, n).wait_send()
     for n in range(1, 16):
         z_copy(n).wait_send()
         c_copy(n).wait_send()
     for w in range(windows):
-        line.drain(w)
-    qkv.drain()
-    proj.drain()
-
-
+        mixl.drain(w)
+        four.drain(w)
+    for copy in halo_f:
+        copy.wait_send()
+    for n in range(4):
+        copy_of(n, 0, f, far).wait_send()
+        copy_of(n, 1, f, near).wait_send()
+        copy_of(n, 2, far, near).wait_send()
+        proj_copy(n, 0, f, far).wait_send()
+        proj_copy(n, 1, f, near).wait_send()
+        proj_copy(n, 2, far, near).wait_send()
+    for member in (up, down, qkv, proj, table):
+        member.drain()
 def finish_body(*refs):
     (
         (home_out, feat, home_in, og, gq, gp, g_up, g_down, gn, gh, gx, gt, uq, up, uu, ud),
@@ -1308,38 +1369,55 @@
     clip_o[...] = step(14)
 
 
-def optimizer(gq, gp, g_up, g_down, small, rows, br, mix, home_in, feat, og, masters, stats, states):
+def whole_step(feat, og, regions, rel_index, masters, stats, states):
     w_qkv, w_proj, w_up, w_down, w_norm, w_heads, w_hidden, w_table = masters
-    windows = br.shape[0]
-    images = windows // 2
+    images = feat.shape[0]
+    windows = 2 * images
     shard, width = w_qkv.shape[1], w_qkv.shape[2]
     hidden = w_up.shape[1]
-    stats = [
-        u if u.ndim == 2 else (u.reshape(-1, 128) if u.shape[0] % 512 == 0 or u.shape[0] == hidden
-                               else u[None])
-        for u in stats
-    ]
+    heads = width // HD
+    stats = [u if u.ndim == 2 else u.reshape(-1, 128) if u.shape[0] == D else u[None] for u in stats]
     like = lambda u: (u.shape, F32)
     mats = (w_qkv, w_proj, w_up, w_down)
     smalls = (w_norm, w_heads, w_hidden, w_table)
     vm, dma = pltpu.VMEM, pltpu.SemaphoreType.DMA
+    flat = windows * TOK
+    halves = (2 * windows, 2, ROWS, HALF)
+    tokens = (windows, TOK, D)
+    rows_of = (images, SHIFT, 24, D)
     outs = [
-        (feat.shape, BF), like(w_qkv), like(w_proj), *map(like, smalls), *map(like, mats),
+        (feat.shape, BF), (feat.shape, BF), *map(like, mats), *map(like, smalls), *map(like, mats),
         *map(like, stats), ((8, 128), F32),
     ]
-    halves = (windows, 2, TOK, HALF)
     scratch = [
+        vm((4, 16, shard), BF), vm((3, D, width), BF), vm((4, D, shard), BF), vm((D, D), BF),
+        vm((D, hidden), BF), vm((D, hidden), BF), vm(rows_of, BF), vm(rows_of, BF), vm(rows_of, BF),
+        vm((heads, TOK, 256), F32), vm((24, D), F32), vm((16, D), F32), vm((192, 256), jnp.int32),
+        vm((8, 640), F32), vm((24, D), F32),
+        vm(tokens, F32), vm(tokens, F32), vm((flat, D), BF), vm((windows, TOK, width), BF),
+        vm((windows, TOK, width), BF), vm((windows, TOK, width), BF),
+        vm((windows, heads, TOK, TOK), F32), vm((windows, 4, TOK, width), BF), vm(halves, F32),
+        vm((flat, D), BF), vm((flat, hidden), BF), vm((flat, hidden), BF),
+        vm(tokens, F32), vm((windows, TOK, 128), F32), vm(halves, BF), vm((D, hidden), F32),
+        vm((D, hidden), F32), vm(tokens, F32), vm((flat, D), BF), vm(halves, F32),
+        vm((3, flat, width), BF), vm((heads, 192, 256), F32), vm((heads, 24, 256), F32),
+        vm(halves, BF),
+        *LineSum.scratch(2 * windows), *LineSum.scratch(2 * windows),
+        *ShardSum.scratch((shard, hidden)), *ShardSum.scratch((shard, hidden)),
         *ShardSum.scratch((3, shard, width)), *ShardSum.scratch((width, shard)),
-        *LineSum.scratch(windows),
-        vm(halves, BF), vm((3, 24, D), F32), vm((3, 24, D), F32), vm((4, 8, shard), F32),
-        vm((4, 8, hidden), F32), vm((16, 8, 128), F32), vm((16, 8, 128), F32),
-        vm((windows, TOK, D), F32), vm((24, D), F32), vm((images, SHIFT, 24, D), BF),
-        dma((3,)), dma((3,)), *[dma((4,))] * 4, *[dma((16,))] * 4, *[dma((images,))] * 2,
+        *TableSum.scratch(heads),
+        vm((3, 24, D), F32), vm((3, 24, D), F32), vm((4, 8, shard), F32), vm((4, 8, hidden), F32),
+        vm((16, 8, 128), F32), vm((16, 8, 128), F32),
+        dma((4, 3)), dma((4, 3)), dma((4, 3)), dma((4, 3)), dma((4,)), dma((4,)),
+        dma((2 * images,)), dma((2 * images,)), *[dma((images,))] * 4,
+        dma((windows, 4)), dma((windows, 4)),
+        dma((3,)), dma((3,)), *[dma((4,))] * 4, *[dma((16,))] * 4,
     ]
-    got = vmem_call(optimizer_body, outs, scratch, "optimizer", 4)(
-        gq, gp, g_up, g_down, small, rows, br, mix, *masters, *stats, *states
-    )
-    home_out, g_qkv, g_proj, gn, gh, gx, gt, uq, up, uu, ud, *new_stats, size = got
+    got = vmem_call(step_body, outs, scratch, "whole_step", 1)(
+        feat, og, regions, rel_index, *masters, *stats, *states
+    )
+    home_out, home_in, g_qkv, g_proj, g_up, g_down, gn, gh, gx, gt, uq, up, uu, ud, *rest = got
+    new_stats, size = rest[:8], rest[8]
     outs = [
         like(og), like(og), *map(like, mats), *map(like, smalls), *map(like, masters),
         *[(u.shape, BF) for u in mats], *map(like, stats), *map(like, smalls), ((1, 1), F32),
@@ -1756,14 +1834,11 @@
     state_hidden,
     state_table,
 ):
-    home_in, gq, gp, small, g_up, g_down, rows, br, mix = forward_backward(
-        features, out_grad, regions, rel_index, w_qkv, w_proj, w_up, w_down.T,
-        norm_vecs, head_bias, hidden_bias, rel_table)
     flip = lambda u: u.transpose(1, 0, 2)
     (block_out, grad_input, g_qkv, g_proj, g_up, g_down, g_norm, g_heads, g_hidden, g_table,
      new_qkv, new_proj, new_up, new_down, new_norm, new_heads, new_hidden, new_table,
-     copy_qkv, copy_proj, copy_up, copy_down, *rest) = optimizer(
-        gq, gp, g_up, g_down, small, rows, br, mix, home_in, features, out_grad,
+     copy_qkv, copy_proj, copy_up, copy_down, *rest) = whole_step(
+        features, out_grad, regions, rel_index,
         (w_qkv, w_proj, w_up, w_down.T, norm_vecs, flip(head_bias), hidden_bias.T, rel_table.T),
         (row_qkv, col_qkv, row_proj, col_proj, row_up, col_up, row_down, col_down),
         (state_norm, flip(state_heads), state_hidden.T, state_table.T))

time: 209 us -> 161 us (0.77)
  Pallas kernels: 199 us -> 158 us
  local copies, waits for them, and re-layouts: 6.97 us -> 1.31 us
    pallas_call x3 -> x2, Pallas kernels: 199 us -> 158 us  [call(): pl.pallas_call(body, out_shape=[jax.ShapeDtypeStruct(s, t) for s, t in ou...]
    pad x2 -> x0, local copies, waits for them, and re-layouts: 2.94 us -> none  [the longest x1 1.6 us: forward_backward(): ridx = jnp.pad(rel_index, ((0, 192 - TOK), (0, 256 - TOK)))]
    another operation x4 -> x0, local copies, waits for them, and re-layouts: 2.34 us -> none  [the longest x1 0.85 us: forward_backward(): region_win[:, :, None]]
where the time goes in v5:
time: 161 us
  Pallas kernels  158 us (98%)
    pallas_call x2, Pallas kernels, call(): pl.pallas_call(body, out_shape=[jax.ShapeDtypeStruct(s, t) for s, t in ou...  158 us

profile of v5, /device:TPU:0, one launch (start us, length us, event | category | flops | bytes accessed | tf_op | source)
XLA Modules:
  0.0 160.6 jit_solution(3611277096481024911)
XLA Ops:
  0.7 1.3 copy.59.refs_2_
  2.0 150.7 %whole_step.1 = (bf16[2,12,24,768]{3,2,1,0:T(8,128)(2,1)}, bf16[2,12,24,768]{3,2,1,0:T(8,128)(2,1)}, f32[3,192,192]{2,1,0:T(8,128)}, f32[192,192]{1,0:T(8,128)},...) custom-call(bf16[2,12,24,768]{3,2,1,0:T(8,128)(2,1)} %refs_1_.3, ...), custom_call_target="tpu_custom_call" | custom-call | tf_op jit(solution)/shard_map/whole_step/pallas_call | solution.py:411
  152.7 7.7 %finish.1 = (f32[2,12,24,768]{3,2,1,0:T(8,128)}, f32[2,12,24,768]{3,2,1,0:T(8,128)}, f32[3,192,192]{2,1,0:T(8,128)}, f32[192,192]{1,0:T(8,128)}, f32[192,768]{1,...) custom-call(bf16[2,12,24,768]{3,2,1,0:T(8,128)(2,1)} %get-tuple-elem, ...), custom_call_target="tpu_custom_call" | custom-call | tf_op jit(solution)/shard_map/finish/pallas_call | solution.py:411

commit v6 on v5

--- a/solution.py
+++ b/solution.py
@@ -267,6 +267,9 @@
         return remote(self.total.at[w, h], self.total.at[w, h], self.s_tot.at[w, h],
                       self.r_tot.at[w, h], {"tp": self.outer})
 
+    def order(self, w):
+        return (2 * w, 2 * w + 1)
+
     def put(self, w, value):
         for s in range(2):
             for h in range(2):
@@ -284,15 +287,15 @@
     def start(self, w):
         @pl.when(self.is_outer)
         def _():
-            for j in (2 * w, 2 * w + 1):
-                for h in (self.other, self.own):
+            for h in (self.other, self.own):
+                for j in self.order(w):
                     self.send[j, h] = self.part[j, h].astype(BF)
                     self._to_mid(j, h).start()
 
     def cross(self, w):
         @pl.when(self.is_mid)
         def _():
-            for j in (2 * w, 2 * w + 1):
+            for j in self.order(w):
                 self._to_mid(j, self.other).wait_recv()
                 self.send[j, self.other] = (
                     self.part[j, self.other] + self.from_outer[j, self.other].astype(F32)
@@ -343,6 +346,54 @@
                 self._total_out(j, 1).wait_send()
 
 
+class TradeSum(LineSum):
+    def __init__(self, base, away, sems):
+        self.__dict__.update(base.__dict__)
+        self.away, (self.s_ctx, self.r_ctx) = away, sems
+        self.ctx = 1 - lax.axis_index("ctx")
+
+    def order(self, w):
+        return (2 * w + 1, 2 * w)
+
+    def _trade(self, w):
+        return remote(self.away.at[w], self.total.at[2 * w + 1, self.own], self.s_ctx.at[w],
+                      self.r_ctx.at[w], {"ctx": self.ctx})
+
+    def settle(self, w):
+        @pl.when(self.is_mid)
+        def _():
+            for s, j in ((1, 2 * w + 1), (0, 2 * w)):
+                self._to_mid(j, self.own).wait_recv()
+                self._across(j).wait_recv()
+                whole = (
+                    self.part[j, self.own]
+                    + self.from_outer[j, self.own].astype(F32)
+                    + self.from_mid[j].astype(F32)
+                ).astype(BF)
+                if s == 1:
+                    self.away[w] = whole
+                    self._trade(w).start()
+                else:
+                    self.total[j, self.own] = whole
+                    self._total_across(j, self.own).start()
+                    self._total_out(j, self.own).start()
+
+    def trade(self, w):
+        @pl.when(self.is_mid)
+        def _():
+            j = 2 * w + 1
+            self._trade(w).wait_recv()
+            self._total_across(j, self.own).start()
+            self._total_out(j, self.own).start()
+
+    def drain(self, w):
+        LineSum.drain(self, w)
+
+        @pl.when(self.is_mid)
+        def _():
+            self._trade(w).wait_send()
+
+
 class ShardSum:
     def __init__(self, block_of, out, refs):
         self.block_of, self.out = block_of, out
@@ -382,13 +433,12 @@
         other = lax.div(self.far, 2)
         self.snd2[...] = (self.block_of(self.far) + self.rcv1[other].astype(F32)).astype(BF)
         self._far().start()
+        mine = lax.div(self.f, 2)
+        self.out[...] = self.block_of(self.f) + self.rcv1[mine].astype(F32)
 
     def cross(self):
         self._far().wait_recv()
-        mine = lax.div(self.f, 2)
-        self.snd3[...] = (
-            self.block_of(self.f) + self.rcv1[mine].astype(F32) + self.rcv2[...].astype(F32)
-        ).astype(BF)
+        self.snd3[...] = (self.out[...] + self.rcv2[...].astype(F32)).astype(BF)
         self._ctx().start()
 
     def finish(self):
@@ -402,7 +452,77 @@
         self._ctx().wait_send()
 
 
-def vmem_call(body, outs, scratch, name, collective_id):
+class BandFirstSum:
+    def __init__(self, block_of, out, refs):
+        self.block_of, self.out = block_of, out
+        self.snd1, self.rcv1, self.sndy, self.rcvy, self.sndx, self.rcvx, self.sndf, self.rcvf = refs[:8]
+        self.s, self.r = refs[8:]
+        f = lax.axis_index("fsdp")
+        self.f, self.core, self.x = f, lax.rem(f, 2), lax.div(f, 2)
+        self.near, self.far = f + 1 - 2 * self.core, lax.rem(f + 2, 4)
+        self.c = lax.axis_index("ctx")
+        self.half = out.shape[0] // 2
+
+    @staticmethod
+    def scratch(shape):
+        two = (2, *shape)
+        half = (shape[0] // 2, shape[1])
+        shapes = [two, two, (2, *half), (2, *half), half, half, half, half]
+        return [*[pltpu.VMEM(u, BF) for u in shapes], pltpu.SemaphoreType.DMA((5,)),
+                pltpu.SemaphoreType.DMA((5,))]
+
+    def _near(self, x):
+        return remote(self.snd1.at[x], self.rcv1.at[x], self.s.at[x], self.r.at[x], {"fsdp": self.near})
+
+    def _copy(self, n):
+        src, dst = ((self.sndy, self.rcvy), (self.sndx, self.rcvx), (self.sndf, self.rcvf))[n]
+        where = {"fsdp": self.far} if n == 1 else {"ctx": 1 - self.c}
+        return remote(src, dst, self.s.at[2 + n], self.r.at[2 + n], where)
+
+    def _rows(self, c):
+        return pl.ds(pl.multiple_of(c * self.half, self.half), self.half)
+
+    def _sum(self, x, c):
+        return self.block_of(2 * x + self.core, c * self.half, self.half) + self.rcv1[
+            x, self._rows(c), :
+        ].astype(F32)
+
+    def start(self):
+        for x in range(2):
+            self.snd1[x] = self.block_of(2 * x + 1 - self.core, 0, 2 * self.half).astype(BF)
+            self._near(x).start()
+
+    def pair(self):
+        for x in range(2):
+            self._near(x).wait_recv()
+            self.sndy[x] = self._sum(x, 1 - self.c).astype(BF)
+        self._copy(0).start()
+
+    def cross(self):
+        self._copy(0).wait_recv()
+        other = 1 - self.x
+        self.sndx[...] = (self._sum(other, self.c) + self.rcvy[other].astype(F32)).astype(BF)
+        self._copy(1).start()
+        self.out[self._rows(self.c), :] = self._sum(self.x, self.c) + self.rcvy[self.x].astype(F32)
+
+    def share(self):
+        self._copy(1).wait_recv()
+        self.sndf[...] = (self.out[self._rows(self.c), :] + self.rcvx[...].astype(F32)).astype(BF)
+        self._copy(2).start()
+
+    def finish(self):
+        self._copy(2).wait_recv()
+        self.out[self._rows(self.c), :] = self.sndf[...].astype(F32)
+        self.out[self._rows(1 - self.c), :] = self.rcvf[...].astype(F32)
+
+    def drain(self):
+        for x in range(2):
+            self._near(x).wait_send()
+        for n in range(3):
+            self._copy(n).wait_send()
+
+
+def vmem_call(body, outs, scratch, name, collective_id, in_place=0, out_place=0):
     remote_kernel = {} if collective_id is None else dict(
         collective_id=collective_id, has_side_effects=True
     )
@@ -411,8 +531,14 @@
         return pl.pallas_call(
             body,
             out_shape=[jax.ShapeDtypeStruct(s, t) for s, t in outs],
-            in_specs=[pl.BlockSpec(memory_space=pltpu.VMEM)] * len(args),
-            out_specs=[pl.BlockSpec(memory_space=pltpu.VMEM)] * len(outs),
+            in_specs=[
+                pl.BlockSpec(memory_space=pl.ANY if n < in_place else pltpu.VMEM)
+                for n in range(len(args))
+            ],
+            out_specs=[
+                pl.BlockSpec(memory_space=pl.ANY if n < out_place else pltpu.VMEM)
+                for n in range(len(outs))
+            ],
             scratch_shapes=scratch,
             compiler_params=pltpu.CompilerParams(vmem_limit_bytes=VMEM_LIMIT, **remote_kernel),
             name=name,
@@ -587,12 +713,23 @@
     return new, grad * lax.rsqrt(new)
 
 
+def update_scales(rq, kq, rp, kp, ru, ku, rd, kd, means):
+    def outer(first, second):
+        return as_column(lax.rsqrt(first)) * lax.rsqrt(second)
+
+    return [
+        *[outer(rq[n : n + 1, :] / means[n], kq[n : n + 1, :]) for n in range(3)],
+        outer(rp / means[3], kp), outer(ru / means[4], ku), outer(kd, rd / means[5]),
+    ]
+
+
 def step_body(*refs):
     (
-        (feat, og, regions, ridx_m, w_qkv, w_proj, w_up, w_down, w_norm, w_heads, w_hidden, w_table),
+        big_inputs,
+        (regions, ridx_m, w_norm, w_heads, w_hidden, w_table),
         (row_qkv, col_qkv, row_proj, col_proj, row_up, col_up, row_down, col_down),
         (s_norm, s_heads, s_hidden, s_table),
-        (home_o, gin_o, gq_o, gp_o, gu_o, gd_o, gn_o, gh_o, gx_o, gt_o, uq_o, up_o, uu_o, ud_o),
+        (home_o, gin_o, gq_o, gp_o, gu_o, gd_o, gn_o, gh_o, gx_o, gt_o),
         (rq_o, kq_o, rp_o, kp_o, ru_o, ku_o, rd_o, kd_o, size_o),
         (sm_g, wq, wp_g, wp, wu, wd, fh, gh, og_low, bias_s, row_tmp, rows, ridx, table_t, small),
         (xw, ogw, n1, q, k, v, probs, ctx, part),
@@ -600,10 +737,11 @@
         (dh_s, dpos_s, chunk_s, tot_four),
         ls_two, ls_four, up_refs, down_refs, qkv_refs, proj_refs, table_refs,
         (sm_s, sm_r, t_s, f_s, z_s, c_s),
+        (feat, og, w_qkv, w_proj, w_up, w_down), (tot_mix, away, y_send, y_recv, i_sem, d_send, d_recv),
         (w_send, w_recv, p_send, p_recv, v_send, v_recv, h_send, h_recv, a_send, a_recv,
-         b_send, b_recv, x_send, x_recv),
+         x_send, x_recv),
         (sm_send, sm_recv, t_send, t_recv, f_send, f_recv, z_send, z_recv, c_send, c_recv),
-    ) = take(refs, (12, 8, 4, 14, 9, 15, 9, 11, 4, 10, 10, 8, 8, 8, 8, 8, 6, 14, 10))
+    ) = take(refs, (6, 6, 8, 4, 10, 9, 15, 9, 11, 4, 10, 10, 8, 10, 24, 8, 8, 6, 6, 7, 12, 10))
     windows, heads = probs.shape[0], probs.shape[1]
     images = windows // 2
     width = q.shape[2]
@@ -615,7 +753,7 @@
     me = f * 4 + t
     two = LineSum.build(part, ls_two, tot_two)
     four = LineSum.build(part, ls_four, tot_four)
-    mixl = LineSum.build(mix, ls_two, tot_two)
+    mixl = TradeSum(LineSum.build(mix, ls_two, tot_mix), away, (y_send, y_recv))
 
     def block(at):
         return pl.ds(pl.multiple_of(at * shard, shard), shard)
@@ -628,15 +766,25 @@
         return {"fsdp": lax.div(at, 4), "tp": lax.rem(at, 4)}
 
     up = ShardSum(lambda at: gu[block(at), :], gu_o, up_refs)
-    down = ShardSum(lambda at: gd[block(at), :], gd_o, down_refs)
-    qkv = ShardSum(
-        lambda at: jnp.stack([gu[block(at), n * 256 : n * 256 + width] for n in range(3)]),
-        gq_o, qkv_refs,
-    )
+    down = BandFirstSum(
+        lambda at, first, size: gd[pl.ds(pl.multiple_of(at * shard + first, 32), size), :], gd_o, down_refs
+    )
+    qkv = [
+        ShardSum(
+            lambda at, n=n: gu[block(at), n * 256 : n * 256 + width], gq_o.at[n], qkv_refs[8 * n : 8 * n + 8]
+        )
+        for n in range(3)
+    ]
     proj = ShardSum(lambda at: gd[block(at), :shard], gp_o, proj_refs)
     table = TableSum(dpos_s, table_refs)
     barrier = pltpu.get_barrier_semaphore()
     greet(barrier, [{"ctx": 1 - c}] + [other(n) for n in range(1, 16)])
+    fetch = [
+        pltpu.make_async_copy(src, dst, i_sem.at[n])
+        for n, (src, dst) in enumerate(zip(big_inputs, (feat, og, w_qkv, w_proj, w_up, w_down)))
+    ]
+    for n in (2, 3, 0, 4, 5, 1):
+        fetch[n].start()
 
     part_of = HD // 4
 
@@ -654,8 +802,6 @@
             axis=0, keepdims=True,
         )
 
-    wq[:, block(f), :] = w_qkv[...].astype(BF)
-    wp_g[f, band(t), :] = w_proj[...].astype(BF)
     units = hidden // HD
     lanes = units * part_of
     spread = dot(
@@ -672,8 +818,16 @@
     for n in range(2):
         small[9 + n : 10 + n, : heads * part_of] = flat_units(w_heads[:, n, :].astype(BF), heads)
     sm_g[f] = small[0:16, :shard].astype(BF)
+    fetch[2].wait()
+    wq[:, block(f), :] = w_qkv[...].astype(BF)
+    fetch[3].wait()
+    wp_g[f, band(t), :] = w_proj[...].astype(BF)
+    fetch[0].wait()
+    fetch[4].wait()
     wu[block(f), :] = w_up[...].astype(BF)
+    fetch[5].wait()
     wd[block(f), :] = w_down[...].astype(BF)
+    fetch[1].wait()
     for i in range(images):
         og_low[i] = og[i, 0:SHIFT].astype(BF)
     pl.semaphore_wait(barrier, 16)
@@ -682,8 +836,20 @@
         lambda at: sm_g.at[at],
         lambda at: wq.at[:, block(at), :],
         lambda at: wu.at[block(at), :],
-        lambda at: wd.at[block(at), :],
     ]
+    half = shard // 2
+
+    def down_copy(n, at, cc, where):
+        ref = wd.at[block(at), :] if cc is None else wd.at[
+            pl.ds(pl.multiple_of(at * shard + cc * half, half), half), :
+        ]
+        return remote(ref, ref, d_send.at[n], d_recv.at[n], where)
+
+    down_copies = (
+        down_copy(0, f, c, {"fsdp": far}), down_copy(1, f, None, {"fsdp": near}),
+        down_copy(2, far, c, {"ctx": 1 - c}), down_copy(3, far, c, {"fsdp": near}),
+        down_copy(4, far, 1 - c, {"fsdp": near}),
+    )
 
     def copy_of(n, kind, at, where):
         ref = items[n](at)
@@ -721,6 +887,8 @@
         proj_line(n).start()
     send_both(1)
     proj_both(0)
+    down_copies[0].start()
+    halo_g[0].start()
 
     def relay(n):
         copy_of(n, 0, f, far).wait_recv()
@@ -759,9 +927,7 @@
         proj_line(n).wait_recv()
         proj_both(n)
     send_both(2)
-    send_both(3)
-    for copy in halo_g:
-        copy.start()
+    down_copies[1].start()
     gathered(0)
     rows[...] = jnp.concatenate([sm_g[n].astype(F32) for n in range(4)], axis=1)
     unit = ints((shard, D), 0)
@@ -821,6 +987,11 @@
         return remote(ref, ref, x_send.at[w, n], x_recv.at[w, n], {"tp": lax.rem(t + n, 4)})
 
     gathered(1)
+    down_copies[0].wait_recv()
+    down_copies[2].start()
+    for copy in halo_g[1:]:
+        copy.start()
+    down_copies[3].start()
 
     def forward(w, carry):
         @pl.when(w == 2)
@@ -856,14 +1027,16 @@
     for n in range(4):
         proj_copy(n, 0, f, far).wait_recv()
         proj_copy(n, 2, far, near).start()
+    down_copies[2].wait_recv()
+    down_copies[4].start()
     relay(2)
-    relay(3)
     for n in range(4):
         proj_copy(n, 1, f, near).wait_recv()
         proj_copy(n, 2, far, near).wait_recv()
     wp[...] = jnp.concatenate([wp_g[n] for n in range(4)], axis=1)
     gathered(2)
-    gathered(3)
+    for n in (1, 3, 4):
+        down_copies[n].wait_recv()
 
     def middle(w, carry):
         for n in range(1, 4):
@@ -895,6 +1068,14 @@
                     row_tmp, n, ogw,
                 )
 
+        @pl.when(w >= 3)
+        def _():
+            two.hand(w - 3)
+
+        @pl.when(w >= 2)
+        def _():
+            two.settle(w - 2)
+
         @pl.when(w >= 1)
         def _():
             two.cross(w - 1)
@@ -921,14 +1102,6 @@
                             + whole[s * ROWS : (s + 1) * ROWS, h * HALF : (h + 1) * HALF]
                         )
 
-        @pl.when(w >= 1)
-        def _():
-            two.settle(w - 1)
-
-        @pl.when(w >= 2)
-        def _():
-            two.hand(w - 2)
-
         return carry
 
     lax.fori_loop(0, windows, middle, 0)
@@ -941,13 +1114,11 @@
         gu[chunk, :] = t_dot(n2_s[:, chunk], dpl_s[...])
         return carry
 
-    lax.fori_loop(0, 1, grad_chunk, 0)
-    two.hand(windows - 2)
-    lax.fori_loop(1, 2, grad_chunk, 0)
-    two.settle(windows - 1)
-    lax.fori_loop(2, D // 256, grad_chunk, 0)
+    lax.fori_loop(0, D // 256, grad_chunk, 0)
     down.start()
     up.start()
+    two.hand(windows - 3)
+    two.settle(windows - 2)
 
     def backward(w, carry):
         two.arrive(w)
@@ -968,16 +1139,6 @@
         d_k = jnp.zeros((TOK, width), F32)
         d_v = jnp.zeros((TOK, width), F32)
         for h in range(heads):
-            if h == heads // 2:
-
-                @pl.when(w >= 1)
-                def _():
-                    four.cross(w - 1)
-
-                @pl.when(w == 0)
-                def _():
-                    two.hand(windows - 1)
-
             d_ctx_h = d_ctx * picks_of[h]
             p = probs[w, h]
             d_p = dot_t(d_ctx_h, v_w)
@@ -997,42 +1158,57 @@
         four.put(w, partial)
         four.start(w)
 
-        @pl.when(w >= 1)
-        def _():
-            four.settle(w - 1)
-
-        @pl.when(w >= 2)
-        def _():
-            four.hand(w - 2)
-
-        @pl.when(w == 1)
+        @pl.when(w == 0)
         def _():
             down.pair()
             up.pair()
-
-        @pl.when(w == windows - 1)
+            two.settle(windows - 1)
+            two.hand(windows - 2)
+
+        @pl.when(w == 1)
+        def _():
+            two.hand(windows - 1)
+
+        @pl.when(w >= 2)
+        def _():
+            four.cross(w - 2)
+
+        @pl.when(w == 2)
         def _():
             down.cross()
+
+        @pl.when(w == 3)
+        def _():
             up.cross()
 
         return carry
 
     lax.fori_loop(0, windows, backward, 0)
+    table.start()
     for n in range(3):
         gu[:, n * 256 : n * 256 + width] = t_dot(n1[...], dh_s[n])
-    qkv.start()
+        qkv[n].start()
+    four.settle(0)
     ctx_own = jnp.concatenate([ctx[w, t] for w in range(windows)], axis=0)
     gp = t_dot(ctx_own, dbr[...])
     for n in range(4):
         gd[n * width : (n + 1) * width, :shard] = gp[:, n * shard : (n + 1) * shard]
     proj.start()
-    four.cross(windows - 1)
-    table.start()
     for w in range(windows):
         two.drain(w)
         mixl.start(w)
-    four.hand(windows - 2)
-    four.settle(windows - 1)
+    table.pair()
+    down.share()
+    four.cross(2)
+    four.settle(1)
+    for member in (*qkv, proj):
+        member.pair()
+    four.hand(0)
+    four.cross(3)
+    table.cross()
+    four.hand(1)
+    four.settle(2)
+    qkv[0].cross()
 
     keep = 1.0 - DECAY_RATE
     first_f = jnp.where(f == 0, 1.0, 0.0)
@@ -1058,9 +1234,34 @@
         total_of(w_hidden[...] * w_hidden[...]),
         first_f * total_of(w_table[...] * w_table[...]),
     ]
-    qkv.pair()
-    proj.pair()
-    table.pair()
+    four.settle(3)
+
+    for copy in halo_g:
+        copy.wait_send()
+    home_in = HomeRows(xhat_s, row_tmp, gin_o, og_low, a_send, a_recv)
+
+    def back(w):
+        four.arrive(w)
+        x = xw[w]
+        centred = x - row_mean(x)
+        rstd = lax.rsqrt(row_mean(centred * centred) + NORM_EPS)
+        xhat = centred * rstd
+        d_one = four.get(w)
+        e = d_one * gain_one
+        xhat_s[w] = dft[w] + (e - row_mean(e) - xhat * row_mean(e * xhat)) * rstd
+        for n, term in ((0, d_one * xhat), (1, d_one)):
+            add_rows(n, term)
+
+    back(0)
+    mixl.cross(0)
+    four.hand(2)
+    qkv[1].cross()
+    qkv[2].cross()
+    back(1)
+    four.hand(3)
+    proj.cross()
+    mixl.settle(0)
+    mixl.cross(1)
     down.finish()
     up.finish()
     t_s[t] = jnp.zeros((8, shard), F32)
@@ -1072,33 +1273,6 @@
     f_s[f, 4:5, :] = jnp.sum(sq_up, axis=0, keepdims=True)
     f_s[f, 5:6, :] = jnp.sum(sq_down, axis=0, keepdims=True)
     tot_up, tot_down = total_of(sq_up), total_of(sq_down)
-
-    for copy in halo_g:
-        copy.wait_send()
-    home_in = HomeRows(xhat_s, row_tmp, gin_o, og_low, a_send, a_recv)
-
-    def back(w):
-        four.arrive(w)
-        x = xw[w]
-        centred = x - row_mean(x)
-        rstd = lax.rsqrt(row_mean(centred * centred) + NORM_EPS)
-        xhat = centred * rstd
-        d_one = four.get(w)
-        e = d_one * gain_one
-        xhat_s[w] = dft[w] + (e - row_mean(e) - xhat * row_mean(e * xhat)) * rstd
-        for n, term in ((0, d_one * xhat), (1, d_one)):
-            add_rows(n, term)
-
-    back(0)
-    back(1)
-    home_in.go(0)
-    four.hand(windows - 1)
-    table.cross()
-    mixl.cross(0)
-    qkv.cross()
-    proj.cross()
-    mixl.settle(0)
-    mixl.cross(1)
     table.finish(chunk_s)
     first = table.first_row()
     ident = ints((640, TOK), 0)
@@ -1117,9 +1291,14 @@
             acc = acc + dot_t(jnp.concatenate([high, low], axis=0), hot)
         return acc
 
-    hist = lax.fori_loop(0, 6, bin_row, jnp.zeros((16, 640), F32))
+    hist = lax.fori_loop(0, 3, bin_row, jnp.zeros((16, 640), F32))
+    mixl.settle(1)
+    back(2)
+    mixl.trade(0)
+    hist = lax.fori_loop(3, 6, bin_row, hist)
     small[16:24, :640] = hist[0:8] + hist[8:16]
-    back(2)
+    mixl.cross(2)
+    home_in.go(0)
     back(3)
     sm_s[0] = small[...]
 
@@ -1128,15 +1307,9 @@
         return remote(sm_s.at[n], sm_r.at[n], sm_send.at[n], sm_recv.at[n], where)
 
     swap(0).start()
-    home_in.go(1)
-    mixl.settle(1)
     mixl.hand(0)
-    mixl.cross(2)
-    swap(0).wait_recv()
-    sm_s[1] = sm_s[0] + sm_r[0]
-    swap(1).start()
-    qkv.finish()
-    proj.finish()
+    for member in (*qkv, proj):
+        member.finish()
 
     tot_q = []
     for n in range(3):
@@ -1166,12 +1339,33 @@
         f_copy(n).start()
     for n in range(1, 16):
         z_copy(n).start()
+    mixl.settle(2)
+    mixl.trade(1)
+    mixl.cross(3)
+    swap(0).wait_recv()
+    sm_s[1] = sm_s[0] + sm_r[0]
+    swap(1).start()
+
+    def lift(w):
+        mixl.arrive(w)
+        dft[w] = mixl.get(w)
+
+    def leave(i):
+        for r in range(WIN):
+            home_o[i, (SHIFT + r) % WIN] = home_row(dft, row_tmp, i, r)
+
+    mixl.hand(1)
+    mixl.settle(3)
+    home_in.go(1)
+    mixl.trade(2)
+    lift(0)
     swap(1).wait_recv()
     sm_s[2] = sm_s[1] + sm_r[1]
     swap(2).start()
-    mixl.settle(2)
-    mixl.hand(1)
-    mixl.cross(3)
+    mixl.trade(3)
+    mixl.hand(2)
+    lift(1)
+    leave(0)
 
     swap(2).wait_recv()
     sm = sm_s[2] + sm_r[2]
@@ -1243,45 +1437,27 @@
             DECAY_RATE * scalar(6 + n) + keep * (scalar(n) / cols_all + rows_all * STAT_EPS)
         ) / rows_all
 
-    scale_q = [
-        as_column(lax.rsqrt(rq[n : n + 1, :] / mean_row(n, D, D))) * lax.rsqrt(kq[n : n + 1, :])
-        for n in range(3)
+    means = [
+        mean_row(0, D, D), mean_row(1, D, D), mean_row(2, D, D), mean_row(3, D, D),
+        mean_row(4, D, ff), mean_row(5, ff, D),
     ]
-    scale_p = as_column(lax.rsqrt(rp / mean_row(3, D, D))) * lax.rsqrt(kp)
-    scale_u = as_column(lax.rsqrt(ru / mean_row(4, D, ff))) * lax.rsqrt(ku)
-    scale_d = as_column(lax.rsqrt(kd)) * lax.rsqrt(rd / mean_row(5, ff, D))
+    scales = update_scales(rq, kq, rp, kp, ru, ku, rd, kd, means)
     big_sq = small_sq
-    for n in range(3):
-        u = gq_o[n] * scale_q[n]
-        uq_o[n] = u
-        big_sq = big_sq + total_of(u * u)
-    for grad, scale, ref in ((gp_o, scale_p, up_o), (gu_o, scale_u, uu_o), (gd_o, scale_d, ud_o)):
-        u = grad[...] * scale
-        ref[...] = u
+    grads = [gq_o[n] for n in range(3)] + [gp_o[...], gu_o[...], gd_o[...]]
+    for grad, scale in zip(grads, scales):
+        u = grad * scale
         big_sq = big_sq + total_of(u * u)
     c_s[me] = jnp.broadcast_to(big_sq, (8, 128))
     for n in range(1, 16):
         c_copy(n).start()
-    mixl.settle(3)
-    mixl.hand(2)
     rq_o[...] = rq
     kq_o[...] = kq
     for ref, row in ((rp_o, rp), (kp_o, kp), (ru_o, ru), (ku_o, ku), (rd_o, rd), (kd_o, kd)):
         put_wide(ref, row)
-
-    home_out = HomeRows(dft, row_tmp, home_o, fh, b_send, b_recv)
-
-    def lift(w):
-        mixl.arrive(w)
-        dft[w] = mixl.get(w)
-
-    lift(0)
-    lift(1)
-    home_out.go(0)
     mixl.hand(3)
     lift(2)
     lift(3)
-    home_out.go(1)
+    leave(1)
 
     counts = [3 * D * D, D * D, D * ff, ff * D] + [D] * 8 + [ff, RELP * HEADS]
     sizes = [jnp.sqrt(scalar(12 + n) / counts[n] + STAT_EPS) for n in range(14)]
@@ -1293,10 +1469,9 @@
     count_all = 4 * D * D + 2 * D * ff + 8 * D + ff + RELP * HEADS
     clip = jnp.sqrt(all_sq[0:1, 0:1] / count_all)
     factor = STEP_RATE / jnp.maximum(1.0, clip / CLIP_LEVEL)
-    size_o[...] = lane_pack([size * factor for size in sizes] + [clip])
+    size_o[...] = lane_pack([size * factor for size in sizes] + [clip] + means)
     for i in range(images):
         home_in.wait(i)
-        home_out.wait(i)
     for n in range(3):
         swap(n).wait_send()
     for n in range(1, 4):
@@ -1313,18 +1488,21 @@
         four.drain(w)
     for copy in halo_f:
         copy.wait_send()
-    for n in range(4):
+    for copy in down_copies:
+        copy.wait_send()
+    for n in range(3):
         copy_of(n, 0, f, far).wait_send()
         copy_of(n, 1, f, near).wait_send()
         copy_of(n, 2, far, near).wait_send()
+    for n in range(4):
         proj_copy(n, 0, f, far).wait_send()
         proj_copy(n, 1, f, near).wait_send()
         proj_copy(n, 2, far, near).wait_send()
-    for member in (up, down, qkv, proj, table):
+    for member in (up, down, *qkv, proj, table):
         member.drain()
 def finish_body(*refs):
     (
-        (home_out, feat, home_in, og, gq, gp, g_up, g_down, gn, gh, gx, gt, uq, up, uu, ud),
+        (home_out, feat, home_in, og, gq, gp, g_up, g_down, gn, gh, gx, gt),
         (w_qkv, w_proj, w_up, w_down, w_norm, w_heads, w_hidden, w_table),
         (s_norm, s_heads, s_hidden, s_table),
         stats, (size,),
@@ -1332,7 +1510,7 @@
         (nq_o, np_o, nu_o, nd_o, nn_o, nh_o, nx_o, nt_o),
         (cq_o, cp_o, cu_o, cd_o),
         stats_o, (sn_o, sh_o, sx_o, st_o), (clip_o,),
-    ) = take(refs, (16, 8, 4, 8, 1, 10, 8, 4, 8, 4, 1))
+    ) = take(refs, (12, 8, 4, 8, 1, 10, 8, 4, 8, 4, 1))
     lane8 = lax.broadcasted_iota(jnp.int32, (8, 128), 1)
     table = size[...]
 
@@ -1346,10 +1524,16 @@
         (gt, gt_o), *zip(stats, stats_o),
     ):
         dst[...] = src[...]
-    for n, (master, u, new_o, low_o) in enumerate(
-        ((w_qkv, uq, nq_o, cq_o), (w_proj, up, np_o, cp_o), (w_up, uu, nu_o, cu_o), (w_down, ud, nd_o, cd_o))
+    rq, kq, *vecs = stats
+    scales = update_scales(rq[...], kq[...], *map(wide, vecs), [step(15 + n) for n in range(6)])
+    for n in range(3):
+        new = w_qkv[n] - step(0) * (gq[n] * scales[n])
+        nq_o[n] = new
+        cq_o[n] = new.astype(BF)
+    for n, (master, grad, new_o, low_o) in enumerate(
+        ((w_proj, gp, np_o, cp_o), (w_up, g_up, nu_o, cu_o), (w_down, g_down, nd_o, cd_o))
     ):
-        new = master[...] - step(n) * u[...]
+        new = master[...] - step(1 + n) * (grad[...] * scales[3 + n])
         new_o[...] = new
         low_o[...] = new.astype(BF)
     sn, un = plain(gn[...], s_norm[...])
@@ -1386,7 +1570,7 @@
     tokens = (windows, TOK, D)
     rows_of = (images, SHIFT, 24, D)
     outs = [
-        (feat.shape, BF), (feat.shape, BF), *map(like, mats), *map(like, smalls), *map(like, mats),
+        (feat.shape, BF), (feat.shape, BF), *map(like, mats), *map(like, smalls),
         *map(like, stats), ((8, 128), F32),
     ]
     scratch = [
@@ -1403,27 +1587,30 @@
         vm((3, flat, width), BF), vm((heads, 192, 256), F32), vm((heads, 24, 256), F32),
         vm(halves, BF),
         *LineSum.scratch(2 * windows), *LineSum.scratch(2 * windows),
-        *ShardSum.scratch((shard, hidden)), *ShardSum.scratch((shard, hidden)),
-        *ShardSum.scratch((3, shard, width)), *ShardSum.scratch((width, shard)),
+        *ShardSum.scratch((shard, hidden)), *BandFirstSum.scratch((shard, hidden)),
+        *[s for _ in range(3) for s in ShardSum.scratch((shard, width))], *ShardSum.scratch((width, shard)),
         *TableSum.scratch(heads),
         vm((3, 24, D), F32), vm((3, 24, D), F32), vm((4, 8, shard), F32), vm((4, 8, hidden), F32),
         vm((16, 8, 128), F32), vm((16, 8, 128), F32),
+        vm(feat.shape, BF), vm(og.shape, F32), *[vm(u.shape, F32) for u in mats],
+        vm(halves, BF), vm((windows, ROWS, HALF), BF), dma((windows,)), dma((windows,)), dma((6,)),
+        dma((5,)), dma((5,)),
         dma((4, 3)), dma((4, 3)), dma((4, 3)), dma((4, 3)), dma((4,)), dma((4,)),
-        dma((2 * images,)), dma((2 * images,)), *[dma((images,))] * 4,
+        dma((2 * images,)), dma((2 * images,)), *[dma((images,))] * 2,
         dma((windows, 4)), dma((windows, 4)),
         dma((3,)), dma((3,)), *[dma((4,))] * 4, *[dma((16,))] * 4,
     ]
-    got = vmem_call(step_body, outs, scratch, "whole_step", 1)(
-        feat, og, regions, rel_index, *masters, *stats, *states
-    )
-    home_out, home_in, g_qkv, g_proj, g_up, g_down, gn, gh, gx, gt, uq, up, uu, ud, *rest = got
+    got = vmem_call(step_body, outs, scratch, "whole_step", 1, 6)(
+        feat, og, *mats, regions, rel_index, *smalls, *stats, *states
+    )
+    home_out, home_in, g_qkv, g_proj, g_up, g_down, gn, gh, gx, gt, *rest = got
     new_stats, size = rest[:8], rest[8]
     outs = [
         like(og), like(og), *map(like, mats), *map(like, smalls), *map(like, masters),
         *[(u.shape, BF) for u in mats], *map(like, stats), *map(like, smalls), ((1, 1), F32),
     ]
     return vmem_call(finish_body, outs, [], "finish", None)(
-        home_out, feat, home_in, og, g_qkv, g_proj, g_up, g_down, gn, gh, gx, gt, uq, up, uu, ud,
+        home_out, feat, home_in, og, g_qkv, g_proj, g_up, g_down, gn, gh, gx, gt,
         *masters, *states, *new_stats, size,
     )
 

time: 161 us -> 144 us (0.89)
  Pallas kernels: 158 us -> 141 us
    pallas_call x2, Pallas kernels: 158 us -> 141 us  [call(): pl.pallas_call(body, out_shape=[jax.ShapeDtypeStruct(s, t) for s, t in ou...]
where the time goes in v6:
time: 144 us
  Pallas kernels  141 us (98%)
    pallas_call x2, Pallas kernels, call(): pl.pallas_call(body, out_shape=[jax.ShapeDtypeStruct(s, t) for s, t in ou...  141 us

profile of v6, /device:TPU:0, one launch (start us, length us, event | category | flops | bytes accessed | tf_op | source)
XLA Modules:
  0.0 143.5 jit_solution(12398271989623451865)
XLA Ops:
  0.7 1.3 copy.59.refs_6_
  2.0 133.3 %whole_step.1 = (bf16[2,12,24,768]{3,2,1,0:T(8,128)(2,1)}, bf16[2,12,24,768]{3,2,1,0:T(8,128)(2,1)}, f32[3,192,192]{2,1,0:T(8,128)}, f32[192,192]{1,0:T(8,128)},...) custom-call(bf16[2,12,24,768]{3,2,1,0:T(8,128)(2,1)} %refs_1_.3, ...), custom_call_target="tpu_custom_call" | custom-call | tf_op jit(solution)/shard_map/whole_step/pallas_call | solution.py:531
  135.3 8.1 %finish.1 = (f32[2,12,24,768]{3,2,1,0:T(8,128)}, f32[2,12,24,768]{3,2,1,0:T(8,128)}, f32[3,192,192]{2,1,0:T(8,128)}, f32[192,192]{1,0:T(8,128)}, f32[192,768]{1,...) custom-call(bf16[2,12,24,768]{3,2,1,0:T(8,128)(2,1)} %get-tuple-elem, ...), custom_call_target="tpu_custom_call" | custom-call | tf_op jit(solution)/shard_map/finish/pallas_call | solution.py:531

commit v7 on v6

--- a/solution.py
+++ b/solution.py
@@ -522,24 +522,50 @@
             self._copy(n).wait_send()
 
 
-def vmem_call(body, outs, scratch, name, collective_id, in_place=0, out_place=0):
+def vmem_call(body, outs, scratch, name, collective_id, in_place, out_place):
     remote_kernel = {} if collective_id is None else dict(
         collective_id=collective_id, has_side_effects=True
     )
+    anywhere = pl.BlockSpec(memory_space=pl.ANY)
 
     def call(*args):
+        few_in = [pltpu.VMEM(u.shape, u.dtype) for u in args[in_place:]]
+        few_out = [pltpu.VMEM(s, t) for s, t in outs[out_place:]]
+
+        def whole(*refs):
+            ins, results, own, vm_in, vm_out, sems = take(
+                refs, (len(args), len(outs), len(scratch), len(few_in), len(few_out), 2)
+            )
+            fetch = [
+                pltpu.make_async_copy(src, dst, sems[0].at[n])
+                for n, (src, dst) in enumerate(zip(ins[in_place:], vm_in))
+            ]
+            for copy in fetch:
+                copy.start()
+
+            def ready():
+                for copy in fetch:
+                    copy.wait()
+
+            body(ready, *ins[:in_place], *vm_in, *results[:out_place], *vm_out, *own)
+            store = [
+                pltpu.make_async_copy(src, dst, sems[1].at[n])
+                for n, (src, dst) in enumerate(zip(vm_out, results[out_place:]))
+            ]
+            for copy in store:
+                copy.start()
+            for copy in store:
+                copy.wait()
+
         return pl.pallas_call(
-            body,
+            whole,
             out_shape=[jax.ShapeDtypeStruct(s, t) for s, t in outs],
-            in_specs=[
-                pl.BlockSpec(memory_space=pl.ANY if n < in_place else pltpu.VMEM)
-                for n in range(len(args))
+            in_specs=[anywhere] * len(args),
+            out_specs=[anywhere] * len(outs),
+            scratch_shapes=[
+                *scratch, *few_in, *few_out,
+                pltpu.SemaphoreType.DMA((len(few_in),)), pltpu.SemaphoreType.DMA((len(few_out),)),
             ],
-            out_specs=[
-                pl.BlockSpec(memory_space=pl.ANY if n < out_place else pltpu.VMEM)
-                for n in range(len(outs))
-            ],
-            scratch_shapes=scratch,
             compiler_params=pltpu.CompilerParams(vmem_limit_bytes=VMEM_LIMIT, **remote_kernel),
             name=name,
         )(*args)
@@ -723,13 +749,13 @@
     ]
 
 
-def step_body(*refs):
+def step_body(ready, *refs):
     (
         big_inputs,
         (regions, ridx_m, w_norm, w_heads, w_hidden, w_table),
         (row_qkv, col_qkv, row_proj, col_proj, row_up, col_up, row_down, col_down),
         (s_norm, s_heads, s_hidden, s_table),
-        (home_o, gin_o, gq_o, gp_o, gu_o, gd_o, gn_o, gh_o, gx_o, gt_o),
+        big_outputs, (gn_o, gh_o, gx_o, gt_o),
         (rq_o, kq_o, rp_o, kp_o, ru_o, ku_o, rd_o, kd_o, size_o),
         (sm_g, wq, wp_g, wp, wu, wd, fh, gh, og_low, bias_s, row_tmp, rows, ridx, table_t, small),
         (xw, ogw, n1, q, k, v, probs, ctx, part),
@@ -738,10 +764,11 @@
         ls_two, ls_four, up_refs, down_refs, qkv_refs, proj_refs, table_refs,
         (sm_s, sm_r, t_s, f_s, z_s, c_s),
         (feat, og, w_qkv, w_proj, w_up, w_down), (tot_mix, away, y_send, y_recv, i_sem, d_send, d_recv),
+        (home_o, gin_o, gq_o, gp_o, gu_o, gd_o, o_sem),
         (w_send, w_recv, p_send, p_recv, v_send, v_recv, h_send, h_recv, a_send, a_recv,
          x_send, x_recv),
         (sm_send, sm_recv, t_send, t_recv, f_send, f_recv, z_send, z_recv, c_send, c_recv),
-    ) = take(refs, (6, 6, 8, 4, 10, 9, 15, 9, 11, 4, 10, 10, 8, 10, 24, 8, 8, 6, 6, 7, 12, 10))
+    ) = take(refs, (6, 6, 8, 4, 6, 4, 9, 15, 9, 11, 4, 10, 10, 8, 10, 24, 8, 8, 6, 6, 7, 7, 12, 10))
     windows, heads = probs.shape[0], probs.shape[1]
     images = windows // 2
     width = q.shape[2]
@@ -785,6 +812,13 @@
     ]
     for n in (2, 3, 0, 4, 5, 1):
         fetch[n].start()
+
+    store = [
+        pltpu.make_async_copy(src, dst, o_sem.at[n])
+        for n, (src, dst) in enumerate(zip((home_o, gin_o, gq_o, gp_o, gu_o, gd_o), big_outputs))
+    ]
+
+    ready()
 
     part_of = HD // 4
 
@@ -835,21 +869,24 @@
     items = [
         lambda at: sm_g.at[at],
         lambda at: wq.at[:, block(at), :],
-        lambda at: wu.at[block(at), :],
     ]
     half = shard // 2
 
-    def down_copy(n, at, cc, where):
-        ref = wd.at[block(at), :] if cc is None else wd.at[
-            pl.ds(pl.multiple_of(at * shard + cc * half, half), half), :
-        ]
-        return remote(ref, ref, d_send.at[n], d_recv.at[n], where)
-
-    down_copies = (
-        down_copy(0, f, c, {"fsdp": far}), down_copy(1, f, None, {"fsdp": near}),
-        down_copy(2, far, c, {"ctx": 1 - c}), down_copy(3, far, c, {"fsdp": near}),
-        down_copy(4, far, 1 - c, {"fsdp": near}),
-    )
+    def split_copies(full, k):
+        def piece(n, at, cc, where):
+            ref = full.at[block(at), :] if cc is None else full.at[
+                pl.ds(pl.multiple_of(at * shard + cc * half, half), half), :
+            ]
+            return remote(ref, ref, d_send.at[k, n], d_recv.at[k, n], where)
+
+        return (
+            piece(0, f, c, {"fsdp": far}), piece(1, f, None, {"fsdp": near}),
+            piece(2, far, c, {"ctx": 1 - c}), piece(3, far, c, {"fsdp": near}),
+            piece(4, far, 1 - c, {"fsdp": near}),
+        )
+
+    down_copies = split_copies(wd, 0)
+    up_copies = split_copies(wu, 1)
 
     def copy_of(n, kind, at, where):
         ref = items[n](at)
@@ -888,7 +925,10 @@
     send_both(1)
     proj_both(0)
     down_copies[0].start()
+    up_copies[0].start()
     halo_g[0].start()
+    down_copies[1].start()
+    up_copies[1].start()
 
     def relay(n):
         copy_of(n, 0, f, far).wait_recv()
@@ -926,8 +966,6 @@
     for n in range(1, 4):
         proj_line(n).wait_recv()
         proj_both(n)
-    send_both(2)
-    down_copies[1].start()
     gathered(0)
     rows[...] = jnp.concatenate([sm_g[n].astype(F32) for n in range(4)], axis=1)
     unit = ints((shard, D), 0)
@@ -962,7 +1000,7 @@
 
     def region_forms(w):
         i, j = lax.div(w, 2), lax.rem(w, 2)
-        both = regions[i].astype(F32)
+        both = jnp.where(i == 0, regions[:, 0, :], regions[:, 1, :]).astype(F32)
         square = jnp.where(j == 0, both[:, :WIN], both[:, WIN:]).astype(BF)
         p_row, r_row = ints((WIN, TOK), 1), ints((WIN, TOK), 0)
         spread_row = dot(square, ones_where(p_row - WIN * over(p_row) == r_row))
@@ -982,16 +1020,26 @@
             term, axis=0, keepdims=True
         )
 
-    def ctx_copy(w, n):
-        ref = ctx.at[w, t]
-        return remote(ref, ref, x_send.at[w, n], x_recv.at[w, n], {"tp": lax.rem(t + n, 4)})
+    def ctx_copy(p, kind, at, where):
+        ref = ctx.at[p, at]
+        return remote(ref, ref, x_send.at[p, kind], x_recv.at[p, at], {"tp": where})
+
+    other_outer = 3 - two.outer
+
+    def ctx_wait(p, at):
+        ctx_copy(p, 0, at, two.mid).wait_recv()
+
+    def pass_in(p):
+        ctx_wait(p, two.outer)
+        ctx_copy(p, 2, two.outer, two.other_mid).start()
+        ctx_wait(p, two.other_mid)
+        ctx_copy(p, 3, two.other_mid, two.outer).start()
+
+    def pass_out(p):
+        ctx_wait(p, other_outer)
+        ctx_copy(p, 4, other_outer, two.outer).start()
 
     gathered(1)
-    down_copies[0].wait_recv()
-    down_copies[2].start()
-    for copy in halo_g[1:]:
-        copy.start()
-    down_copies[3].start()
 
     def forward(w, carry):
         @pl.when(w == 2)
@@ -1018,32 +1066,71 @@
             p = lifted / jnp.sum(lifted, axis=-1, keepdims=True)
             probs[w, h] = p
             context = context + dot(p.astype(BF), v_w * picks_of[h])
-        ctx[w, t] = context.astype(BF)
-        for n in (2, 1, 3):
-            ctx_copy(w, n).start()
+        low = context.astype(BF)
+        p_at = lax.div(w, 2)
+
+        @pl.when(lax.rem(w, 2) == 0)
+        def _():
+            ctx[p_at, t, :, :width] = low
+
+        @pl.when(lax.rem(w, 2) == 1)
+        def _():
+            ctx[p_at, t, :, width:] = low
+            ctx_copy(p_at, 0, t, jnp.where(two.is_mid, two.outer, two.mid)).start()
+
+            @pl.when(two.is_mid)
+            def _():
+                ctx_copy(p_at, 1, t, two.other_mid).start()
+
         return carry
 
     lax.fori_loop(0, windows, forward, 0)
+    for copies in (down_copies, up_copies):
+        copies[0].wait_recv()
+        copies[2].start()
+        copies[3].start()
+    for copy in halo_g[1:]:
+        copy.start()
+
+    @pl.when(two.is_mid)
+    def _():
+        pass_in(0)
+
     for n in range(4):
         proj_copy(n, 0, f, far).wait_recv()
         proj_copy(n, 2, far, near).start()
+
+    @pl.when(two.is_mid)
+    def _():
+        pass_out(0)
+        pass_in(1)
+
     down_copies[2].wait_recv()
     down_copies[4].start()
-    relay(2)
+
     for n in range(4):
         proj_copy(n, 1, f, near).wait_recv()
         proj_copy(n, 2, far, near).wait_recv()
     wp[...] = jnp.concatenate([wp_g[n] for n in range(4)], axis=1)
-    gathered(2)
+    up_copies[2].wait_recv()
+    up_copies[4].start()
     for n in (1, 3, 4):
         down_copies[n].wait_recv()
+        up_copies[n].wait_recv()
 
     def middle(w, carry):
-        for n in range(1, 4):
-            ctx_copy(w, n).wait_recv()
+        p_at, odd = lax.div(w, 2), lax.rem(w, 2) == 1
+
+        @pl.when(jnp.logical_and(two.is_outer, jnp.logical_not(odd)))
+        def _():
+            for at in (two.mid, two.other_mid, other_outer):
+                ctx_wait(p_at, at)
+
         branch = jnp.zeros((TOK, D), F32) + bias_proj
         for n in range(4):
-            branch = branch + dot(ctx[w, n], wp[n * width : (n + 1) * width, :])
+            both = ctx[p_at, n]
+            low = jnp.where(odd, both[:, width:], both[:, :width])
+            branch = branch + dot(low, wp[n * width : (n + 1) * width, :])
         resid = xw[w] + branch
         centred = resid - row_mean(resid)
         rstd = lax.rsqrt(row_mean(centred * centred) + NORM_EPS)
@@ -1068,6 +1155,10 @@
                     row_tmp, n, ogw,
                 )
 
+        @pl.when(jnp.logical_and(two.is_mid, w == 0))
+        def _():
+            pass_out(1)
+
         @pl.when(w >= 3)
         def _():
             two.hand(w - 3)
@@ -1114,11 +1205,11 @@
         gu[chunk, :] = t_dot(n2_s[:, chunk], dpl_s[...])
         return carry
 
+    two.hand(windows - 3)
+    two.settle(windows - 2)
     lax.fori_loop(0, D // 256, grad_chunk, 0)
     down.start()
     up.start()
-    two.hand(windows - 3)
-    two.settle(windows - 2)
 
     def backward(w, carry):
         two.arrive(w)
@@ -1189,7 +1280,9 @@
         gu[:, n * 256 : n * 256 + width] = t_dot(n1[...], dh_s[n])
         qkv[n].start()
     four.settle(0)
-    ctx_own = jnp.concatenate([ctx[w, t] for w in range(windows)], axis=0)
+    ctx_own = jnp.concatenate(
+        [ctx[w // 2, t, :, (w % 2) * width : (w % 2 + 1) * width] for w in range(windows)], axis=0
+    )
     gp = t_dot(ctx_own, dbr[...])
     for n in range(4):
         gd[n * width : (n + 1) * width, :shard] = gp[:, n * shard : (n + 1) * shard]
@@ -1264,6 +1357,8 @@
     mixl.cross(1)
     down.finish()
     up.finish()
+    store[4].start()
+    store[5].start()
     t_s[t] = jnp.zeros((8, shard), F32)
     f_s[f] = jnp.zeros((8, hidden), F32)
     sq_up = gu_o[...] * gu_o[...]
@@ -1310,6 +1405,8 @@
     mixl.hand(0)
     for member in (*qkv, proj):
         member.finish()
+    store[2].start()
+    store[3].start()
 
     tot_q = []
     for n in range(3):
@@ -1458,6 +1555,10 @@
     lift(2)
     lift(3)
     leave(1)
+    store[0].start()
+    for i in range(images):
+        home_in.wait(i)
+    store[1].start()
 
     counts = [3 * D * D, D * D, D * ff, ff * D] + [D] * 8 + [ff, RELP * HEADS]
     sizes = [jnp.sqrt(scalar(12 + n) / counts[n] + STAT_EPS) for n in range(14)]
@@ -1470,16 +1571,20 @@
     clip = jnp.sqrt(all_sq[0:1, 0:1] / count_all)
     factor = STEP_RATE / jnp.maximum(1.0, clip / CLIP_LEVEL)
     size_o[...] = lane_pack([size * factor for size in sizes] + [clip] + means)
-    for i in range(images):
-        home_in.wait(i)
     for n in range(3):
         swap(n).wait_send()
     for n in range(1, 4):
         t_copy(n).wait_send()
         f_copy(n).wait_send()
         proj_line(n).wait_send()
-        for w in range(windows):
-            ctx_copy(w, n).wait_send()
+    for p in range(windows // 2):
+        ctx_copy(p, 0, t, two.mid).wait_send()
+
+        @pl.when(two.is_mid)
+        def _():
+            for kind in range(1, 5):
+                ctx_copy(p, kind, t, two.mid).wait_send()
+
     for n in range(1, 16):
         z_copy(n).wait_send()
         c_copy(n).wait_send()
@@ -1488,9 +1593,9 @@
         four.drain(w)
     for copy in halo_f:
         copy.wait_send()
-    for copy in down_copies:
+    for copy in (*down_copies, *up_copies):
         copy.wait_send()
-    for n in range(3):
+    for n in range(2):
         copy_of(n, 0, f, far).wait_send()
         copy_of(n, 1, f, near).wait_send()
         copy_of(n, 2, far, near).wait_send()
@@ -1500,42 +1605,61 @@
         proj_copy(n, 2, far, near).wait_send()
     for member in (up, down, *qkv, proj, table):
         member.drain()
-def finish_body(*refs):
+    for copy in store:
+        copy.wait()
+def finish_body(ready, *refs):
     (
-        (home_out, feat, home_in, og, gq, gp, g_up, g_down, gn, gh, gx, gt),
-        (w_qkv, w_proj, w_up, w_down, w_norm, w_heads, w_hidden, w_table),
-        (s_norm, s_heads, s_hidden, s_table),
-        stats, (size,),
-        (out_o, gin_o, gq_o, gp_o, gu_o, gd_o, gn_o, gh_o, gx_o, gt_o),
-        (nq_o, np_o, nu_o, nd_o, nn_o, nh_o, nx_o, nt_o),
-        (cq_o, cp_o, cu_o, cd_o),
-        stats_o, (sn_o, sh_o, sx_o, st_o), (clip_o,),
-    ) = take(refs, (12, 8, 4, 8, 1, 10, 8, 4, 8, 4, 1))
+        big_in, (gn, gh, gx, gt), (w_norm, w_heads, w_hidden, w_table),
+        (s_norm, s_heads, s_hidden, s_table), stats, (size,),
+        big_out, (gn_o, gh_o, gx_o, gt_o), (nn_o, nh_o, nx_o, nt_o), stats_o,
+        (sn_o, sh_o, sx_o, st_o), (clip_o,), held, made, (i_sem, o_sem),
+    ) = take(refs, (12, 4, 4, 4, 8, 1, 14, 4, 4, 8, 4, 1, 12, 10, 2))
+    home_out, feat, home_in, og = held[:4]
+    grads, masters = held[4:8], held[8:12]
+    fetch = [
+        pltpu.make_async_copy(src, dst, i_sem.at[n]) for n, (src, dst) in enumerate(zip(big_in, held))
+    ]
+    for n in (4, 8, 5, 9, 6, 10, 7, 11, 0, 1, 2, 3):
+        fetch[n].start()
+    sources = [*made[:2], *grads, *made[2:]]
+    store = [
+        pltpu.make_async_copy(src, dst, o_sem.at[n]) for n, (src, dst) in enumerate(zip(sources, big_out))
+    ]
+    ready()
     lane8 = lax.broadcasted_iota(jnp.int32, (8, 128), 1)
     table = size[...]
 
     def step(n):
         return jnp.sum(jnp.where(lane8 == n, table, 0.0)[0:1], axis=1, keepdims=True)
 
-    out_o[...] = feat[...].astype(F32) + home_out[...].astype(F32)
-    gin_o[...] = og[...] + home_in[...].astype(F32)
-    for src, dst in (
-        (gq, gq_o), (gp, gp_o), (g_up, gu_o), (g_down, gd_o), (gn, gn_o), (gh, gh_o), (gx, gx_o),
-        (gt, gt_o), *zip(stats, stats_o),
-    ):
-        dst[...] = src[...]
     rq, kq, *vecs = stats
     scales = update_scales(rq[...], kq[...], *map(wide, vecs), [step(15 + n) for n in range(6)])
-    for n in range(3):
-        new = w_qkv[n] - step(0) * (gq[n] * scales[n])
-        nq_o[n] = new
-        cq_o[n] = new.astype(BF)
-    for n, (master, grad, new_o, low_o) in enumerate(
-        ((w_proj, gp, np_o, cp_o), (w_up, g_up, nu_o, cu_o), (w_down, g_down, nd_o, cd_o))
-    ):
-        new = master[...] - step(1 + n) * (grad[...] * scales[3 + n])
-        new_o[...] = new
-        low_o[...] = new.astype(BF)
+    for n in range(4):
+        fetch[4 + n].wait()
+        store[2 + n].start()
+        fetch[8 + n].wait()
+        new_o, low_o = made[2 + n], made[6 + n]
+        if n == 0:
+            for m in range(3):
+                new = masters[0][m] - step(0) * (grads[0][m] * scales[m])
+                new_o[m] = new
+                low_o[m] = new.astype(BF)
+        else:
+            new = masters[n][...] - step(n) * (grads[n][...] * scales[2 + n])
+            new_o[...] = new
+            low_o[...] = new.astype(BF)
+        store[6 + n].start()
+        store[10 + n].start()
+    for n in (0, 1):
+        fetch[n].wait()
+    made[0][...] = feat[...].astype(F32) + home_out[...].astype(F32)
+    store[0].start()
+    for n in (2, 3):
+        fetch[n].wait()
+    made[1][...] = og[...] + home_in[...].astype(F32)
+    store[1].start()
+    for src, dst in ((gn, gn_o), (gh, gh_o), (gx, gx_o), (gt, gt_o), *zip(stats, stats_o)):
+        dst[...] = src[...]
     sn, un = plain(gn[...], s_norm[...])
     sn_o[...] = sn
     for n in range(6):
@@ -1551,6 +1675,8 @@
     st_o[...] = st
     nt_o[...] = w_table[...] - step(13) * ut
     clip_o[...] = step(14)
+    for copy in store:
+        copy.wait()
 
 
 def whole_step(feat, og, regions, rel_index, masters, stats, states):
@@ -1580,7 +1706,7 @@
         vm((8, 640), F32), vm((24, D), F32),
         vm(tokens, F32), vm(tokens, F32), vm((flat, D), BF), vm((windows, TOK, width), BF),
         vm((windows, TOK, width), BF), vm((windows, TOK, width), BF),
-        vm((windows, heads, TOK, TOK), F32), vm((windows, 4, TOK, width), BF), vm(halves, F32),
+        vm((windows, heads, TOK, TOK), F32), vm((windows // 2, 4, TOK, 2 * width), BF), vm(halves, F32),
         vm((flat, D), BF), vm((flat, hidden), BF), vm((flat, hidden), BF),
         vm(tokens, F32), vm((windows, TOK, 128), F32), vm(halves, BF), vm((D, hidden), F32),
         vm((D, hidden), F32), vm(tokens, F32), vm((flat, D), BF), vm(halves, F32),
@@ -1594,24 +1720,31 @@
         vm((16, 8, 128), F32), vm((16, 8, 128), F32),
         vm(feat.shape, BF), vm(og.shape, F32), *[vm(u.shape, F32) for u in mats],
         vm(halves, BF), vm((windows, ROWS, HALF), BF), dma((windows,)), dma((windows,)), dma((6,)),
-        dma((5,)), dma((5,)),
-        dma((4, 3)), dma((4, 3)), dma((4, 3)), dma((4, 3)), dma((4,)), dma((4,)),
+        dma((2, 5)), dma((2, 5)),
+        vm(feat.shape, BF), vm(feat.shape, BF), *[vm(u.shape, F32) for u in mats], dma((6,)),
+        dma((2, 3)), dma((2, 3)), dma((4, 3)), dma((4, 3)), dma((4,)), dma((4,)),
         dma((2 * images,)), dma((2 * images,)), *[dma((images,))] * 2,
-        dma((windows, 4)), dma((windows, 4)),
+        dma((windows // 2, 5)), dma((windows // 2, 4)),
         dma((3,)), dma((3,)), *[dma((4,))] * 4, *[dma((16,))] * 4,
     ]
-    got = vmem_call(step_body, outs, scratch, "whole_step", 1, 6)(
+    got = vmem_call(step_body, outs, scratch, "whole_step", 1, 6, 6)(
         feat, og, *mats, regions, rel_index, *smalls, *stats, *states
     )
     home_out, home_in, g_qkv, g_proj, g_up, g_down, gn, gh, gx, gt, *rest = got
     new_stats, size = rest[:8], rest[8]
     outs = [
-        like(og), like(og), *map(like, mats), *map(like, smalls), *map(like, masters),
-        *[(u.shape, BF) for u in mats], *map(like, stats), *map(like, smalls), ((1, 1), F32),
+        like(og), like(og), *map(like, mats), *map(like, mats), *[(u.shape, BF) for u in mats],
+        *map(like, smalls), *map(like, smalls), *map(like, stats), *map(like, smalls), ((1, 1), F32),
     ]
-    return vmem_call(finish_body, outs, [], "finish", None)(
-        home_out, feat, home_in, og, g_qkv, g_proj, g_up, g_down, gn, gh, gx, gt,
-        *masters, *states, *new_stats, size,
+    scratch = [
+        vm(feat.shape, BF), vm(feat.shape, BF), vm(feat.shape, BF), vm(og.shape, F32),
+        *[vm(u.shape, F32) for u in mats], *[vm(u.shape, F32) for u in mats],
+        vm(og.shape, F32), vm(og.shape, F32), *[vm(u.shape, F32) for u in mats],
+        *[vm(u.shape, BF) for u in mats], dma((12,)), dma((14,)),
+    ]
+    return vmem_call(finish_body, outs, scratch, "finish", None, 12, 14)(
+        home_out, feat, home_in, og, g_qkv, g_proj, g_up, g_down, *mats, gn, gh, gx, gt,
+        *smalls, *states, *new_stats, size,
     )
 
 
@@ -2022,10 +2155,10 @@
     state_table,
 ):
     flip = lambda u: u.transpose(1, 0, 2)
-    (block_out, grad_input, g_qkv, g_proj, g_up, g_down, g_norm, g_heads, g_hidden, g_table,
-     new_qkv, new_proj, new_up, new_down, new_norm, new_heads, new_hidden, new_table,
-     copy_qkv, copy_proj, copy_up, copy_down, *rest) = whole_step(
-        features, out_grad, regions, rel_index,
+    (block_out, grad_input, g_qkv, g_proj, g_up, g_down, new_qkv, new_proj, new_up, new_down,
+     copy_qkv, copy_proj, copy_up, copy_down, g_norm, g_heads, g_hidden, g_table,
+     new_norm, new_heads, new_hidden, new_table, *rest) = whole_step(
+        features, out_grad, flip(regions), rel_index,
         (w_qkv, w_proj, w_up, w_down.T, norm_vecs, flip(head_bias), hidden_bias.T, rel_table.T),
         (row_qkv, col_qkv, row_proj, col_proj, row_up, col_up, row_down, col_down),
         (state_norm, flip(state_heads), state_hidden.T, state_table.T))

time: 144 us -> 138 us (0.958)
  Pallas kernels: 141 us -> 137 us
    pallas_call x2, Pallas kernels: 141 us -> 137 us  [call(): pl.pallas_call(whole, out_shape=[jax.ShapeDtypeStruct(s, t) for s, t in o...]
where the time goes in v7:
time: 138 us
  Pallas kernels  137 us (99%)
    pallas_call x2, Pallas kernels, call(): pl.pallas_call(whole, out_shape=[jax.ShapeDtypeStruct(s, t) for s, t in o...  137 us

profile of v7, /device:TPU:0, one launch (start us, length us, event | category | flops | bytes accessed | tf_op | source)
XLA Modules:
  0.0 138.0 jit_solution(10504976799246156028)
XLA Ops:
  0.7 128.8 %whole_step.1 = (bf16[2,12,24,768]{3,2,1,0:T(8,128)(2,1)}, bf16[2,12,24,768]{3,2,1,0:T(8,128)(2,1)}, f32[3,192,192]{2,1,0:T(8,128)}, f32[192,192]{1,0:T(8,128)},...) custom-call(bf16[2,12,24,768]{3,2,1,0:T(8,128)(2,1)} %refs_1_.3, ...), custom_call_target="tpu_custom_call" | custom-call | tf_op jit(solution)/shard_map/whole_step/pallas_call | solution.py:560
  129.5 8.4 %finish.1 = (f32[2,12,24,768]{3,2,1,0:T(8,128)}, f32[2,12,24,768]{3,2,1,0:T(8,128)}, f32[3,192,192]{2,1,0:T(8,128)}, f32[192,192]{1,0:T(8,128)}, f32[192,768]{1,...) custom-call(bf16[2,12,24,768]{3,2,1,0:T(8,128)(2,1)} %get-tuple-elem, ...), custom_call_target="tpu_custom_call" | custom-call | tf_op jit(solution)/shard_map/finish/pallas_call | solution.py:560

commit v8 on v7

--- a/solution.py
+++ b/solution.py
@@ -1196,7 +1196,6 @@
         return carry
 
     lax.fori_loop(0, windows, middle, 0)
-    two.cross(windows - 1)
 
     def grad_chunk(m, carry):
         chunk = pl.ds(pl.multiple_of(m * 256, 256), 256)
@@ -1205,11 +1204,12 @@
         gu[chunk, :] = t_dot(n2_s[:, chunk], dpl_s[...])
         return carry
 
-    two.hand(windows - 3)
-    two.settle(windows - 2)
     lax.fori_loop(0, D // 256, grad_chunk, 0)
     down.start()
     up.start()
+    two.hand(windows - 3)
+    two.cross(windows - 1)
+    two.settle(windows - 2)
 
     def backward(w, carry):
         two.arrive(w)
@@ -1259,13 +1259,12 @@
         @pl.when(w == 1)
         def _():
             two.hand(windows - 1)
-
-        @pl.when(w >= 2)
-        def _():
-            four.cross(w - 2)
+            four.cross(0)
 
         @pl.when(w == 2)
         def _():
+            four.settle(0)
+            four.cross(1)
             down.cross()
 
         @pl.when(w == 3)
@@ -1279,7 +1278,8 @@
     for n in range(3):
         gu[:, n * 256 : n * 256 + width] = t_dot(n1[...], dh_s[n])
         qkv[n].start()
-    four.settle(0)
+    four.hand(0)
+    four.settle(1)
     ctx_own = jnp.concatenate(
         [ctx[w // 2, t, :, (w % 2) * width : (w % 2 + 1) * width] for w in range(windows)], axis=0
     )
@@ -1293,14 +1293,12 @@
     table.pair()
     down.share()
     four.cross(2)
-    four.settle(1)
     for member in (*qkv, proj):
         member.pair()
-    four.hand(0)
+    four.hand(1)
     four.cross(3)
+    four.settle(2)
     table.cross()
-    four.hand(1)
-    four.settle(2)
     qkv[0].cross()
 
     keep = 1.0 - DECAY_RATE
@@ -1346,15 +1344,15 @@
             add_rows(n, term)
 
     back(0)
-    mixl.cross(0)
     four.hand(2)
     qkv[1].cross()
+    mixl.cross(0)
     qkv[2].cross()
     back(1)
     four.hand(3)
+    mixl.cross(1)
+    mixl.settle(0)
     proj.cross()
-    mixl.settle(0)
-    mixl.cross(1)
     down.finish()
     up.finish()
     store[4].start()
@@ -1387,13 +1385,12 @@
         return acc
 
     hist = lax.fori_loop(0, 3, bin_row, jnp.zeros((16, 640), F32))
+    mixl.cross(2)
     mixl.settle(1)
-    back(2)
     mixl.trade(0)
     hist = lax.fori_loop(3, 6, bin_row, hist)
     small[16:24, :640] = hist[0:8] + hist[8:16]
-    mixl.cross(2)
-    home_in.go(0)
+    back(2)
     back(3)
     sm_s[0] = small[...]
 
@@ -1402,7 +1399,10 @@
         return remote(sm_s.at[n], sm_r.at[n], sm_send.at[n], sm_recv.at[n], where)
 
     swap(0).start()
+    mixl.cross(3)
+    mixl.settle(2)
     mixl.hand(0)
+    mixl.trade(1)
     for member in (*qkv, proj):
         member.finish()
     store[2].start()
@@ -1436,9 +1436,11 @@
         f_copy(n).start()
     for n in range(1, 16):
         z_copy(n).start()
-    mixl.settle(2)
-    mixl.trade(1)
-    mixl.cross(3)
+    mixl.settle(3)
+    home_in.go(0)
+    home_in.go(1)
+    mixl.hand(1)
+    mixl.trade(2)
     swap(0).wait_recv()
     sm_s[1] = sm_s[0] + sm_r[0]
     swap(1).start()
@@ -1451,10 +1453,6 @@
         for r in range(WIN):
             home_o[i, (SHIFT + r) % WIN] = home_row(dft, row_tmp, i, r)
 
-    mixl.hand(1)
-    mixl.settle(3)
-    home_in.go(1)
-    mixl.trade(2)
     lift(0)
     swap(1).wait_recv()
     sm_s[2] = sm_s[1] + sm_r[1]
@@ -1619,12 +1617,23 @@
     fetch = [
         pltpu.make_async_copy(src, dst, i_sem.at[n]) for n, (src, dst) in enumerate(zip(big_in, held))
     ]
-    for n in (4, 8, 5, 9, 6, 10, 7, 11, 0, 1, 2, 3):
+    for n in (4, 5, 6, 7, 1, 0, 3, 2, 8, 9, 10, 11):
         fetch[n].start()
     sources = [*made[:2], *grads, *made[2:]]
     store = [
         pltpu.make_async_copy(src, dst, o_sem.at[n]) for n, (src, dst) in enumerate(zip(sources, big_out))
     ]
+    for n in range(4):
+        fetch[4 + n].wait()
+        store[2 + n].start()
+    for n in (0, 1):
+        fetch[n].wait()
+    made[0][...] = feat[...].astype(F32) + home_out[...].astype(F32)
+    store[0].start()
+    for n in (2, 3):
+        fetch[n].wait()
+    made[1][...] = og[...] + home_in[...].astype(F32)
+    store[1].start()
     ready()
     lane8 = lax.broadcasted_iota(jnp.int32, (8, 128), 1)
     table = size[...]
@@ -1635,8 +1644,6 @@
     rq, kq, *vecs = stats
     scales = update_scales(rq[...], kq[...], *map(wide, vecs), [step(15 + n) for n in range(6)])
     for n in range(4):
-        fetch[4 + n].wait()
-        store[2 + n].start()
         fetch[8 + n].wait()
         new_o, low_o = made[2 + n], made[6 + n]
         if n == 0:
@@ -1650,14 +1657,6 @@
             low_o[...] = new.astype(BF)
         store[6 + n].start()
         store[10 + n].start()
-    for n in (0, 1):
-        fetch[n].wait()
-    made[0][...] = feat[...].astype(F32) + home_out[...].astype(F32)
-    store[0].start()
-    for n in (2, 3):
-        fetch[n].wait()
-    made[1][...] = og[...] + home_in[...].astype(F32)
-    store[1].start()
     for src, dst in ((gn, gn_o), (gh, gh_o), (gx, gx_o), (gt, gt_o), *zip(stats, stats_o)):
         dst[...] = src[...]
     sn, un = plain(gn[...], s_norm[...])

time: 138 us -> 133 us (0.964)
  Pallas kernels: 137 us -> 132 us
    pallas_call x2, Pallas kernels: 137 us -> 132 us  [call(): pl.pallas_call(whole, out_shape=[jax.ShapeDtypeStruct(s, t) for s, t in o...]
where the time goes in v8:
time: 133 us
  Pallas kernels  132 us (99%)
    pallas_call x2, Pallas kernels, call(): pl.pallas_call(whole, out_shape=[jax.ShapeDtypeStruct(s, t) for s, t in o...  132 us

profile of v8, /device:TPU:0, one launch (start us, length us, event | category | flops | bytes accessed | tf_op | source)
XLA Modules:
  0.0 133.0 jit_solution(9407363294145853101)
XLA Ops:
  0.7 123.7 %whole_step.1 = (bf16[2,12,24,768]{3,2,1,0:T(8,128)(2,1)}, bf16[2,12,24,768]{3,2,1,0:T(8,128)(2,1)}, f32[3,192,192]{2,1,0:T(8,128)}, f32[192,192]{1,0:T(8,128)},...) custom-call(bf16[2,12,24,768]{3,2,1,0:T(8,128)(2,1)} %refs_1_.3, ...), custom_call_target="tpu_custom_call" | custom-call | tf_op jit(solution)/shard_map/whole_step/pallas_call | solution.py:560
  124.4 8.4 %finish.1 = (f32[2,12,24,768]{3,2,1,0:T(8,128)}, f32[2,12,24,768]{3,2,1,0:T(8,128)}, f32[3,192,192]{2,1,0:T(8,128)}, f32[192,192]{1,0:T(8,128)}, f32[192,768]{1,...) custom-call(bf16[2,12,24,768]{3,2,1,0:T(8,128)(2,1)} %get-tuple-elem, ...), custom_call_target="tpu_custom_call" | custom-call | tf_op jit(solution)/shard_map/finish/pallas_call | solution.py:560

commit v9 on v8

--- a/solution.py
+++ b/solution.py
@@ -1403,6 +1403,9 @@
     mixl.settle(2)
     mixl.hand(0)
     mixl.trade(1)
+    swap(0).wait_recv()
+    sm_s[1] = sm_s[0] + sm_r[0]
+    swap(1).start()
     for member in (*qkv, proj):
         member.finish()
     store[2].start()
@@ -1437,13 +1440,13 @@
     for n in range(1, 16):
         z_copy(n).start()
     mixl.settle(3)
+    mixl.hand(1)
+    swap(1).wait_recv()
+    sm_s[2] = sm_s[1] + sm_r[1]
+    swap(2).start()
     home_in.go(0)
     home_in.go(1)
-    mixl.hand(1)
     mixl.trade(2)
-    swap(0).wait_recv()
-    sm_s[1] = sm_s[0] + sm_r[0]
-    swap(1).start()
 
     def lift(w):
         mixl.arrive(w)
@@ -1454,9 +1457,6 @@
             home_o[i, (SHIFT + r) % WIN] = home_row(dft, row_tmp, i, r)
 
     lift(0)
-    swap(1).wait_recv()
-    sm_s[2] = sm_s[1] + sm_r[1]
-    swap(2).start()
     mixl.trade(3)
     mixl.hand(2)
     lift(1)

time: 133 us -> 130 us (0.977)
  Pallas kernels: 132 us -> 129 us
    pallas_call x2, Pallas kernels: 132 us -> 129 us  [call(): pl.pallas_call(whole, out_shape=[jax.ShapeDtypeStruct(s, t) for s, t in o...]
where the time goes in v9:
time: 130 us
  Pallas kernels  129 us (99%)
    pallas_call x2, Pallas kernels, call(): pl.pallas_call(whole, out_shape=[jax.ShapeDtypeStruct(s, t) for s, t in o...  129 us

profile of v9, /device:TPU:0, one launch (start us, length us, event | category | flops | bytes accessed | tf_op | source)
XLA Modules:
  0.0 129.8 jit_solution(13077406171734587878)
XLA Ops:
  0.7 120.5 %whole_step.1 = (bf16[2,12,24,768]{3,2,1,0:T(8,128)(2,1)}, bf16[2,12,24,768]{3,2,1,0:T(8,128)(2,1)}, f32[3,192,192]{2,1,0:T(8,128)}, f32[192,192]{1,0:T(8,128)},...) custom-call(bf16[2,12,24,768]{3,2,1,0:T(8,128)(2,1)} %refs_1_.3, ...), custom_call_target="tpu_custom_call" | custom-call | tf_op jit(solution)/shard_map/whole_step/pallas_call | solution.py:560
  121.2 8.4 %finish.1 = (f32[2,12,24,768]{3,2,1,0:T(8,128)}, f32[2,12,24,768]{3,2,1,0:T(8,128)}, f32[3,192,192]{2,1,0:T(8,128)}, f32[192,192]{1,0:T(8,128)}, f32[192,768]{1,...) custom-call(bf16[2,12,24,768]{3,2,1,0:T(8,128)(2,1)} %get-tuple-elem, ...), custom_call_target="tpu_custom_call" | custom-call | tf_op jit(solution)/shard_map/finish/pallas_call | solution.py:560
